TPU v7x, 32 devices: a whole 2x2x4 slice. The times are simulated.
32 devices in a mesh: rep: 2 (over y), grp: 16 (over z, x, core).
Axes of the slice: x: 2, y: 2, z: 4, core: 2. Of those that a mesh axis runs over, the one named last changes fastest.
Arguments:
- hidden: bfloat16 [2, 3072, 2048], P('rep', 'grp'), may hold values from -6 to 6
- grad_out: bfloat16 [2, 3072, 2048], P('rep', 'grp'), may hold values from -6 to 6
- expert_ids: int32 [2, 3072, 6], P('rep', 'grp'), may hold values from 0 to 15, all different within a row; in each aligned block of 192 rows (0 to 191, 192 to 383, ..., all dimensions but the last counted through in order) at most 90 rows name the same one
- prefix_len: int32 [2], P('rep'), may hold values from 1 to 1536
- adapter_id: int32 [2], P('rep'), may hold values from 0 to 7
- attn_gain: float32 [2048], replicated, may hold values from 0.1 to 1.9
- kv_gain: float32 [512], replicated, may hold values from 0.1 to 1.9
- ffn_gain: float32 [2048], replicated, may hold values from 0.1 to 1.9
- w_q: bfloat16 [2048, 3072], P('grp'), may hold values from -0.125 to 0.125
- w_kva: bfloat16 [2048, 576], P('grp'), may hold values from -0.125 to 0.125
- w_kvb: bfloat16 [512, 4096], P('grp'), may hold values from -0.25 to 0.25
- w_o: bfloat16 [2048, 2048], P('grp'), may hold values from -1 to 1
- w_router: bfloat16 [2048, 16], P('grp'), may hold values from -0.125 to 0.125
- shared_gate: bfloat16 [2048, 2816], P('grp'), may hold values from -0.125 to 0.125
- shared_up: bfloat16 [2048, 2816], P('grp'), may hold values from -0.125 to 0.125
- shared_down: bfloat16 [2816, 2048], P('grp'), may hold values from -0.109375 to 0.109375
- expert_gate: bfloat16 [16, 2048, 1408], P('grp'), may hold values from -0.125 to 0.125
- expert_up_weight: bfloat16 [16, 2048, 1408], P('grp'), may hold values from -0.125 to 0.125
- expert_down: bfloat16 [16, 1408, 2048], P('grp'), may hold values from -0.625 to 0.625
- q_down: bfloat16 [8, 2048, 16], replicated, may hold values from -0.125 to 0.125
- q_up: bfloat16 [8, 16, 3072], replicated, may hold values from -0.59765625 to 0.59765625
- o_down: bfloat16 [8, 2048, 16], replicated, may hold values from -1 to 1
- o_up: bfloat16 [8, 16, 2048], replicated, may hold values from -0.59765625 to 0.59765625
Outputs:
- output: bfloat16 [2, 3072, 2048], P('rep', 'grp')
- grad_hidden: bfloat16 [2, 3072, 2048], P('rep', 'grp')
- grad_q_down: float32 [8, 2048, 16], P(None, 'grp')
- grad_q_up: float32 [8, 16, 3072], P(None, None, 'grp')
- grad_o_down: float32 [8, 2048, 16], P(None, 'grp')
- grad_o_up: float32 [8, 16, 2048], P(None, None, 'grp')
Inputs may be any that keep to these rules, and one draw needn't show every extreme that they name: `expert_ids`: each row names 6 different experts; among the rows of one device no expert is named more than 90 times, and that count is reached.
All inputs are finite; a program needn't handle non-finite values.
Results may differ from a plain program's by a relative error of at most 0.024.
Values may be sent and summed in bfloat16 or wider, within the bound.
A program may use at most 384 MiB of HBM per device.

v0:
```python
import math

import jax
import jax.numpy as jnp
from jax import lax
from jax.sharding import PartitionSpec as P

H = 16
NOPE = 128
ROPE = 64
VD = 128
KVR = 512
TOP = 6


EPS = 1e-06
HIGHEST = lax.Precision.HIGHEST


def product(former, latter):
    return jnp.dot(former, latter, preferred_element_type=jnp.float32)


def product_t(former, latter):
    return lax.dot_general(
        former, latter, (((1,), (1,)), ((), ())), preferred_element_type=jnp.float32
    )


def inner_rows(former, latter):
    return lax.dot_general(
        former, latter, (((0,), (0,)), ((), ())), preferred_element_type=jnp.float32
    )


def root_norm(array_value, gains):
    factor = lax.rsqrt(jnp.mean(array_value * array_value, axis=-1, keepdims=True) + EPS)
    return array_value * factor * gains


def norm_back(array_value, gains, gradient):
    factor = lax.rsqrt(jnp.mean(array_value * array_value, axis=-1, keepdims=True) + EPS)
    weighted = gradient * gains
    return factor * weighted - array_value * (factor * factor * factor) * jnp.mean(
        weighted * array_value, axis=-1, keepdims=True
    )


def gated_slope(array_value):
    logistic = jax.nn.sigmoid(array_value)
    return logistic * (1.0 + array_value * (1.0 - logistic))


def angles(positions, width):
    frequency = 10000.0 ** (-jnp.arange(0, width, 2, dtype=jnp.float32) / width)
    phases = positions.astype(jnp.float32)[:, None] * frequency[None, :]
    return (jnp.cos(phases), jnp.sin(phases))


def rotate(array_value, cosine, sine_part):
    midway = array_value.shape[-1] // 2
    leading = array_value[..., :midway]
    trailing = array_value[..., midway:]
    return jnp.concatenate(
        [leading * cosine - trailing * sine_part, trailing * cosine + leading * sine_part], axis=-1
    )


def unrotate(gradient, cosine, sine_part):
    midway = gradient.shape[-1] // 2
    leading = gradient[..., :midway]
    trailing = gradient[..., midway:]
    return jnp.concatenate(
        [leading * cosine + trailing * sine_part, trailing * cosine - leading * sine_part], axis=-1
    )


def per_device(
    hidden,
    grad_out,
    expert_ids,
    prefix_len,
    adapter_id,
    attn_gain,
    kv_gain,
    ffn_gain,
    w_q,
    w_kva,
    w_kvb,
    w_o,
    w_router,
    shared_gate,
    shared_up,
    shared_down,
    expert_gate,
    expert_up_weight,
    expert_down,
    q_down,
    q_up,
    o_down,
    o_up,
):
    tokens = hidden.shape[1]
    members = lax.axis_size("grp")
    length = tokens * members
    experts = expert_gate.shape[0] * members
    capacity = tokens * TOP * 5 // (4 * experts)
    group_size = math.gcd(H, 4)
    groups = H // group_size
    factor = (NOPE + ROPE) ** (-0.5)
    inputs = hidden[0].astype(jnp.float32)
    cotangent = grad_out[0]
    routes = expert_ids[0]
    prefix = prefix_len[0]
    adapter = adapter_id[0]
    qa_down = lax.dynamic_index_in_dim(q_down, adapter, 0, keepdims=False)
    qa_up = lax.dynamic_index_in_dim(q_up, adapter, 0, keepdims=False)
    oa_down = lax.dynamic_index_in_dim(o_down, adapter, 0, keepdims=False)
    oa_up = lax.dynamic_index_in_dim(o_up, adapter, 0, keepdims=False)
    full_q, full_kva, full_kvb, full_o, full_router, full_sgate, full_sup, full_sdown = (
        lax.all_gather(w_q, "grp", axis=0, tiled=True),
        lax.all_gather(w_kva, "grp", axis=0, tiled=True),
        lax.all_gather(w_kvb, "grp", axis=0, tiled=True),
        lax.all_gather(w_o, "grp", axis=0, tiled=True),
        lax.all_gather(w_router, "grp", axis=0, tiled=True),
        lax.all_gather(shared_gate, "grp", axis=0, tiled=True),
        lax.all_gather(shared_up, "grp", axis=0, tiled=True),
        lax.all_gather(shared_down, "grp", axis=0, tiled=True),
    )
    positions = lax.axis_index("grp") * tokens + jnp.arange(tokens, dtype=jnp.int32)
    cosine, sine_part = angles(positions, ROPE)
    normed = root_norm(inputs, attn_gain).astype(jnp.bfloat16)
    q_small = product(normed, qa_down).astype(jnp.bfloat16)
    query = (product(normed, full_q) + product(q_small, qa_up)).reshape(tokens, H, NOPE + ROPE)
    q_nope = query[:, :, :NOPE].astype(jnp.bfloat16)
    q_rope = rotate(query[:, :, NOPE:], cosine[:, None, :], sine_part[:, None, :]).astype(
        jnp.bfloat16
    )
    latent = product(normed, full_kva)
    compressed = root_norm(latent[:, :KVR], kv_gain).astype(jnp.bfloat16)
    k_rope = rotate(latent[:, KVR:], cosine, sine_part).astype(jnp.bfloat16)
    expanded = (
        product(compressed, full_kvb)
        .astype(jnp.bfloat16)
        .reshape(tokens, H, NOPE + VD)
        .transpose(1, 0, 2)
    )
    all_keys, all_rope = (
        lax.all_gather(expanded, "grp", axis=1, tiled=True),
        lax.all_gather(k_rope, "grp", axis=0, tiled=True),
    )
    key_blocks = all_keys.reshape(groups, group_size, length, NOPE + VD)
    key_index = jnp.arange(length, dtype=jnp.int32)
    allowed = (key_index[None, :] <= positions[:, None]) | (positions[:, None] < prefix) & (
        key_index[None, :] < prefix
    )
    query_nope = q_nope.transpose(1, 0, 2).reshape(groups, group_size, tokens, NOPE)
    query_rope = q_rope.transpose(1, 0, 2).reshape(groups, group_size, tokens, ROPE)

    def scores_of(q_part, rank_portion, k_part):
        dots = jnp.einsum(
            "hid,hjd->hij", q_part, k_part[:, :, :NOPE], preferred_element_type=jnp.float32
        )
        dots = dots + jnp.einsum(
            "hid,jd->hij", rank_portion, all_rope, preferred_element_type=jnp.float32
        )
        return jnp.where(allowed[None], dots * factor, -1e30)

    def attend(blocks):
        q_part, rank_portion, k_part = blocks
        scores = scores_of(q_part, rank_portion, k_part)
        maxima = jnp.max(scores, axis=-1, keepdims=True)
        weights = jnp.exp(scores - maxima)
        totals = jnp.sum(weights, axis=-1, keepdims=True)
        chances = (weights / totals).astype(jnp.bfloat16)
        mixture = jnp.einsum(
            "hij,hjd->hid", chances, k_part[:, :, NOPE:], preferred_element_type=jnp.float32
        )
        return (mixture, maxima, totals)

    mixture, maxima, totals = lax.map(attend, (query_nope, query_rope, key_blocks))
    mixed_low = (
        mixture.reshape(H, tokens, VD)
        .transpose(1, 0, 2)
        .reshape(tokens, H * VD)
        .astype(jnp.bfloat16)
    )
    o_small = product(mixed_low, oa_down).astype(jnp.bfloat16)
    middle = inputs + product(mixed_low, full_o) + product(o_small, oa_up)
    ffn_in = root_norm(middle, ffn_gain).astype(jnp.bfloat16)
    route_probs = jax.nn.softmax(product(ffn_in, full_router), axis=-1)
    gate_weight = jnp.take_along_axis(route_probs, routes, axis=1)
    s_gate = product(ffn_in, full_sgate)
    s_up = product(ffn_in, full_sup)
    s_hidden = (jax.nn.silu(s_gate) * s_up).astype(jnp.bfloat16)
    shared_out = product(s_hidden, full_sdown)
    pair_count = tokens * TOP
    flattened_identities = routes.reshape(pair_count)
    onehot = (
        flattened_identities[:, None] == jnp.arange(experts, dtype=jnp.int32)[None, :]
    ).astype(jnp.int32)
    ranks = jnp.sum(
        (jnp.cumsum(onehot, axis=0, dtype=jnp.int32) - 1) * onehot, axis=1, dtype=jnp.int32
    )
    slots = ranks * experts + flattened_identities
    source = (
        jnp.full((capacity * experts,), pair_count, jnp.int32)
        .at[slots]
        .set(jnp.arange(pair_count, dtype=jnp.int32))
    )
    width = ffn_in.shape[1]
    padded = jnp.concatenate([ffn_in, jnp.zeros((1, width), jnp.bfloat16)], axis=0)
    outgoing = padded[source // TOP].reshape(capacity, experts, width)
    received = lax.all_to_all(outgoing, "grp", split_axis=1, concat_axis=0, tiled=True)
    expert_gate_rows = jnp.einsum(
        "rxd,xdf->rxf", received, expert_gate, preferred_element_type=jnp.float32
    )
    e_up = jnp.einsum(
        "rxd,xdf->rxf", received, expert_up_weight, preferred_element_type=jnp.float32
    )
    e_hidden = (jax.nn.silu(expert_gate_rows) * e_up).astype(jnp.bfloat16)
    e_out = jnp.einsum(
        "rxf,xfd->rxd", e_hidden, expert_down, preferred_element_type=jnp.float32
    ).astype(jnp.bfloat16)
    returned = lax.all_to_all(e_out, "grp", split_axis=0, concat_axis=1, tiled=True)
    picked = returned.reshape(capacity * experts, width)[slots].reshape(tokens, TOP, width)
    routed = jnp.sum(gate_weight[:, :, None] * picked.astype(jnp.float32), axis=1)
    output = (middle + shared_out + routed).astype(jnp.bfloat16)
    top_choice_gradient = cotangent.astype(jnp.float32)
    d_gate = jnp.sum(top_choice_gradient[:, None, :] * picked.astype(jnp.float32), axis=2)
    d_pairs = (
        (gate_weight[:, :, None] * top_choice_gradient[:, None, :])
        .astype(jnp.bfloat16)
        .reshape(pair_count, width)
    )
    d_padded = jnp.concatenate([d_pairs, jnp.zeros((1, width), jnp.bfloat16)], axis=0)
    d_outgoing = d_padded[source].reshape(capacity, experts, width)
    d_received = lax.all_to_all(d_outgoing, "grp", split_axis=1, concat_axis=0, tiled=True)
    expert_hidden_gradient = jnp.einsum(
        "rxd,xfd->rxf", d_received, expert_down, preferred_element_type=jnp.float32
    )
    d_egate = (expert_hidden_gradient * e_up * gated_slope(expert_gate_rows)).astype(jnp.bfloat16)
    expert_up_gradient = (expert_hidden_gradient * jax.nn.silu(expert_gate_rows)).astype(
        jnp.bfloat16
    )
    d_rows = (
        jnp.einsum("ktj,tzj->ktz", d_egate, expert_gate, preferred_element_type=jnp.float32)
        + jnp.einsum(
            "ktj,tzj->ktz", expert_up_gradient, expert_up_weight, preferred_element_type=jnp.float32
        )
    ).astype(jnp.bfloat16)
    d_returned = lax.all_to_all(d_rows, "grp", split_axis=0, concat_axis=1, tiled=True)
    d_routed = jnp.sum(
        d_returned.reshape(capacity * experts, width)[slots]
        .reshape(tokens, TOP, width)
        .astype(jnp.float32),
        axis=1,
    )
    expert_match = (
        routes[:, :, None] == jnp.arange(experts, dtype=jnp.int32)[None, None, :]
    ).astype(jnp.float32)
    d_route = jnp.sum(d_gate[:, :, None] * expert_match, axis=1)
    d_logits = (
        route_probs * (d_route - jnp.sum(route_probs * d_route, axis=-1, keepdims=True))
    ).astype(jnp.bfloat16)
    d_shidden = product_t(cotangent, full_sdown)
    d_sgate = (d_shidden * s_up * gated_slope(s_gate)).astype(jnp.bfloat16)
    d_sup = (d_shidden * jax.nn.silu(s_gate)).astype(jnp.bfloat16)
    d_ffn = (
        d_routed
        + product_t(d_logits, full_router)
        + product_t(d_sgate, full_sgate)
        + product_t(d_sup, full_sup)
    )
    d_middle = top_choice_gradient + norm_back(middle, ffn_gain, d_ffn)
    d_attn = d_middle.astype(jnp.bfloat16)
    grad_oup = inner_rows(o_small, d_attn)
    d_osmall = product_t(d_attn, oa_up).astype(jnp.bfloat16)
    grad_odown = inner_rows(mixed_low, d_osmall)
    d_mixed = (product_t(d_attn, full_o) + product_t(d_osmall, oa_down)).astype(jnp.bfloat16)
    d_mixture = (
        d_mixed.reshape(tokens, H, VD).transpose(1, 0, 2).reshape(groups, group_size, tokens, VD)
    )

    def attend_back(blocks):
        q_part, rank_portion, k_part, d_part, maxima_part, totals_part = blocks
        scores = scores_of(q_part, rank_portion, k_part)
        chances = jnp.exp(scores - maxima_part) / totals_part
        d_chances = jnp.einsum(
            "hid,hjd->hij", d_part, k_part[:, :, NOPE:], preferred_element_type=jnp.float32
        )
        d_scores = (
            chances * (d_chances - jnp.sum(chances * d_chances, axis=-1, keepdims=True))
        ).astype(jnp.bfloat16)
        d_qnope = (
            jnp.einsum(
                "hij,hjd->hid", d_scores, k_part[:, :, :NOPE], preferred_element_type=jnp.float32
            )
            * factor
        )
        d_qrope = (
            jnp.einsum("hij,jd->hid", d_scores, all_rope, preferred_element_type=jnp.float32)
            * factor
        )
        d_knope = (
            jnp.einsum("hij,hid->hjd", d_scores, q_part, preferred_element_type=jnp.float32)
            * factor
        )
        d_values = jnp.einsum(
            "hij,hid->hjd", chances.astype(jnp.bfloat16), d_part, preferred_element_type=jnp.float32
        )
        d_krope = (
            jnp.einsum("hij,hid->jd", d_scores, rank_portion, preferred_element_type=jnp.float32)
            * factor
        )
        return (d_qnope, d_qrope, jnp.concatenate([d_knope, d_values], axis=-1), d_krope)

    d_qnope, d_qrope, d_keys, d_krope = lax.map(
        attend_back, (query_nope, query_rope, key_blocks, d_mixture, maxima, totals)
    )
    expansion = full_kvb.astype(jnp.float32).reshape(KVR, H, NOPE + VD).transpose(1, 2, 0)
    own_keys, own_rope = (
        lax.psum_scatter(
            d_keys.reshape(H, length, NOPE + VD).astype(jnp.bfloat16),
            "grp",
            scatter_dimension=1,
            tiled=True,
        ).astype(jnp.float32),
        lax.psum_scatter(
            jnp.sum(d_krope, axis=0).astype(jnp.bfloat16), "grp", scatter_dimension=0, tiled=True
        ).astype(jnp.float32),
    )
    d_compressed = jnp.einsum(
        "hjc,hcr->jr", own_keys, expansion, precision=HIGHEST, preferred_element_type=jnp.float32
    )
    d_latent = jnp.concatenate(
        [norm_back(latent[:, :KVR], kv_gain, d_compressed), unrotate(own_rope, cosine, sine_part)],
        axis=-1,
    ).astype(jnp.bfloat16)
    d_qrope_rows = d_qrope.reshape(H, tokens, ROPE).transpose(1, 0, 2)
    d_qnope_rows = d_qnope.reshape(H, tokens, NOPE).transpose(1, 0, 2)
    d_query = (
        jnp.concatenate(
            [d_qnope_rows, unrotate(d_qrope_rows, cosine[:, None, :], sine_part[:, None, :])],
            axis=-1,
        )
        .reshape(tokens, H * (NOPE + ROPE))
        .astype(jnp.bfloat16)
    )
    grad_qup = inner_rows(q_small, d_query)
    d_qsmall = product_t(d_query, qa_up).astype(jnp.bfloat16)
    grad_qdown = inner_rows(normed, d_qsmall)
    d_normed = (
        product_t(d_query, full_q) + product_t(d_qsmall, qa_down) + product_t(d_latent, full_kva)
    )
    grad_inputs = (d_middle + norm_back(inputs, attn_gain, d_normed)).astype(jnp.bfloat16)
    selector = (jnp.arange(q_down.shape[0], dtype=jnp.int32) == adapter).astype(jnp.float32)[
        :, None, None
    ]
    term_qdown = selector * grad_qdown[None]
    term_qup = selector * grad_qup[None]
    term_odown = selector * grad_odown[None]
    term_oup = selector * grad_oup[None]
    shares = (
        lax.psum_scatter(
            term_qdown.astype(jnp.bfloat16), "grp", scatter_dimension=1, tiled=True
        ).astype(jnp.float32),
        lax.psum_scatter(
            term_qup.astype(jnp.bfloat16), "grp", scatter_dimension=2, tiled=True
        ).astype(jnp.float32),
        lax.psum_scatter(
            term_odown.astype(jnp.bfloat16), "grp", scatter_dimension=1, tiled=True
        ).astype(jnp.float32),
        lax.psum_scatter(
            term_oup.astype(jnp.bfloat16), "grp", scatter_dimension=2, tiled=True
        ).astype(jnp.float32),
    )
    summed = (
        lax.psum(shares[0].astype(jnp.bfloat16), "rep").astype(jnp.float32),
        lax.psum(shares[1].astype(jnp.bfloat16), "rep").astype(jnp.float32),
        lax.psum(shares[2].astype(jnp.bfloat16), "rep").astype(jnp.float32),
        lax.psum(shares[3].astype(jnp.bfloat16), "rep").astype(jnp.float32),
    )
    return (output[None], grad_inputs[None], summed[0], summed[1], summed[2], summed[3])


def solution(mesh):
    in_specs = (
        P("rep", "grp", None),
        P("rep", "grp", None),
        P("rep", "grp", None),
        P("rep"),
        P("rep"),
        P(),
        P(),
        P(),
        P("grp", None),
        P("grp", None),
        P("grp", None),
        P("grp", None),
        P("grp", None),
        P("grp", None),
        P("grp", None),
        P("grp", None),
        P("grp", None, None),
        P("grp", None, None),
        P("grp", None, None),
        P(),
        P(),
        P(),
        P(),
    )
    out_specs = (
        P("rep", "grp", None),
        P("rep", "grp", None),
        P(None, "grp", None),
        P(None, None, "grp"),
        P(None, "grp", None),
        P(None, None, "grp"),
    )
    return jax.shard_map(
        per_device, mesh=mesh, in_specs=in_specs, out_specs=out_specs, check_vma=False
    )
```

profile of v0, /device:TPU:0, one launch (start us, length us, event | category | flops | bytes accessed | tf_op | source)
XLA Modules:
  0.0 2312.4 jit_solution(11316234938025665880)
XLA Ops:
  11.4 43.5 %all-gather.12.cloned.1.call-done = bf16[2048,576]{0,1:T(8,128)(2,1)} async-done(((bf16[128,576]{0,1:T(8,128)(2,1)}), bf16[2048,576]{0,1:T(8,128)(2,1)}) %all-gather.12.cloned.1.call-update) | async-done | bytes 2359312 | tf_op jit(solution)/shard_map/all_gather | solution.py:122
  58.7 47.7 %all-gather.14.cloned.1.call-done = bf16[512,4096]{1,0:T(8,128)(2,1)} async-done(((bf16[32,4096]{1,0:T(8,128)(2,1)}), bf16[512,4096]{1,0:T(8,128)(2,1)}) %all-gather.14.cloned.1.call-update) | async-done | bytes 4194320 | tf_op jit(solution)/shard_map/all_gather | solution.py:123
  132.2 22.5 all-gather
  155.5 53.9 %all-gather.10.cloned.1.call-done = bf16[2048,3072]{1,0:T(8,128)(2,1)} async-done(((bf16[128,3072]{1,0:T(8,128)(2,1)}), bf16[2048,3072]{1,0:T(8,128)(2,1)}) %all-gather.10.cloned.1.call-update) | async-done | bytes 12582928 | tf_op jit(solution)/shard_map/all_gather | solution.py:121
  224.1 113.6 %all-gather.16.cloned.1.call-done = bf16[16,3072,256]{2,0,1:T(8,128)(2,1)} async-done(((bf16[16,192,256]{2,0,1:T(8,128)(2,1)}), bf16[16,3072,256]{2,0,1:T(8,128)(2,1)}) %all-gather.16.cloned.1.call-update) | async-done | bytes 25165840 | tf_op jit(solution)/shard_map/all_gather | solution.py:149
  337.7 23.2 %copy.233 = bf16[16,3072,256]{2,1,0:T(8,128)(2,1)} copy(bf16[16,3072,256]{2,0,1:T(8,128)(2,1)} %all-gather.16.cloned.1.call-done) | data formatting | bytes 50331648
  361.9 51.4 %while.32 = (s32[]{:T(128)}, bf16[4,4,192,128]{3,2,1,0:T(8,128)(2,1)}, f32[4,4,192,1]{2,1,3,0:T(4,128)}, f32[4,4,192,1]{2,1,3,0:T(4,128)}, bf16[4,4,192,128]{3,2...) while((s32[]{:T(128)}, ...), condition=%wide.region_5.6_spmd.clone, body=%wide.region_2.5_spmd.clone.sunk | while | flops 1532951040 | bytes 74681480 | solution.py:181
  454.6 10.9 mul.554
  465.6 145.6 %all_gather.39 = bf16[2048,16]{0,1:T(8,128)(2,1)S(1)} all-gather(bf16[128,16]{0,1:T(8,128)(2,1)S(1)} %copy-done.93), channel_id=1, replica_groups=mesh['rep'=2,'grp'=16] {'grp'}, dimensions={0}, use_global_device_ids=true | all-gather | bytes 69632 | tf_op jit(solution)/shard_map/all_gather | solution.py:125
  612.4 9.3 gather_fusion.4
  628.7 15.6 gather_fusion.2
  652.9 68.1 %all-to-all-start.2 = ((bf16[90,16,2048]{2,0,1:T(8,128)(2,1)}), bf16[90,16,2048]{2,0,1:T(8,128)(2,1)}, u32[]{:S(2)}, u32[]{:S(2)}) async-start(bf16[90,16,2048]{2,0,1:T(8,128)(2,1)} %copy.209), calls=%async_computation.2 | async-start | bytes 12582912 | tf_op jit(solution)/shard_map/all_to_all | solution.py:238
  728.5 15.0 convolution_bitcast_fusion.2
  743.6 11.4 convolution_bitcast_fusion.3
  755.0 14.7 fusion.68
  779.5 10.3 reshape.501
  789.8 114.8 %all-to-all-done.2 = bf16[90,16,2048]{2,0,1:T(8,128)(2,1)} async-done(((bf16[90,16,2048]{2,0,1:T(8,128)(2,1)}), bf16[90,16,2048]{2,0,1:T(8,128)(2,1)}, u32[]{:S(2)}, u32[]{:S(2)}) %all-to-all-start.2) | async-done | bytes 5898272 | tf_op jit(solution)/shard_map/all_to_all | solution.py:238
  904.5 28.3 %all-to-all-start.1 = ((bf16[16,2,92160]{2,1,0:T(2,128)(2,1)}), bf16[16,2,92160]{2,1,0:T(2,128)(2,1)}, u32[]{:S(2)}, u32[]{:S(2)}) async-start(bf16[16,2,92160]{2,1,0:T(2,128)(2,1)} %reshape.501), calls=%async_computation.1 | async-start | bytes 11796480 | tf_op jit(solution)/shard_map/all_to_all | solution.py:225
  939.2 15.1 convolution_bitcast_fusion.1
  954.3 21.7 fusion.74
  976.0 20.0 fusion.69
  1005.1 10.3 reshape.503
  1015.5 24.6 %all-to-all-done.1 = bf16[16,2,92160]{2,1,0:T(2,128)(2,1)} async-done(((bf16[16,2,92160]{2,1,0:T(2,128)(2,1)}), bf16[16,2,92160]{2,1,0:T(2,128)(2,1)}, u32[]{:S(2)}, u32[]{:S(2)}) %all-to-all-start.1) | async-done | bytes 5898272 | tf_op jit(solution)/shard_map/all_to_all | solution.py:225
  1040.1 26.5 %all-to-all-start.3 = ((bf16[16,2,92160]{2,1,0:T(2,128)(2,1)}), bf16[16,2,92160]{2,1,0:T(2,128)(2,1)}, u32[]{:S(2)}, u32[]{:S(2)}) async-start(bf16[16,2,92160]{2,1,0:T(2,128)(2,1)} %reshape.503), calls=%async_computation.3 | async-start | bytes 11796480 | tf_op jit(solution)/shard_map/all_to_all | solution.py:252
  1067.3 9.6 fusion.121
  1092.0 10.1 fusion.111
  1111.3 14.2 reshape.502
  1125.4 126.3 %reduce.6 = bf16[1440,2048]{1,0:T(8,128)(2,1)} reduce(bf16[1440,1,2048]{2,1,0:T(2,128)(2,1)} %reshape.502, bf16[]{:T(256)} %constant.186), dimensions={1}, to_apply=%all_to_all.47.reduce_sub_computation | reduce | bytes 11796482 | tf_op jit(solution)/shard_map/all_to_all | solution.py:225
  1266.6 14.3 gather_fusion.1
  1290.1 14.0 reshape.504
  1304.1 126.2 %reduce.7 = bf16[1440,2048]{1,0:T(8,128)(2,1)} reduce(bf16[1440,1,2048]{2,1,0:T(2,128)(2,1)} %reshape.504, bf16[]{:T(256)} %constant.186), dimensions={1}, to_apply=%all_to_all.53.reduce_sub_computation | reduce | bytes 11796482 | tf_op jit(solution)/shard_map/all_to_all | solution.py:252
  1445.6 14.1 gather_fusion.3
  1459.6 9.3 reshape.429
  1468.9 9.9 multiply_reduce_fusion.1
  1479.0 9.8 reduce_sum.162
  1500.9 208.8 %while.33 = (s32[]{:T(128)}, bf16[4,4,192,128]{3,2,1,0:T(8,128)(2,1)}, f32[4,4,192,64]{2,3,1,0:T(8,128)}, bf16[4,4,3072,256]{2,3,1,0:T(8,128)(2,1)}, f32[4,3072,...) while((s32[]{:T(128)}, ...), condition=%wide.region_21.22_spmd.clone, body=%wide.region_19.21_spmd.clone.sunk | while | flops 3969662208 | bytes 232567952 | solution.py:318
  1522.4 11.0 multiply_convert_fusion.22
  1574.5 11.0 multiply_convert_fusion.22
  1626.6 11.0 multiply_convert_fusion.22
  1678.6 11.0 multiply_convert_fusion.22
  1777.1 11.5 reduce-scatter.21.cloned.1.call-done
  1792.0 55.2 %reduce-scatter.25.cloned.1.call-done = bf16[128,128]{1,0:T(8,128)(2,1)} async-done(((bf16[2048,128]{1,0:T(8,128)(2,1)}), bf16[128,128]{1,0:T(8,128)(2,1)}) %reduce-scatter.25.cloned.1.call-update) | async-done | bytes 32784
  1850.6 55.4 %reduce-scatter.27.cloned.1.call-done = bf16[128,128]{1,0:T(8,128)(2,1)} async-done(((bf16[2048,128]{1,0:T(8,128)(2,1)}), bf16[128,128]{1,0:T(8,128)(2,1)}) %reduce-scatter.27.cloned.1.call-update) | async-done | bytes 32784
  1909.4 56.4 %reduce-scatter.23.cloned.1.call-done = bf16[192,128]{1,0:T(8,128)(2,1)} async-done(((bf16[3072,128]{1,0:T(8,128)(2,1)}), bf16[192,128]{1,0:T(8,128)(2,1)}) %reduce-scatter.23.cloned.1.call-update) | async-done | bytes 49168
  1969.6 32.7 %copy.218 = bf16[16,3072,256]{2,1,0:T(8,128)(2,1)} copy(bf16[16,3072,256]{1,2,0:T(8,128)(2,1)} %bitcast.397) | data formatting | bytes 50331648 | tf_op jit(solution)/shard_map/convert_element_type | solution.py:324
  2008.8 10.2 fusion.216
  2028.5 21.3 all-reduce.5.cloned.1.call-done
  2055.5 241.8 %reduce-scatter.17.cloned.1.call-done = bf16[16,192,256]{2,1,0:T(8,128)(2,1)} async-done(((bf16[16,3072,256]{2,1,0:T(8,128)(2,1)}), bf16[16,192,256]{2,1,0:T(8,128)(2,1)}) %reduce-scatter.17.cloned.1.call-update) | async-done | bytes 1572880 | tf_op jit(solution)/shard_map/reduce_scatter | solution.py:323
  (545 shorter events, 540.5 us)
Async XLA Ops:
  7.2 208.3 %copy-start = (bf16[8,16,3072]{2,1,0:T(8,128)(2,1)S(1)}, bf16[8,16,3072]{2,1,0:T(8,128)(2,1)}, u32[]{:S(2)}) copy-start(bf16[8,16,3072]{2,1,0:T(8,128)(2,1)} %param.47) | copy-start | bytes 2359300
  7.2 99.2 %copy-start.81 = (f32[512]{0:T(512)S(1)}, f32[512]{0:T(512)}, u32[]{:S(2)}) copy-start(f32[512]{0:T(512)} %param.33) | copy-start | bytes 6148
  7.2 47.8 %all-gather.12.cloned.1.call-start = ((), (), s32[]{:S(2)}) async-start(), calls=%async_computation.11 | async-start | bytes 2506752 | tf_op jit(solution)/shard_map/all_gather | solution.py:122
  7.9 98.5 %all-gather.14.cloned.1.call-start = ((), (), s32[]{:S(2)}) async-start(), calls=%async_computation.12 | async-start | bytes 4456448 | tf_op jit(solution)/shard_map/all_gather | solution.py:123
  8.7 200.7 %all-gather.10.cloned.1.call-start = ((), (), s32[]{:S(2)}) async-start(), calls=%async_computation.10 | async-start | bytes 13369344 | tf_op jit(solution)/shard_map/all_gather | solution.py:121
  9.4 328.3 %all-gather.16.cloned.1.call-start = ((), (), s32[]{:S(2)}) async-start(), calls=%async_computation.13 | async-start | bytes 26738688 | tf_op jit(solution)/shard_map/all_gather | solution.py:149
  11.4 198.0 %copy-start.90 = (f32[192]{0:T(256)}, f32[192]{0:T(256)S(1)}, u32[]{:S(2)}) copy-start(f32[192]{0:T(256)S(1)} %get-tuple-element.483) | copy-start | bytes 2308
  57.9 72.3 %copy-start.26 = (f32[192,576]{1,0:T(8,128)}, f32[192,576]{1,0:T(8,128)S(1)}, u32[]{:S(2)}) copy-start(f32[192,576]{1,0:T(8,128)S(1)} %fusion.207) | copy-start | bytes 1327108
  58.7 52.7 %copy-start.75 = (f32[192]{0:T(256)}, f32[192]{0:T(256)S(1)}, u32[]{:S(2)}) copy-start(f32[192]{0:T(256)S(1)} %get-tuple-element.485) | copy-start | bytes 2308
  109.6 18.1 copy-start.19
  109.6 18.1 copy-start.83
  111.4 306.3 %all-gather.18.cloned.1.call-start = ((), (), s32[]{:S(2)}) async-start(), calls=%async_computation.14 | async-start | bytes 8912896 | tf_op jit(solution)/shard_map/all_gather | solution.py:124
  112.0 955.3 %all-gather.24.cloned.1.call-start = ((), (), s32[]{:S(2)}) async-start(), calls=%async_computation.17 | async-start | bytes 12255232 | tf_op jit(solution)/shard_map/all_gather | solution.py:128
  112.6 964.5 %all-gather.22.cloned.1.call-start = ((), (), s32[]{:S(2)}) async-start(), calls=%async_computation.16 | async-start | bytes 12255232 | tf_op jit(solution)/shard_map/all_gather | solution.py:127
  113.4 18.8 copy-start.95
  113.4 18.8 copy-start.87
  113.5 41.1 %copy-start.36 = (s32[1,192,6]{2,1,0:T(8,128)}, s32[1,192,6]{2,1,0:T(8,128)S(1)}, u32[]{:S(2)}) copy-start(s32[1,192,6]{2,1,0:T(8,128)S(1)} %copy.201) | copy-start | bytes 13828
  114.0 16.4 copy-start.55
  361.9 55.8 %copy-start.20 = (bf16[1,192,2048]{2,1,0:T(8,128)(2,1)S(1)}, bf16[1,192,2048]{2,1,0:T(8,128)(2,1)}, u32[]{:S(2)}) copy-start(bf16[1,192,2048]{2,1,0:T(8,128)(2,1)} %param.27) | copy-start | bytes 2359300
  426.0 185.2 %copy-start.23 = (bf16[192,2048]{1,0:T(8,128)(2,1)}, bf16[192,2048]{1,0:T(8,128)(2,1)S(1)}, u32[]{:S(2)}) copy-start(bf16[192,2048]{1,0:T(8,128)(2,1)S(1)} %multiply_convert_fusion.10) | copy-start | bytes 2359300
  441.9 211.0 %all-to-all-start = ((bf16[90,16,2048]{2,0,1:T(8,128)(2,1)}), bf16[90,16,2048]{2,0,1:T(8,128)(2,1)}, u32[]{:S(2)}, u32[]{:S(2)}) async-start(bf16[90,16,2048]{2,0,1:T(8,128)(2,1)} %copy.206), calls=%async_computation | async-start | bytes 12582912 | tf_op jit(solution)/shard_map/all_to_all | solution.py:214
  652.9 251.7 %all-to-all-start.2 = ((bf16[90,16,2048]{2,0,1:T(8,128)(2,1)}), bf16[90,16,2048]{2,0,1:T(8,128)(2,1)}, u32[]{:S(2)}, u32[]{:S(2)}) async-start(bf16[90,16,2048]{2,0,1:T(8,128)(2,1)} %copy.209), calls=%async_computation.2 | async-start | bytes 12582912 | tf_op jit(solution)/shard_map/all_to_all | solution.py:238
  721.0 364.2 %all-gather.20.cloned.1.call-start = ((), (), s32[]{:S(2)}) async-start(), calls=%async_computation.15 | async-start | bytes 12255232 | tf_op jit(solution)/shard_map/all_gather | solution.py:126
  721.7 21.8 slice-start.4
  728.5 15.0 copy-start.28
  728.5 15.0 slice-start.5
  728.5 26.5 %slice-start.2 = ((s8[5767168]{0:T(1024)(128)(4,1)}), s8[4194304]{0:T(1024)(128)(4,1)S(1)}, s32[]{:S(2)}) async-start(s8[5767168]{0:T(1024)(128)(4,1)} %bitcast.430), calls=%async_computation.27 | async-start | bytes 8388608
  904.5 135.5 %all-to-all-start.1 = ((bf16[16,2,92160]{2,1,0:T(2,128)(2,1)}), bf16[16,2,92160]{2,1,0:T(2,128)(2,1)}, u32[]{:S(2)}, u32[]{:S(2)}) async-start(bf16[16,2,92160]{2,1,0:T(2,128)(2,1)} %reshape.501), calls=%async_computation.1 | async-start | bytes 11796480 | tf_op jit(solution)/shard_map/all_to_all | solution.py:225
  1015.5 51.2 %copy-start.59 = (s32[1,192,6]{1,0,2:T(1,128)S(1)}, s32[1,192,6]{1,0,2:T(1,128)}, u32[]{:S(2)}) copy-start(s32[1,192,6]{1,0,2:T(1,128)} %param.29) | copy-start | bytes 13828
  1015.5 51.8 %copy-start.68 = (s32[1152]{0:T(1024)S(1)}, s32[1152]{0:T(1024)}, u32[]{:S(2)}) copy-start(s32[1152]{0:T(1024)} %copy-done.67) | copy-start | bytes 13828
  1015.5 51.8 %copy-start.35 = (bf16[1,192,2048]{2,1,0:T(8,128)(2,1)S(1)}, bf16[1,192,2048]{2,1,0:T(8,128)(2,1)}, u32[]{:S(2)}) copy-start(bf16[1,192,2048]{2,1,0:T(8,128)(2,1)} %param.28) | copy-start | bytes 2359300
  1040.1 250.0 %all-to-all-start.3 = ((bf16[16,2,92160]{2,1,0:T(2,128)(2,1)}), bf16[16,2,92160]{2,1,0:T(2,128)(2,1)}, u32[]{:S(2)}, u32[]{:S(2)}) async-start(bf16[16,2,92160]{2,1,0:T(2,128)(2,1)} %reshape.503), calls=%async_computation.3 | async-start | bytes 11796480 | tf_op jit(solution)/shard_map/all_to_all | solution.py:252
  1066.6 722.0 %reduce-scatter.21.cloned.1.call-start = ((), (), s32[]{:S(2)}) async-start(), calls=%async_computation.20 | async-start | bytes 557056
  1500.9 211.0 %copy-start.43 = (f32[192,32]{1,0:T(8,128)S(1)}, f32[192,32]{1,0:T(8,128)}, u32[]{:S(2)}) copy-start(f32[192,32]{1,0:T(8,128)} %copy.194) | copy-start | bytes 73732
  1501.1 40.2 %copy-start.17 = (bf16[4,4,192,128]{3,2,1,0:T(8,128)(2,1)}, bf16[4,4,192,128]{3,2,1,0:T(8,128)(2,1)S(1)}, u32[]{:S(2)}) copy-start(bf16[4,4,192,128]{3,2,1,0:T(8,128)(2,1)S(1)} %get-tuple-element.755) | copy-start | bytes 2359300 | tf_op jit(solution)/shard_map/while
  1553.1 40.2 %copy-start.17 = (bf16[4,4,192,128]{3,2,1,0:T(8,128)(2,1)}, bf16[4,4,192,128]{3,2,1,0:T(8,128)(2,1)S(1)}, u32[]{:S(2)}) copy-start(bf16[4,4,192,128]{3,2,1,0:T(8,128)(2,1)S(1)} %get-tuple-element.755) | copy-start | bytes 2359300 | tf_op jit(solution)/shard_map/while
  1605.2 40.2 %copy-start.17 = (bf16[4,4,192,128]{3,2,1,0:T(8,128)(2,1)}, bf16[4,4,192,128]{3,2,1,0:T(8,128)(2,1)S(1)}, u32[]{:S(2)}) copy-start(bf16[4,4,192,128]{3,2,1,0:T(8,128)(2,1)S(1)} %get-tuple-element.755) | copy-start | bytes 2359300 | tf_op jit(solution)/shard_map/while
  1657.2 40.3 %copy-start.17 = (bf16[4,4,192,128]{3,2,1,0:T(8,128)(2,1)}, bf16[4,4,192,128]{3,2,1,0:T(8,128)(2,1)S(1)}, u32[]{:S(2)}) copy-start(bf16[4,4,192,128]{3,2,1,0:T(8,128)(2,1)S(1)} %get-tuple-element.755) | copy-start | bytes 2359300 | tf_op jit(solution)/shard_map/while
  1731.1 116.2 %reduce-scatter.25.cloned.1.call-start = ((), (), s32[]{:S(2)}) async-start(), calls=%async_computation.22 | async-start | bytes 557056
  1742.4 163.6 %reduce-scatter.27.cloned.1.call-start = ((), (), s32[]{:S(2)}) async-start(), calls=%async_computation.23 | async-start | bytes 557056
  1755.4 210.4 %reduce-scatter.23.cloned.1.call-start = ((), (), s32[]{:S(2)}) async-start(), calls=%async_computation.21 | async-start | bytes 835584
  1771.7 255.4 %reduce-scatter.19.cloned.1.call-start = ((), (), s32[]{:S(2)}) async-start(), calls=%async_computation.19 | async-start | bytes 835584
  1776.9 272.9 %all-reduce.5.cloned.1.call-start = ((), (), s32[]{:S(2)}) async-start(), calls=%async_computation.24 | async-start | bytes 327680 | tf_op jit(solution)/shard_map/psum | solution.py:379
  1969.5 327.8 %reduce-scatter.17.cloned.1.call-start = ((), (), s32[]{:S(2)}) async-start(), calls=%async_computation.18 | async-start | bytes 26738688 | tf_op jit(solution)/shard_map/reduce_scatter | solution.py:323
  2019.1 278.3 %copy-start.27 = (f32[192,576]{1,0:T(8,128)S(1)}, f32[192,576]{1,0:T(8,128)}, u32[]{:S(2)}) copy-start(f32[192,576]{1,0:T(8,128)} %copy-done.26) | copy-start | bytes 1327108
  2019.1 278.2 %copy-start.82 = (f32[512]{0:T(512)S(1)}, f32[512]{0:T(512)}, u32[]{:S(2)}) copy-start(f32[512]{0:T(512)} %param.33) | copy-start | bytes 6148
  2027.1 274.2 %copy-start.76 = (f32[192]{0:T(256)S(1)}, f32[192]{0:T(256)}, u32[]{:S(2)}) copy-start(f32[192]{0:T(256)} %copy-done.75) | copy-start | bytes 2308
  2027.1 274.2 %copy-start.92 = (f32[192]{0:T(256)S(1)}, f32[192]{0:T(256)}, u32[]{:S(2)}) copy-start(f32[192]{0:T(256)} %get-tuple-element.484) | copy-start | bytes 2308
  (109 other events, 605.5 us)
Sparse Core Ops, SparseCore 0:
  10.2 44.7 all-gather.11
  57.1 49.2 all-gather.13
  108.7 100.7 all-gather.9
  210.9 126.7 all-gather.15
  339.7 74.2 all-gather.17
  416.1 174.6 all-gather.23
  593.1 112.2 all-gather.21
  724.1 177.0 all-gather.19
  1731.2 57.4 reduce-scatter.20
  1792.0 55.1 reduce-scatter.24
  1850.8 55.1 reduce-scatter.26
  1910.0 55.7 reduce-scatter.22
  1969.9 55.7 reduce-scatter.18
  2028.6 21.1 all-reduce.4
  2053.7 243.5 reduce-scatter.16
where the time goes:
time: 2320 us; the launch traced here: 2310 us
  waiting for transfers between devices  845 us (36%)
  local copies, waits for them, and re-layouts  402 us (17%)
  other arithmetic  393 us (17%)
  matrix products  357 us (15%)
  blocking collectives  168 us (7%)
  starting transfers between devices  129 us (6%)
    reduce_scatter x1, waiting for transfers between devices, per_device(): lax.psum_scatter(d_keys.reshape(H, length, NOPE + VD).astype(jnp.bfloat16...  242 us
    unnamed x20, waiting for transfers between devices  183 us
    all_gather x1, blocking collectives, per_device(): lax.all_gather(w_router, 'grp', axis=0, tiled=True)  146 us
    unnamed x225, local copies, waits for them, and re-layouts  143 us
    all_to_all x1, other arithmetic, per_device(): lax.all_to_all(e_out, 'grp', split_axis=0, concat_axis=1, tiled=True)  126 us
    all_to_all x1, other arithmetic, per_device(): lax.all_to_all(d_rows, 'grp', split_axis=0, concat_axis=1, tiled=True)  126 us
    all_to_all x1, waiting for transfers between devices, per_device(): lax.all_to_all(d_outgoing, 'grp', split_axis=1, concat_axis=0, tiled=True)  115 us
    all_gather x1, waiting for transfers between devices, per_device(): lax.all_gather(expanded, 'grp', axis=1, tiled=True)  114 us
  transfers between devices with their start and end apart: 19, of which 12 were waited for; matrix products, arithmetic and copies ran while one was open for 30% of the time, Pallas kernels for 0%

commit v1 on v0

v1 whole, which is shorter than its diff:
```python
import functools

import jax
import jax.numpy as jnp
from jax import lax
from jax.experimental import pallas as pl
from jax.experimental.pallas import tpu as pltpu
from jax.sharding import PartitionSpec as P

H = 16
NOPE = 128
ROPE = 64
VD = 128
KVR = 512
TOP = 6
QK = NOPE + ROPE
EPS = 1e-06
F32 = jnp.float32
BF16 = jnp.bfloat16


def dot(former, latter):
    return jnp.dot(former, latter, preferred_element_type=F32)


def dot_t(former, latter):
    return lax.dot_general(
        former, latter, (((1,), (1,)), ((), ())), preferred_element_type=F32
    )


def t_dot(former, latter):
    return lax.dot_general(
        former, latter, (((0,), (0,)), ((), ())), preferred_element_type=F32
    )


def root_norm(v, gains):
    factor = lax.rsqrt(jnp.mean(v * v, axis=-1, keepdims=True) + EPS)
    return v * factor * gains


def norm_back(v, gains, gradient):
    factor = lax.rsqrt(jnp.mean(v * v, axis=-1, keepdims=True) + EPS)
    weighted = gradient * gains
    return factor * weighted - v * (factor * factor * factor) * jnp.mean(
        weighted * v, axis=-1, keepdims=True
    )


def gated_slope(v):
    logistic = jax.nn.sigmoid(v)
    return logistic * (1.0 + v * (1.0 - logistic))


def angles(positions, width):
    frequency = 10000.0 ** (-jnp.arange(0, width, 2, dtype=F32) / width)
    phases = positions.astype(F32)[:, None] * frequency[None, :]
    return (jnp.cos(phases), jnp.sin(phases))


def rotate(v, cosine, sine):
    half = v.shape[-1] // 2
    a, b = v[..., :half], v[..., half:]
    return jnp.concatenate([a * cosine - b * sine, b * cosine + a * sine], axis=-1)


def unrotate(v, cosine, sine):
    half = v.shape[-1] // 2
    a, b = v[..., :half], v[..., half:]
    return jnp.concatenate([a * cosine + b * sine, b * cosine - a * sine], axis=-1)


def gather(v, axis=0):
    return lax.all_gather(v, "grp", axis=axis, tiled=True)


def exchange(v):
    return lax.all_to_all(v, "grp", split_axis=0, concat_axis=0, tiled=True)


def scatter_sum(v):
    return lax.psum_scatter(v, "grp", scatter_dimension=0, tiled=True)


def block_of(length):
    return next(b for b in (512, 384, 256, 128) if length % b == 0)


def attend_kernel(prefix_ref, q_ref, k_ref, v_ref, o_ref, lse_ref, *, block, factor):
    i = pl.program_id(0)
    prefix = prefix_ref[0]
    start = i * block
    q = q_ref[...]
    seen = jnp.where(start < prefix, (prefix + block - 1) // block, 0)
    stop = jnp.maximum(i + 1, seen)
    rows = start + lax.broadcasted_iota(jnp.int32, (block, block), 0)

    def step(j, carry):
        top, total, acc = carry
        at = pl.multiple_of(j * block, block)
        k = k_ref[pl.ds(at, block), :]
        v = v_ref[pl.ds(at, block), :]
        s = dot_t(q, k) * factor
        cols = at + lax.broadcasted_iota(jnp.int32, (block, block), 1)
        limit = jnp.where(rows < prefix, jnp.maximum(rows, prefix - 1), rows)
        s = jnp.where(cols <= limit, s, -1e30)
        fresh = jnp.maximum(top, jnp.max(s, axis=1, keepdims=True))
        p = jnp.exp(s - fresh)
        scale = jnp.exp(top - fresh)
        total = total * scale + jnp.sum(p, axis=1, keepdims=True)
        acc = acc * scale + dot(p.astype(BF16), v)
        return fresh, total, acc

    top, total, acc = lax.fori_loop(
        0,
        stop,
        step,
        (
            jnp.full((block, 1), -1e30, F32),
            jnp.zeros((block, 1), F32),
            jnp.zeros((block, VD), F32),
        ),
    )
    o_ref[...] = acc / total
    lse_ref[...] = top + jnp.log(total)


def attend(prefix, q, k, v):
    length = q.shape[0]
    block = block_of(length)
    return pl.pallas_call(
        functools.partial(attend_kernel, block=block, factor=QK**-0.5),
        grid=(length // block,),
        in_specs=[
            pl.BlockSpec(memory_space=pltpu.SMEM),
            pl.BlockSpec((block, QK), lambda i: (i, 0)),
            pl.BlockSpec((length, QK), lambda i: (0, 0)),
            pl.BlockSpec((length, VD), lambda i: (0, 0)),
        ],
        out_specs=[
            pl.BlockSpec((block, VD), lambda i: (i, 0)),
            pl.BlockSpec((block, 1), lambda i: (i, 0)),
        ],
        out_shape=[
            jax.ShapeDtypeStruct((length, VD), F32),
            jax.ShapeDtypeStruct((length, 1), F32),
        ],
        cost_estimate=pl.CostEstimate(
            flops=length * length * (QK + VD), bytes_accessed=length * 1000, transcendentals=length * length // 2
        ),
        name="attend",
    )(prefix, q, k, v)


def attend_back_kernel(
    prefix_ref, q_ref, k_ref, v_ref, d_ref, lse_ref, delta_ref, dq_ref, dk_ref, dv_ref, *, block, factor
):
    i = pl.program_id(0)
    prefix = prefix_ref[0]
    start = i * block

    @pl.when(i == 0)
    def _():
        dk_ref[...] = jnp.zeros_like(dk_ref)
        dv_ref[...] = jnp.zeros_like(dv_ref)

    q = q_ref[...]
    d = d_ref[...]
    lse = lse_ref[...]
    delta = delta_ref[...]
    seen = jnp.where(start < prefix, (prefix + block - 1) // block, 0)
    stop = jnp.maximum(i + 1, seen)
    rows = start + lax.broadcasted_iota(jnp.int32, (block, block), 1)

    def step(j, dq):
        at = pl.multiple_of(j * block, block)
        k = k_ref[pl.ds(at, block), :]
        v = v_ref[pl.ds(at, block), :]
        s = dot_t(k, q) * factor
        cols = at + lax.broadcasted_iota(jnp.int32, (block, block), 0)
        limit = jnp.where(rows < prefix, jnp.maximum(rows, prefix - 1), rows)
        p = jnp.where(cols <= limit, jnp.exp(s - lse), 0.0)
        dp = dot_t(v, d)
        ds = (p * (dp - delta)).astype(BF16)
        dv_ref[pl.ds(at, block), :] += dot(p.astype(BF16), d)
        dk_ref[pl.ds(at, block), :] += dot(ds, q) * factor
        return dq + t_dot(ds, k)

    dq = lax.fori_loop(0, stop, step, jnp.zeros((block, QK), F32))
    dq_ref[...] = dq * factor


def attend_back(prefix, q, k, v, d, lse, delta):
    length = q.shape[0]
    block = block_of(length)
    whole = lambda i: (0, 0)
    return pl.pallas_call(
        functools.partial(attend_back_kernel, block=block, factor=QK**-0.5),
        grid=(length // block,),
        in_specs=[
            pl.BlockSpec(memory_space=pltpu.SMEM),
            pl.BlockSpec((block, QK), lambda i: (i, 0)),
            pl.BlockSpec((length, QK), whole),
            pl.BlockSpec((length, VD), whole),
            pl.BlockSpec((block, VD), lambda i: (i, 0)),
            pl.BlockSpec((1, block), lambda i: (0, i)),
            pl.BlockSpec((1, block), lambda i: (0, i)),
        ],
        out_specs=[
            pl.BlockSpec((block, QK), lambda i: (i, 0)),
            pl.BlockSpec((length, QK), whole),
            pl.BlockSpec((length, VD), whole),
        ],
        out_shape=[
            jax.ShapeDtypeStruct((length, QK), F32),
            jax.ShapeDtypeStruct((length, QK), F32),
            jax.ShapeDtypeStruct((length, VD), F32),
        ],
        cost_estimate=pl.CostEstimate(
            flops=length * length * (3 * QK + 2 * VD), bytes_accessed=length * 2000, transcendentals=length * length // 2
        ),
        name="attend_back",
    )(prefix, q, k, v, d, lse, delta)


def split_two(v):
    high = v.astype(BF16)
    low = (v - high.astype(F32)).astype(BF16)
    return high, low


def per_device(
    hidden,
    grad_out,
    expert_ids,
    prefix_len,
    adapter_id,
    attn_gain,
    kv_gain,
    ffn_gain,
    w_q,
    w_kva,
    w_kvb,
    w_o,
    w_router,
    shared_gate,
    shared_up,
    shared_down,
    expert_gate,
    expert_up_weight,
    expert_down,
    q_down,
    q_up,
    o_down,
    o_up,
):
    tokens = hidden.shape[1]
    width = hidden.shape[2]
    members = lax.axis_size("grp")
    length = tokens * members
    experts = expert_gate.shape[0] * members
    capacity = tokens * TOP * 5 // (4 * experts)
    slots = -(-capacity // 16) * 16
    me = lax.axis_index("grp")

    inputs = hidden[0].astype(F32)
    cotangent = grad_out[0]
    c32 = cotangent.astype(F32)
    routes = expert_ids[0]
    adapter = adapter_id[0]
    pick = lambda table: lax.dynamic_index_in_dim(table, adapter, 0, keepdims=False)
    qa_down, qa_up, oa_down, oa_up = pick(q_down), pick(q_up), pick(o_down), pick(o_up)

    full_kva = gather(w_kva)
    full_q = gather(w_q)
    hidden_slice = shared_down.shape[0]
    kvb_cols = w_kvb.shape[1] // members
    own_kvb = exchange(
        w_kvb.reshape(w_kvb.shape[0], members, kvb_cols).transpose(1, 0, 2)
    ).reshape(KVR, kvb_cols)
    shared = jnp.stack([shared_gate, shared_up], axis=1)
    shared = shared.reshape(shared.shape[0], 2, members, hidden_slice).transpose(2, 0, 1, 3)
    own_shared = exchange(shared.reshape(members, -1, 2 * hidden_slice)).reshape(width, 2 * hidden_slice)
    full_o = gather(w_o)
    full_router = gather(w_router)

    positions = me * tokens + jnp.arange(tokens, dtype=jnp.int32)
    cosine, sine = angles(positions, ROPE)
    normed = root_norm(inputs, attn_gain).astype(BF16)
    latent = dot(normed, full_kva)
    compressed = root_norm(latent[:, :KVR], kv_gain).astype(BF16)
    k_rope = rotate(latent[:, KVR:], cosine, sine).astype(BF16)
    all_latent = gather(jnp.concatenate([compressed, k_rope], axis=-1))
    q_small = dot(normed, qa_down).astype(BF16)
    query = (dot(normed, full_q) + dot(q_small, qa_up)).reshape(tokens, H, QK)
    query = jnp.concatenate(
        [query[:, :, :NOPE], rotate(query[:, :, NOPE:], cosine[:, None], sine[:, None])], axis=-1
    ).astype(BF16)
    q_head = exchange(query.transpose(1, 0, 2)).reshape(length, QK)
    expanded = dot(all_latent[:, :KVR], own_kvb).astype(BF16)
    k_head = jnp.concatenate([expanded[:, :NOPE], all_latent[:, KVR:]], axis=-1)
    v_head = expanded[:, NOPE:]
    mixture, lse = attend(prefix_len, q_head, k_head, v_head)
    mixed = (
        exchange(mixture.astype(BF16).reshape(members, tokens, VD))
        .transpose(1, 0, 2)
        .reshape(tokens, H * VD)
    )
    o_small = dot(mixed, oa_down).astype(BF16)
    middle = inputs + dot(mixed, full_o) + dot(o_small, oa_up)
    ffn_in = root_norm(middle, ffn_gain).astype(BF16)
    route_probs = jax.nn.softmax(dot(ffn_in, full_router), axis=-1)

    lanes = 128
    high, low = split_two(route_probs)
    extra = jnp.concatenate(
        [high, low, jnp.zeros((tokens, lanes - 2 * experts), BF16)], axis=-1
    )
    all_in = gather(jnp.concatenate([ffn_in, extra], axis=-1))
    all_ids = gather(routes)
    all_c = gather(cotangent)
    ffn_all = all_in[:, :width]
    mine = jnp.arange(experts, dtype=jnp.int32)[None, :] == me
    probs = jnp.sum(
        jnp.where(
            mine,
            all_in[:, width : width + experts].astype(F32)
            + all_in[:, width + experts : width + 2 * experts].astype(F32),
            0.0,
        ),
        axis=-1,
    ).reshape(members, tokens)
    chosen = jnp.any(all_ids == me, axis=-1).reshape(members, tokens)
    order = jnp.arange(tokens, dtype=jnp.int32)
    before = (order[:, None] < order[None, :]).astype(BF16)
    rank = dot(chosen.astype(BF16), before).astype(jnp.int32)
    place = (rank[:, None, :] == jnp.arange(slots, dtype=jnp.int32)[None, :, None]) & chosen[:, None, :]
    select = place.astype(BF16)
    weight_rows = jnp.sum(jnp.where(place, probs[:, None, :], 0.0), axis=-1)

    def compact(rows):
        return lax.dot_general(
            select,
            rows.reshape(members, tokens, width),
            (((2,), (1,)), ((0,), (0,))),
            preferred_element_type=F32,
        ).astype(BF16).reshape(members * slots, width)

    def spread(rows):
        return lax.dot_general(
            select,
            rows.reshape(members, slots, width),
            (((1,), (1,)), ((0,), (0,))),
            preferred_element_type=F32,
        ).reshape(length, width)

    rows_in = compact(ffn_all)
    e_gate = dot(rows_in, expert_gate[0])
    e_up = dot(rows_in, expert_up_weight[0])
    e_hidden = (jax.nn.silu(e_gate) * e_up).astype(BF16)
    e_out = dot(e_hidden, expert_down[0]).astype(BF16)
    gates = weight_rows.reshape(members * slots, 1)
    s_gate = dot(ffn_all, own_shared[:, :hidden_slice])
    s_up = dot(ffn_all, own_shared[:, hidden_slice:])
    s_hidden = (jax.nn.silu(s_gate) * s_up).astype(BF16)
    partial = spread((gates * e_out.astype(F32)).astype(BF16)) + dot(s_hidden, shared_down)
    ffn_out = scatter_sum(partial.astype(BF16))
    output = (middle + ffn_out.astype(F32)).astype(BF16)

    rows_c = compact(all_c)
    rows_c32 = rows_c.astype(F32)
    d_gate = jnp.sum(rows_c32 * e_out.astype(F32), axis=-1).reshape(members, slots)
    d_eout = (gates * rows_c32).astype(BF16)
    d_eh = dot_t(d_eout, expert_down[0])
    d_egate = (d_eh * e_up * gated_slope(e_gate)).astype(BF16)
    d_eup = (d_eh * jax.nn.silu(e_gate)).astype(BF16)
    d_rows = (dot_t(d_egate, expert_gate[0]) + dot_t(d_eup, expert_up_weight[0])).astype(BF16)
    d_sh = dot_t(all_c, shared_down)
    d_sgate = (d_sh * s_up * gated_slope(s_gate)).astype(BF16)
    d_sup = (d_sh * jax.nn.silu(s_gate)).astype(BF16)
    d_shared = jnp.concatenate([d_sgate, d_sup], axis=-1)
    d_partial = spread(d_rows) + dot_t(d_shared, own_shared)
    d_gate_all = jnp.sum(jnp.where(place, d_gate[:, :, None], 0.0), axis=1).reshape(length, 1)
    g_high, g_low = split_two(d_gate_all)
    d_extra = jnp.concatenate(
        [
            jnp.where(mine, g_high, 0).astype(BF16),
            jnp.where(mine, g_low, 0).astype(BF16),
            jnp.zeros((length, lanes - 2 * experts), BF16),
        ],
        axis=-1,
    )
    d_own = scatter_sum(jnp.concatenate([d_partial.astype(BF16), d_extra], axis=-1))
    d_route = d_own[:, width : width + experts].astype(F32) + d_own[
        :, width + experts : width + 2 * experts
    ].astype(F32)
    d_logits = (
        route_probs * (d_route - jnp.sum(route_probs * d_route, axis=-1, keepdims=True))
    ).astype(BF16)
    d_ffn = d_own[:, :width].astype(F32) + dot_t(d_logits, full_router)
    d_middle = c32 + norm_back(middle, ffn_gain, d_ffn)
    d_attn = d_middle.astype(BF16)
    grad_oup = t_dot(o_small, d_attn)
    d_osmall = dot_t(d_attn, oa_up).astype(BF16)
    grad_odown = t_dot(d_osmall, mixed)
    d_mixed = (dot_t(d_attn, full_o) + dot_t(d_osmall, oa_down)).astype(BF16)
    d_head = exchange(d_mixed.reshape(tokens, H, VD).transpose(1, 0, 2)).reshape(length, VD)
    delta = jnp.sum(d_head.astype(F32) * mixture, axis=-1)
    dq, dk, dv = attend_back(
        prefix_len, q_head, k_head, v_head, d_head, lse.reshape(1, length), delta.reshape(1, length)
    )
    d_query = exchange(dq.astype(BF16).reshape(members, tokens, QK)).transpose(1, 0, 2).astype(F32)
    d_expanded = jnp.concatenate([dk[:, :NOPE], dv], axis=-1).astype(BF16)
    d_latents = scatter_sum(
        jnp.concatenate([dot_t(d_expanded, own_kvb), dk[:, NOPE:]], axis=-1).astype(BF16)
    ).astype(F32)
    d_latent = jnp.concatenate(
        [
            norm_back(latent[:, :KVR], kv_gain, d_latents[:, :KVR]),
            unrotate(d_latents[:, KVR:], cosine, sine),
        ],
        axis=-1,
    ).astype(BF16)
    d_query = (
        jnp.concatenate(
            [d_query[:, :, :NOPE], unrotate(d_query[:, :, NOPE:], cosine[:, None], sine[:, None])],
            axis=-1,
        )
        .reshape(tokens, H * QK)
        .astype(BF16)
    )
    grad_qup = t_dot(q_small, d_query)
    d_qsmall = dot_t(d_query, qa_up).astype(BF16)
    grad_qdown = t_dot(d_qsmall, normed)
    d_normed = dot_t(d_query, full_q) + dot_t(d_qsmall, qa_down) + dot_t(d_latent, full_kva)
    grad_inputs = (d_middle + norm_back(inputs, attn_gain, d_normed)).astype(BF16)

    rank_of = qa_up.shape[0]
    parts = [
        g.astype(BF16).reshape(rank_of, members, -1).transpose(1, 0, 2)
        for g in (grad_qdown, grad_qup, grad_odown, grad_oup)
    ]
    sizes = [g.shape[2] for g in parts]
    share = jnp.sum(exchange(jnp.concatenate(parts, axis=-1)).astype(F32), axis=0)
    selector = (jnp.arange(q_down.shape[0], dtype=jnp.int32) == adapter).astype(F32)[:, None, None]
    summed = lax.psum((selector * share[None]).astype(BF16), "rep").astype(F32)
    ends = [sum(sizes[: n + 1]) for n in range(4)]
    outs = [summed[:, :, e - s : e] for e, s in zip(ends, sizes)]
    return (
        output[None],
        grad_inputs[None],
        outs[0].transpose(0, 2, 1),
        outs[1],
        outs[2].transpose(0, 2, 1),
        outs[3],
    )


def solution(mesh):
    seq = P("rep", "grp", None)
    rows = P("grp", None)
    in_specs = (
        (seq, seq, seq, P("rep"), P("rep"), P(), P(), P())
        + (rows,) * 8
        + (P("grp", None, None),) * 3
        + (P(),) * 4
    )
    out_specs = (
        seq,
        seq,
        P(None, "grp", None),
        P(None, None, "grp"),
        P(None, "grp", None),
        P(None, None, "grp"),
    )
    return jax.shard_map(
        per_device, mesh=mesh, in_specs=in_specs, out_specs=out_specs, check_vma=False
    )
```

time: 2320 us -> 1340 us (0.58)
  local copies, waits for them, and re-layouts: 402 us -> 84 us
  other arithmetic: 393 us -> 137 us
  waiting for transfers between devices: 845 us -> 630 us
  matrix products: 357 us -> 258 us
  starting transfers between devices: 129 us -> 37.6 us
  blocking collectives: 168 us -> 113 us
  Pallas kernels: 0 us -> 49.3 us
    all_to_all x2 -> x0, other arithmetic: 253 us -> none  [the longest x1 126 us: per_device(): lax.all_to_all(e_out, 'grp', split_axis=0, concat_axis=1, tiled=True)]
    unnamed x20 -> x10, waiting for transfers between devices: 183 us -> 2.53 us
    unnamed x225 -> x150, local copies, waits for them, and re-layouts: 143 us -> 23.4 us
    dot_general x78 -> x38, matrix products: 357 us -> 258 us  [the longest x14 108 us: dot_t(): lax.dot_general(former, latter, (((1,), (1,)), ((), ())), preferred_eleme...]
    all_to_all x4 -> x7, starting transfers between devices: 128 us -> 36.9 us  [exchange(): return lax.all_to_all(v, 'grp', split_axis=0, concat_axis=0, tiled=True)]
    all_to_all x4 -> x7, waiting for transfers between devices: 139 us -> 50.6 us  [exchange(): return lax.all_to_all(v, 'grp', split_axis=0, concat_axis=0, tiled=True)]
    reduce_or x0 -> x1, other arithmetic: none -> 65.3 us  [per_device(): chosen = jnp.any(all_ids == me, axis=-1).reshape(members, tokens)]
    reduce_scatter x1 -> x3, waiting for transfers between devices: 242 us -> 307 us  [scatter_sum(): return lax.psum_scatter(v, 'grp', scatter_dimension=0, tiled=True)]
  transfers between devices with their start and end apart: 19 -> 17, of which waited for: 12 -> 12; matrix products, arithmetic and copies ran while one was open for 30% -> 15% of each run, Pallas kernels for 0% -> 2%
where the time goes in v1:
time: 1340 us; the launch traced here: 1330 us
  waiting for transfers between devices  630 us (47%)
  matrix products  258 us (19%)
  other arithmetic  137 us (10%)
  blocking collectives  113 us (8%)
  local copies, waits for them, and re-layouts  84 us (6%)
  Pallas kernels  49.3 us (4%)
  starting transfers between devices  37.6 us (3%)
  between operations  17 us (1%)
    reduce_scatter x3, waiting for transfers between devices, scatter_sum(): return lax.psum_scatter(v, 'grp', scatter_dimension=0, tiled=True)  307 us
    all_gather x6, waiting for transfers between devices, gather(): return lax.all_gather(v, 'grp', axis=axis, tiled=True)  266 us
    all_gather x2, blocking collectives, gather(): return lax.all_gather(v, 'grp', axis=axis, tiled=True)  113 us
    dot_general x14, matrix products, dot_t(): lax.dot_general(former, latter, (((1,), (1,)), ((), ())), preferred_eleme...  108 us
    dot_general x16, matrix products, dot(): return jnp.dot(former, latter, preferred_element_type=F32)  106 us
    reduce_or x1, other arithmetic, per_device(): chosen = jnp.any(all_ids == me, axis=-1).reshape(members, tokens)  65.3 us
    all_to_all x7, waiting for transfers between devices, exchange(): return lax.all_to_all(v, 'grp', split_axis=0, concat_axis=0, tiled=True)  50.6 us
    all_to_all x7, starting transfers between devices, exchange(): return lax.all_to_all(v, 'grp', split_axis=0, concat_axis=0, tiled=True)  36.9 us
  transfers between devices with their start and end apart: 17, of which 12 were waited for; matrix products, arithmetic and copies ran while one was open for 15% of the time, Pallas kernels for 2%

profile of v1, /device:TPU:0, one launch (start us, length us, event | category | flops | bytes accessed | tf_op | source)
XLA Modules:
  0.0 1326.1 jit_solution(12241553895608569507)
XLA Ops:
  10.7 44.2 %all-gather.11.cloned.1.call-done = bf16[2048,576]{0,1:T(8,128)(2,1)} async-done(((bf16[128,576]{0,1:T(8,128)(2,1)}), bf16[2048,576]{0,1:T(8,128)(2,1)}) %all-gather.11.cloned.1.call-update) | async-done | bytes 2359312 | tf_op jit(solution)/shard_map/all_gather | solution.py:75
  62.1 4.2 all-to-all-start.1
  68.2 93.9 %all-gather.9.cloned.1.call-done = bf16[2048,3072]{1,0:T(8,128)(2,1)} async-done(((bf16[128,3072]{1,0:T(8,128)(2,1)}), bf16[2048,3072]{1,0:T(8,128)(2,1)}) %all-gather.9.cloned.1.call-update) | async-done | bytes 12582928 | tf_op jit(solution)/shard_map/all_gather | solution.py:75
  162.1 6.1 fusion.145
  178.2 3.7 all-to-all-start
  182.6 46.6 %all-gather.13.cloned.1.call-done = bf16[3072,576]{1,0:T(8,128)(2,1)} async-done(((bf16[192,576]{1,0:T(8,128)(2,1)}), bf16[3072,576]{1,0:T(8,128)(2,1)}) %all-gather.13.cloned.1.call-update) | async-done | bytes 3538960 | tf_op jit(solution)/shard_map/all_gather | solution.py:75
  236.0 20.9 %attend.1 = (f32[3072,128]{1,0:T(8,128)}, f32[3072,1]{1,0:T(8,128)}) custom-call(s32[1]{0:T(128)S(6)} %copy.239.prefix_ref, bf16[3072,192]{1,0:T(8,128)(2,1)} %bitcast.235, bf16[3072,192]{1,0:T(8,128)(2,1)} %pad_maximum_fusion.1.k_ref, bf16[3072,128]{1,0:T(8,128)(2,1)} %get-tuple-element.44.v_ref), custom_call_target="tpu_custom_call" | custom-call | flops 3019898880 | bytes 3072000 | tf_op jit(solution)/shard_map/attend/pallas_call | solution.py:132
  259.4 6.2 all-to-all-start.2
  265.6 42.6 %all_gather.29 = bf16[2048,16]{0,1:T(8,128)(2,1)S(1)} all-gather(bf16[128,16]{0,1:T(8,128)(2,1)S(1)} %copy-done.62), channel_id=1, replica_groups=mesh['rep'=2,'grp'=16] {'grp'}, dimensions={0}, use_global_device_ids=true | all-gather | bytes 69632 | tf_op jit(solution)/shard_map/all_gather | solution.py:75
  309.4 12.6 all-gather.15.cloned.1.call-done
  322.0 5.2 convolution_add_fusion.5
  334.8 3.9 all-to-all-start.3
  338.9 70.7 %all-gather = s32[1,3072,6]{2,0,1:T(1,128)S(1)} all-gather(s32[1,192,6]{2,0,1:T(1,128)S(1)} %copy.166), channel_id=2, replica_groups=mesh['rep'=2,'grp'=16] {'grp'}, dimensions={1}, use_global_device_ids=true | all-gather | bytes 78336 | tf_op jit(solution)/shard_map/all_gather | solution.py:75
  409.6 65.3 %compare_reduce_fusion = pred[3072]{0:T(1024)(128)(4,1)S(1)} fusion(s32[1,3072,6]{2,0,1:T(1,128)S(1)} %all-gather, s32[]{:T(128)S(6)} %axis_index.12), kind=kLoop, calls=%fused_computation.19 | loop fusion | flops 33792 | bytes 76804 | tf_op jit(solution)/shard_map/reduce_or | solution.py:334
  477.3 11.8 convert_convert_fusion
  489.5 5.6 fusion.3
  495.1 68.3 %all-gather.17.cloned.1.call-done = bf16[3072,2176]{1,0:T(8,128)(2,1)} async-done(((bf16[192,2176]{1,0:T(8,128)(2,1)}), bf16[3072,2176]{1,0:T(8,128)(2,1)}) %all-gather.17.cloned.1.call-update) | async-done | bytes 13369360 | tf_op jit(solution)/shard_map/all_gather | solution.py:75
  566.1 4.6 slice-done
  574.3 13.6 %fusion.14 = f32[1536,1408]{1,0:T(8,128)} fusion(bf16[1536,2048]{1,0:T(8,128)(2,1)S(1)} %bitcast.226, bf16[1,2048,1408]{2,1,0:T(8,128)(2,1)} %param.39), kind=kOutput, calls=%fused_computation.28 | convolution fusion | flops 8858370048 | bytes 20709376 | tf_op jit(solution)/shard_map/dot_general | solution.py:23
  587.9 12.1 fusion.10
  600.0 20.3 %fusion.2 = (f32[1536]{0:T(1024)S(1)}, bf16[1536,2048]{1,0:T(8,128)(2,1)}) fusion(f32[16,96,2048]{2,1,0:T(8,128)} %convert_convert_fusion, bf16[1,1408,2048]{2,1,0:T(8,128)(2,1)} %param.41, f32[1536,1408]{1,0:T(8,128)} %fusion.10, f32[1536,1408]{1,0:T(8,128)} %fusion.14), kind=kOutput, calls=%fused_computation.7 | convolution fusion | flops 8883927040 | bytes 41949184 | tf_op jit(solution)/shard_map/dot_general | solution.py:23
  622.7 7.9 multiply_convert_fusion
  630.7 15.3 %fusion.6 = f32[1536,1408]{1,0:T(8,128)} fusion(bf16[1536,2048]{1,0:T(8,128)(2,1)} %bitcast.230, bf16[1,1408,2048]{2,1,0:T(8,128)(2,1)} %param.41), kind=kOutput, calls=%fused_computation.20 | convolution fusion | flops 8858370048 | bytes 20709376 | tf_op jit(solution)/shard_map/dot_general | solution.py:27
  645.9 22.9 %fusion.12 = f32[1536,2048]{1,0:T(8,128)} fusion(bf16[1,2048,1408]{2,1,0:T(8,128)(2,1)} %param.39, f32[1536,1408]{1,0:T(8,128)} %fusion.14, f32[1536,1408]{1,0:T(8,128)} %fusion.6, f32[1536,1408]{1,0:T(8,128)} %fusion.10), kind=kOutput, calls=%fused_computation.26 | convolution fusion | flops 8879996928 | bytes 44302336 | tf_op jit(solution)/shard_map/dot_general | solution.py:27
  668.8 21.1 %add_convert_fusion.1 = bf16[1536,2048]{1,0:T(8,128)(2,1)} fusion(f32[1536,2048]{1,0:T(8,128)} %fusion.12, bf16[1,2048,1408]{2,1,0:T(8,128)(2,1)} %param.40, f32[1536,1408]{1,0:T(8,128)} %fusion.6, f32[1536,1408]{1,0:T(8,128)} %fusion.14), kind=kOutput, calls=%fused_computation.10 | convolution fusion | flops 8877637632 | bytes 41943040 | tf_op jit(solution)/shard_map/dot_general | solution.py:27
  689.9 12.4 fusion.43
  702.3 24.9 %copy.179 = f32[3072,2048]{0,1:T(8,128)} copy(f32[3072,2048]{1,0:T(8,128)} %bitcast.222) | data formatting | bytes 50331648 | tf_op jit(solution)/shard_map/reshape | solution.py:356
  727.3 7.4 fusion.72
  734.8 12.4 multiply_convert_fusion.8
  747.2 15.3 %add_convert_fusion = bf16[3072,2048]{0,1:T(8,128)(2,1)} fusion(f32[3072,2048]{0,1:T(8,128)} %copy.179, bf16[3072,176]{0,1:T(8,128)(2,1)} %get-tuple-element.35, bf16[3072,176]{0,1:T(8,128)(2,1)} %get-tuple-element.34, bf16[16,128,352]{1,2,0:T(8,128)(2,1)S(1)} %copy-done.5), kind=kOutput, calls=%fused_computation.2 | convolution fusion | flops 4446093312 | bytes 41353216 | tf_op jit(solution)/shard_map/dot_general | solution.py:27
  762.5 15.7 %maximum_maximum_fusion = bf16[3072,2176]{0,1:T(8,128)(2,1)} fusion(bf16[3072,16]{0,1:T(8,128)(2,1)S(1)} %get-tuple-element.65, bf16[3072,16]{0,1:T(8,128)(2,1)S(1)} %get-tuple-element.64, bf16[3072,2048]{0,1:T(8,128)(2,1)} %add_convert_fusion, bf16[2176]{0:T(1024)(128)(2,1)S(1)} %copy-done.43), kind=kLoop, calls=%fused_computation.5 | loop fusion | flops 53477376 | bytes 26153216 | tf_op jit(solution)/shard_map/concatenate | solution.py:394
  778.2 16.8 %copy.194 = bf16[3072,2176]{1,0:T(8,128)(2,1)} copy(bf16[3072,2176]{0,1:T(8,128)(2,1)} %maximum_maximum_fusion) | data formatting | bytes 26738688
  795.1 3.9 fusion.1
  799.0 13.5 %fusion.46 = f32[16,192,2048]{2,1,0:T(8,128)} fusion(bf16[16,96,2048]{2,1,0:T(8,128)(2,1)S(1)} %bitcast.224, s32[16,192]{1,0:T(8,128)S(1)} %convolution_convert_fusion.8, pred[16,192]{1,0:T(8,128)(4,1)S(1)} %reshape.291), kind=kOutput, calls=%fused_computation.96 | convolution fusion | flops 1208549376 | bytes 31472640 | tf_op jit(solution)/shard_map/dot_general | solution.py:351
  812.5 18.0 %fusion = bf16[3072,2048]{1,0:T(8,128)(2,1)} fusion(f32[16,192,2048]{2,1,0:T(8,128)} %fusion.46, bf16[176,2048]{1,0:T(8,128)(2,1)} %param.38, f32[3072,176]{0,1:T(8,128)S(1)} %copy-done.12, f32[3072,176]{0,1:T(8,128)} %get-tuple-element.72), kind=kOutput, calls=%fused_computation.1 | convolution fusion | flops 2230419456 | bytes 42795008 | tf_op jit(solution)/shard_map/dot_general | solution.py:23
  830.6 103.0 %reduce-scatter.12.cloned.1.call-done = bf16[192,2176]{1,0:T(8,128)(2,1)} async-done(((bf16[3072,2176]{1,0:T(8,128)(2,1)}), bf16[192,2176]{1,0:T(8,128)(2,1)}) %reduce-scatter.12.cloned.1.call-update) | async-done | bytes 835600 | tf_op jit(solution)/shard_map/reduce_scatter | solution.py:83
  937.6 134.3 %reduce-scatter.10.cloned.1.call-done = bf16[192,2048]{1,0:T(8,128)(2,1)} async-done(((bf16[3072,2048]{1,0:T(8,128)(2,1)}), bf16[192,2048]{1,0:T(8,128)(2,1)}) %reduce-scatter.10.cloned.1.call-update) | async-done | bytes 786448 | tf_op jit(solution)/shard_map/reduce_scatter | solution.py:83
  1076.5 6.3 fusion.134
  1085.1 4.0 all-to-all-start.4
  1091.6 16.2 %all-to-all-done.4 = bf16[16,192,128]{2,1,0:T(8,128)(2,1)S(1)} async-done(((bf16[16,192,128]{2,1,0:T(8,128)(2,1)}), bf16[16,192,128]{2,1,0:T(8,128)(2,1)S(1)}, u32[]{:S(2)}, u32[]{:S(2)}) %all-to-all-start.4) | async-done | bytes 786464 | tf_op jit(solution)/shard_map/all_to_all | solution.py:79
  1110.5 28.5 %attend_back.1 = (f32[3072,192]{1,0:T(8,128)}, f32[3072,192]{1,0:T(8,128)}, f32[3072,128]{1,0:T(8,128)}) custom-call(s32[1]{0:T(128)S(6)} %copy.239.prefix_ref, bf16[3072,192]{1,0:T(8,128)(2,1)} %bitcast.236, bf16[3072,192]{1,0:T(8,128)(2,1)} %pad_maximum_fusion.1.k_ref, bf16[3072,128]{1,0:T(8,128)(2,1)} %get-tuple-element.44.v_ref, ...), custom_call_target="tpu_custom_call" | custom-call | flops 7851737088 | bytes 6144000 | tf_op jit(solution)/shard_map/attend_back/pallas_call | solution.py:198
  1142.2 5.8 all-to-all-start.5
  1149.2 30.8 %all-to-all-done.5 = bf16[16,192,192]{2,1,0:T(8,128)(2,1)} async-done(((bf16[16,192,192]{2,1,0:T(8,128)(2,1)}), bf16[16,192,192]{2,1,0:T(8,128)(2,1)}, u32[]{:S(2)}, u32[]{:S(2)}) %all-to-all-start.5) | async-done | bytes 1179680 | tf_op jit(solution)/shard_map/all_to_all | solution.py:79
  1195.3 9.1 all-to-all-start.6
  1217.8 4.5 pad_maximum_fusion
  1222.3 10.1 fusion.154
  1232.4 4.7 all-reduce.2.cloned.1.call-done
  1241.8 69.5 %reduce-scatter.8.cloned.1.call-done = bf16[192,576]{1,0:T(8,128)(2,1)} async-done(((bf16[3072,576]{1,0:T(8,128)(2,1)}), bf16[192,576]{1,0:T(8,128)(2,1)}) %reduce-scatter.8.cloned.1.call-update) | async-done | bytes 221200 | tf_op jit(solution)/shard_map/reduce_scatter | solution.py:83
  (278 shorter events, 112.7 us)
Async XLA Ops:
  7.2 161.0 %copy-start = (bf16[8,16,3072]{2,1,0:T(8,128)(2,1)S(1)}, bf16[8,16,3072]{2,1,0:T(8,128)(2,1)}, u32[]{:S(2)}) copy-start(bf16[8,16,3072]{2,1,0:T(8,128)(2,1)} %param.43) | copy-start | bytes 2359300
  7.2 47.8 %all-gather.11.cloned.1.call-start = ((), (), s32[]{:S(2)}) async-start(), calls=%async_computation.11 | async-start | bytes 2506752 | tf_op jit(solution)/shard_map/all_gather | solution.py:75
  7.9 154.2 %all-gather.9.cloned.1.call-start = ((), (), s32[]{:S(2)}) async-start(), calls=%async_computation.10 | async-start | bytes 13369344 | tf_op jit(solution)/shard_map/all_gather | solution.py:75
  8.7 220.5 %all-gather.13.cloned.1.call-start = ((), (), s32[]{:S(2)}) async-start(), calls=%async_computation.12 | async-start | bytes 4177920 | tf_op jit(solution)/shard_map/all_gather | solution.py:75
  8.7 49.9 %copy-start.63 = (f32[32]{0:T(128)}, f32[32]{0:T(128)S(1)}, u32[]{:S(2)}) copy-start(f32[32]{0:T(128)S(1)} %multiply_power_fusion) | copy-start | bytes 388
  8.8 49.9 %copy-start.55 = (f32[192]{0:T(256)}, f32[192]{0:T(256)S(1)}, u32[]{:S(2)}) copy-start(f32[192]{0:T(256)S(1)} %add_convert_fusion.4) | copy-start | bytes 2308
  10.7 151.4 %copy-start.58 = (f32[192]{0:T(256)}, f32[192]{0:T(256)S(1)}, u32[]{:S(2)}) copy-start(f32[192]{0:T(256)S(1)} %get-tuple-element.59) | copy-start | bytes 2308
  59.1 116.4 %copy-start.23 = (f32[192,32]{1,0:T(8,128)}, f32[192,32]{1,0:T(8,128)S(1)}, u32[]{:S(2)}) copy-start(f32[192,32]{1,0:T(8,128)S(1)} %get-tuple-element.56) | copy-start | bytes 73732
  59.1 116.4 %copy-start.25 = (f32[192,32]{1,0:T(8,128)}, f32[192,32]{1,0:T(8,128)S(1)}, u32[]{:S(2)}) copy-start(f32[192,32]{1,0:T(8,128)S(1)} %get-tuple-element.57) | copy-start | bytes 73732
  60.1 261.9 %all-gather.15.cloned.1.call-start = ((), (), s32[]{:S(2)}) async-start(), calls=%async_computation.13 | async-start | bytes 8912896 | tf_op jit(solution)/shard_map/all_gather | solution.py:75
  60.7 416.6 %all-gather.19.cloned.1.call-start = ((), (), s32[]{:S(2)}) async-start(), calls=%async_computation.17 | async-start | bytes 13369344 | tf_op jit(solution)/shard_map/all_gather | solution.py:75
  62.1 116.1 %all-to-all-start.1 = ((bf16[16,32,256]{2,1,0:T(8,128)(2,1)}), bf16[16,32,256]{2,1,0:T(8,128)(2,1)}, u32[]{:S(2)}, u32[]{:S(2)}) async-start(bf16[16,32,256]{2,1,0:T(8,128)(2,1)} %copy.163), calls=%async_computation.1 | async-start | bytes 524288 | tf_op jit(solution)/shard_map/all_to_all | solution.py:79
  68.2 99.9 %copy-start.37 = (bf16[192,16]{0,1:T(8,128)(2,1)}, bf16[192,16]{0,1:T(8,128)(2,1)S(1)}, u32[]{:S(2)}) copy-start(bf16[192,16]{0,1:T(8,128)(2,1)S(1)} %convolution_convert_fusion.12) | copy-start | bytes 18436
  178.2 56.7 %all-to-all-start = ((bf16[16,192,192]{2,1,0:T(8,128)(2,1)}), bf16[16,192,192]{2,1,0:T(8,128)(2,1)S(1)}, u32[]{:S(2)}, u32[]{:S(2)}) async-start(bf16[16,192,192]{2,1,0:T(8,128)(2,1)} %maximum_bitcast_fusion), calls=%async_computation | async-start | bytes 3145728 | tf_op jit(solution)/shard_map/all_to_all | solution.py:79
  256.9 65.1 %copy-start.7 = (bf16[1,192,2048]{2,1,0:T(8,128)(2,1)S(1)}, bf16[1,192,2048]{2,1,0:T(8,128)(2,1)}, u32[]{:S(2)}) copy-start(bf16[1,192,2048]{2,1,0:T(8,128)(2,1)} %param.23) | copy-start | bytes 2359300
  259.4 48.9 %all-to-all-start.2 = ((bf16[16,192,128]{2,1,0:T(8,128)(2,1)}), bf16[16,192,128]{2,1,0:T(8,128)(2,1)S(1)}, u32[]{:S(2)}, u32[]{:S(2)}) async-start(bf16[16,192,128]{2,1,0:T(8,128)(2,1)} %bitcast.9), calls=%async_computation.2 | async-start | bytes 1572864 | tf_op jit(solution)/shard_map/all_to_all | solution.py:79
  265.6 297.9 %all-gather.17.cloned.1.call-start = ((), (), s32[]{:S(2)}) async-start(), calls=%async_computation.14 | async-start | bytes 14204928 | tf_op jit(solution)/shard_map/all_gather | solution.py:75
  308.2 21.8 %copy-start.30 = (bf16[2048,16]{0,1:T(8,128)(2,1)}, bf16[2048,16]{0,1:T(8,128)(2,1)S(1)}, u32[]{:S(2)}) copy-start(bf16[2048,16]{0,1:T(8,128)(2,1)S(1)} %all_gather.29) | copy-start | bytes 196612
  308.2 19.0 %copy-start.13 = (bf16[16,192,128]{2,1,0:T(8,128)(2,1)}, bf16[16,192,128]{2,1,0:T(8,128)(2,1)S(1)}, u32[]{:S(2)}) copy-start(bf16[16,192,128]{2,1,0:T(8,128)(2,1)S(1)} %all-to-all-done.2) | copy-start | bytes 2359300
  309.4 17.8 %copy-start.39 = (bf16[192,16]{0,1:T(8,128)(2,1)}, bf16[192,16]{0,1:T(8,128)(2,1)S(1)}, u32[]{:S(2)}) copy-start(bf16[192,16]{0,1:T(8,128)(2,1)S(1)} %convolution_convert_fusion.11) | copy-start | bytes 18436
  334.8 141.0 %all-to-all-start.3 = ((bf16[16,128,352]{1,2,0:T(8,128)(2,1)}), bf16[16,128,352]{1,2,0:T(8,128)(2,1)S(1)}, u32[]{:S(2)}, u32[]{:S(2)}) async-start(bf16[16,128,352]{1,2,0:T(8,128)(2,1)} %bitcast.231), calls=%async_computation.3 | async-start | bytes 2883584 | tf_op jit(solution)/shard_map/all_to_all | solution.py:79
  338.7 594.9 %reduce-scatter.12.cloned.1.call-start = ((), (), s32[]{:S(2)}) async-start(), calls=%async_computation.19 | async-start | bytes 14204928 | tf_op jit(solution)/shard_map/reduce_scatter | solution.py:83
  475.7 90.2 %copy-start.65 = (pred[16]{0:T(512)(128)(4,1)}, pred[16]{0:T(512)(128)(4,1)S(1)}, u32[]{:S(2)}) copy-start(pred[16]{0:T(512)(128)(4,1)S(1)} %iota_compare_fusion.3) | copy-start | bytes 52
  702.3 24.9 %copy-start.66 = (pred[16]{0:T(512)(128)(4,1)S(1)}, pred[16]{0:T(512)(128)(4,1)}, u32[]{:S(2)}) copy-start(pred[16]{0:T(512)(128)(4,1)} %copy-done.65) | copy-start | bytes 52
  702.3 25.0 %copy-start.21 = (bf16[2048,352]{0,1:T(8,128)(2,1)S(1)}, bf16[2048,352]{0,1:T(8,128)(2,1)}, u32[]{:S(2)}) copy-start(bf16[2048,352]{0,1:T(8,128)(2,1)} %copy_bitcast_fusion) | copy-start | bytes 4325380
  795.0 276.9 %reduce-scatter.10.cloned.1.call-start = ((), (), s32[]{:S(2)}) async-start(), calls=%async_computation.18 | async-start | bytes 13369344 | tf_op jit(solution)/shard_map/reduce_scatter | solution.py:83
  830.5 104.2 %copy-start.33 = (f32[192,16]{0,1:T(8,128)S(1)}, f32[192,16]{0,1:T(8,128)}, u32[]{:S(2)}) copy-start(f32[192,16]{0,1:T(8,128)} %copy-done.32) | copy-start | bytes 36868
  830.6 104.2 %copy-start.42 = (f32[192]{0:T(256)S(1)}, f32[192]{0:T(256)}, u32[]{:S(2)}) copy-start(f32[192]{0:T(256)} %copy-done.41) | copy-start | bytes 2308
  830.6 104.3 %copy-start.47 = (f32[192]{0:T(256)S(1)}, f32[192]{0:T(256)}, u32[]{:S(2)}) copy-start(f32[192]{0:T(256)} %copy-done.46) | copy-start | bytes 2308
  830.6 104.3 %copy-start.2 = (f32[192,2048]{1,0:T(8,128)S(1)}, f32[192,2048]{1,0:T(8,128)}, u32[]{:S(2)}) copy-start(f32[192,2048]{1,0:T(8,128)} %copy-done.1) | copy-start | bytes 4718596
  830.6 104.3 %copy-start.31 = (bf16[2048,16]{0,1:T(8,128)(2,1)S(1)}, bf16[2048,16]{0,1:T(8,128)(2,1)}, u32[]{:S(2)}) copy-start(bf16[2048,16]{0,1:T(8,128)(2,1)} %copy-done.30) | copy-start | bytes 196612
  830.6 104.3 %copy-start.36 = (f32[2048]{0:T(1024)S(1)}, f32[2048]{0:T(1024)}, u32[]{:S(2)}) copy-start(f32[2048]{0:T(1024)} %param.30) | copy-start | bytes 24580
  830.6 241.3 %copy-start.16 = (bf16[1,192,2048]{2,1,0:T(8,128)(2,1)S(1)}, bf16[1,192,2048]{2,1,0:T(8,128)(2,1)}, u32[]{:S(2)}) copy-start(bf16[1,192,2048]{2,1,0:T(8,128)(2,1)} %param.24) | copy-start | bytes 2359300
  830.6 241.3 %copy-start.51 = (f32[192]{0:T(256)S(1)}, f32[192]{0:T(256)}, u32[]{:S(2)}) copy-start(f32[192]{0:T(256)} %copy-done.50) | copy-start | bytes 2308
  830.6 241.3 %copy-start.61 = (f32[192]{0:T(256)S(1)}, f32[192]{0:T(256)}, u32[]{:S(2)}) copy-start(f32[192]{0:T(256)} %get-tuple-element.62) | copy-start | bytes 2308
  1085.1 22.6 %all-to-all-start.4 = ((bf16[16,192,128]{2,1,0:T(8,128)(2,1)}), bf16[16,192,128]{2,1,0:T(8,128)(2,1)S(1)}, u32[]{:S(2)}, u32[]{:S(2)}) async-start(bf16[16,192,128]{2,1,0:T(8,128)(2,1)} %bitcast.214), calls=%async_computation.4 | async-start | bytes 1572864 | tf_op jit(solution)/shard_map/all_to_all | solution.py:79
  1142.2 37.7 %all-to-all-start.5 = ((bf16[16,192,192]{2,1,0:T(8,128)(2,1)}), bf16[16,192,192]{2,1,0:T(8,128)(2,1)}, u32[]{:S(2)}, u32[]{:S(2)}) async-start(bf16[16,192,192]{2,1,0:T(8,128)(2,1)} %bitcast.229), calls=%async_computation.5 | async-start | bytes 3145728 | tf_op jit(solution)/shard_map/all_to_all | solution.py:79
  1149.2 32.6 %copy-start.24 = (f32[192,32]{1,0:T(8,128)S(1)}, f32[192,32]{1,0:T(8,128)}, u32[]{:S(2)}) copy-start(f32[192,32]{1,0:T(8,128)} %copy-done.23) | copy-start | bytes 73732
  1149.2 32.6 %copy-start.26 = (f32[192,32]{1,0:T(8,128)S(1)}, f32[192,32]{1,0:T(8,128)}, u32[]{:S(2)}) copy-start(f32[192,32]{1,0:T(8,128)} %copy-done.25) | copy-start | bytes 73732
  1195.3 20.3 %all-to-all-start.6 = ((bf16[16,16,576]{2,1,0:T(8,128)(2,1)}), bf16[16,16,576]{2,1,0:T(8,128)(2,1)}, u32[]{:S(2)}, u32[]{:S(2)}) async-start(bf16[16,16,576]{2,1,0:T(8,128)(2,1)} %pad_maximum_fusion.2), calls=%async_computation.7 | async-start | bytes 655360 | tf_op jit(solution)/shard_map/all_to_all | solution.py:79
  1204.5 32.6 %all-reduce.2.cloned.1.call-start = ((), (), s32[]{:S(2)}) async-start(), calls=%async_computation.16 | async-start | bytes 327680 | tf_op jit(solution)/shard_map/psum | solution.py:447
  1217.4 93.9 %reduce-scatter.8.cloned.1.call-start = ((), (), s32[]{:S(2)}) async-start(), calls=%async_computation.15 | async-start | bytes 4177920 | tf_op jit(solution)/shard_map/reduce_scatter | solution.py:83
  1222.3 90.2 %copy-start.45 = (f32[512]{0:T(512)S(1)}, f32[512]{0:T(512)}, u32[]{:S(2)}) copy-start(f32[512]{0:T(512)} %param.29) | copy-start | bytes 6148
  1232.3 81.3 %copy-start.56 = (f32[192]{0:T(256)S(1)}, f32[192]{0:T(256)}, u32[]{:S(2)}) copy-start(f32[192]{0:T(256)} %copy-done.55) | copy-start | bytes 2308
  1232.3 81.3 %copy-start.64 = (f32[32]{0:T(128)S(1)}, f32[32]{0:T(128)}, u32[]{:S(2)}) copy-start(f32[32]{0:T(128)} %copy-done.63) | copy-start | bytes 388
  1232.3 81.8 %copy-start.10 = (f32[192,576]{1,0:T(8,128)S(1)}, f32[192,576]{1,0:T(8,128)}, u32[]{:S(2)}) copy-start(f32[192,576]{1,0:T(8,128)} %copy-done.9) | copy-start | bytes 1327108
  1232.3 81.8 %copy-start.49 = (f32[192]{0:T(256)S(1)}, f32[192]{0:T(256)}, u32[]{:S(2)}) copy-start(f32[192]{0:T(256)} %copy-done.48) | copy-start | bytes 2308
  1232.4 81.8 %copy-start.60 = (f32[192]{0:T(256)S(1)}, f32[192]{0:T(256)}, u32[]{:S(2)}) copy-start(f32[192]{0:T(256)} %get-tuple-element.60) | copy-start | bytes 2308
  (41 other events, 226.5 us)
Sparse Core Ops, SparseCore 0:
  10.1 44.7 all-gather.10
  57.2 104.8 all-gather.8
  165.0 64.1 all-gather.12
  231.2 90.7 all-gather.14
  324.1 133.6 all-gather.18
  460.0 103.4 all-gather.16
  795.1 138.5 reduce-scatter.11
  937.7 134.0 reduce-scatter.9
  1217.6 19.5 all-reduce.1
  1240.8 70.4 reduce-scatter.7

commit v2 on v1

--- a/solution.py
+++ b/solution.py
@@ -71,8 +71,436 @@
     return jnp.concatenate([a * cosine + b * sine, b * cosine - a * sine], axis=-1)
 
 
-def gather(v, axis=0):
-    return lax.all_gather(v, "grp", axis=axis, tiled=True)
+SIDE = 2
+CORES = 2
+
+
+def place_of(members):
+    me = lax.axis_index("grp")
+    return me // (SIDE * CORES), (me // CORES) % SIDE, me % CORES
+
+
+def index_of(z, x, c):
+    return (z * SIDE + x) * CORES + c
+
+
+def send(src, dst, sent, got, to):
+    return pltpu.make_async_remote_copy(
+        src_ref=src,
+        dst_ref=dst,
+        send_sem=sent,
+        recv_sem=got,
+        device_id={"grp": to},
+        device_id_type=pl.DeviceIdType.MESH,
+    )
+
+
+def meet(members):
+    barrier = pltpu.get_barrier_semaphore()
+    me = lax.axis_index("grp")
+
+    @pl.loop(1, members)
+    def _(d):
+        pl.semaphore_signal(
+            barrier, 1, device_id={"grp": lax.rem(me + d, members)}, device_id_type=pl.DeviceIdType.MESH
+        )
+
+    pl.semaphore_wait(barrier, members - 1)
+
+
+def gather_steps(src, out, sent, got, members):
+    levels = members // (SIDE * CORES)
+    z, x, c = place_of(members)
+    me = lax.axis_index("grp")
+    up, down = index_of(z + 1, x, c), index_of(z - 1, x, c)
+    side, twin = index_of(z, 1 - x, c), index_of(z, x, 1 - c)
+
+    def copy(slot, kind, to, own=False):
+        return send(src if own else out.at[slot], out.at[slot], sent.at[kind, slot], got.at[slot], to)
+
+    def arrive(slot):
+        copy(slot, 0, twin).wait_recv()
+
+    def first():
+        @pl.when(z < levels - 1)
+        def _():
+            copy(me, 0, up, True).start()
+
+        @pl.when(z > 0)
+        def _():
+            copy(me, 1, down, True).start()
+
+        copy(me, 2, side, True).start()
+        copy(me, 3, twin, True).start()
+
+    def step(s):
+        @pl.when(z >= s)
+        def _():
+            slot = index_of(z - s, x, c)
+            arrive(slot)
+
+            @pl.when(z < levels - 1)
+            def _():
+                copy(slot, 0, up).start()
+
+            copy(slot, 2, side).start()
+            copy(slot, 3, twin).start()
+
+        @pl.when(z + s < levels)
+        def _():
+            slot = index_of(z + s, x, c)
+            arrive(slot)
+
+            @pl.when(z > 0)
+            def _():
+                copy(slot, 1, down).start()
+
+            copy(slot, 2, side).start()
+            copy(slot, 3, twin).start()
+
+    def pass_on(s):
+        @pl.when(z >= s)
+        def _():
+            slot = index_of(z - s, 1 - x, c)
+            arrive(slot)
+            copy(slot, 3, twin).start()
+
+        if s > 0:
+
+            @pl.when(z + s < levels)
+            def _():
+                slot = index_of(z + s, 1 - x, c)
+                arrive(slot)
+                copy(slot, 3, twin).start()
+
+    def finish():
+        @pl.loop(0, members // CORES)
+        def _(i):
+            arrive(i * CORES + 1 - c)
+
+        @pl.loop(0, levels)
+        def _(k):
+            slot = index_of(k, x, c)
+            copy(slot, 2, side).wait_send()
+
+            @pl.when((k <= z) & (z < levels - 1))
+            def _():
+                copy(slot, 0, up).wait_send()
+
+            @pl.when((k >= z) & (z > 0))
+            def _():
+                copy(slot, 1, down).wait_send()
+
+        @pl.loop(0, members // CORES)
+        def _(i):
+            copy(i * CORES + c, 3, twin).wait_send()
+
+    return first, step, pass_on, finish, levels
+
+
+def comm_kernel(*refs, members, n_g, n_e):
+    n = n_g + n_e
+    ins, outs = refs[:n], refs[n : 2 * n]
+    stage = refs[2 * n : 3 * n]
+    local = refs[3 * n]
+    g_sem = refs[3 * n + 1 : 3 * n + 1 + 2 * n_g]
+    e_sem = refs[3 * n + 1 + 2 * n_g :]
+    me = lax.axis_index("grp")
+    own = [r if k < n_g else r.at[me] for k, r in enumerate(ins)]
+    into = [pltpu.make_async_copy(own[k], stage[k], local.at[k]) for k in range(n)]
+    out_of = [pltpu.make_async_copy(stage[k], outs[k].at[me], local.at[k]) for k in range(n)]
+    for k in range(n):
+        into[k].start()
+    meet(members)
+
+    plans = [
+        gather_steps(ins[k], outs[k], g_sem[2 * k], g_sem[2 * k + 1], members) for k in range(n_g)
+    ]
+
+    def exchange_copy(k, d):
+        to = lax.rem(me + d, members)
+        return send(ins[n_g + k].at[to], outs[n_g + k].at[me], e_sem[2 * k].at[d], e_sem[2 * k + 1].at[d], to)
+
+    for first, *_ in plans:
+        first()
+    for k in range(n_e):
+
+        @pl.loop(1, members)
+        def _(d):
+            exchange_copy(k, d).start()
+
+    for k in range(n):
+        into[k].wait()
+        out_of[k].start()
+    levels = members // (SIDE * CORES)
+    for s in range(1, levels):
+        for _, step, *_ in plans:
+            step(s)
+    for s in range(levels):
+        for _, _, pass_on, *_ in plans:
+            pass_on(s)
+    for *_, finish, _ in plans:
+        finish()
+    for k in range(n_e):
+
+        @pl.loop(1, members)
+        def _(d):
+            exchange_copy(k, d).wait()
+
+    for k in range(n):
+        out_of[k].wait()
+
+
+def communicate(gathers, exchanges, members, collective_id):
+    gathers, exchanges = list(gathers), list(exchanges)
+    n_g, n_e = len(gathers), len(exchanges)
+    blocks = [g.shape for g in gathers] + [e.shape[1:] for e in exchanges]
+    kinds = [a.dtype for a in gathers + exchanges]
+    anywhere = pl.BlockSpec(memory_space=pl.ANY)
+    sem = pltpu.SemaphoreType.DMA
+    moved = sum(members * b[0] * b[1] * 2 for b in blocks)
+    outs = pl.pallas_call(
+        functools.partial(comm_kernel, members=members, n_g=n_g, n_e=n_e),
+        in_specs=[anywhere] * (n_g + n_e),
+        out_specs=[anywhere] * (n_g + n_e),
+        out_shape=[jax.ShapeDtypeStruct((members, *b), k) for b, k in zip(blocks, kinds)],
+        scratch_shapes=[pltpu.VMEM(b, k) for b, k in zip(blocks, kinds)]
+        + [sem((n_g + n_e,))]
+        + [sem((4, members)), sem((members,))] * n_g
+        + [sem((members,)), sem((members,))] * n_e,
+        compiler_params=pltpu.CompilerParams(collective_id=collective_id, has_side_effects=True),
+        cost_estimate=pl.CostEstimate(flops=0, bytes_accessed=moved * 8, transcendentals=0),
+        name=f"communicate_{collective_id}",
+    )(*gathers, *exchanges)
+    return outs[:n_g], outs[n_g:]
+
+
+def reduce_kernel(*refs, members, n_e):
+    p, extra, out, landed = refs[0], refs[1 : 1 + n_e], refs[1 + n_e], refs[2 + n_e : 2 + 2 * n_e]
+    twin_in, side_in, up_in, down_in = refs[2 + 2 * n_e : 6 + 2 * n_e]
+    sems = refs[6 + 2 * n_e :]
+    twin_sent, twin_got, side_sent, side_got, up_sent, up_got, down_sent, down_got = sems[:8]
+    stage, local, e_sem = sems[8 : 8 + n_e], sems[8 + n_e : 8 + 2 * n_e], sems[8 + 2 * n_e :]
+    me = lax.axis_index("grp")
+    levels = members // (SIDE * CORES)
+    z, x, c = place_of(members)
+    up, down = index_of(z + 1, x, c), index_of(z - 1, x, c)
+    side, twin = index_of(z, 1 - x, c), index_of(z, x, 1 - c)
+
+    def level(s):
+        orders = []
+        for k in range(levels):
+            far = sorted((v for v in range(levels) if v != k), key=lambda v: (-abs(v - k), v))
+            orders.append(far + [k])
+        v = 0
+        for k in range(levels):
+            v = v + jnp.where(z == k, orders[k][s], 0)
+        return v
+
+    steps = [level(s) for s in range(levels)]
+    into = [pltpu.make_async_copy(extra[k].at[me], stage[k], local[k]) for k in range(n_e)]
+    out_of = [pltpu.make_async_copy(stage[k], landed[k].at[me], local[k]) for k in range(n_e)]
+    for k in range(n_e):
+        into[k].start()
+    meet(members)
+
+    def exchange_copy(k, d):
+        to = lax.rem(me + d, members)
+        return send(extra[k].at[to], landed[k].at[me], e_sem[2 * k].at[d], e_sem[2 * k + 1].at[d], to)
+
+    def to_twin(k, w):
+        return send(
+            p.at[index_of(k, w, 1 - c)], twin_in.at[k * SIDE + w], twin_sent.at[k * SIDE + w], twin_got.at[k * SIDE + w], twin
+        )
+
+    def to_side(k):
+        return send(p.at[index_of(k, 1 - x, c)], side_in.at[k], side_sent.at[k], side_got.at[k], side)
+
+    def to_up(k):
+        return send(p.at[index_of(k, x, c)], up_in.at[k], up_sent.at[k], up_got.at[k], up)
+
+    def to_down(k):
+        return send(p.at[index_of(k, x, c)], down_in.at[k], down_sent.at[k], down_got.at[k], down)
+
+    def add(slot, ref):
+        rows = p.shape[1]
+        chunk = next(r for r in (32, 16, 8) if rows % r == 0)
+
+        @pl.loop(0, rows // chunk)
+        def _(i):
+            at = pl.ds(pl.multiple_of(i * chunk, chunk), chunk)
+            p[slot, at, :] = (p[slot, at, :].astype(F32) + ref[at, :].astype(F32)).astype(p.dtype)
+
+    for k in steps:
+        to_twin(k, x).start()
+        to_twin(k, 1 - x).start()
+    for k in range(n_e):
+
+        @pl.loop(1, members)
+        def _(d):
+            exchange_copy(k, d).start()
+
+        into[k].wait()
+        out_of[k].start()
+    for k in steps:
+        w = 1 - x
+        to_twin(k, w).wait_recv()
+        add(index_of(k, w, c), twin_in.at[k * SIDE + w])
+        to_side(k).start()
+        to_twin(k, x).wait_recv()
+        add(index_of(k, x, c), twin_in.at[k * SIDE + x])
+    for s, k in enumerate(steps):
+        mine = index_of(k, x, c)
+        to_side(k).wait_recv()
+        add(mine, side_in.at[k])
+        if s < levels - 1:
+
+            @pl.when((k > z) & (z > 0))
+            def _():
+                to_up(k).wait_recv()
+                add(mine, up_in.at[k])
+
+            @pl.when((k < z) & (z < levels - 1))
+            def _():
+                to_down(k).wait_recv()
+                add(mine, down_in.at[k])
+
+            @pl.when(k > z)
+            def _():
+                to_up(k).start()
+
+            @pl.when(k < z)
+            def _():
+                to_down(k).start()
+
+        else:
+
+            @pl.when(z > 0)
+            def _():
+                to_up(k).wait_recv()
+                add(mine, up_in.at[k])
+
+            @pl.when(z < levels - 1)
+            def _():
+                to_down(k).wait_recv()
+                add(mine, down_in.at[k])
+
+            out[...] = p[mine]
+    for s, k in enumerate(steps):
+        to_twin(k, x).wait_send()
+        to_twin(k, 1 - x).wait_send()
+        to_side(k).wait_send()
+        if s < levels - 1:
+
+            @pl.when(k > z)
+            def _():
+                to_up(k).wait_send()
+
+            @pl.when(k < z)
+            def _():
+                to_down(k).wait_send()
+
+    for k in range(n_e):
+
+        @pl.loop(1, members)
+        def _(d):
+            exchange_copy(k, d).wait()
+
+        out_of[k].wait()
+
+
+def reduce_blocks(p, extra, members, collective_id):
+    extra = list(extra)
+    n_e = len(extra)
+    anywhere = pl.BlockSpec(memory_space=pl.ANY)
+    _, r, c = p.shape
+    levels = members // (SIDE * CORES)
+    sem = pltpu.SemaphoreType.DMA
+    vmem = pl.BlockSpec(memory_space=pltpu.VMEM)
+    out, *landed = pl.pallas_call(
+        functools.partial(reduce_kernel, members=members, n_e=n_e),
+        in_specs=[vmem] + [anywhere] * n_e,
+        out_specs=[vmem] + [anywhere] * n_e,
+        out_shape=[jax.ShapeDtypeStruct((r, c), p.dtype)] + [jax.ShapeDtypeStruct(e.shape, e.dtype) for e in extra],
+        scratch_shapes=[
+            pltpu.VMEM((members // CORES, r, c), p.dtype),
+            pltpu.VMEM((levels, r, c), p.dtype),
+            pltpu.VMEM((levels, r, c), p.dtype),
+            pltpu.VMEM((levels, r, c), p.dtype),
+        ]
+        + [sem((members // CORES,))] * 2
+        + [sem((levels,))] * 6
+        + [pltpu.VMEM(e.shape[1:], e.dtype) for e in extra]
+        + [sem] * n_e
+        + [sem((members,)), sem((members,))] * n_e,
+        compiler_params=pltpu.CompilerParams(
+            collective_id=collective_id, has_side_effects=True, vmem_limit_bytes=60 * 1024 * 1024
+        ),
+        cost_estimate=pl.CostEstimate(flops=0, bytes_accessed=members * r * c * 16, transcendentals=0),
+        name=f"reduce_{collective_id}",
+    )(p, *extra)
+    return out, landed
+
+
+def spread_kernel(src, out, stage, sent, got, local, *, members, sequences):
+    me, mine = lax.axis_index("grp"), lax.axis_index("rep")
+    barrier = pltpu.get_barrier_semaphore()
+    into = pltpu.make_async_copy(src.at[me], stage, local)
+    out_of = pltpu.make_async_copy(stage, out.at[mine, me], local)
+    into.start()
+
+    def other(n):
+        return lax.rem(mine + n // members, sequences), lax.rem(me + n % members, members)
+
+    @pl.loop(1, members * sequences)
+    def _(n):
+        r, to = other(n)
+        pl.semaphore_signal(barrier, 1, device_id={"rep": r, "grp": to}, device_id_type=pl.DeviceIdType.MESH)
+
+    pl.semaphore_wait(barrier, members * sequences - 1)
+
+    def copy(n):
+        r, to = other(n)
+        return pltpu.make_async_remote_copy(
+            src_ref=src.at[to],
+            dst_ref=out.at[mine, me],
+            send_sem=sent.at[n],
+            recv_sem=got.at[n],
+            device_id={"rep": r, "grp": to},
+            device_id_type=pl.DeviceIdType.MESH,
+        )
+
+    @pl.loop(1, members * sequences)
+    def _(n):
+        copy(n).start()
+
+    into.wait()
+    out_of.start()
+
+    @pl.loop(1, members * sequences)
+    def _(n):
+        copy(n).wait()
+
+    out_of.wait()
+
+
+def spread_blocks(v, members, sequences, collective_id):
+    anywhere = pl.BlockSpec(memory_space=pl.ANY)
+    sem = pltpu.SemaphoreType.DMA
+    return pl.pallas_call(
+        functools.partial(spread_kernel, members=members, sequences=sequences),
+        in_specs=[anywhere],
+        out_specs=anywhere,
+        out_shape=jax.ShapeDtypeStruct((sequences, *v.shape), v.dtype),
+        scratch_shapes=[pltpu.VMEM(v.shape[1:], v.dtype), sem((members * sequences,)), sem((members * sequences,)), sem],
+        compiler_params=pltpu.CompilerParams(collective_id=collective_id, has_side_effects=True),
+        cost_estimate=pl.CostEstimate(flops=0, bytes_accessed=v.size * 16, transcendentals=0),
+        name=f"spread_{collective_id}",
+    )(v)
+
+
+def gather(v):
+    return lax.all_gather(v, "grp", axis=0, tiled=True)
 
 
 def exchange(v):
@@ -81,6 +509,10 @@
 
 def scatter_sum(v):
     return lax.psum_scatter(v, "grp", scatter_dimension=0, tiled=True)
+
+
+def after(v, *others):
+    return lax.optimization_barrier((v, *others))[0]
 
 
 def block_of(length):
@@ -224,10 +656,16 @@
     )(prefix, q, k, v, d, lse, delta)
 
 
-def split_two(v):
-    high = v.astype(BF16)
-    low = (v - high.astype(F32)).astype(BF16)
-    return high, low
+def pack(v):
+    half = v.shape[1] // 2
+    rope = jnp.concatenate([v[:, :half, NOPE:], v[:, half:, NOPE:]], axis=-1)
+    return jnp.concatenate([v[:, :, :NOPE], rope], axis=1)
+
+
+def unpack(v):
+    rows = v.shape[1] * 2 // 3
+    rope = jnp.concatenate([v[:, rows:, :ROPE], v[:, rows:, ROPE:]], axis=1)
+    return jnp.concatenate([v[:, :rows], rope], axis=-1)
 
 
 def per_device(
@@ -272,18 +710,25 @@
     pick = lambda table: lax.dynamic_index_in_dim(table, adapter, 0, keepdims=False)
     qa_down, qa_up, oa_down, oa_up = pick(q_down), pick(q_up), pick(o_down), pick(o_up)
 
-    full_kva = gather(w_kva)
-    full_q = gather(w_q)
+    chosen_by = jnp.sum(
+        (routes[:, :, None] == jnp.arange(experts, dtype=jnp.int32)[None, None, :]).astype(F32), axis=1
+    )
+    (all_kva, all_q, all_router), (kvb_parts, chosen_all) = communicate(
+        [w_kva, w_q, w_router],
+        [
+            w_kvb.reshape(w_kvb.shape[0], members, -1).transpose(1, 0, 2),
+            jnp.broadcast_to(chosen_by.T[:, None, :], (experts, 8, tokens)),
+        ],
+        members,
+        1,
+    )
+    full_kva, full_q, full_router = (v.reshape(-1, v.shape[2]) for v in (all_kva, all_q, all_router))
+    own_kvb = kvb_parts.reshape(KVR, -1)
     hidden_slice = shared_down.shape[0]
-    kvb_cols = w_kvb.shape[1] // members
-    own_kvb = exchange(
-        w_kvb.reshape(w_kvb.shape[0], members, kvb_cols).transpose(1, 0, 2)
-    ).reshape(KVR, kvb_cols)
-    shared = jnp.stack([shared_gate, shared_up], axis=1)
+    shared = after(jnp.stack([shared_gate, shared_up], axis=1), all_q)
     shared = shared.reshape(shared.shape[0], 2, members, hidden_slice).transpose(2, 0, 1, 3)
     own_shared = exchange(shared.reshape(members, -1, 2 * hidden_slice)).reshape(width, 2 * hidden_slice)
-    full_o = gather(w_o)
-    full_router = gather(w_router)
+    full_o = gather(after(w_o, all_q))
 
     positions = me * tokens + jnp.arange(tokens, dtype=jnp.int32)
     cosine, sine = angles(positions, ROPE)
@@ -291,47 +736,37 @@
     latent = dot(normed, full_kva)
     compressed = root_norm(latent[:, :KVR], kv_gain).astype(BF16)
     k_rope = rotate(latent[:, KVR:], cosine, sine).astype(BF16)
-    all_latent = gather(jnp.concatenate([compressed, k_rope], axis=-1))
     q_small = dot(normed, qa_down).astype(BF16)
     query = (dot(normed, full_q) + dot(q_small, qa_up)).reshape(tokens, H, QK)
     query = jnp.concatenate(
         [query[:, :, :NOPE], rotate(query[:, :, NOPE:], cosine[:, None], sine[:, None])], axis=-1
     ).astype(BF16)
-    q_head = exchange(query.transpose(1, 0, 2)).reshape(length, QK)
+    (all_latent,), (q_packed,) = communicate(
+        [jnp.concatenate([compressed, k_rope], axis=-1)], [pack(query.transpose(1, 0, 2))], members, 2
+    )
+    all_latent = all_latent.reshape(length, KVR + ROPE)
+    q_head = unpack(q_packed).reshape(length, QK)
     expanded = dot(all_latent[:, :KVR], own_kvb).astype(BF16)
     k_head = jnp.concatenate([expanded[:, :NOPE], all_latent[:, KVR:]], axis=-1)
     v_head = expanded[:, NOPE:]
     mixture, lse = attend(prefix_len, q_head, k_head, v_head)
-    mixed = (
-        exchange(mixture.astype(BF16).reshape(members, tokens, VD))
-        .transpose(1, 0, 2)
-        .reshape(tokens, H * VD)
-    )
+    _, (mixed,) = communicate([], [mixture.astype(BF16).reshape(members, tokens, VD)], members, 3)
+    mixed = mixed.transpose(1, 0, 2).reshape(tokens, H * VD)
     o_small = dot(mixed, oa_down).astype(BF16)
     middle = inputs + dot(mixed, full_o) + dot(o_small, oa_up)
     ffn_in = root_norm(middle, ffn_gain).astype(BF16)
     route_probs = jax.nn.softmax(dot(ffn_in, full_router), axis=-1)
 
-    lanes = 128
-    high, low = split_two(route_probs)
-    extra = jnp.concatenate(
-        [high, low, jnp.zeros((tokens, lanes - 2 * experts), BF16)], axis=-1
-    )
-    all_in = gather(jnp.concatenate([ffn_in, extra], axis=-1))
-    all_ids = gather(routes)
-    all_c = gather(cotangent)
-    ffn_all = all_in[:, :width]
-    mine = jnp.arange(experts, dtype=jnp.int32)[None, :] == me
-    probs = jnp.sum(
-        jnp.where(
-            mine,
-            all_in[:, width : width + experts].astype(F32)
-            + all_in[:, width + experts : width + 2 * experts].astype(F32),
-            0.0,
-        ),
-        axis=-1,
-    ).reshape(members, tokens)
-    chosen = jnp.any(all_ids == me, axis=-1).reshape(members, tokens)
+    (all_in,), (prob_parts,) = communicate(
+        [ffn_in],
+        [jnp.broadcast_to(route_probs.T[:, None, :], (experts, 8, tokens))],
+        members,
+        4,
+    )
+    all_c = gather(after(cotangent, all_in))
+    ffn_all = all_in.reshape(length, width)
+    probs = prob_parts[:, 0]
+    chosen = chosen_all[:, 0] > 0.5
     order = jnp.arange(tokens, dtype=jnp.int32)
     before = (order[:, None] < order[None, :]).astype(BF16)
     rank = dot(chosen.astype(BF16), before).astype(jnp.int32)
@@ -381,40 +816,41 @@
     d_sup = (d_sh * jax.nn.silu(s_gate)).astype(BF16)
     d_shared = jnp.concatenate([d_sgate, d_sup], axis=-1)
     d_partial = spread(d_rows) + dot_t(d_shared, own_shared)
-    d_gate_all = jnp.sum(jnp.where(place, d_gate[:, :, None], 0.0), axis=1).reshape(length, 1)
-    g_high, g_low = split_two(d_gate_all)
-    d_extra = jnp.concatenate(
-        [
-            jnp.where(mine, g_high, 0).astype(BF16),
-            jnp.where(mine, g_low, 0).astype(BF16),
-            jnp.zeros((length, lanes - 2 * experts), BF16),
-        ],
-        axis=-1,
-    )
-    d_own = scatter_sum(jnp.concatenate([d_partial.astype(BF16), d_extra], axis=-1))
-    d_route = d_own[:, width : width + experts].astype(F32) + d_own[
-        :, width + experts : width + 2 * experts
-    ].astype(F32)
+    d_gate_all = jnp.sum(jnp.where(place, d_gate[:, :, None], 0.0), axis=1)
+    d_own, (d_route,) = reduce_blocks(
+        d_partial.astype(BF16).reshape(members, tokens, width),
+        [jnp.broadcast_to(d_gate_all[:, None, :], (members, 8, tokens))],
+        members,
+        5,
+    )
+    d_route = d_route[:, 0].T
     d_logits = (
         route_probs * (d_route - jnp.sum(route_probs * d_route, axis=-1, keepdims=True))
     ).astype(BF16)
-    d_ffn = d_own[:, :width].astype(F32) + dot_t(d_logits, full_router)
+    d_ffn = d_own.astype(F32) + dot_t(d_logits, full_router)
     d_middle = c32 + norm_back(middle, ffn_gain, d_ffn)
     d_attn = d_middle.astype(BF16)
     grad_oup = t_dot(o_small, d_attn)
     d_osmall = dot_t(d_attn, oa_up).astype(BF16)
     grad_odown = t_dot(d_osmall, mixed)
     d_mixed = (dot_t(d_attn, full_o) + dot_t(d_osmall, oa_down)).astype(BF16)
-    d_head = exchange(d_mixed.reshape(tokens, H, VD).transpose(1, 0, 2)).reshape(length, VD)
+    _, (d_head,) = communicate([], [d_mixed.reshape(tokens, H, VD).transpose(1, 0, 2)], members, 6)
+    d_head = d_head.reshape(length, VD)
     delta = jnp.sum(d_head.astype(F32) * mixture, axis=-1)
     dq, dk, dv = attend_back(
         prefix_len, q_head, k_head, v_head, d_head, lse.reshape(1, length), delta.reshape(1, length)
     )
-    d_query = exchange(dq.astype(BF16).reshape(members, tokens, QK)).transpose(1, 0, 2).astype(F32)
     d_expanded = jnp.concatenate([dk[:, :NOPE], dv], axis=-1).astype(BF16)
-    d_latents = scatter_sum(
-        jnp.concatenate([dot_t(d_expanded, own_kvb), dk[:, NOPE:]], axis=-1).astype(BF16)
-    ).astype(F32)
+    d_latents, (d_query,) = reduce_blocks(
+        jnp.concatenate([dot_t(d_expanded, own_kvb), dk[:, NOPE:]], axis=-1)
+        .astype(BF16)
+        .reshape(members, tokens, KVR + ROPE),
+        [pack(dq.astype(BF16).reshape(members, tokens, QK))],
+        members,
+        7,
+    )
+    d_latents = d_latents.astype(F32)
+    d_query = unpack(d_query).transpose(1, 0, 2).astype(F32)
     d_latent = jnp.concatenate(
         [
             norm_back(latent[:, :KVR], kv_gain, d_latents[:, :KVR]),
@@ -442,9 +878,14 @@
         for g in (grad_qdown, grad_qup, grad_odown, grad_oup)
     ]
     sizes = [g.shape[2] for g in parts]
-    share = jnp.sum(exchange(jnp.concatenate(parts, axis=-1)).astype(F32), axis=0)
-    selector = (jnp.arange(q_down.shape[0], dtype=jnp.int32) == adapter).astype(F32)[:, None, None]
-    summed = lax.psum((selector * share[None]).astype(BF16), "rep").astype(F32)
+    lanes = 128
+    named = jnp.broadcast_to(adapter.astype(BF16), (members, rank_of, lanes))
+    sequences = lax.axis_size("rep")
+    shares = spread_blocks(jnp.concatenate(parts + [named], axis=-1), members, sequences, 8)
+    numbers = shares[:, 0, 0, -1].astype(jnp.int32)
+    share = jnp.sum(shares[..., :-lanes].astype(F32), axis=1)
+    selector = (jnp.arange(q_down.shape[0], dtype=jnp.int32)[:, None] == numbers[None, :]).astype(F32)
+    summed = jnp.sum(selector[:, :, None, None] * share[None], axis=1)
     ends = [sum(sizes[: n + 1]) for n in range(4)]
     outs = [summed[:, :, e - s : e] for e, s in zip(ends, sizes)]
     return (

time: 1340 us -> 992 us (0.74)
  waiting for transfers between devices: 630 us -> 81.2 us
  Pallas kernels: 49.3 us -> 529 us
  blocking collectives: 113 us -> 0 us
  other arithmetic: 137 us -> 50.8 us
  local copies, waits for them, and re-layouts: 84 us -> 43.3 us
  starting transfers between devices: 37.6 us -> 5.12 us
    pallas_call x0 -> x8, Pallas kernels: none -> 480 us  [the longest x5 319 us: communicate(): pl.pallas_call(functools.partial(comm_kernel, members=members, n_g=n_g, n...]
    reduce_scatter x3 -> x1, waiting for transfers between devices: 307 us -> 0.01 us  [scatter_sum(): return lax.psum_scatter(v, 'grp', scatter_dimension=0, tiled=True)]
    all_gather x6 -> x2, waiting for transfers between devices: 266 us -> 30.9 us  [gather(): return lax.all_gather(v, 'grp', axis=0, tiled=True)]
    all_gather x2 -> x0, blocking collectives: 113 us -> none  [gather(): return lax.all_gather(v, 'grp', axis=axis, tiled=True)]
    reduce_or x1 -> x0, other arithmetic: 65.3 us -> none  [per_device(): chosen = jnp.any(all_ids == me, axis=-1).reshape(members, tokens)]
    all_to_all x7 -> x1, starting transfers between devices: 36.9 us -> 5 us  [exchange(): return lax.all_to_all(v, 'grp', split_axis=0, concat_axis=0, tiled=True)]
    reshape x3 -> x1, local copies, waits for them, and re-layouts: 25 us -> 1.68 us  [per_device(): w_kvb.reshape(w_kvb.shape[0], members, -1).transpose(1, 0, 2)]
    all_to_all x7 -> x1, waiting for transfers between devices: 50.6 us -> 50.2 us  [exchange(): return lax.all_to_all(v, 'grp', split_axis=0, concat_axis=0, tiled=True)]
  transfers between devices with their start and end apart: 17 -> 4, of which waited for: 12 -> 2; matrix products, arithmetic and copies ran while one was open for 15% -> 18% of each run, Pallas kernels for 2% -> 23%
where the time goes in v2:
time: 992 us; the launch traced here: 979 us
  Pallas kernels  529 us (53%)
  matrix products  252 us (25%)
  waiting for transfers between devices  81.2 us (8%)
  other arithmetic  50.8 us (5%)
  local copies, waits for them, and re-layouts  43.3 us (4%)
  between operations  16.5 us (2%)
    pallas_call x5, Pallas kernels, communicate(): pl.pallas_call(functools.partial(comm_kernel, members=members, n_g=n_g, n...  319 us
    pallas_call x2, Pallas kernels, reduce_blocks(): pl.pallas_call(functools.partial(reduce_kernel, members=members, n_e=n_e)...  139 us
    dot_general x14, matrix products, dot_t(): lax.dot_general(former, latter, (((1,), (1,)), ((), ())), preferred_eleme...  111 us
    dot_general x16, matrix products, dot(): return jnp.dot(former, latter, preferred_element_type=F32)  98.3 us
    all_to_all x1, waiting for transfers between devices, exchange(): return lax.all_to_all(v, 'grp', split_axis=0, concat_axis=0, tiled=True)  50.2 us
    all_gather x2, waiting for transfers between devices, gather(): return lax.all_gather(v, 'grp', axis=0, tiled=True)  30.9 us
    pallas_call x1, Pallas kernels, attend_back(): pl.pallas_call(functools.partial(attend_back_kernel, block=block, factor=...  28.5 us
    dot_general x2, matrix products, spread(): lax.dot_general(select, rows.reshape(members, slots, width), (((1,), (1,)...  23.3 us
  transfers between devices with their start and end apart: 4, of which 2 were waited for; matrix products, arithmetic and copies ran while one was open for 18% of the time, Pallas kernels for 23%

profile of v2, /device:TPU:0, one launch (start us, length us, event | category | flops | bytes accessed | tf_op | source)
XLA Modules:
  0.0 978.5 jit_solution(7794783937105497639)
XLA Ops:
  9.5 1.7 copy.97.refs_0_
  13.5 101.4 %communicate_1.1 = (bf16[16,128,576]{2,1,0:T(8,128)(2,1)}, bf16[16,128,3072]{2,1,0:T(8,128)(2,1)}, bf16[16,128,16]{2,1,0:T(8,128)(2,1)}, bf16[16,32,256]{2,1,0:T(8,128)(2,1)}, f32[16,8,192]{2,1,0:T(8,128)}) custom-call(bf16[128,576]{1,0:T(8,128)(2,1)} %copy.97.refs_0_, bf16[128,3072]{1,0:T(8,128)(2,1)} %refs_1_.1, bf16[128,16]{1,0:T(8,128)(2,1)} %copy.98.refs_2_, ...), custom_call_target="tpu_custom_call" | custom-call | bytes 122552320 | tf_op jit(solution)/shard_map/communicate_1/pallas_call | solution.py:262
  118.4 6.6 fusion.145
  125.6 2.6 reshape.335
  130.1 2.7 fusion.147
  139.2 88.9 %communicate_2.1 = (bf16[16,192,576]{2,1,0:T(8,128)(2,1)}, bf16[16,288,128]{2,1,0:T(8,128)(2,1)}) custom-call(bf16[192,576]{1,0:T(8,128)(2,1)} %pad_maximum_fusion.3.refs_0_, bf16[16,288,128]{2,1,0:T(8,128)(2,1)} %maximum_maximum_fusion.1.refs_1_), custom_call_target="tpu_custom_call" | custom-call | bytes 37748736 | tf_op jit(solution)/shard_map/communicate_2/pallas_call | solution.py:262
  236.8 20.9 %attend.1 = (f32[3072,128]{1,0:T(8,128)}, f32[3072,1]{1,0:T(8,128)}) custom-call(s32[1]{0:T(128)S(6)} %copy.175.prefix_ref, bf16[3072,192]{1,0:T(8,128)(2,1)} %bitcast.288, bf16[3072,192]{1,0:T(8,128)(2,1)} %pad_maximum_fusion.1.k_ref, bf16[3072,128]{1,0:T(8,128)(2,1)} %get-tuple-element.62.v_ref), custom_call_target="tpu_custom_call" | custom-call | flops 3019898880 | bytes 3072000 | tf_op jit(solution)/shard_map/attend/pallas_call | solution.py:564
  257.7 2.4 convert_element_type.227
  260.1 27.9 %communicate_3.1 = bf16[16,192,128]{2,1,0:T(8,128)(2,1)} custom-call(bf16[16,192,128]{2,1,0:T(8,128)(2,1)} %bitcast.280), custom_call_target="tpu_custom_call" | custom-call | bytes 6291456 | tf_op jit(solution)/shard_map/communicate_3/pallas_call | solution.py:262
  289.4 5.4 convolution_add_fusion.6
  299.9 84.9 %communicate_4.1 = (bf16[16,192,2048]{2,1,0:T(8,128)(2,1)}, f32[16,8,192]{2,1,0:T(8,128)}) custom-call(bf16[192,2048]{1,0:T(8,128)(2,1)} %copy-done.6, f32[16,8,192]{2,1,0:T(8,128)} %broadcast_in_dim.35.refs_1_), custom_call_target="tpu_custom_call" | custom-call | bytes 101056512 | tf_op jit(solution)/shard_map/communicate_4/pallas_call | solution.py:262
  386.9 5.0 all-to-all-start
  393.1 50.2 %all-to-all-done = bf16[16,128,352]{1,2,0:T(8,128)(2,1)S(1)} async-done(((bf16[16,128,352]{1,2,0:T(8,128)(2,1)}), bf16[16,128,352]{1,2,0:T(8,128)(2,1)S(1)}, u32[]{:S(2)}, u32[]{:S(2)}) %all-to-all-start) | async-done | bytes 1441824 | tf_op jit(solution)/shard_map/all_to_all | solution.py:507
  443.5 1.9 slice.156
  445.4 6.5 convolution_convert_fusion.1
  452.9 4.3 fusion.70
  457.2 13.5 %fusion.13 = f32[1536,1408]{1,0:T(8,128)} fusion(bf16[1536,2048]{1,0:T(8,128)(2,1)S(1)} %bitcast.267, bf16[1,2048,1408]{2,1,0:T(8,128)(2,1)} %param.39), kind=kOutput, calls=%fused_computation.25 | convolution fusion | flops 8858370048 | bytes 20709376 | tf_op jit(solution)/shard_map/dot_general | solution.py:23
  470.7 12.1 %fusion.9 = f32[1536,1408]{1,0:T(8,128)} fusion(bf16[1536,2048]{1,0:T(8,128)(2,1)S(1)} %bitcast.268, bf16[1,2048,1408]{2,1,0:T(8,128)(2,1)S(1)} %bitcast.312), kind=kOutput, calls=%fused_computation.21 | convolution fusion | flops 8858370048 | bytes 20709376 | tf_op jit(solution)/shard_map/dot_general | solution.py:23
  482.8 30.9 %all-gather.5.cloned.1.call-done = bf16[3072,2048]{1,0:T(8,128)(2,1)} async-done(((bf16[192,2048]{1,0:T(8,128)(2,1)}), bf16[3072,2048]{1,0:T(8,128)(2,1)}) %all-gather.5.cloned.1.call-update) | async-done | bytes 12582928 | tf_op jit(solution)/shard_map/all_gather | solution.py:503
  513.8 8.9 convert_convert_fusion
  522.7 20.4 %fusion.3 = (f32[1536]{0:T(1024)S(1)}, bf16[1536,2048]{1,0:T(8,128)(2,1)}) fusion(f32[16,96,2048]{2,1,0:T(8,128)} %convert_convert_fusion, bf16[1,1408,2048]{2,1,0:T(8,128)(2,1)} %param.41, f32[1536,1408]{1,0:T(8,128)} %fusion.9, f32[1536,1408]{1,0:T(8,128)} %fusion.13), kind=kOutput, calls=%fused_computation.7 | convolution fusion | flops 8883927040 | bytes 41949184 | tf_op jit(solution)/shard_map/dot_general | solution.py:23
  543.1 2.9 select_reduce_fusion
  546.1 3.9 fusion.2
  550.0 10.1 %fusion.44 = f32[16,192,2048]{2,1,0:T(8,128)} fusion(bf16[16,96,2048]{2,1,0:T(8,128)(2,1)S(1)} %bitcast.261, s32[16,192]{1,0:T(8,128)S(1)} %convolution_convert_fusion.8, pred[16,192]{1,0:T(8,128)(4,1)S(1)} %bitcast.295), kind=kOutput, calls=%fused_computation.94 | convolution fusion | flops 1208549376 | bytes 31472640 | tf_op jit(solution)/shard_map/dot_general | solution.py:786
  560.0 9.0 fusion.157
  569.1 11.4 %multiply_convert_fusion.8 = (bf16[3072,176]{0,1:T(8,128)(2,1)}, bf16[3072,176]{0,1:T(8,128)(2,1)}, f32[3072,176]{0,1:T(8,128)}) fusion(f32[3072,176]{0,1:T(8,128)S(1)} %fusion.157, f32[3072,176]{0,1:T(8,128)S(1)} %fusion.70, bf16[3072,2048]{1,0:T(8,128)(2,1)} %bitcast.263, bf16[2048,352]{0,1:T(8,128)(2,1)S(1)} %copy-done.28), kind=kOutput, calls=%fused_computation.52 | convolution fusion | flops 2221621248 | bytes 21954560 | tf_op jit(solution)/shard_map/dot_general | solution.py:23
  580.5 15.8 %fusion.1 = bf16[3072,2048]{1,0:T(8,128)(2,1)} fusion(f32[16,192,2048]{2,1,0:T(8,128)} %fusion.44, bf16[176,2048]{1,0:T(8,128)(2,1)} %param.38, f32[3072,176]{0,1:T(8,128)S(1)} %fusion.70, f32[3072,176]{0,1:T(8,128)} %get-tuple-element.93), kind=kOutput, calls=%fused_computation.3 | convolution fusion | flops 2230419456 | bytes 42795008 | tf_op jit(solution)/shard_map/dot_general | solution.py:23
  598.8 9.8 %multiply_convert_fusion = bf16[16,96,2048]{2,1,0:T(8,128)(2,1)} fusion(f32[16,96,2048]{2,1,0:T(8,128)} %convert_convert_fusion, f32[16,96]{1,0:T(8,128)S(1)} %get-tuple-element.49), kind=kLoop, calls=%fused_computation.9 | loop fusion | flops 6291456 | bytes 18880512 | tf_op jit(solution)/shard_map/convert_element_type | solution.py:809
  608.6 16.4 %fusion.5 = f32[1536,1408]{1,0:T(8,128)} fusion(bf16[1536,2048]{1,0:T(8,128)(2,1)} %bitcast.274, bf16[1,1408,2048]{2,1,0:T(8,128)(2,1)} %param.41), kind=kOutput, calls=%fused_computation.17 | convolution fusion | flops 8858370048 | bytes 20709376 | tf_op jit(solution)/shard_map/dot_general | solution.py:27
  625.0 23.9 %fusion.11 = f32[1536,2048]{1,0:T(8,128)} fusion(bf16[1,2048,1408]{2,1,0:T(8,128)(2,1)} %param.39, f32[1536,1408]{1,0:T(8,128)} %fusion.13, f32[1536,1408]{1,0:T(8,128)} %fusion.5, f32[1536,1408]{1,0:T(8,128)} %fusion.9), kind=kOutput, calls=%fused_computation.23 | convolution fusion | flops 8879996928 | bytes 44302336 | tf_op jit(solution)/shard_map/dot_general | solution.py:27
  649.0 21.0 %add_convert_fusion = bf16[1536,2048]{1,0:T(8,128)(2,1)} fusion(f32[1536,2048]{1,0:T(8,128)} %fusion.11, bf16[1,2048,1408]{2,1,0:T(8,128)(2,1)} %param.40, f32[1536,1408]{1,0:T(8,128)} %fusion.5, f32[1536,1408]{1,0:T(8,128)} %fusion.13), kind=kOutput, calls=%fused_computation.8 | convolution fusion | flops 8877637632 | bytes 41943040 | tf_op jit(solution)/shard_map/dot_general | solution.py:27
  670.0 13.2 %fusion.41 = f32[16,192,2048]{2,1,0:T(8,128)} fusion(bf16[16,96,2048]{2,1,0:T(8,128)(2,1)} %bitcast.269, s32[16,192]{1,0:T(8,128)S(1)} %convolution_convert_fusion.8, pred[16,192]{1,0:T(8,128)(4,1)S(1)} %bitcast.296), kind=kOutput, calls=%fused_computation.93 | convolution fusion | flops 1208549376 | bytes 31472640 | tf_op jit(solution)/shard_map/dot_general | solution.py:786
  683.3 15.1 %fusion = bf16[3072,2048]{1,0:T(8,128)(2,1)} fusion(f32[16,192,2048]{2,1,0:T(8,128)} %fusion.41, bf16[3072,176]{0,1:T(8,128)(2,1)} %get-tuple-element.51, bf16[3072,176]{0,1:T(8,128)(2,1)} %get-tuple-element.50, bf16[16,128,352]{1,2,0:T(8,128)(2,1)S(1)} %copy-done.5), kind=kOutput, calls=%fused_computation.1 | convolution fusion | flops 4446093312 | bytes 41353216 | tf_op jit(solution)/shard_map/dot_general | solution.py:27
  699.1 88.9 %reduce_5.1 = (bf16[192,2048]{1,0:T(8,128)(2,1)}, f32[16,8,192]{2,1,0:T(8,128)}) custom-call(bf16[16,192,2048]{2,1,0:T(8,128)(2,1)} %bitcast.260, f32[16,8,192]{2,1,0:T(8,128)} %broadcast_in_dim.46.refs_1_), custom_call_target="tpu_custom_call" | custom-call | bytes 100663296 | tf_op jit(solution)/shard_map/reduce_5/pallas_call | solution.py:420
  789.0 2.9 multiply_reduce_fusion.1
  791.9 3.4 subtract_add_fusion
  798.3 6.3 fusion.136
  806.9 16.0 %communicate_6.1 = bf16[16,192,128]{2,1,0:T(8,128)(2,1)} custom-call(bf16[16,192,128]{2,1,0:T(8,128)(2,1)} %bitcast.278), custom_call_target="tpu_custom_call" | custom-call | bytes 6291456 | tf_op jit(solution)/shard_map/communicate_6/pallas_call | solution.py:262
  822.9 2.7 multiply_reduce_fusion
  825.6 28.5 %attend_back.1 = (f32[3072,192]{1,0:T(8,128)}, f32[3072,192]{1,0:T(8,128)}, f32[3072,128]{1,0:T(8,128)}) custom-call(s32[1]{0:T(128)S(6)} %copy.175.prefix_ref, bf16[3072,192]{1,0:T(8,128)(2,1)} %bitcast.289, bf16[3072,192]{1,0:T(8,128)(2,1)} %pad_maximum_fusion.1.k_ref, bf16[3072,128]{1,0:T(8,128)(2,1)} %get-tuple-element.62.v_ref, ...), custom_call_target="tpu_custom_call" | custom-call | flops 7851737088 | bytes 6144000 | tf_op jit(solution)/shard_map/attend_back/pallas_call | solution.py:630
  854.1 2.0 convert.49
  856.2 2.4 copy-done.16
  861.6 2.4 pad_maximum_fusion.refs_0_
  865.3 49.9 %reduce_7.1 = (bf16[192,576]{1,0:T(8,128)(2,1)}, bf16[16,288,128]{2,1,0:T(8,128)(2,1)}) custom-call(bf16[16,192,576]{2,1,0:T(8,128)(2,1)} %pad_maximum_fusion.refs_0_, bf16[16,288,128]{2,1,0:T(8,128)(2,1)} %maximum_maximum_fusion.2.refs_1_), custom_call_target="tpu_custom_call" | custom-call | bytes 28311552 | tf_op jit(solution)/shard_map/reduce_7/pallas_call | solution.py:420
  920.6 2.1 copy.112
  922.7 3.0 convert_element_type.263
  925.7 10.1 %fusion.158 = f32[192,2048]{1,0:T(8,128)} fusion(bf16[192,3072]{1,0:T(8,128)(2,1)S(1)} %convert_element_type.263, bf16[2048,3072]{1,0:T(8,128)(2,1)} %bitcast.310), kind=kOutput, calls=%fused_computation.247 | convolution fusion | flops 2415919104 | bytes 15335424 | tf_op jit(solution)/shard_map/dot_general | solution.py:27
  941.6 21.8 %spread_8.1 = bf16[2,16,16,704]{3,2,1,0:T(8,128)(2,1)} custom-call(bf16[16,16,704]{2,1,0:T(8,128)(2,1)} %concatenate.85.src), custom_call_target="tpu_custom_call" | custom-call | bytes 2883584 | tf_op jit(solution)/shard_map/spread_8/pallas_call | solution.py:490
  (263 shorter events, 67.7 us)
Async XLA Ops:
  7.2 117.9 %copy-start = (bf16[8,16,3072]{2,1,0:T(8,128)(2,1)S(1)}, bf16[8,16,3072]{2,1,0:T(8,128)(2,1)}, u32[]{:S(2)}) copy-start(bf16[8,16,3072]{2,1,0:T(8,128)(2,1)} %param.43) | copy-start | bytes 2359300
  7.2 109.2 %copy-start.7 = (bf16[1,192,2048]{2,1,0:T(8,128)(2,1)S(1)}, bf16[1,192,2048]{2,1,0:T(8,128)(2,1)}, u32[]{:S(2)}) copy-start(bf16[1,192,2048]{2,1,0:T(8,128)(2,1)} %param.23) | copy-start | bytes 2359300
  7.2 110.0 %copy-start.60 = (f32[2048]{0:T(1024)S(1)}, f32[2048]{0:T(1024)}, u32[]{:S(2)}) copy-start(f32[2048]{0:T(1024)} %param.28) | copy-start | bytes 24580
  7.2 282.2 %all-gather.3.cloned.1.call-start = ((), (), s32[]{:S(2)}) async-start(), calls=%async_computation.2 | async-start | bytes 8912896 | tf_op jit(solution)/shard_map/all_gather | solution.py:503
  115.0 398.7 %all-gather.5.cloned.1.call-start = ((), (), s32[]{:S(2)}) async-start(), calls=%async_computation.4 | async-start | bytes 13369344 | tf_op jit(solution)/shard_map/all_gather | solution.py:503
  117.2 12.8 %copy-start.65 = (f32[192]{0:T(256)}, f32[192]{0:T(256)S(1)}, u32[]{:S(2)}) copy-start(f32[192]{0:T(256)S(1)} %get-tuple-element.82) | copy-start | bytes 2308
  118.4 6.6 copy-start.46
  130.0 3.2 copy-start.3
  132.8 3.6 copy-start.10
  289.4 5.5 copy-start.48
  297.7 87.2 %copy-start.34 = (bf16[128,2816]{1,0:T(8,128)(2,1)S(1)}, bf16[128,2816]{1,0:T(8,128)(2,1)}, u32[]{:S(2)}) copy-start(bf16[128,2816]{1,0:T(8,128)(2,1)} %param.36) | copy-start | bytes 2162692
  297.7 87.5 %copy-start.35 = (bf16[128,2816]{1,0:T(8,128)(2,1)S(1)}, bf16[128,2816]{1,0:T(8,128)(2,1)}, u32[]{:S(2)}) copy-start(bf16[128,2816]{1,0:T(8,128)(2,1)} %param.37) | copy-start | bytes 2162692
  386.9 56.3 %all-to-all-start = ((bf16[16,128,352]{1,2,0:T(8,128)(2,1)}), bf16[16,128,352]{1,2,0:T(8,128)(2,1)S(1)}, u32[]{:S(2)}, u32[]{:S(2)}) async-start(bf16[16,128,352]{1,2,0:T(8,128)(2,1)} %bitcast.275), calls=%async_computation | async-start | bytes 2883584 | tf_op jit(solution)/shard_map/all_to_all | solution.py:507
  392.0 399.9 %reduce-scatter.2.cloned.1.call-start = ((), (), s32[]{:S(2)}) async-start(), calls=%async_computation.3 | async-start | bytes 13369344 | tf_op jit(solution)/shard_map/reduce_scatter | solution.py:511
  443.3 8.6 copy-start.4
  443.3 8.7 slice-start
  443.5 8.5 copy-start.27
  445.3 6.6 slice-start.1
  445.4 7.5 slice-start.2
  452.9 17.8 %slice-start.5 = ((s8[5767168]{0:T(1024)(128)(4,1)}), s8[1572864]{0:T(1024)(128)(4,1)S(1)}, s32[]{:S(2)}) async-start(s8[5767168]{0:T(1024)(128)(4,1)} %bitcast.311), calls=%async_computation.10 | async-start | bytes 3145728
  457.2 13.6 %slice-start.6 = ((s8[5767168]{0:T(1024)(128)(4,1)}), s8[4194304]{0:T(1024)(128)(4,1)S(1)}, s32[]{:S(2)}) async-start(s8[5767168]{0:T(1024)(128)(4,1)} %bitcast.311), calls=%async_computation.11 | async-start | bytes 8388608
  549.9 10.1 %copy-start.33 = (bf16[176,2048]{1,0:T(8,128)(2,1)S(1)}, bf16[176,2048]{1,0:T(8,128)(2,1)}, u32[]{:S(2)}) copy-start(bf16[176,2048]{1,0:T(8,128)(2,1)} %param.38) | copy-start | bytes 2162692
  560.0 9.0 copy-start.28
  670.0 13.3 %copy-start.5 = (bf16[16,128,352]{1,2,0:T(8,128)(2,1)S(1)}, bf16[16,128,352]{1,2,0:T(8,128)(2,1)}, u32[]{:S(2)}) copy-start(bf16[16,128,352]{1,2,0:T(8,128)(2,1)} %copy-done.4) | copy-start | bytes 4325380
  683.3 15.1 %copy-start.43 = (f32[16,192]{1,0:T(8,128)S(1)}, f32[16,192]{1,0:T(8,128)}, u32[]{:S(2)}) copy-start(f32[16,192]{1,0:T(8,128)} %get-tuple-element.48) | copy-start | bytes 36868
  699.1 89.8 %copy-start.37 = (f32[192,16]{0,1:T(8,128)S(1)}, f32[192,16]{0,1:T(8,128)}, u32[]{:S(2)}) copy-start(f32[192,16]{0,1:T(8,128)} %copy-done.36) | copy-start | bytes 36868
  699.1 89.8 %copy-start.51 = (f32[192]{0:T(256)S(1)}, f32[192]{0:T(256)}, u32[]{:S(2)}) copy-start(f32[192]{0:T(256)} %copy-done.50) | copy-start | bytes 2308
  699.1 89.8 %copy-start.55 = (f32[192]{0:T(256)S(1)}, f32[192]{0:T(256)}, u32[]{:S(2)}) copy-start(f32[192]{0:T(256)} %copy-done.54) | copy-start | bytes 2308
  699.1 89.9 %copy-start.2 = (f32[192,2048]{1,0:T(8,128)S(1)}, f32[192,2048]{1,0:T(8,128)}, u32[]{:S(2)}) copy-start(f32[192,2048]{1,0:T(8,128)} %copy-done.1) | copy-start | bytes 4718596
  699.1 89.9 %copy-start.21 = (bf16[16,128,16]{2,1,0:T(8,128)(2,1)S(1)}, bf16[16,128,16]{2,1,0:T(8,128)(2,1)}, u32[]{:S(2)}) copy-start(bf16[16,128,16]{2,1,0:T(8,128)(2,1)} %get-tuple-element.35) | copy-start | bytes 196612
  699.1 89.9 %copy-start.45 = (f32[2048]{0:T(1024)S(1)}, f32[2048]{0:T(1024)}, u32[]{:S(2)}) copy-start(f32[2048]{0:T(1024)} %param.30) | copy-start | bytes 24580
  789.0 2.9 copy-start.18
  789.0 2.9 copy-start.59
  789.0 2.9 copy-start.68
  791.9 4.7 copy-start.49
  865.3 51.0 %copy-start.11 = (f32[192,576]{1,0:T(8,128)S(1)}, f32[192,576]{1,0:T(8,128)}, u32[]{:S(2)}) copy-start(f32[192,576]{1,0:T(8,128)} %copy-done.10) | copy-start | bytes 1327108
  865.3 51.0 %copy-start.53 = (f32[512]{0:T(512)S(1)}, f32[512]{0:T(512)}, u32[]{:S(2)}) copy-start(f32[512]{0:T(512)} %param.29) | copy-start | bytes 6148
  865.3 51.8 %copy-start.63 = (f32[192]{0:T(256)S(1)}, f32[192]{0:T(256)}, u32[]{:S(2)}) copy-start(f32[192]{0:T(256)} %copy-done.62) | copy-start | bytes 2308
  865.3 51.8 %copy-start.71 = (f32[32]{0:T(128)S(1)}, f32[32]{0:T(128)}, u32[]{:S(2)}) copy-start(f32[32]{0:T(128)} %copy-done.70) | copy-start | bytes 388
  915.2 3.0 copy-start.22
  925.6 10.5 %copy-start.47 = (bf16[192,16]{0,1:T(8,128)(2,1)S(1)}, bf16[192,16]{0,1:T(8,128)(2,1)}, u32[]{:S(2)}) copy-start(bf16[192,16]{0,1:T(8,128)(2,1)} %copy-done.46) | copy-start | bytes 18436
  939.7 27.5 %copy-start.69 = (f32[192]{0:T(256)S(1)}, f32[192]{0:T(256)}, u32[]{:S(2)}) copy-start(f32[192]{0:T(256)} %multiply_reduce_fusion.4) | copy-start | bytes 2308
  941.6 27.3 %copy-start.41 = (bf16[192,32]{1,0:T(8,128)(2,1)S(1)}, bf16[192,32]{1,0:T(8,128)(2,1)}, u32[]{:S(2)}) copy-start(bf16[192,32]{1,0:T(8,128)(2,1)} %get-tuple-element.71) | copy-start | bytes 36868
  963.4 3.8 copy-start.26
  965.6 3.0 copy-start.12
  965.6 3.0 copy-start.15
  965.7 3.0 copy-start.57
  965.7 3.0 copy-start.67
  (35 other events, 58.3 us)
Sparse Core Ops, SparseCore 0:
  115.1 100.5 all-gather.2
  385.0 128.6 all-gather.4
  596.4 136.1 reduce-scatter.1

commit v3 on v1

--- a/solution.py
+++ b/solution.py
@@ -48,11 +48,6 @@
     )
 
 
-def gated_slope(v):
-    logistic = jax.nn.sigmoid(v)
-    return logistic * (1.0 + v * (1.0 - logistic))
-
-
 def angles(positions, width):
     frequency = 10000.0 ** (-jnp.arange(0, width, 2, dtype=F32) / width)
     phases = positions.astype(F32)[:, None] * frequency[None, :]
@@ -71,8 +66,529 @@
     return jnp.concatenate([a * cosine + b * sine, b * cosine - a * sine], axis=-1)
 
 
-def gather(v, axis=0):
-    return lax.all_gather(v, "grp", axis=axis, tiled=True)
+SIDE = 2
+CORES = 2
+MESH = pl.DeviceIdType.MESH
+
+
+def place_of():
+    me = lax.axis_index("grp")
+    return me // (SIDE * CORES), (me // CORES) % SIDE, me % CORES
+
+
+def index_of(z, x, c):
+    return (z * SIDE + x) * CORES + c
+
+
+def send(src, dst, sent, got, to):
+    return pltpu.make_async_remote_copy(
+        src_ref=src,
+        dst_ref=dst,
+        send_sem=sent,
+        recv_sem=got,
+        device_id=to if isinstance(to, dict) else {"grp": to},
+        device_id_type=MESH,
+    )
+
+
+def meet(members, partner=None):
+    barrier = pltpu.get_barrier_semaphore()
+    me = lax.axis_index("grp")
+
+    @pl.loop(1, members)
+    def _(d):
+        pl.semaphore_signal(barrier, 1, device_id={"grp": lax.rem(me + d, members)}, device_id_type=MESH)
+
+    if partner is not None:
+        pl.semaphore_signal(barrier, 1, device_id=partner, device_id_type=MESH)
+    pl.semaphore_wait(barrier, members - 1 + (partner is not None))
+
+
+def pick_from(table, z, s):
+    v = 0
+    for i, row in enumerate(table):
+        for j, entry in enumerate(row):
+            if entry:
+                v = v + jnp.where((z == i) & (s == j), entry, 0)
+    return v
+
+
+def near_first(levels):
+    return [sorted(range(levels), key=lambda v: (abs(v - k), v)) for k in range(levels)]
+
+
+def far_first(levels):
+    return [sorted((v for v in range(levels) if v != k), key=lambda v: (-abs(v - k), v)) + [k] for k in range(levels)]
+
+
+class Gather:
+    def __init__(self, src, out, sent, got, members, split=0):
+        self.src, self.out, self.sent, self.got = src, out, sent, got
+        self.members, self.split = members, split
+        self.levels = members // (SIDE * CORES)
+        self.z, self.x, self.c = z, x, c = place_of()
+        self.me = lax.axis_index("grp")
+        self.up, self.down = index_of(z + 1, x, c), index_of(z - 1, x, c)
+        self.side, self.twin = index_of(z, 1 - x, c), index_of(z, x, 1 - c)
+        if split:
+            rows = src.shape[0]
+            rep = lax.axis_index("rep")
+            odd = rep % 2
+            self.partner = {"rep": rep + 1 - 2 * odd, "grp": self.me}
+            self.window = pl.ds(pl.multiple_of(odd * split, 16), rows - split)
+            self.given = pl.ds(pl.multiple_of(odd * (rows - split), 16), split)
+            self.lacked = pl.ds(pl.multiple_of((1 - odd) * (rows - split), 16), split)
+
+    def copy(self, slot, kind, to, own=False, rows=None):
+        rows = rows or (self.window if self.split else None)
+        other = rows is not None and self.split and rows is not self.window
+        src = self.src if own else self.out.at[slot]
+        dst = self.out.at[slot]
+        if rows is not None:
+            src, dst = src.at[rows], dst.at[rows]
+        return send(src, dst, self.sent.at[kind, slot], self.got.at[int(bool(other)), slot], to)
+
+    def arrive(self, slot):
+        self.copy(slot, 0, self.twin).wait_recv()
+
+    def to_partner(self, slot):
+        return self.copy(slot, 4, self.partner, rows=self.given)
+
+    def lacked_to_twin(self, slot, own=False):
+        return self.copy(slot, 5, self.twin, own, rows=self.lacked)
+
+    def first(self):
+        @pl.when(self.z < self.levels - 1)
+        def _():
+            self.copy(self.me, 0, self.up, True).start()
+
+        @pl.when(self.z > 0)
+        def _():
+            self.copy(self.me, 1, self.down, True).start()
+
+        self.copy(self.me, 2, self.side, True).start()
+        self.copy(self.me, 3, self.twin, True).start()
+        if self.split:
+            self.lacked_to_twin(self.me, True).start()
+
+    def relay(self, s):
+        @pl.when(self.z >= s)
+        def _():
+            slot = index_of(self.z - s, self.x, self.c)
+            self.arrive(slot)
+
+            @pl.when(self.z < self.levels - 1)
+            def _():
+                self.copy(slot, 0, self.up).start()
+
+            self.spread(slot)
+
+        @pl.when(self.z + s < self.levels)
+        def _():
+            slot = index_of(self.z + s, self.x, self.c)
+            self.arrive(slot)
+
+            @pl.when(self.z > 0)
+            def _():
+                self.copy(slot, 1, self.down).start()
+
+            self.spread(slot)
+
+    def spread(self, slot):
+        self.copy(slot, 2, self.side).start()
+        self.copy(slot, 3, self.twin).start()
+        if self.split:
+            self.to_partner(slot).start()
+
+    def pass_on(self, k):
+        slot = index_of(k, 1 - self.x, self.c)
+        self.arrive(slot)
+        self.copy(slot, 3, self.twin).start()
+        if self.split:
+            self.to_partner(slot).start()
+
+    def take_lacked(self, k, x):
+        slot = index_of(k, x, self.c)
+
+        @pl.when(slot != self.me)
+        def _():
+            self.copy(slot, 4, self.partner, rows=self.lacked).wait_recv()
+            self.lacked_to_twin(slot).start()
+
+    def take_twin(self, k):
+        for x in range(SIDE):
+            self.arrive(index_of(k, x, 1 - self.c))
+
+    def take_twin_lacked(self):
+        @pl.loop(0, self.members // CORES)
+        def _(i):
+            self.lacked_to_twin(i * CORES + 1 - self.c).wait_recv()
+
+    def finish(self):
+        @pl.loop(0, self.levels)
+        def _(k):
+            slot = index_of(k, self.x, self.c)
+            self.copy(slot, 2, self.side).wait_send()
+
+            @pl.when((k <= self.z) & (self.z < self.levels - 1))
+            def _():
+                self.copy(slot, 0, self.up).wait_send()
+
+            @pl.when((k >= self.z) & (self.z > 0))
+            def _():
+                self.copy(slot, 1, self.down).wait_send()
+
+        @pl.loop(0, self.members // CORES)
+        def _(i):
+            slot = i * CORES + self.c
+            self.copy(slot, 3, self.twin).wait_send()
+            if self.split:
+                self.lacked_to_twin(slot).wait_send()
+
+                @pl.when(slot != self.me)
+                def _():
+                    self.to_partner(slot).wait_send()
+
+
+class Exchange:
+    def __init__(self, src, out, sent, got, members):
+        self.src, self.out, self.sent, self.got, self.members = src, out, sent, got, members
+        self.me = lax.axis_index("grp")
+
+    def copy(self, d):
+        to = lax.rem(self.me + d, self.members)
+        return send(self.src.at[to], self.out.at[self.me], self.sent.at[d], self.got.at[d], to)
+
+    def start(self):
+        @pl.loop(1, self.members)
+        def _(d):
+            self.copy(d).start()
+
+    def wait(self):
+        @pl.loop(1, self.members)
+        def _(d):
+            self.copy(d).wait()
+
+
+def comm_kernel(*refs, members, splits, n_e):
+    n_g = len(splits)
+    n = n_g + n_e
+    ins, outs = refs[:n], refs[n : 2 * n]
+    stage = refs[2 * n : 3 * n]
+    local = refs[3 * n]
+    sems = refs[3 * n + 1 :]
+    me = lax.axis_index("grp")
+    into = [
+        pltpu.make_async_copy(r if k < n_g else r.at[me], stage[k], local.at[k]) for k, r in enumerate(ins)
+    ]
+    out_of = [pltpu.make_async_copy(stage[k], outs[k].at[me], local.at[k]) for k in range(n)]
+    gathers = [
+        Gather(ins[k], outs[k], sems[2 * k], sems[2 * k + 1], members, splits[k]) for k in range(n_g)
+    ]
+    exchanges = [Exchange(ins[k], outs[k], sems[2 * k], sems[2 * k + 1], members) for k in range(n_g, n)]
+    for copy in into:
+        copy.start()
+    split = [g for g in gathers if g.split]
+    meet(members, split[0].partner if split else None)
+    for g in gathers:
+        g.first()
+    for e in exchanges:
+        e.start()
+    for a, b in zip(into, out_of):
+        a.wait()
+        b.start()
+    levels = members // (SIDE * CORES)
+    z = me // (SIDE * CORES)
+    order = near_first(levels)
+    for s in range(1, levels):
+        for g in gathers:
+            g.relay(s)
+    for s in range(levels):
+        for g in gathers:
+            g.pass_on(pick_from(order, z, s))
+    for g in split:
+
+        @pl.loop(0, levels)
+        def _(s):
+            k = pick_from(order, z, s)
+            g.take_lacked(k, g.x)
+            g.take_lacked(k, 1 - g.x)
+
+    for g in gathers:
+
+        @pl.loop(0, levels)
+        def _(k):
+            g.take_twin(k)
+
+        if g.split:
+            g.take_twin_lacked()
+        g.finish()
+    for e in exchanges:
+        e.wait()
+    for copy in out_of:
+        copy.wait()
+
+
+def communicate(gathers, exchanges, members, collective_id, splits=None):
+    gathers, exchanges = list(gathers), list(exchanges)
+    n_g, n_e = len(gathers), len(exchanges)
+    splits = splits or [0] * n_g
+    blocks = [g.shape for g in gathers] + [e.shape[1:] for e in exchanges]
+    kinds = [a.dtype for a in gathers + exchanges]
+    anywhere = pl.BlockSpec(memory_space=pl.ANY)
+    sem = pltpu.SemaphoreType.DMA
+    moved = sum(members * b[0] * b[1] * 2 for b in blocks)
+    outs = pl.pallas_call(
+        functools.partial(comm_kernel, members=members, splits=tuple(splits), n_e=n_e),
+        in_specs=[anywhere] * (n_g + n_e),
+        out_specs=[anywhere] * (n_g + n_e),
+        out_shape=[jax.ShapeDtypeStruct((members, *b), k) for b, k in zip(blocks, kinds)],
+        scratch_shapes=[pltpu.VMEM(b, k) for b, k in zip(blocks, kinds)]
+        + [sem((n_g + n_e,))]
+        + [sem((6, members)), sem((2, members))] * n_g
+        + [sem((members,)), sem((members,))] * n_e,
+        compiler_params=pltpu.CompilerParams(collective_id=collective_id, has_side_effects=True),
+        cost_estimate=pl.CostEstimate(flops=0, bytes_accessed=moved * 8, transcendentals=0),
+        name=f"communicate_{collective_id}",
+    )(*gathers, *exchanges)
+    return outs[:n_g], outs[n_g:]
+
+
+class Reduce:
+    def __init__(self, p, twin_in, side_in, line_in, sems, members):
+        self.p, self.twin_in, self.side_in, self.line_in = p, twin_in, side_in, line_in
+        self.sems = sems
+        self.levels = members // (SIDE * CORES)
+        self.z, self.x, self.c = place_of()
+
+    def copy(self, kind, slot, dst, n, to):
+        sent, got = self.sems[2 * kind], self.sems[2 * kind + 1]
+        return send(self.p.at[slot], dst.at[n], sent.at[n], got.at[n], to)
+
+    def to_twin(self, k, w):
+        twin = index_of(self.z, self.x, 1 - self.c)
+        return self.copy(0, index_of(k, w, 1 - self.c), self.twin_in, k * SIDE + w, twin)
+
+    def to_side(self, k):
+        return self.copy(1, index_of(k, 1 - self.x, self.c), self.side_in, k, index_of(self.z, 1 - self.x, self.c))
+
+    def to_up(self, k):
+        return self.copy(2, index_of(k, self.x, self.c), self.line_in, k + 1, index_of(self.z + 1, self.x, self.c))
+
+    def to_down(self, k):
+        return self.copy(3, index_of(k, self.x, self.c), self.line_in, k, index_of(self.z - 1, self.x, self.c))
+
+    def add(self, slot, ref):
+        rows = self.p.shape[1]
+        chunk = next(r for r in (32, 16, 8) if rows % r == 0)
+
+        @pl.loop(0, rows // chunk)
+        def _(i):
+            at = pl.ds(pl.multiple_of(i * chunk, chunk), chunk)
+            self.p[slot, at, :] = (self.p[slot, at, :].astype(F32) + ref[at, :].astype(F32)).astype(self.p.dtype)
+
+    def start(self, k):
+        self.to_twin(k, self.x).start()
+        self.to_twin(k, 1 - self.x).start()
+
+    def chip(self, k):
+        w = 1 - self.x
+        self.to_twin(k, w).wait_recv()
+        self.add(index_of(k, w, self.c), self.twin_in.at[k * SIDE + w])
+        self.to_side(k).start()
+        self.to_twin(k, self.x).wait_recv()
+        self.add(index_of(k, self.x, self.c), self.twin_in.at[k * SIDE + self.x])
+
+    def line(self, k):
+        z, mine = self.z, index_of(k, self.x, self.c)
+        self.to_side(k).wait_recv()
+        self.add(mine, self.side_in.at[k])
+
+        @pl.when((k > z) & (z > 0))
+        def _():
+            self.to_up(k).wait_recv()
+            self.add(mine, self.line_in.at[k + 1])
+
+        @pl.when((k < z) & (z < self.levels - 1))
+        def _():
+            self.to_down(k).wait_recv()
+            self.add(mine, self.line_in.at[k])
+
+        @pl.when(k > z)
+        def _():
+            self.to_up(k).start()
+
+        @pl.when(k < z)
+        def _():
+            self.to_down(k).start()
+
+    def last(self, out):
+        z, mine = self.z, index_of(self.z, self.x, self.c)
+        self.to_side(z).wait_recv()
+        self.add(mine, self.side_in.at[z])
+
+        @pl.when(z > 0)
+        def _():
+            self.to_up(z).wait_recv()
+            self.add(mine, self.line_in.at[z + 1])
+
+        @pl.when(z < self.levels - 1)
+        def _():
+            self.to_down(z).wait_recv()
+            self.add(mine, self.line_in.at[z])
+
+        out[...] = self.p[mine]
+
+    def finish(self):
+        z = self.z
+
+        @pl.loop(0, self.levels)
+        def _(k):
+            self.to_twin(k, 0).wait_send()
+            self.to_twin(k, 1).wait_send()
+            self.to_side(k).wait_send()
+
+            @pl.when(k > z)
+            def _():
+                self.to_up(k).wait_send()
+
+            @pl.when(k < z)
+            def _():
+                self.to_down(k).wait_send()
+
+    @staticmethod
+    def scratch(members, r, c, kind):
+        levels = members // (SIDE * CORES)
+        sem = pltpu.SemaphoreType.DMA
+        return [
+            pltpu.VMEM((members // CORES, r, c), kind),
+            pltpu.VMEM((levels, r, c), kind),
+            pltpu.VMEM((levels + 1, r, c), kind),
+        ] + [sem((n,)) for n in (members // CORES,) * 2 + (levels,) * 2 + (levels + 1,) * 4]
+
+
+def reduce_kernel(*refs, members, n_e):
+    p, extra, out, landed = refs[0], refs[1 : 1 + n_e], refs[1 + n_e], refs[2 + n_e : 2 + 2 * n_e]
+    bufs = refs[2 + 2 * n_e :]
+    r = Reduce(p, *bufs[:3], bufs[3:11], members)
+    stage, local, sems = bufs[11 : 11 + n_e], bufs[11 + n_e : 11 + 2 * n_e], bufs[11 + 2 * n_e :]
+    me = lax.axis_index("grp")
+    order = far_first(r.levels)
+    into = [pltpu.make_async_copy(extra[k].at[me], stage[k], local[k]) for k in range(n_e)]
+    out_of = [pltpu.make_async_copy(stage[k], landed[k].at[me], local[k]) for k in range(n_e)]
+    exchanges = [Exchange(extra[k], landed[k], sems[2 * k], sems[2 * k + 1], members) for k in range(n_e)]
+    for k in range(n_e):
+        into[k].start()
+    meet(members)
+
+    @pl.loop(0, r.levels)
+    def _(s):
+        r.start(pick_from(order, r.z, s))
+
+    for k in range(n_e):
+        exchanges[k].start()
+        into[k].wait()
+        out_of[k].start()
+
+    @pl.loop(0, r.levels)
+    def _(s):
+        r.chip(pick_from(order, r.z, s))
+
+    @pl.loop(0, r.levels - 1)
+    def _(s):
+        r.line(pick_from(order, r.z, s))
+
+    r.last(out)
+    r.finish()
+    for k in range(n_e):
+        exchanges[k].wait()
+        out_of[k].wait()
+
+
+def reduce_blocks(p, extra, members, collective_id):
+    extra = list(extra)
+    n_e = len(extra)
+    anywhere = pl.BlockSpec(memory_space=pl.ANY)
+    _, r, c = p.shape
+    sem = pltpu.SemaphoreType.DMA
+    vmem = pl.BlockSpec(memory_space=pltpu.VMEM)
+    out, *landed = pl.pallas_call(
+        functools.partial(reduce_kernel, members=members, n_e=n_e),
+        in_specs=[vmem] + [anywhere] * n_e,
+        out_specs=[vmem] + [anywhere] * n_e,
+        out_shape=[jax.ShapeDtypeStruct((r, c), p.dtype)] + [jax.ShapeDtypeStruct(e.shape, e.dtype) for e in extra],
+        scratch_shapes=Reduce.scratch(members, r, c, p.dtype)
+        + [pltpu.VMEM(e.shape[1:], e.dtype) for e in extra]
+        + [sem] * n_e
+        + [sem((members,)), sem((members,))] * n_e,
+        compiler_params=pltpu.CompilerParams(
+            collective_id=collective_id, has_side_effects=True, vmem_limit_bytes=60 * 1024 * 1024
+        ),
+        cost_estimate=pl.CostEstimate(flops=0, bytes_accessed=members * r * c * 16, transcendentals=0),
+        name=f"reduce_{collective_id}",
+    )(p, *extra)
+    return out, landed
+
+
+def spread_kernel(src, out, stage, sent, got, local, *, members, sequences):
+    me, mine = lax.axis_index("grp"), lax.axis_index("rep")
+    barrier = pltpu.get_barrier_semaphore()
+    into = pltpu.make_async_copy(src.at[me], stage, local)
+    out_of = pltpu.make_async_copy(stage, out.at[mine, me], local)
+    into.start()
+
+    def other(n):
+        return lax.rem(mine + n // members, sequences), lax.rem(me + n % members, members)
+
+    @pl.loop(1, members * sequences)
+    def _(n):
+        r, to = other(n)
+        pl.semaphore_signal(barrier, 1, device_id={"rep": r, "grp": to}, device_id_type=MESH)
+
+    pl.semaphore_wait(barrier, members * sequences - 1)
+
+    def copy(n):
+        r, to = other(n)
+        return pltpu.make_async_remote_copy(
+            src_ref=src.at[to],
+            dst_ref=out.at[mine, me],
+            send_sem=sent.at[n],
+            recv_sem=got.at[n],
+            device_id={"rep": r, "grp": to},
+            device_id_type=MESH,
+        )
+
+    @pl.loop(1, members * sequences)
+    def _(n):
+        copy(n).start()
+
+    into.wait()
+    out_of.start()
+
+    @pl.loop(1, members * sequences)
+    def _(n):
+        copy(n).wait()
+
+    out_of.wait()
+
+
+def spread_blocks(v, members, sequences, collective_id):
+    anywhere = pl.BlockSpec(memory_space=pl.ANY)
+    sem = pltpu.SemaphoreType.DMA
+    return pl.pallas_call(
+        functools.partial(spread_kernel, members=members, sequences=sequences),
+        in_specs=[anywhere],
+        out_specs=anywhere,
+        out_shape=jax.ShapeDtypeStruct((sequences, *v.shape), v.dtype),
+        scratch_shapes=[pltpu.VMEM(v.shape[1:], v.dtype), sem((members * sequences,)), sem((members * sequences,)), sem],
+        compiler_params=pltpu.CompilerParams(collective_id=collective_id, has_side_effects=True),
+        cost_estimate=pl.CostEstimate(flops=0, bytes_accessed=v.size * 16, transcendentals=0),
+        name=f"spread_{collective_id}",
+    )(v)
+
+
+def gather(v):
+    return lax.all_gather(v, "grp", axis=0, tiled=True)
 
 
 def exchange(v):
@@ -81,6 +597,10 @@
 
 def scatter_sum(v):
     return lax.psum_scatter(v, "grp", scatter_dimension=0, tiled=True)
+
+
+def after(v, *others):
+    return lax.optimization_barrier((v, *others))[0]
 
 
 def block_of(length):
@@ -224,10 +744,392 @@
     )(prefix, q, k, v, d, lse, delta)
 
 
-def split_two(v):
-    high = v.astype(BF16)
-    low = (v - high.astype(F32)).astype(BF16)
-    return high, low
+def silu_parts(v):
+    logistic = 1.0 / (1.0 + jnp.exp(-v))
+    return v * logistic, logistic * (1.0 + v * (1.0 - logistic))
+
+
+def picks(rank, slots):
+    at = lax.broadcasted_iota(jnp.int32, (slots, rank.shape[1]), 0).astype(F32)
+    return at == rank
+
+
+def picks_back(rank, slots):
+    at = lax.broadcasted_iota(jnp.int32, (rank.shape[0], slots), 1).astype(F32)
+    return at == rank
+
+
+def tiles(width, size):
+    return pl.ds(pl.multiple_of(width * size, size), size)
+
+
+def experts_kernel(
+    x_hbm, prob_hbm, rank_ref, back_ref, gate_hbm, up_hbm, down_hbm, own_hbm, sdown_hbm,
+    part_hbm, eg_hbm, eu_hbm, eo_hbm, sh_hbm, prob_out,
+    xs, probs, gate, up, down, own, sdown, tail, rows, acts, part_st, eg_st, eu_st, eo_st, sh_st,
+    sent, got, e_sent, e_got, load, store,
+    *, members, slots, tile, wide
+):
+    me = lax.axis_index("grp")
+    levels = members // (SIDE * CORES)
+    group = SIDE * CORES
+    width, hidden = gate.shape
+    half, whole = hidden % tile, hidden // tile
+    units = own.shape[1] // 2
+    z = me // group
+    order = near_first(levels)
+    loads = [
+        pltpu.make_async_copy(a, b, load.at[n])
+        for n, (a, b) in enumerate(
+            [
+                (x_hbm, xs.at[me]),
+                (prob_hbm.at[me], probs.at[me]),
+                (own_hbm, own),
+                (gate_hbm, gate),
+                (up_hbm, up),
+                (down_hbm, down),
+                (sdown_hbm, sdown),
+            ]
+        )
+    ]
+    gather = Gather(x_hbm, xs, sent, got, members)
+    exchange = Exchange(prob_hbm, probs, e_sent, e_got, members)
+    for copy in loads:
+        copy.start()
+    meet(members)
+    gather.first()
+    exchange.start()
+    for copy in loads:
+        copy.wait()
+    tail[:, :half] = gate[:, hidden - half :]
+    tail[:, half:] = up[:, hidden - half :]
+    gather.pass_on(z)
+    gather.relay(1)
+    exchange.wait()
+    prob_out[...] = probs[...]
+
+    def stores(s, k):
+        n = s % 2
+        return [
+            pltpu.make_async_copy(a.at[n], b.at[k], store.at[n, m])
+            for m, (a, b) in enumerate(
+                [(part_st, part_hbm), (eg_st, eg_hbm), (eu_st, eu_hbm), (eo_st, eo_hbm), (sh_st, sh_hbm)]
+            )
+        ]
+
+    @pl.loop(0, levels)
+    def _(s):
+        k = pick_from(order, z, s)
+        n = s % 2
+        gather.take_twin(k)
+
+        @pl.when(s >= 2)
+        def _():
+            for copy in stores(s, pick_from(order, z, s - 2)):
+                copy.wait()
+
+        for b in range(group):
+            pick = picks(rank_ref[k * group + b, 0:1, :], slots).astype(BF16)
+            rows[b * slots : (b + 1) * slots, :] = dot(pick, xs[k * group + b]).astype(BF16)
+
+        def keep(at, g, u):
+            eg_st[n, :, at] = g.astype(BF16)
+            eu_st[n, :, at] = u.astype(BF16)
+            acts[:, at] = (silu_parts(g)[0] * u).astype(BF16)
+
+        @pl.loop(0, whole)
+        def _(j):
+            at = tiles(j, tile)
+            x = rows[...]
+            keep(at, dot(x, gate[:, at]), dot(x, up[:, at]))
+
+        last = dot(rows[...], tail[...])
+        keep(pl.ds(whole * tile, half), last[:, :half], last[:, half:])
+
+        gather.relay(s + 2)
+
+        @pl.when(s + 1 < levels)
+        def _():
+            gather.pass_on(pick_from(order, z, s + 1))
+
+        @pl.loop(0, width // wide)
+        def _(j):
+            at = tiles(j, wide)
+            eo_st[n, :, at] = dot(acts[...], down[:, at]).astype(BF16)
+
+        for b in range(group):
+            i = k * group + b
+            pick = picks(rank_ref[i, 0:1, :], slots)
+            back = picks_back(back_ref[i], slots).astype(BF16)
+            g = jnp.sum(jnp.where(pick, probs[i, 0:1, :], 0.0), axis=1, keepdims=True)
+            pre = dot(xs[i], own[...])
+            sh_st[n, b] = pre.astype(BF16)
+            act = (silu_parts(pre[:, :units])[0] * pre[:, units:]).astype(BF16)
+
+            @pl.loop(0, width // wide)
+            def _(j):
+                at = tiles(j, wide)
+                weighted = (g * eo_st[n, b * slots : (b + 1) * slots, at].astype(F32)).astype(BF16)
+                part_st[n, b, :, at] = (dot(back, weighted) + dot(act, sdown[:, at])).astype(BF16)
+
+        for copy in stores(s, k):
+            copy.start()
+
+    @pl.loop(levels - 2, levels)
+    def _(s):
+        for copy in stores(s, pick_from(order, z, s)):
+            copy.wait()
+
+    gather.finish()
+
+
+def experts_forward(x, prob, rank, back, gate, up, down, own, sdown, slots, members, collective_id):
+    tokens, width = x.shape
+    hidden = gate.shape[1]
+    group = SIDE * CORES
+    levels = members // group
+    packed = group * slots
+    anywhere = pl.BlockSpec(memory_space=pl.ANY)
+    vmem = pl.BlockSpec(memory_space=pltpu.VMEM)
+    sem = pltpu.SemaphoreType.DMA
+    tile = 256
+    shapes = [
+        (levels, group, tokens, width),
+        (levels, packed, hidden),
+        (levels, packed, hidden),
+        (levels, packed, width),
+        (levels, group, tokens, own.shape[1]),
+    ]
+    return pl.pallas_call(
+        functools.partial(experts_kernel, members=members, slots=slots, tile=tile, wide=512),
+        in_specs=[anywhere, anywhere, vmem, vmem] + [anywhere] * 5,
+        out_specs=[anywhere] * 5 + [vmem],
+        out_shape=[jax.ShapeDtypeStruct(s, BF16) for s in shapes] + [jax.ShapeDtypeStruct(prob.shape, F32)],
+        scratch_shapes=[
+            pltpu.VMEM((members, tokens, width), BF16),
+            pltpu.VMEM(prob.shape, F32),
+            pltpu.VMEM(gate.shape, BF16),
+            pltpu.VMEM(up.shape, BF16),
+            pltpu.VMEM(down.shape, BF16),
+            pltpu.VMEM(own.shape, BF16),
+            pltpu.VMEM(sdown.shape, BF16),
+            pltpu.VMEM((width, tile), BF16),
+            pltpu.VMEM((packed, width), BF16),
+            pltpu.VMEM((packed, hidden), BF16),
+        ]
+        + [pltpu.VMEM((2, *s[1:]), BF16) for s in shapes]
+        + [sem((6, members)), sem((2, members)), sem((members,)), sem((members,)), sem((7,)), sem((2, 5))],
+        compiler_params=pltpu.CompilerParams(
+            collective_id=collective_id, has_side_effects=True, vmem_limit_bytes=63 * 1024 * 1024
+        ),
+        cost_estimate=pl.CostEstimate(
+            flops=12 * members * slots * width * hidden, bytes_accessed=60_000_000, transcendentals=0
+        ),
+        name="experts_forward",
+    )(x, prob, rank, back, gate, up, down, own, sdown)
+
+
+def experts_back_kernel(
+    c_hbm, rank_ref, back_ref, prob_ref, eg_hbm, eu_hbm, eo_hbm, sh_hbm, gate_hbm, up_hbm, down_hbm, own_hbm, sdown_hbm,
+    out, dg_out,
+    part, cs, eg, eu, eo, sh, gate, up, down, own, sdown, rows, d_gate, d_up, dg_st, dg_in,
+    *sems, members, slots, tile, wide
+):
+    twin_in, side_in, line_in = sems[:3]
+    e_sent, e_got, load, fetch = sems[11:15]
+    me = lax.axis_index("grp")
+    levels = members // (SIDE * CORES)
+    group = SIDE * CORES
+    width, hidden = gate.shape
+    half, whole = hidden % tile, hidden // tile
+    units = own.shape[1] // 2
+    z = me // group
+    order = far_first(levels)
+    reduce = Reduce(part, twin_in, side_in, line_in, sems[3:11], members)
+    exchange = Exchange(dg_st, dg_in, e_sent, e_got, members)
+
+    def cotangents(s):
+        return pltpu.make_async_copy(c_hbm.at[pick_from(order, z, s)], cs.at[s % 2], fetch.at[s % 2])
+
+    def kept(s):
+        k = pick_from(order, z, s)
+        return [
+            pltpu.make_async_copy(a.at[k], b, fetch.at[2 + m])
+            for m, (a, b) in enumerate([(eo_hbm, eo), (eg_hbm, eg), (eu_hbm, eu), (sh_hbm, sh)])
+        ]
+
+    loads = [
+        pltpu.make_async_copy(a, b, load.at[n])
+        for n, (a, b) in enumerate(
+            [(down_hbm, down), (gate_hbm, gate), (up_hbm, up), (own_hbm, own), (sdown_hbm, sdown)]
+        )
+    ]
+    cotangents(0).start()
+    for copy in kept(0):
+        copy.start()
+    for copy in loads:
+        copy.start()
+    meet(members)
+
+    def early(s):
+        return (z == 0) | (z == levels - 1)
+
+    @pl.loop(0, levels)
+    def _(s):
+        k = pick_from(order, z, s)
+        n = s % 2
+        cotangents(s).wait()
+        load_eo, load_eg, load_eu, load_sh = kept(s)
+
+        @pl.when(s + 1 < levels)
+        def _():
+            cotangents(s + 1).start()
+
+        load_eo.wait()
+        for b in range(group):
+            i = k * group + b
+            at = slice(b * slots, (b + 1) * slots)
+            pick = picks(rank_ref[i, 0:1, :], slots)
+            c = dot(pick.astype(BF16), cs[n, b])
+            g = jnp.sum(jnp.where(pick, prob_ref[i, 0:1, :], 0.0), axis=1, keepdims=True)
+            along = jnp.sum(c * eo[at, :].astype(F32), axis=1, keepdims=True)
+            dg_st[i] = jnp.broadcast_to(
+                jnp.sum(jnp.where(pick, along, 0.0), axis=0, keepdims=True), dg_st.shape[1:]
+            )
+            rows[at, :] = (g * c).astype(BF16)
+
+        @pl.when(s == 0)
+        def _():
+            for copy in loads:
+                copy.wait()
+
+        load_eg.wait()
+        load_eu.wait()
+
+        def slopes(at):
+            d = dot_t(rows[...], down[at, :])
+            act, slope = silu_parts(eg[:, at].astype(F32))
+            d_gate[:, at] = (d * eu[:, at].astype(F32) * slope).astype(BF16)
+            d_up[:, at] = (d * act).astype(BF16)
+
+        @pl.loop(0, whole)
+        def _(j):
+            slopes(tiles(j, tile))
+
+        slopes(pl.ds(whole * tile, half))
+
+        @pl.when(s >= 1)
+        def _():
+            reduce.chip(pick_from(order, z, s - 1))
+
+        @pl.when((s >= 2) & ~early(s))
+        def _():
+            reduce.line(pick_from(order, z, s - 2))
+
+        @pl.loop(0, width // tile)
+        def _(j):
+            at = tiles(j, tile)
+            eo[:, at] = (dot_t(d_gate[...], gate[at, :]) + dot_t(d_up[...], up[at, :])).astype(BF16)
+
+        load_sh.wait()
+        for b in range(group):
+            i = k * group + b
+            back = picks_back(back_ref[i], slots).astype(BF16)
+            d = dot_t(cs[n, b], sdown[...])
+            pre = sh[b].astype(F32)
+            act, slope = silu_parts(pre[:, :units])
+            both = jnp.concatenate([d * pre[:, units:] * slope, d * act], axis=1).astype(BF16)
+
+            @pl.loop(0, width // wide)
+            def _(j):
+                at = tiles(j, wide)
+                part[i, :, at] = (
+                    dot(back, eo[b * slots : (b + 1) * slots, at]) + dot_t(both, own[at, :])
+                ).astype(BF16)
+
+        reduce.start(k)
+
+        @pl.when(s + 1 < levels)
+        def _():
+            for copy in kept(s + 1):
+                copy.start()
+
+        @pl.when((s >= 1) & early(s))
+        def _():
+            reduce.line(pick_from(order, z, s - 1))
+
+    exchange.start()
+    dg_in[me] = dg_st[me]
+    reduce.chip(z)
+
+    @pl.when(~early(0))
+    def _():
+        reduce.line(pick_from(order, z, levels - 2))
+
+    reduce.last(out)
+    reduce.finish()
+    exchange.wait()
+    dg_out[...] = dg_in[...]
+
+
+def experts_backward(c, rank, back, prob, kept, gate, up, down, own, sdown, slots, members, collective_id):
+    _, tokens, width = c.shape
+    hidden = gate.shape[1]
+    group = SIDE * CORES
+    levels = members // group
+    packed = group * slots
+    anywhere = pl.BlockSpec(memory_space=pl.ANY)
+    vmem = pl.BlockSpec(memory_space=pltpu.VMEM)
+    sem = pltpu.SemaphoreType.DMA
+    eg, eu, eo, sh = kept
+    return pl.pallas_call(
+        functools.partial(experts_back_kernel, members=members, slots=slots, tile=256, wide=512),
+        in_specs=[anywhere, vmem, vmem, vmem] + [anywhere] * 9,
+        out_specs=[vmem, vmem],
+        out_shape=[
+            jax.ShapeDtypeStruct((tokens, width), BF16),
+            jax.ShapeDtypeStruct((members, 8, tokens), F32),
+        ],
+        scratch_shapes=[
+            pltpu.VMEM((members, tokens, width), BF16),
+            pltpu.VMEM((2, group, tokens, width), BF16),
+            pltpu.VMEM(eg.shape[1:], BF16),
+            pltpu.VMEM(eu.shape[1:], BF16),
+            pltpu.VMEM(eo.shape[1:], BF16),
+            pltpu.VMEM(sh.shape[1:], BF16),
+            pltpu.VMEM(gate.shape, BF16),
+            pltpu.VMEM(up.shape, BF16),
+            pltpu.VMEM(down.shape, BF16),
+            pltpu.VMEM(own.shape, BF16),
+            pltpu.VMEM(sdown.shape, BF16),
+            pltpu.VMEM((packed, width), BF16),
+            pltpu.VMEM((packed, hidden), BF16),
+            pltpu.VMEM((packed, hidden), BF16),
+            pltpu.VMEM((members, 8, tokens), F32),
+            pltpu.VMEM((members, 8, tokens), F32),
+        ]
+        + Reduce.scratch(members, tokens, width, BF16)
+        + [sem((members,)), sem((members,)), sem((5,)), sem((6,))],
+        compiler_params=pltpu.CompilerParams(
+            collective_id=collective_id, has_side_effects=True, vmem_limit_bytes=67_043_328
+        ),
+        cost_estimate=pl.CostEstimate(
+            flops=12 * members * slots * width * hidden, bytes_accessed=60_000_000, transcendentals=0
+        ),
+        name="experts_backward",
+    )(c.reshape(levels, group, tokens, width), rank, back, prob, *kept, gate, up, down, own, sdown)
+
+
+def pack(v):
+    half = v.shape[1] // 2
+    rope = jnp.concatenate([v[:, :half, NOPE:], v[:, half:, NOPE:]], axis=-1)
+    return jnp.concatenate([v[:, :, :NOPE], rope], axis=1)
+
+
+def unpack(v):
+    rows = v.shape[1] * 2 // 3
+    rope = jnp.concatenate([v[:, rows:, :ROPE], v[:, rows:, ROPE:]], axis=1)
+    return jnp.concatenate([v[:, :rows], rope], axis=-1)
 
 
 def per_device(
@@ -272,18 +1174,29 @@
     pick = lambda table: lax.dynamic_index_in_dim(table, adapter, 0, keepdims=False)
     qa_down, qa_up, oa_down, oa_up = pick(q_down), pick(q_up), pick(o_down), pick(o_up)
 
-    full_kva = gather(w_kva)
-    full_q = gather(w_q)
+    chosen_by = jnp.sum(
+        (routes[:, :, None] == jnp.arange(experts, dtype=jnp.int32)[None, None, :]).astype(F32), axis=1
+    )
+    sequences = lax.axis_size("rep")
+    split = w_q.shape[0] * 3 // 128 * 16 if sequences % 2 == 0 else 0
+    (all_kva, all_q, all_o, all_router), (kvb_parts, chosen_all) = communicate(
+        [w_kva, w_q, w_o, w_router],
+        [
+            w_kvb.reshape(w_kvb.shape[0], members, -1).transpose(1, 0, 2),
+            jnp.broadcast_to(chosen_by.T[:, None, :], (experts, 8, tokens)),
+        ],
+        members,
+        1,
+        [split, split, split, 0],
+    )
+    full_kva, full_q, full_o, full_router = (
+        v.reshape(-1, v.shape[2]) for v in (all_kva, all_q, all_o, all_router)
+    )
+    own_kvb = kvb_parts.reshape(KVR, -1)
     hidden_slice = shared_down.shape[0]
-    kvb_cols = w_kvb.shape[1] // members
-    own_kvb = exchange(
-        w_kvb.reshape(w_kvb.shape[0], members, kvb_cols).transpose(1, 0, 2)
-    ).reshape(KVR, kvb_cols)
-    shared = jnp.stack([shared_gate, shared_up], axis=1)
+    shared = after(jnp.stack([shared_gate, shared_up], axis=1), all_q)
     shared = shared.reshape(shared.shape[0], 2, members, hidden_slice).transpose(2, 0, 1, 3)
     own_shared = exchange(shared.reshape(members, -1, 2 * hidden_slice)).reshape(width, 2 * hidden_slice)
-    full_o = gather(w_o)
-    full_router = gather(w_router)
 
     positions = me * tokens + jnp.arange(tokens, dtype=jnp.int32)
     cosine, sine = angles(positions, ROPE)
@@ -291,130 +1204,72 @@
     latent = dot(normed, full_kva)
     compressed = root_norm(latent[:, :KVR], kv_gain).astype(BF16)
     k_rope = rotate(latent[:, KVR:], cosine, sine).astype(BF16)
-    all_latent = gather(jnp.concatenate([compressed, k_rope], axis=-1))
     q_small = dot(normed, qa_down).astype(BF16)
     query = (dot(normed, full_q) + dot(q_small, qa_up)).reshape(tokens, H, QK)
     query = jnp.concatenate(
         [query[:, :, :NOPE], rotate(query[:, :, NOPE:], cosine[:, None], sine[:, None])], axis=-1
     ).astype(BF16)
-    q_head = exchange(query.transpose(1, 0, 2)).reshape(length, QK)
+    (all_latent,), (q_packed,) = communicate(
+        [jnp.concatenate([compressed, k_rope], axis=-1)], [pack(query.transpose(1, 0, 2))], members, 2
+    )
+    all_latent = all_latent.reshape(length, KVR + ROPE)
+    q_head = unpack(q_packed).reshape(length, QK)
     expanded = dot(all_latent[:, :KVR], own_kvb).astype(BF16)
     k_head = jnp.concatenate([expanded[:, :NOPE], all_latent[:, KVR:]], axis=-1)
     v_head = expanded[:, NOPE:]
     mixture, lse = attend(prefix_len, q_head, k_head, v_head)
-    mixed = (
-        exchange(mixture.astype(BF16).reshape(members, tokens, VD))
-        .transpose(1, 0, 2)
-        .reshape(tokens, H * VD)
-    )
+    _, (mixed,) = communicate([], [mixture.astype(BF16).reshape(members, tokens, VD)], members, 3)
+    mixed = mixed.transpose(1, 0, 2).reshape(tokens, H * VD)
     o_small = dot(mixed, oa_down).astype(BF16)
     middle = inputs + dot(mixed, full_o) + dot(o_small, oa_up)
     ffn_in = root_norm(middle, ffn_gain).astype(BF16)
     route_probs = jax.nn.softmax(dot(ffn_in, full_router), axis=-1)
 
-    lanes = 128
-    high, low = split_two(route_probs)
-    extra = jnp.concatenate(
-        [high, low, jnp.zeros((tokens, lanes - 2 * experts), BF16)], axis=-1
-    )
-    all_in = gather(jnp.concatenate([ffn_in, extra], axis=-1))
-    all_ids = gather(routes)
-    all_c = gather(cotangent)
-    ffn_all = all_in[:, :width]
-    mine = jnp.arange(experts, dtype=jnp.int32)[None, :] == me
-    probs = jnp.sum(
-        jnp.where(
-            mine,
-            all_in[:, width : width + experts].astype(F32)
-            + all_in[:, width + experts : width + 2 * experts].astype(F32),
-            0.0,
-        ),
-        axis=-1,
-    ).reshape(members, tokens)
-    chosen = jnp.any(all_ids == me, axis=-1).reshape(members, tokens)
+    all_c = gather(after(cotangent, q_head))
+    chosen = chosen_all[:, 0] > 0.5
     order = jnp.arange(tokens, dtype=jnp.int32)
     before = (order[:, None] < order[None, :]).astype(BF16)
-    rank = dot(chosen.astype(BF16), before).astype(jnp.int32)
-    place = (rank[:, None, :] == jnp.arange(slots, dtype=jnp.int32)[None, :, None]) & chosen[:, None, :]
-    select = place.astype(BF16)
-    weight_rows = jnp.sum(jnp.where(place, probs[:, None, :], 0.0), axis=-1)
-
-    def compact(rows):
-        return lax.dot_general(
-            select,
-            rows.reshape(members, tokens, width),
-            (((2,), (1,)), ((0,), (0,))),
-            preferred_element_type=F32,
-        ).astype(BF16).reshape(members * slots, width)
-
-    def spread(rows):
-        return lax.dot_general(
-            select,
-            rows.reshape(members, slots, width),
-            (((1,), (1,)), ((0,), (0,))),
-            preferred_element_type=F32,
-        ).reshape(length, width)
-
-    rows_in = compact(ffn_all)
-    e_gate = dot(rows_in, expert_gate[0])
-    e_up = dot(rows_in, expert_up_weight[0])
-    e_hidden = (jax.nn.silu(e_gate) * e_up).astype(BF16)
-    e_out = dot(e_hidden, expert_down[0]).astype(BF16)
-    gates = weight_rows.reshape(members * slots, 1)
-    s_gate = dot(ffn_all, own_shared[:, :hidden_slice])
-    s_up = dot(ffn_all, own_shared[:, hidden_slice:])
-    s_hidden = (jax.nn.silu(s_gate) * s_up).astype(BF16)
-    partial = spread((gates * e_out.astype(F32)).astype(BF16)) + dot(s_hidden, shared_down)
-    ffn_out = scatter_sum(partial.astype(BF16))
+    rank = jnp.where(chosen, dot(chosen.astype(BF16), before), -1.0)
+    back = rank[:, :, None]
+    rank = jnp.broadcast_to(rank[:, None, :], (members, 8, tokens))
+    weights = (expert_gate[0], expert_up_weight[0], expert_down[0], own_shared, shared_down)
+    prob_blocks = jnp.broadcast_to(route_probs.T[:, None, :], (experts, 8, tokens))
+    partial, *kept, prob_parts = experts_forward(
+        ffn_in, prob_blocks, rank, back, *weights, slots, members, 4
+    )
+    ffn_out = scatter_sum(partial.reshape(length, width))
     output = (middle + ffn_out.astype(F32)).astype(BF16)
-
-    rows_c = compact(all_c)
-    rows_c32 = rows_c.astype(F32)
-    d_gate = jnp.sum(rows_c32 * e_out.astype(F32), axis=-1).reshape(members, slots)
-    d_eout = (gates * rows_c32).astype(BF16)
-    d_eh = dot_t(d_eout, expert_down[0])
-    d_egate = (d_eh * e_up * gated_slope(e_gate)).astype(BF16)
-    d_eup = (d_eh * jax.nn.silu(e_gate)).astype(BF16)
-    d_rows = (dot_t(d_egate, expert_gate[0]) + dot_t(d_eup, expert_up_weight[0])).astype(BF16)
-    d_sh = dot_t(all_c, shared_down)
-    d_sgate = (d_sh * s_up * gated_slope(s_gate)).astype(BF16)
-    d_sup = (d_sh * jax.nn.silu(s_gate)).astype(BF16)
-    d_shared = jnp.concatenate([d_sgate, d_sup], axis=-1)
-    d_partial = spread(d_rows) + dot_t(d_shared, own_shared)
-    d_gate_all = jnp.sum(jnp.where(place, d_gate[:, :, None], 0.0), axis=1).reshape(length, 1)
-    g_high, g_low = split_two(d_gate_all)
-    d_extra = jnp.concatenate(
-        [
-            jnp.where(mine, g_high, 0).astype(BF16),
-            jnp.where(mine, g_low, 0).astype(BF16),
-            jnp.zeros((length, lanes - 2 * experts), BF16),
-        ],
-        axis=-1,
-    )
-    d_own = scatter_sum(jnp.concatenate([d_partial.astype(BF16), d_extra], axis=-1))
-    d_route = d_own[:, width : width + experts].astype(F32) + d_own[
-        :, width + experts : width + 2 * experts
-    ].astype(F32)
+    d_own, d_route = experts_backward(
+        all_c.reshape(members, tokens, width), rank, back, prob_parts, kept, *weights, slots, members, 5
+    )
+    d_route = d_route[:, 0].T
     d_logits = (
         route_probs * (d_route - jnp.sum(route_probs * d_route, axis=-1, keepdims=True))
     ).astype(BF16)
-    d_ffn = d_own[:, :width].astype(F32) + dot_t(d_logits, full_router)
+    d_ffn = d_own.astype(F32) + dot_t(d_logits, full_router)
     d_middle = c32 + norm_back(middle, ffn_gain, d_ffn)
     d_attn = d_middle.astype(BF16)
     grad_oup = t_dot(o_small, d_attn)
     d_osmall = dot_t(d_attn, oa_up).astype(BF16)
     grad_odown = t_dot(d_osmall, mixed)
     d_mixed = (dot_t(d_attn, full_o) + dot_t(d_osmall, oa_down)).astype(BF16)
-    d_head = exchange(d_mixed.reshape(tokens, H, VD).transpose(1, 0, 2)).reshape(length, VD)
+    _, (d_head,) = communicate([], [d_mixed.reshape(tokens, H, VD).transpose(1, 0, 2)], members, 6)
+    d_head = d_head.reshape(length, VD)
     delta = jnp.sum(d_head.astype(F32) * mixture, axis=-1)
     dq, dk, dv = attend_back(
         prefix_len, q_head, k_head, v_head, d_head, lse.reshape(1, length), delta.reshape(1, length)
     )
-    d_query = exchange(dq.astype(BF16).reshape(members, tokens, QK)).transpose(1, 0, 2).astype(F32)
     d_expanded = jnp.concatenate([dk[:, :NOPE], dv], axis=-1).astype(BF16)
-    d_latents = scatter_sum(
-        jnp.concatenate([dot_t(d_expanded, own_kvb), dk[:, NOPE:]], axis=-1).astype(BF16)
-    ).astype(F32)
+    d_latents, (d_query,) = reduce_blocks(
+        jnp.concatenate([dot_t(d_expanded, own_kvb), dk[:, NOPE:]], axis=-1)
+        .astype(BF16)
+        .reshape(members, tokens, KVR + ROPE),
+        [pack(dq.astype(BF16).reshape(members, tokens, QK))],
+        members,
+        7,
+    )
+    d_latents = d_latents.astype(F32)
+    d_query = unpack(d_query).transpose(1, 0, 2).astype(F32)
     d_latent = jnp.concatenate(
         [
             norm_back(latent[:, :KVR], kv_gain, d_latents[:, :KVR]),
@@ -442,9 +1297,13 @@
         for g in (grad_qdown, grad_qup, grad_odown, grad_oup)
     ]
     sizes = [g.shape[2] for g in parts]
-    share = jnp.sum(exchange(jnp.concatenate(parts, axis=-1)).astype(F32), axis=0)
-    selector = (jnp.arange(q_down.shape[0], dtype=jnp.int32) == adapter).astype(F32)[:, None, None]
-    summed = lax.psum((selector * share[None]).astype(BF16), "rep").astype(F32)
+    lanes = 128
+    named = jnp.broadcast_to(adapter.astype(BF16), (members, rank_of, lanes))
+    shares = spread_blocks(jnp.concatenate(parts + [named], axis=-1), members, sequences, 8)
+    numbers = shares[:, 0, 0, -1].astype(jnp.int32)
+    share = jnp.sum(shares[..., :-lanes].astype(F32), axis=1)
+    selector = (jnp.arange(q_down.shape[0], dtype=jnp.int32)[:, None] == numbers[None, :]).astype(F32)
+    summed = jnp.sum(selector[:, :, None, None] * share[None], axis=1)
     ends = [sum(sizes[: n + 1]) for n in range(4)]
     outs = [summed[:, :, e - s : e] for e, s in zip(ends, sizes)]
     return (

time: 1340 us -> 858 us (0.64)
  Pallas kernels: 49.3 us -> 690 us
  waiting for transfers between devices: 630 us -> 0.04 us
  matrix products: 258 us -> 54.9 us
  blocking collectives: 113 us -> 0 us
  other arithmetic: 137 us -> 35.2 us
  local copies, waits for them, and re-layouts: 84 us -> 45.1 us
  starting transfers between devices: 37.6 us -> 4.06 us
    pallas_call x0 -> x8, Pallas kernels: none -> 637 us  [the longest x4 246 us: communicate(): pl.pallas_call(functools.partial(comm_kernel, members=members, splits=tup...]
    reduce_scatter x3 -> x1, waiting for transfers between devices: 307 us -> 0.01 us  [scatter_sum(): return lax.psum_scatter(v, 'grp', scatter_dimension=0, tiled=True)]
    all_gather x6 -> x1, waiting for transfers between devices: 266 us -> 0.01 us  [gather(): return lax.all_gather(v, 'grp', axis=0, tiled=True)]
    all_gather x2 -> x0, blocking collectives: 113 us -> none  [gather(): return lax.all_gather(v, 'grp', axis=axis, tiled=True)]
    dot_general x16 -> x10, matrix products: 106 us -> 24 us  [dot(): return jnp.dot(former, latter, preferred_element_type=F32)]
    dot_general x14 -> x9, matrix products: 108 us -> 27.2 us  [dot_t(): lax.dot_general(former, latter, (((1,), (1,)), ((), ())), preferred_eleme...]
    reduce_or x1 -> x0, other arithmetic: 65.3 us -> none  [per_device(): chosen = jnp.any(all_ids == me, axis=-1).reshape(members, tokens)]
    all_to_all x7 -> x1, waiting for transfers between devices: 50.6 us -> 0.01 us  [exchange(): return lax.all_to_all(v, 'grp', split_axis=0, concat_axis=0, tiled=True)]
  transfers between devices with their start and end apart: 17 -> 3, of which waited for: 12 -> 0; matrix products, arithmetic and copies ran while one was open for 15% -> 4% of each run, Pallas kernels for 2% -> 45%
where the time goes in v3:
time: 858 us; the launch traced here: 846 us
  Pallas kernels  690 us (80%)
  matrix products  54.9 us (6%)
  local copies, waits for them, and re-layouts  45.1 us (5%)
  other arithmetic  35.2 us (4%)
  between operations  16.8 us (2%)
    pallas_call x4, Pallas kernels, communicate(): pl.pallas_call(functools.partial(comm_kernel, members=members, splits=tup...  246 us
    pallas_call x1, Pallas kernels, experts_backward(): pl.pallas_call(functools.partial(experts_back_kernel, members=members, sl...  172 us
    pallas_call x1, Pallas kernels, experts_forward(): pl.pallas_call(functools.partial(experts_kernel, members=members, slots=s...  147 us
    pallas_call x1, Pallas kernels, reduce_blocks(): pl.pallas_call(functools.partial(reduce_kernel, members=members, n_e=n_e)...  49.7 us
    pallas_call x1, Pallas kernels, attend_back(): pl.pallas_call(functools.partial(attend_back_kernel, block=block, factor=...  30.5 us
    dot_general x9, matrix products, dot_t(): lax.dot_general(former, latter, (((1,), (1,)), ((), ())), preferred_eleme...  27.2 us
    dot_general x10, matrix products, dot(): return jnp.dot(former, latter, preferred_element_type=F32)  24 us
    pallas_call x1, Pallas kernels, attend(): pl.pallas_call(functools.partial(attend_kernel, block=block, factor=QK **...  22.4 us
  transfers between devices with their start and end apart: 3, of which 0 were waited for; matrix products, arithmetic and copies ran while one was open for 4% of the time, Pallas kernels for 45%

profile of v3, /device:TPU:0, one launch (start us, length us, event | category | flops | bytes accessed | tf_op | source)
XLA Modules:
  0.0 846.4 jit_solution(17919875013366865133)
XLA Ops:
  7.9 1.4 fusion.9
  10.6 1.4 copy.99.refs_3_
  12.0 1.7 copy.98.refs_0_
  13.7 1.7 copy.162
  16.1 135.8 %communicate_1.1 = (bf16[16,128,576]{2,1,0:T(8,128)(2,1)}, bf16[16,128,3072]{2,1,0:T(8,128)(2,1)}, bf16[16,128,2048]{2,1,0:T(8,128)(2,1)}, bf16[16,128,16]{2,1,0...) custom-call(bf16[128,576]{1,0:T(8,128)(2,1)} %copy.98.refs_0_, bf16[128,3072]{1,0:T(8,128)(2,1)} %refs_1_.1, ...), custom_call_target="tpu_custom_call" | custom-call | bytes 189661184 | tf_op jit(solution)/shard_map/communicate_1/pallas_call | solution.py:341
  151.9 6.1 fusion.101
  157.9 1.2 convolution_convert_fusion.9
  159.8 2.8 convolution_add_fusion
  162.5 3.1 reshape.304
  166.7 2.2 fusion.105
  168.9 3.0 fusion.103
  177.9 1.3 maximum_maximum_fusion.1.refs_1_
  179.1 56.7 %communicate_2.1 = (bf16[16,192,576]{2,1,0:T(8,128)(2,1)}, bf16[16,288,128]{2,1,0:T(8,128)(2,1)}) custom-call(bf16[192,576]{1,0:T(8,128)(2,1)} %pad_maximum_fusion.3.refs_0_, bf16[16,288,128]{2,1,0:T(8,128)(2,1)} %maximum_maximum_fusion.1.refs_1_), custom_call_target="tpu_custom_call" | custom-call | bytes 37748736 | tf_op jit(solution)/shard_map/communicate_2/pallas_call | solution.py:341
  235.8 1.3 slice.139
  237.5 1.5 maximum_maximum_fusion
  240.6 1.2 copy.108
  241.9 3.7 all-to-all-start
  247.6 1.7 copy.110.back_ref
  250.5 2.9 convolution_convert_fusion
  254.4 1.5 pad_maximum_fusion.1.k_ref
  255.8 22.4 %attend.1 = (f32[3072,128]{1,0:T(8,128)}, f32[3072,1]{1,0:T(8,128)}) custom-call(s32[1]{0:T(128)S(6)} %copy.166.prefix_ref, bf16[3072,192]{1,0:T(8,128)(2,1)} %bitcast.229, bf16[3072,192]{1,0:T(8,128)(2,1)} %pad_maximum_fusion.1.k_ref, bf16[3072,128]{1,0:T(8,128)(2,1)} %get-tuple-element.66.v_ref), custom_call_target="tpu_custom_call" | custom-call | flops 3019898880 | bytes 3072000 | tf_op jit(solution)/shard_map/attend/pallas_call | solution.py:652
  278.2 2.4 convert_element_type.165
  280.6 35.6 %communicate_3.1 = bf16[16,192,128]{2,1,0:T(8,128)(2,1)} custom-call(bf16[16,192,128]{2,1,0:T(8,128)(2,1)} %bitcast.221), custom_call_target="tpu_custom_call" | custom-call | bytes 6291456 | tf_op jit(solution)/shard_map/communicate_3/pallas_call | solution.py:341
  316.2 1.5 convolution_convert_fusion.8
  317.7 4.7 fusion.3
  322.5 1.3 multiply_reduce_fusion.2
  325.7 1.6 copy.109
  328.6 147.3 %experts_forward.1 = (bf16[4,4,192,2048]{3,2,1,0:T(8,128)(2,1)}, bf16[4,384,1408]{2,1,0:T(8,128)(2,1)}, bf16[4,384,1408]{2,1,0:T(8,128)(2,1)}, bf16[4,384,2048]{...) custom-call(bf16[192,2048]{1,0:T(8,128)(2,1)} %copy-done.18, ...), custom_call_target="tpu_custom_call" | custom-call | flops 53150220288 | bytes 60000000 | tf_op jit(solution)/shard_map/experts_forward/pallas_call | solution.py:903
  476.0 1.4 copy-done.23
  478.4 171.8 %experts_backward.1 = (bf16[192,2048]{1,0:T(8,128)(2,1)}, f32[16,8,192]{2,1,0:T(8,128)}) custom-call(bf16[4,4,192,2048]{3,2,1,0:T(8,128)(2,1)} %bitcast.248, f32[16,8,192]{2,1,0:T(8,128)} %broadcast_in_dim.21.rank_ref, f32[16,192,1]{2,1,0:T(8,128)} %copy.110.back_ref, f32[16,8,192]{2,1,0:T(8,128)} %get-tuple-element.43.prob_ref, ...), custom_call_target="tpu_custom_call" | custom-call | flops 53150220288 | bytes 60000000 | tf_op jit(solution)/shard_map/experts_backward/pallas_call | solution.py:1085
  652.0 3.5 multiply_reduce_fusion.1
  655.5 3.2 subtract_add_fusion
  660.8 6.4 fusion.96
  670.3 18.3 %communicate_6.1 = bf16[16,192,128]{2,1,0:T(8,128)(2,1)} custom-call(bf16[16,192,128]{2,1,0:T(8,128)(2,1)} %bitcast.219), custom_call_target="tpu_custom_call" | custom-call | bytes 6291456 | tf_op jit(solution)/shard_map/communicate_6/pallas_call | solution.py:341
  688.7 2.2 multiply_reduce_fusion
  690.9 30.5 %attend_back.1 = (f32[3072,192]{1,0:T(8,128)}, f32[3072,192]{1,0:T(8,128)}, f32[3072,128]{1,0:T(8,128)}) custom-call(s32[1]{0:T(128)S(6)} %copy.166.prefix_ref, bf16[3072,192]{1,0:T(8,128)(2,1)} %bitcast.230, bf16[3072,192]{1,0:T(8,128)(2,1)} %pad_maximum_fusion.1.k_ref, bf16[3072,128]{1,0:T(8,128)(2,1)} %get-tuple-element.66.v_ref, ...), custom_call_target="tpu_custom_call" | custom-call | flops 7851737088 | bytes 6144000 | tf_op jit(solution)/shard_map/attend_back/pallas_call | solution.py:718
  721.5 2.0 convert.48
  724.7 1.3 copy-done.15
  729.0 2.4 pad_maximum_fusion.refs_0_
  731.3 1.3 maximum_maximum_fusion.2.refs_1_
  732.6 49.7 %reduce_7.1 = (bf16[192,576]{1,0:T(8,128)(2,1)}, bf16[16,288,128]{2,1,0:T(8,128)(2,1)}) custom-call(bf16[16,192,576]{2,1,0:T(8,128)(2,1)} %pad_maximum_fusion.refs_0_, bf16[16,288,128]{2,1,0:T(8,128)(2,1)} %maximum_maximum_fusion.2.refs_1_), custom_call_target="tpu_custom_call" | custom-call | bytes 28311552 | tf_op jit(solution)/shard_map/reduce_7/pallas_call | solution.py:515
  788.0 2.0 copy.113
  790.0 3.0 convert_element_type.181
  793.0 10.0 %fusion.113 = f32[192,2048]{1,0:T(8,128)} fusion(bf16[192,3072]{1,0:T(8,128)(2,1)S(1)} %convert_element_type.181, bf16[2048,3072]{1,0:T(8,128)(2,1)} %bitcast.247), kind=kOutput, calls=%fused_computation.186 | convolution fusion | flops 2415919104 | bytes 15335424 | tf_op jit(solution)/shard_map/dot_general | solution.py:27
  803.0 1.4 convolution_convert_fusion.6
  808.6 22.1 %spread_8.1 = bf16[2,16,16,704]{3,2,1,0:T(8,128)(2,1)} custom-call(bf16[16,16,704]{2,1,0:T(8,128)(2,1)} %concatenate.81.src), custom_call_target="tpu_custom_call" | custom-call | bytes 2883584 | tf_op jit(solution)/shard_map/spread_8/pallas_call | solution.py:578
  834.6 1.4 convolution_add_fusion.3
  837.8 1.3 fusion.29
  (211 shorter events, 45.7 us)
Async XLA Ops:
  7.2 471.2 %all-gather.2.cloned.1.call-start = ((), (), s32[]{:S(2)}) async-start(), calls=%async_computation.3 | async-start | bytes 13369344 | tf_op jit(solution)/shard_map/all_gather | solution.py:591
  7.2 165.0 %copy-start.62 = (f32[32]{0:T(128)}, f32[32]{0:T(128)S(1)}, u32[]{:S(2)}) copy-start(f32[32]{0:T(128)S(1)} %multiply_power_fusion) | copy-start | bytes 388
  9.3 142.6 %copy-start.2 = (bf16[1,192,2048]{2,1,0:T(8,128)(2,1)S(1)}, bf16[1,192,2048]{2,1,0:T(8,128)(2,1)}, u32[]{:S(2)}) copy-start(bf16[1,192,2048]{2,1,0:T(8,128)(2,1)} %param.23) | copy-start | bytes 2359300
  9.3 142.6 %copy-start.52 = (f32[2048]{0:T(1024)S(1)}, f32[2048]{0:T(1024)}, u32[]{:S(2)}) copy-start(f32[2048]{0:T(1024)} %param.28) | copy-start | bytes 24580
  9.9 159.0 %copy-start.57 = (f32[192]{0:T(256)}, f32[192]{0:T(256)S(1)}, u32[]{:S(2)}) copy-start(f32[192]{0:T(256)S(1)} %get-tuple-element.86) | copy-start | bytes 2308
  168.9 3.4 copy-start.54
  168.9 3.1 copy-start.17
  168.9 3.8 copy-start.12
  171.8 4.9 copy-start.5
  171.9 1.6 copy-start.11
  172.7 1.8 copy-start.26
  172.7 1.8 copy-start.28
  175.0 1.7 copy-start.45
  241.9 83.8 %all-to-all-start = ((bf16[16,128,352]{1,2,0:T(8,128)(2,1)}), bf16[16,128,352]{1,2,0:T(8,128)(2,1)S(1)}, u32[]{:S(2)}, u32[]{:S(2)}) async-start(bf16[16,128,352]{1,2,0:T(8,128)(2,1)} %bitcast.216), calls=%async_computation | async-start | bytes 2883584 | tf_op jit(solution)/shard_map/all_to_all | solution.py:595
  245.6 409.9 %reduce-scatter.2.cloned.1.call-start = ((), (), s32[]{:S(2)}) async-start(), calls=%async_computation.2 | async-start | bytes 13369344 | tf_op jit(solution)/shard_map/reduce_scatter | solution.py:599
  247.6 2.9 copy-start.33
  280.6 37.1 %copy-start.3 = (bf16[1,192,2048]{2,1,0:T(8,128)(2,1)S(1)}, bf16[1,192,2048]{2,1,0:T(8,128)(2,1)}, u32[]{:S(2)}) copy-start(bf16[1,192,2048]{2,1,0:T(8,128)(2,1)} %param.23) | copy-start | bytes 2359300
  317.7 4.8 copy-start.42
  322.5 1.9 copy-start.39
  323.8 1.8 copy-start
  324.6 2.7 copy-start.18
  325.6 2.3 copy-start.32
  325.6 2.3 copy-start.44
  325.7 2.3 copy-start.47
  651.9 3.6 copy-start.1
  651.9 3.6 copy-start.51
  652.0 3.6 copy-start.60
  660.8 6.4 copy-start.16
  669.2 19.5 %copy-start.8 = (f32[3072,128]{1,0:T(8,128)S(1)}, f32[3072,128]{1,0:T(8,128)}, u32[]{:S(2)}) copy-start(f32[3072,128]{1,0:T(8,128)} %get-tuple-element.36) | copy-start | bytes 4718596
  723.5 2.5 copy-start.15
  732.6 50.8 %copy-start.6 = (f32[192,576]{1,0:T(8,128)S(1)}, f32[192,576]{1,0:T(8,128)}, u32[]{:S(2)}) copy-start(f32[192,576]{1,0:T(8,128)} %copy-done.5) | copy-start | bytes 1327108
  732.6 50.8 %copy-start.46 = (f32[512]{0:T(512)S(1)}, f32[512]{0:T(512)}, u32[]{:S(2)}) copy-start(f32[512]{0:T(512)} %param.29) | copy-start | bytes 6148
  732.6 51.6 %copy-start.55 = (f32[192]{0:T(256)S(1)}, f32[192]{0:T(256)}, u32[]{:S(2)}) copy-start(f32[192]{0:T(256)} %copy-done.54) | copy-start | bytes 2308
  732.6 51.6 %copy-start.63 = (f32[32]{0:T(128)S(1)}, f32[32]{0:T(128)}, u32[]{:S(2)}) copy-start(f32[32]{0:T(128)} %copy-done.62) | copy-start | bytes 388
  782.3 3.0 copy-start.21
  793.0 11.4 %copy-start.41 = (bf16[192,16]{0,1:T(8,128)(2,1)S(1)}, bf16[192,16]{0,1:T(8,128)(2,1)}, u32[]{:S(2)}) copy-start(bf16[192,16]{0,1:T(8,128)(2,1)} %copy-done.40) | copy-start | bytes 18436
  803.0 3.5 copy-start.4
  803.0 3.5 copy-start.58
  805.4 2.3 copy-start.35
  805.4 2.3 copy-start.36
  808.6 25.9 %copy-start.61 = (f32[192]{0:T(256)S(1)}, f32[192]{0:T(256)}, u32[]{:S(2)}) copy-start(f32[192]{0:T(256)} %multiply_reduce_fusion.4) | copy-start | bytes 2308
  830.7 3.8 copy-start.25
  831.7 4.2 copy-start.49
  831.7 4.2 copy-start.59
  834.5 2.1 copy-start.19
  834.5 2.1 copy-start.37
  834.5 2.1 copy-start.38
  834.6 2.0 copy-start.53
  (22 other events, 25.8 us)
Sparse Core Ops, SparseCore 0:
  239.2 147.8 all-gather.1
  476.1 162.6 reduce-scatter.1

commit v4 on v3

--- a/solution.py
+++ b/solution.py
@@ -1,4 +1,5 @@
 import functools
+import math
 
 import jax
 import jax.numpy as jnp
@@ -300,20 +301,28 @@
     levels = members // (SIDE * CORES)
     z = me // (SIDE * CORES)
     order = near_first(levels)
-    for s in range(1, levels):
-        for g in gathers:
-            g.relay(s)
-    for s in range(levels):
-        for g in gathers:
-            g.pass_on(pick_from(order, z, s))
-    for g in split:
+
+    def lacked(g, s):
+        k = pick_from(order, z, s)
+        g.take_lacked(k, g.x)
+        g.take_lacked(k, 1 - g.x)
+
+    if gathers:
 
         @pl.loop(0, levels)
         def _(s):
-            k = pick_from(order, z, s)
-            g.take_lacked(k, g.x)
-            g.take_lacked(k, 1 - g.x)
-
+            for g in gathers:
+                g.relay(s + 1)
+            for g in gathers:
+                g.pass_on(pick_from(order, z, s))
+
+            @pl.when(s >= 1)
+            def _():
+                for g in split:
+                    lacked(g, s - 1)
+
+    for g in split:
+        lacked(g, levels - 1)
     for g in gathers:
 
         @pl.loop(0, levels)
@@ -530,12 +539,19 @@
     return out, landed
 
 
-def spread_kernel(src, out, stage, sent, got, local, *, members, sequences):
+def spread_kernel(src, common, out, commons, stage, stage2, sent, got, sent2, got2, local, *, members, sequences):
     me, mine = lax.axis_index("grp"), lax.axis_index("rep")
     barrier = pltpu.get_barrier_semaphore()
-    into = pltpu.make_async_copy(src.at[me], stage, local)
-    out_of = pltpu.make_async_copy(stage, out.at[mine, me], local)
-    into.start()
+    into = [
+        pltpu.make_async_copy(src.at[me], stage, local.at[0]),
+        pltpu.make_async_copy(common, stage2, local.at[1]),
+    ]
+    out_of = [
+        pltpu.make_async_copy(stage, out.at[mine, me], local.at[0]),
+        pltpu.make_async_copy(stage2, commons.at[mine], local.at[1]),
+    ]
+    for copy in into:
+        copy.start()
 
     def other(n):
         return lax.rem(mine + n // members, sequences), lax.rem(me + n % members, members)
@@ -547,44 +563,62 @@
 
     pl.semaphore_wait(barrier, members * sequences - 1)
 
-    def copy(n):
+    def block(n):
         r, to = other(n)
-        return pltpu.make_async_remote_copy(
-            src_ref=src.at[to],
-            dst_ref=out.at[mine, me],
-            send_sem=sent.at[n],
-            recv_sem=got.at[n],
-            device_id={"rep": r, "grp": to},
-            device_id_type=MESH,
-        )
+        return send(src.at[to], out.at[mine, me], sent.at[n], got.at[n], {"rep": r, "grp": to})
+
+    def whole(n):
+        r, to = other(n * members)
+        return send(common, commons.at[mine], sent2.at[n], got2.at[n], {"rep": r, "grp": to})
+
+    @pl.loop(1, sequences)
+    def _(n):
+        whole(n).start()
 
     @pl.loop(1, members * sequences)
     def _(n):
-        copy(n).start()
-
-    into.wait()
-    out_of.start()
+        block(n).start()
+
+    for a, b in zip(into, out_of):
+        a.wait()
+        b.start()
+
+    @pl.loop(1, sequences)
+    def _(n):
+        whole(n).wait()
 
     @pl.loop(1, members * sequences)
     def _(n):
-        copy(n).wait()
-
-    out_of.wait()
-
-
-def spread_blocks(v, members, sequences, collective_id):
+        block(n).wait()
+
+    for copy in out_of:
+        copy.wait()
+
+
+def spread_blocks(v, common, members, sequences, collective_id):
     anywhere = pl.BlockSpec(memory_space=pl.ANY)
     sem = pltpu.SemaphoreType.DMA
     return pl.pallas_call(
         functools.partial(spread_kernel, members=members, sequences=sequences),
-        in_specs=[anywhere],
-        out_specs=anywhere,
-        out_shape=jax.ShapeDtypeStruct((sequences, *v.shape), v.dtype),
-        scratch_shapes=[pltpu.VMEM(v.shape[1:], v.dtype), sem((members * sequences,)), sem((members * sequences,)), sem],
+        in_specs=[anywhere, anywhere],
+        out_specs=[anywhere, anywhere],
+        out_shape=[
+            jax.ShapeDtypeStruct((sequences, *v.shape), v.dtype),
+            jax.ShapeDtypeStruct((sequences, *common.shape), common.dtype),
+        ],
+        scratch_shapes=[
+            pltpu.VMEM(v.shape[1:], v.dtype),
+            pltpu.VMEM(common.shape, common.dtype),
+            sem((members * sequences,)),
+            sem((members * sequences,)),
+            sem((sequences,)),
+            sem((sequences,)),
+            sem((2,)),
+        ],
         compiler_params=pltpu.CompilerParams(collective_id=collective_id, has_side_effects=True),
         cost_estimate=pl.CostEstimate(flops=0, bytes_accessed=v.size * 16, transcendentals=0),
         name=f"spread_{collective_id}",
-    )(v)
+    )(v, common)
 
 
 def gather(v):
@@ -603,54 +637,58 @@
     return lax.optimization_barrier((v, *others))[0]
 
 
+def tie(v, other):
+    first = other[(0,) * other.ndim]
+    return v + jnp.minimum(jnp.abs(first), 0).astype(v.dtype)
+
+
 def block_of(length):
     return next(b for b in (512, 384, 256, 128) if length % b == 0)
 
 
-def attend_kernel(prefix_ref, q_ref, k_ref, v_ref, o_ref, lse_ref, *, block, factor):
+def attend_kernel(prefix_ref, q_ref, k_ref, v_ref, o_ref, lse_ref, *, block, unit):
     i = pl.program_id(0)
     prefix = prefix_ref[0]
     start = i * block
     q = q_ref[...]
-    seen = jnp.where(start < prefix, (prefix + block - 1) // block, 0)
-    stop = jnp.maximum(i + 1, seen)
-    rows = start + lax.broadcasted_iota(jnp.int32, (block, block), 0)
-
-    def step(j, carry):
+    inside = start < prefix
+    stop = jnp.maximum(i + 1, jnp.where(inside, (prefix + block - 1) // block, 0))
+    full = (jnp.where(inside, prefix - 1, start) + 1) // block
+    rows = start + lax.broadcasted_iota(jnp.int32, (block, 1), 0)
+    limit = jnp.where(rows < prefix, prefix - 1, rows)
+
+    def step(j, carry, masked):
         top, total, acc = carry
         at = pl.multiple_of(j * block, block)
         k = k_ref[pl.ds(at, block), :]
         v = v_ref[pl.ds(at, block), :]
-        s = dot_t(q, k) * factor
-        cols = at + lax.broadcasted_iota(jnp.int32, (block, block), 1)
-        limit = jnp.where(rows < prefix, jnp.maximum(rows, prefix - 1), rows)
-        s = jnp.where(cols <= limit, s, -1e30)
+        s = dot_t(q, k)
+        if masked:
+            cols = at + lax.broadcasted_iota(jnp.int32, (1, block), 1)
+            s = jnp.where(cols <= limit, s, -1e30)
         fresh = jnp.maximum(top, jnp.max(s, axis=1, keepdims=True))
-        p = jnp.exp(s - fresh)
-        scale = jnp.exp(top - fresh)
+        p = jnp.exp2((s - fresh) * unit)
+        scale = jnp.exp2((top - fresh) * unit)
         total = total * scale + jnp.sum(p, axis=1, keepdims=True)
         acc = acc * scale + dot(p.astype(BF16), v)
         return fresh, total, acc
 
-    top, total, acc = lax.fori_loop(
-        0,
-        stop,
-        step,
-        (
-            jnp.full((block, 1), -1e30, F32),
-            jnp.zeros((block, 1), F32),
-            jnp.zeros((block, VD), F32),
-        ),
-    )
+    carry = (
+        jnp.full((block, 1), -1e30, F32),
+        jnp.zeros((block, 1), F32),
+        jnp.zeros((block, VD), F32),
+    )
+    carry = lax.fori_loop(0, full, functools.partial(step, masked=False), carry)
+    top, total, acc = lax.fori_loop(full, stop, functools.partial(step, masked=True), carry)
     o_ref[...] = acc / total
-    lse_ref[...] = top + jnp.log(total)
+    lse_ref[...] = top * unit + jnp.log2(total)
 
 
 def attend(prefix, q, k, v):
     length = q.shape[0]
     block = block_of(length)
     return pl.pallas_call(
-        functools.partial(attend_kernel, block=block, factor=QK**-0.5),
+        functools.partial(attend_kernel, block=block, unit=QK**-0.5 * math.log2(math.e)),
         grid=(length // block,),
         in_specs=[
             pl.BlockSpec(memory_space=pltpu.SMEM),
@@ -674,7 +712,7 @@
 
 
 def attend_back_kernel(
-    prefix_ref, q_ref, k_ref, v_ref, d_ref, lse_ref, delta_ref, dq_ref, dk_ref, dv_ref, *, block, factor
+    prefix_ref, q_ref, k_ref, v_ref, d_ref, lse_ref, delta_ref, dq_ref, dk_ref, dv_ref, *, block, factor, unit
 ):
     i = pl.program_id(0)
     prefix = prefix_ref[0]
@@ -689,34 +727,42 @@
     d = d_ref[...]
     lse = lse_ref[...]
     delta = delta_ref[...]
-    seen = jnp.where(start < prefix, (prefix + block - 1) // block, 0)
-    stop = jnp.maximum(i + 1, seen)
-    rows = start + lax.broadcasted_iota(jnp.int32, (block, block), 1)
-
-    def step(j, dq):
+    inside = start < prefix
+    stop = jnp.maximum(i + 1, jnp.where(inside, (prefix + block - 1) // block, 0))
+    full = (jnp.where(inside, prefix - 1, start) + 1) // block
+    rows = start + lax.broadcasted_iota(jnp.int32, (1, block), 1)
+    limit = jnp.where(rows < prefix, prefix - 1, rows)
+
+    def step(j, dq, masked):
         at = pl.multiple_of(j * block, block)
         k = k_ref[pl.ds(at, block), :]
         v = v_ref[pl.ds(at, block), :]
-        s = dot_t(k, q) * factor
-        cols = at + lax.broadcasted_iota(jnp.int32, (block, block), 0)
-        limit = jnp.where(rows < prefix, jnp.maximum(rows, prefix - 1), rows)
-        p = jnp.where(cols <= limit, jnp.exp(s - lse), 0.0)
+        p = jnp.exp2(dot_t(k, q) * unit - lse)
+        if masked:
+            cols = at + lax.broadcasted_iota(jnp.int32, (block, 1), 0)
+            p = jnp.where(cols <= limit, p, 0.0)
         dp = dot_t(v, d)
         ds = (p * (dp - delta)).astype(BF16)
         dv_ref[pl.ds(at, block), :] += dot(p.astype(BF16), d)
-        dk_ref[pl.ds(at, block), :] += dot(ds, q) * factor
+        dk_ref[pl.ds(at, block), :] += dot(ds, q)
         return dq + t_dot(ds, k)
 
-    dq = lax.fori_loop(0, stop, step, jnp.zeros((block, QK), F32))
-    dq_ref[...] = dq * factor
+    dq = lax.fori_loop(0, full, functools.partial(step, masked=False), jnp.zeros((block, QK), F32))
+    dq = lax.fori_loop(full, stop, functools.partial(step, masked=True), dq)
+    dq_ref[...] = (dq * factor).astype(dq_ref.dtype)
+
+    @pl.when(i == pl.num_programs(0) - 1)
+    def _():
+        dk_ref[...] = dk_ref[...] * factor
 
 
 def attend_back(prefix, q, k, v, d, lse, delta):
     length = q.shape[0]
     block = block_of(length)
     whole = lambda i: (0, 0)
+    factor = QK**-0.5
     return pl.pallas_call(
-        functools.partial(attend_back_kernel, block=block, factor=QK**-0.5),
+        functools.partial(attend_back_kernel, block=block, factor=factor, unit=factor * math.log2(math.e)),
         grid=(length // block,),
         in_specs=[
             pl.BlockSpec(memory_space=pltpu.SMEM),
@@ -733,7 +779,7 @@
             pl.BlockSpec((length, VD), whole),
         ],
         out_shape=[
-            jax.ShapeDtypeStruct((length, QK), F32),
+            jax.ShapeDtypeStruct((length, QK), BF16),
             jax.ShapeDtypeStruct((length, QK), F32),
             jax.ShapeDtypeStruct((length, VD), F32),
         ],
@@ -765,8 +811,8 @@
 
 def experts_kernel(
     x_hbm, prob_hbm, rank_ref, back_ref, gate_hbm, up_hbm, down_hbm, own_hbm, sdown_hbm,
-    part_hbm, eg_hbm, eu_hbm, eo_hbm, sh_hbm, prob_out,
-    xs, probs, gate, up, down, own, sdown, tail, rows, acts, part_st, eg_st, eu_st, eo_st, sh_st,
+    part_hbm, part2_hbm, eg_hbm, eu_hbm, eo_hbm, sh_hbm, prob_out,
+    xs, probs, gate, up, down, own, sdown, tail, rows, acts, sacts, part_st, eg_st, eu_st, eo_st, sh_st,
     sent, got, e_sent, e_got, load, store,
     *, members, slots, tile, wide
 ):
@@ -811,9 +857,16 @@
     def stores(s, k):
         n = s % 2
         return [
-            pltpu.make_async_copy(a.at[n], b.at[k], store.at[n, m])
+            pltpu.make_async_copy(a, b.at[k], store.at[n, m])
             for m, (a, b) in enumerate(
-                [(part_st, part_hbm), (eg_st, eg_hbm), (eu_st, eu_hbm), (eo_st, eo_hbm), (sh_st, sh_hbm)]
+                [
+                    (part_st.at[n, :, :, pl.ds(0, width // 2)], part_hbm),
+                    (part_st.at[n, :, :, pl.ds(width // 2, width // 2)], part2_hbm),
+                    (eg_st.at[n], eg_hbm),
+                    (eu_st.at[n], eu_hbm),
+                    (eo_st.at[n], eo_hbm),
+                    (sh_st.at[n], sh_hbm),
+                ]
             )
         ]
 
@@ -828,9 +881,10 @@
             for copy in stores(s, pick_from(order, z, s - 2)):
                 copy.wait()
 
-        for b in range(group):
+        @pl.loop(0, group)
+        def _(b):
             pick = picks(rank_ref[k * group + b, 0:1, :], slots).astype(BF16)
-            rows[b * slots : (b + 1) * slots, :] = dot(pick, xs[k * group + b]).astype(BF16)
+            rows[tiles(b, slots), :] = dot(pick, xs[k * group + b]).astype(BF16)
 
         def keep(at, g, u):
             eg_st[n, :, at] = g.astype(BF16)
@@ -857,19 +911,24 @@
             at = tiles(j, wide)
             eo_st[n, :, at] = dot(acts[...], down[:, at]).astype(BF16)
 
-        for b in range(group):
+        @pl.loop(0, group // 2)
+        def _(h):
+            x = xs[pl.ds(k * group + 2 * h, 2)].reshape(-1, width)
+            pre = dot(x, own[...])
+            sh_st[n, pl.ds(2 * h, 2)] = pre.astype(BF16).reshape(2, -1, 2 * units)
+            act = (silu_parts(pre[:, :units])[0] * pre[:, units:]).astype(BF16)
+            sacts[pl.ds(2 * h, 2)] = act.reshape(2, -1, units)
+
+        @pl.loop(0, group)
+        def _(b):
             i = k * group + b
             pick = picks(rank_ref[i, 0:1, :], slots)
             back = picks_back(back_ref[i], slots).astype(BF16)
             g = jnp.sum(jnp.where(pick, probs[i, 0:1, :], 0.0), axis=1, keepdims=True)
-            pre = dot(xs[i], own[...])
-            sh_st[n, b] = pre.astype(BF16)
-            act = (silu_parts(pre[:, :units])[0] * pre[:, units:]).astype(BF16)
-
-            @pl.loop(0, width // wide)
-            def _(j):
-                at = tiles(j, wide)
-                weighted = (g * eo_st[n, b * slots : (b + 1) * slots, at].astype(F32)).astype(BF16)
+            act = sacts[b]
+            for j in range(width // wide):
+                at = slice(j * wide, (j + 1) * wide)
+                weighted = (g * eo_st[n, tiles(b, slots), at].astype(F32)).astype(BF16)
                 part_st[n, b, :, at] = (dot(back, weighted) + dot(act, sdown[:, at])).astype(BF16)
 
         for copy in stores(s, k):
@@ -903,8 +962,9 @@
     return pl.pallas_call(
         functools.partial(experts_kernel, members=members, slots=slots, tile=tile, wide=512),
         in_specs=[anywhere, anywhere, vmem, vmem] + [anywhere] * 5,
-        out_specs=[anywhere] * 5 + [vmem],
-        out_shape=[jax.ShapeDtypeStruct(s, BF16) for s in shapes] + [jax.ShapeDtypeStruct(prob.shape, F32)],
+        out_specs=[anywhere] * 6 + [vmem],
+        out_shape=[jax.ShapeDtypeStruct((*shapes[0][:3], width // 2), BF16)] * 2
+        + [jax.ShapeDtypeStruct(s, BF16) for s in shapes[1:]] + [jax.ShapeDtypeStruct(prob.shape, F32)],
         scratch_shapes=[
             pltpu.VMEM((members, tokens, width), BF16),
             pltpu.VMEM(prob.shape, F32),
@@ -916,9 +976,10 @@
             pltpu.VMEM((width, tile), BF16),
             pltpu.VMEM((packed, width), BF16),
             pltpu.VMEM((packed, hidden), BF16),
+            pltpu.VMEM((group, tokens, own.shape[1] // 2), BF16),
         ]
         + [pltpu.VMEM((2, *s[1:]), BF16) for s in shapes]
-        + [sem((6, members)), sem((2, members)), sem((members,)), sem((members,)), sem((7,)), sem((2, 5))],
+        + [sem((6, members)), sem((2, members)), sem((members,)), sem((members,)), sem((7,)), sem((2, 6))],
         compiler_params=pltpu.CompilerParams(
             collective_id=collective_id, has_side_effects=True, vmem_limit_bytes=63 * 1024 * 1024
         ),
@@ -930,7 +991,7 @@
 
 
 def experts_back_kernel(
-    c_hbm, rank_ref, back_ref, prob_ref, eg_hbm, eu_hbm, eo_hbm, sh_hbm, gate_hbm, up_hbm, down_hbm, own_hbm, sdown_hbm,
+    c_hbm, c2_hbm, rank_ref, back_ref, prob_ref, eg_hbm, eu_hbm, eo_hbm, sh_hbm, gate_hbm, up_hbm, down_hbm, own_hbm, sdown_hbm,
     out, dg_out,
     part, cs, eg, eu, eo, sh, gate, up, down, own, sdown, rows, d_gate, d_up, dg_st, dg_in,
     *sems, members, slots, tile, wide
@@ -949,12 +1010,18 @@
     exchange = Exchange(dg_st, dg_in, e_sent, e_got, members)
 
     def cotangents(s):
-        return pltpu.make_async_copy(c_hbm.at[pick_from(order, z, s)], cs.at[s % 2], fetch.at[s % 2])
+        k = pick_from(order, z, s)
+        return [
+            pltpu.make_async_copy(
+                a.at[k], cs.at[s % 2, :, :, pl.ds(h * (width // 2), width // 2)], fetch.at[4 + s % 2 * 2 + h]
+            )
+            for h, a in enumerate([c_hbm, c2_hbm])
+        ]
 
     def kept(s):
         k = pick_from(order, z, s)
         return [
-            pltpu.make_async_copy(a.at[k], b, fetch.at[2 + m])
+            pltpu.make_async_copy(a.at[k], b, fetch.at[m])
             for m, (a, b) in enumerate([(eo_hbm, eo), (eg_hbm, eg), (eu_hbm, eu), (sh_hbm, sh)])
         ]
 
@@ -964,8 +1031,7 @@
             [(down_hbm, down), (gate_hbm, gate), (up_hbm, up), (own_hbm, own), (sdown_hbm, sdown)]
         )
     ]
-    cotangents(0).start()
-    for copy in kept(0):
+    for copy in cotangents(0) + kept(0):
         copy.start()
     for copy in loads:
         copy.start()
@@ -978,17 +1044,20 @@
     def _(s):
         k = pick_from(order, z, s)
         n = s % 2
-        cotangents(s).wait()
+        for copy in cotangents(s):
+            copy.wait()
         load_eo, load_eg, load_eu, load_sh = kept(s)
 
         @pl.when(s + 1 < levels)
         def _():
-            cotangents(s + 1).start()
+            for copy in cotangents(s + 1):
+                copy.start()
 
         load_eo.wait()
-        for b in range(group):
+        @pl.loop(0, group)
+        def _(b):
             i = k * group + b
-            at = slice(b * slots, (b + 1) * slots)
+            at = tiles(b, slots)
             pick = picks(rank_ref[i, 0:1, :], slots)
             c = dot(pick.astype(BF16), cs[n, b])
             g = jnp.sum(jnp.where(pick, prob_ref[i, 0:1, :], 0.0), axis=1, keepdims=True)
@@ -1032,19 +1101,18 @@
             eo[:, at] = (dot_t(d_gate[...], gate[at, :]) + dot_t(d_up[...], up[at, :])).astype(BF16)
 
         load_sh.wait()
-        for b in range(group):
+        @pl.loop(0, group)
+        def _(b):
             i = k * group + b
             back = picks_back(back_ref[i], slots).astype(BF16)
             d = dot_t(cs[n, b], sdown[...])
             pre = sh[b].astype(F32)
             act, slope = silu_parts(pre[:, :units])
             both = jnp.concatenate([d * pre[:, units:] * slope, d * act], axis=1).astype(BF16)
-
-            @pl.loop(0, width // wide)
-            def _(j):
-                at = tiles(j, wide)
+            for j in range(width // wide):
+                at = slice(j * wide, (j + 1) * wide)
                 part[i, :, at] = (
-                    dot(back, eo[b * slots : (b + 1) * slots, at]) + dot_t(both, own[at, :])
+                    dot(back, eo[tiles(b, slots), at]) + dot_t(both, own[at, :])
                 ).astype(BF16)
 
         reduce.start(k)
@@ -1072,8 +1140,8 @@
     dg_out[...] = dg_in[...]
 
 
-def experts_backward(c, rank, back, prob, kept, gate, up, down, own, sdown, slots, members, collective_id):
-    _, tokens, width = c.shape
+def experts_backward(cs, rank, back, prob, kept, gate, up, down, own, sdown, slots, members, collective_id):
+    tokens, width = cs[0].shape[1], cs[0].shape[2] * 2
     hidden = gate.shape[1]
     group = SIDE * CORES
     levels = members // group
@@ -1084,7 +1152,7 @@
     eg, eu, eo, sh = kept
     return pl.pallas_call(
         functools.partial(experts_back_kernel, members=members, slots=slots, tile=256, wide=512),
-        in_specs=[anywhere, vmem, vmem, vmem] + [anywhere] * 9,
+        in_specs=[anywhere, anywhere, vmem, vmem, vmem] + [anywhere] * 9,
         out_specs=[vmem, vmem],
         out_shape=[
             jax.ShapeDtypeStruct((tokens, width), BF16),
@@ -1109,7 +1177,7 @@
             pltpu.VMEM((members, 8, tokens), F32),
         ]
         + Reduce.scratch(members, tokens, width, BF16)
-        + [sem((members,)), sem((members,)), sem((5,)), sem((6,))],
+        + [sem((members,)), sem((members,)), sem((5,)), sem((8,))],
         compiler_params=pltpu.CompilerParams(
             collective_id=collective_id, has_side_effects=True, vmem_limit_bytes=67_043_328
         ),
@@ -1117,7 +1185,11 @@
             flops=12 * members * slots * width * hidden, bytes_accessed=60_000_000, transcendentals=0
         ),
         name="experts_backward",
-    )(c.reshape(levels, group, tokens, width), rank, back, prob, *kept, gate, up, down, own, sdown)
+    )(*(c.reshape(levels, group, tokens, -1) for c in cs), rank, back, prob, *kept, gate, up, down, own, sdown)
+
+
+def by_owner(gradient, members):
+    return gradient.astype(BF16).reshape(gradient.shape[0], members, -1).transpose(1, 0, 2)
 
 
 def pack(v):
@@ -1210,22 +1282,27 @@
         [query[:, :, :NOPE], rotate(query[:, :, NOPE:], cosine[:, None], sine[:, None])], axis=-1
     ).astype(BF16)
     (all_latent,), (q_packed,) = communicate(
-        [jnp.concatenate([compressed, k_rope], axis=-1)], [pack(query.transpose(1, 0, 2))], members, 2
+        [jnp.concatenate([compressed, k_rope], axis=-1)], [after(pack(query.transpose(1, 0, 2)), own_shared)], members, 2
     )
     all_latent = all_latent.reshape(length, KVR + ROPE)
     q_head = unpack(q_packed).reshape(length, QK)
+    q_head, c_first = lax.optimization_barrier((q_head, cotangent[:, : width // 2]))
     expanded = dot(all_latent[:, :KVR], own_kvb).astype(BF16)
     k_head = jnp.concatenate([expanded[:, :NOPE], all_latent[:, KVR:]], axis=-1)
     v_head = expanded[:, NOPE:]
     mixture, lse = attend(prefix_len, q_head, k_head, v_head)
-    _, (mixed,) = communicate([], [mixture.astype(BF16).reshape(members, tokens, VD)], members, 3)
-    mixed = mixed.transpose(1, 0, 2).reshape(tokens, H * VD)
+    _, (mixed_parts,) = communicate([], [mixture.astype(BF16).reshape(members, tokens, VD)], members, 3)
+    mixed = mixed_parts.transpose(1, 0, 2).reshape(tokens, H * VD)
     o_small = dot(mixed, oa_down).astype(BF16)
     middle = inputs + dot(mixed, full_o) + dot(o_small, oa_up)
     ffn_in = root_norm(middle, ffn_gain).astype(BF16)
     route_probs = jax.nn.softmax(dot(ffn_in, full_router), axis=-1)
 
-    all_c = gather(after(cotangent, q_head))
+    half = width // 2
+    all_c = [
+        gather(c_first).reshape(members, tokens, half),
+        gather(tie(cotangent[:, half:], mixed_parts)).reshape(members, tokens, half),
+    ]
     chosen = chosen_all[:, 0] > 0.5
     order = jnp.arange(tokens, dtype=jnp.int32)
     before = (order[:, None] < order[None, :]).astype(BF16)
@@ -1234,14 +1311,16 @@
     rank = jnp.broadcast_to(rank[:, None, :], (members, 8, tokens))
     weights = (expert_gate[0], expert_up_weight[0], expert_down[0], own_shared, shared_down)
     prob_blocks = jnp.broadcast_to(route_probs.T[:, None, :], (experts, 8, tokens))
-    partial, *kept, prob_parts = experts_forward(
+    *partial, kept_gate, kept_up, kept_out, kept_shared, prob_parts = experts_forward(
         ffn_in, prob_blocks, rank, back, *weights, slots, members, 4
     )
-    ffn_out = scatter_sum(partial.reshape(length, width))
-    output = (middle + ffn_out.astype(F32)).astype(BF16)
+    kept = (kept_gate, kept_up, kept_out, kept_shared)
+    partial = [part.reshape(length, half) for part in partial]
+    ffn_out = [scatter_sum(partial[0])]
     d_own, d_route = experts_backward(
-        all_c.reshape(members, tokens, width), rank, back, prob_parts, kept, *weights, slots, members, 5
-    )
+        all_c, rank, back, prob_parts, kept, *weights, slots, members, 5
+    )
+    ffn_out.append(scatter_sum(after(partial[1], d_own)))
     d_route = d_route[:, 0].T
     d_logits = (
         route_probs * (d_route - jnp.sum(route_probs * d_route, axis=-1, keepdims=True))
@@ -1260,11 +1339,12 @@
         prefix_len, q_head, k_head, v_head, d_head, lse.reshape(1, length), delta.reshape(1, length)
     )
     d_expanded = jnp.concatenate([dk[:, :NOPE], dv], axis=-1).astype(BF16)
-    d_latents, (d_query,) = reduce_blocks(
+    o_parts = jnp.concatenate([by_owner(g, members) for g in (grad_odown, grad_oup)], axis=-1)
+    d_latents, (d_query, o_landed) = reduce_blocks(
         jnp.concatenate([dot_t(d_expanded, own_kvb), dk[:, NOPE:]], axis=-1)
         .astype(BF16)
         .reshape(members, tokens, KVR + ROPE),
-        [pack(dq.astype(BF16).reshape(members, tokens, QK))],
+        [pack(dq.reshape(members, tokens, QK)), o_parts],
         members,
         7,
     )
@@ -1285,25 +1365,25 @@
         .reshape(tokens, H * QK)
         .astype(BF16)
     )
+    first, second, _ = lax.optimization_barrier((*ffn_out, d_query))
+    output = (middle + jnp.concatenate([first, second], axis=-1).astype(F32)).astype(BF16)
     grad_qup = t_dot(q_small, d_query)
     d_qsmall = dot_t(d_query, qa_up).astype(BF16)
     grad_qdown = t_dot(d_qsmall, normed)
     d_normed = dot_t(d_query, full_q) + dot_t(d_qsmall, qa_down) + dot_t(d_latent, full_kva)
     grad_inputs = (d_middle + norm_back(inputs, attn_gain, d_normed)).astype(BF16)
 
-    rank_of = qa_up.shape[0]
-    parts = [
-        g.astype(BF16).reshape(rank_of, members, -1).transpose(1, 0, 2)
-        for g in (grad_qdown, grad_qup, grad_odown, grad_oup)
-    ]
-    sizes = [g.shape[2] for g in parts]
-    lanes = 128
-    named = jnp.broadcast_to(adapter.astype(BF16), (members, rank_of, lanes))
-    shares = spread_blocks(jnp.concatenate(parts + [named], axis=-1), members, sequences, 8)
-    numbers = shares[:, 0, 0, -1].astype(jnp.int32)
-    share = jnp.sum(shares[..., :-lanes].astype(F32), axis=1)
+    q_parts = jnp.concatenate([by_owner(g, members) for g in (grad_qdown, grad_qup)], axis=-1)
+    o_share = jnp.sum(o_landed.astype(F32), axis=0)
+    named = jnp.broadcast_to(adapter.astype(F32), (o_share.shape[0], 128))
+    q_shares, o_shares = spread_blocks(
+        q_parts, jnp.concatenate([o_share, named], axis=-1), members, sequences, 8
+    )
+    numbers = o_shares[:, 0, -1].astype(jnp.int32)
+    shares = jnp.concatenate([jnp.sum(q_shares.astype(F32), axis=1), o_shares[:, :, :-128]], axis=-1)
     selector = (jnp.arange(q_down.shape[0], dtype=jnp.int32)[:, None] == numbers[None, :]).astype(F32)
-    summed = jnp.sum(selector[:, :, None, None] * share[None], axis=1)
+    summed = jnp.sum(selector[:, :, None, None] * shares[None], axis=1)
+    sizes = [g.shape[1] // members for g in (grad_qdown, grad_qup, grad_odown, grad_oup)]
     ends = [sum(sizes[: n + 1]) for n in range(4)]
     outs = [summed[:, :, e - s : e] for e, s in zip(ends, sizes)]
     return (

time: 858 us -> 820 us (0.956)
  Pallas kernels: 690 us -> 653 us
    pallas_call x1, Pallas kernels: 172 us -> 140 us  [experts_backward(): pl.pallas_call(functools.partial(experts_back_kernel, members=members, sl...]
    pallas_call x1, Pallas kernels: 49.7 us -> 63.3 us  [reduce_blocks(): pl.pallas_call(functools.partial(reduce_kernel, members=members, n_e=n_e)...]
    pallas_call x4, Pallas kernels: 246 us -> 235 us  [communicate(): pl.pallas_call(functools.partial(comm_kernel, members=members, splits=tup...]
    unnamed x134 -> x122, local copies, waits for them, and re-layouts: 15.1 us -> 17.7 us
  transfers between devices with their start and end apart: 3 -> 5, of which waited for: 0 -> 1; matrix products, arithmetic and copies ran while one was open for 4% -> 13% of each run, Pallas kernels for 45% -> 59%
where the time goes in v4:
time: 820 us; the launch traced here: 815 us
  Pallas kernels  653 us (80%)
  matrix products  51.7 us (6%)
  local copies, waits for them, and re-layouts  49.9 us (6%)
  other arithmetic  36.4 us (4%)
  between operations  17.1 us (2%)
    pallas_call x4, Pallas kernels, communicate(): pl.pallas_call(functools.partial(comm_kernel, members=members, splits=tup...  235 us
    pallas_call x1, Pallas kernels, experts_forward(): pl.pallas_call(functools.partial(experts_kernel, members=members, slots=s...  149 us
    pallas_call x1, Pallas kernels, experts_backward(): pl.pallas_call(functools.partial(experts_back_kernel, members=members, sl...  140 us
    pallas_call x1, Pallas kernels, reduce_blocks(): pl.pallas_call(functools.partial(reduce_kernel, members=members, n_e=n_e)...  63.3 us
    pallas_call x1, Pallas kernels, attend_back(): pl.pallas_call(functools.partial(attend_back_kernel, block=block, factor=...  29.6 us
    dot_general x9, matrix products, dot_t(): lax.dot_general(former, latter, (((1,), (1,)), ((), ())), preferred_eleme...  24.9 us
    dot_general x10, matrix products, dot(): return jnp.dot(former, latter, preferred_element_type=F32)  23.4 us
    pallas_call x1, Pallas kernels, attend(): pl.pallas_call(functools.partial(attend_kernel, block=block, unit=QK ** (...  21.9 us
  transfers between devices with their start and end apart: 5, of which 1 were waited for; matrix products, arithmetic and copies ran while one was open for 13% of the time, Pallas kernels for 59%

profile of v4, /device:TPU:0, one launch (start us, length us, event | category | flops | bytes accessed | tf_op | source)
XLA Modules:
  0.0 815.0 jit_solution(4761499466422277611)
XLA Ops:
  7.2 1.8 copy.98.refs_0_
  9.0 1.4 copy.99.refs_3_
  10.4 1.7 copy.162
  12.8 1.5 copy.105
  15.4 115.3 %communicate_1.1 = (bf16[16,128,576]{2,1,0:T(8,128)(2,1)}, bf16[16,128,3072]{2,1,0:T(8,128)(2,1)}, bf16[16,128,2048]{2,1,0:T(8,128)(2,1)}, bf16[16,128,16]{2,1,0...) custom-call(bf16[128,576]{1,0:T(8,128)(2,1)} %copy.98.refs_0_, bf16[128,3072]{1,0:T(8,128)(2,1)} %refs_1_.1, ...), custom_call_target="tpu_custom_call" | custom-call | bytes 189661184 | tf_op jit(solution)/shard_map/communicate_1/pallas_call | solution.py:350
  130.7 1.3 copy.106
  132.0 4.5 all-to-all-start
  138.7 6.1 fusion.101
  146.6 2.8 convolution_add_fusion
  149.4 3.1 reshape.309
  153.8 2.8 fusion.103
  166.1 2.6 copy.107
  168.7 61.0 %communicate_2.1 = (bf16[16,192,576]{2,1,0:T(8,128)(2,1)}, bf16[16,288,128]{2,1,0:T(8,128)(2,1)}) custom-call(bf16[192,576]{1,0:T(8,128)(2,1)} %pad_maximum_fusion.3.refs_0_, bf16[16,288,128]{2,1,0:T(8,128)(2,1)} %maximum_maximum_fusion.1.refs_1_), custom_call_target="tpu_custom_call" | custom-call | bytes 37748736 | tf_op jit(solution)/shard_map/communicate_2/pallas_call | solution.py:350
  229.7 1.4 fusion.110
  231.3 1.5 maximum_maximum_fusion
  234.9 2.9 convolution_convert_fusion
  238.7 1.5 pad_maximum_fusion.1.k_ref
  240.2 21.9 %attend.1 = (f32[3072,128]{1,0:T(8,128)}, f32[3072,1]{1,0:T(8,128)}) custom-call(s32[1]{0:T(128)S(6)} %copy.166.prefix_ref, bf16[3072,192]{1,0:T(8,128)(2,1)} %bitcast.231, bf16[3072,192]{1,0:T(8,128)(2,1)} %pad_maximum_fusion.1.k_ref, bf16[3072,128]{1,0:T(8,128)(2,1)} %get-tuple-element.82.v_ref), custom_call_target="tpu_custom_call" | custom-call | flops 3019898880 | bytes 3072000 | tf_op jit(solution)/shard_map/attend/pallas_call | solution.py:690
  262.1 2.4 convert_element_type.165
  264.5 27.5 %communicate_3.1 = bf16[16,192,128]{2,1,0:T(8,128)(2,1)} custom-call(bf16[16,192,128]{2,1,0:T(8,128)(2,1)} %bitcast.222), custom_call_target="tpu_custom_call" | custom-call | bytes 6291456 | tf_op jit(solution)/shard_map/communicate_3/pallas_call | solution.py:350
  295.9 1.7 copy.110.back_ref
  298.8 4.6 fusion.3
  303.4 1.3 multiply_reduce_fusion.2
  308.5 149.0 %experts_forward.1 = (bf16[4,4,192,1024]{3,2,1,0:T(8,128)(2,1)}, bf16[4,4,192,1024]{3,2,1,0:T(8,128)(2,1)}, bf16[4,384,1408]{2,1,0:T(8,128)(2,1)}, bf16[4,384,14...) custom-call(bf16[192,2048]{1,0:T(8,128)(2,1)} %copy-done.13, ...), custom_call_target="tpu_custom_call" | custom-call | flops 53150220288 | bytes 60000000 | tf_op jit(solution)/shard_map/experts_forward/pallas_call | solution.py:962
  457.6 1.3 copy-done.21
  460.0 140.3 %experts_backward.1 = (bf16[192,2048]{1,0:T(8,128)(2,1)}, f32[16,8,192]{2,1,0:T(8,128)}) custom-call(bf16[4,4,192,1024]{3,2,1,0:T(8,128)(2,1)} %bitcast.252, bf16[4,4,192,1024]{3,2,1,0:T(8,128)(2,1)} %bitcast.253, f32[16,8,192]{2,1,0:T(8,128)} %broadcast_in_dim.18.rank_ref, f32[16,192,1]{2,1,0:T(8,128)} %copy.110.back_ref, ...), custom_call_target="tpu_custom_call" | custom-call | flops 53150220288 | bytes 60000000 | tf_op jit(solution)/shard_map/experts_backward/pallas_call | solution.py:1153
  602.0 3.4 multiply_reduce_fusion.1
  605.5 1.4 copy-done.1
  606.9 2.0 subtract_add_fusion
  610.1 6.3 fusion.96
  618.7 31.3 %communicate_6.1 = bf16[16,192,128]{2,1,0:T(8,128)(2,1)} custom-call(bf16[16,192,128]{2,1,0:T(8,128)(2,1)} %bitcast.220), custom_call_target="tpu_custom_call" | custom-call | bytes 6291456 | tf_op jit(solution)/shard_map/communicate_6/pallas_call | solution.py:350
  650.0 2.8 multiply_reduce_fusion
  652.8 29.6 %attend_back.1 = (bf16[3072,192]{1,0:T(8,128)(2,1)}, f32[3072,192]{1,0:T(8,128)}, f32[3072,128]{1,0:T(8,128)}) custom-call(s32[1]{0:T(128)S(6)} %copy.166.prefix_ref, bf16[3072,192]{1,0:T(8,128)(2,1)} %bitcast.232, bf16[3072,192]{1,0:T(8,128)(2,1)} %pad_maximum_fusion.1.k_ref, bf16[3072,128]{1,0:T(8,128)(2,1)} %get-tuple-element.82.v_ref, ...), custom_call_target="tpu_custom_call" | custom-call | flops 7851737088 | bytes 6144000 | tf_op jit(solution)/shard_map/attend_back/pallas_call | solution.py:764
  682.4 2.1 convert.47
  689.0 1.3 maximum_maximum_fusion.2.refs_1_
  691.9 2.4 pad_maximum_fusion.refs_0_
  694.3 63.3 %reduce_7.1 = (bf16[192,576]{1,0:T(8,128)(2,1)}, bf16[16,288,128]{2,1,0:T(8,128)(2,1)}, bf16[16,16,256]{2,1,0:T(8,128)(2,1)}) custom-call(bf16[16,192,576]{2,1,0:T(8,128)(2,1)} %pad_maximum_fusion.refs_0_, bf16[16,288,128]{2,1,0:T(8,128)(2,1)} %maximum_maximum_fusion.2.refs_1_, bf16[16,16,256]{2,1,0:T(8,128)(2,1)} %pad_maximum_fusion.5.refs_2_), custom_call_target="tpu_custom_call" | custom-call | bytes 28311552 | tf_op jit(solution)/shard_map/reduce_7/pallas_call | solution.py:524
  757.6 1.3 slice.165
  761.7 2.0 copy.115
  763.8 3.9 convert_element_type.180
  768.5 1.5 convolution_convert_fusion.1
  770.3 1.7 convolution_convert_fusion.6
  772.0 1.5 fusion.25
  774.9 14.1 %spread_8.1 = (bf16[2,16,16,320]{3,2,1,0:T(8,128)(2,1)}, f32[2,16,384]{2,1,0:T(8,128)}) custom-call(bf16[16,16,320]{2,1,0:T(8,128)(2,1)} %pad_maximum_fusion.4.src, f32[16,384]{1,0:T(8,128)} %concatenate.96.common), custom_call_target="tpu_custom_call" | custom-call | bytes 1310720 | tf_op jit(solution)/shard_map/spread_8/pallas_call | solution.py:601
  793.6 7.6 fusion.113
  801.2 1.3 convolution_add_fusion.3
  804.6 1.3 fusion.29
  805.9 2.2 fusion.26
  (211 shorter events, 50.5 us)
Async XLA Ops:
  7.2 7.0 copy-start.28
  132.0 5.1 copy-start.3
  132.0 6.6 copy-start.47
  132.0 34.1 %all-to-all-start = ((bf16[16,128,352]{1,2,0:T(8,128)(2,1)}), bf16[16,128,352]{1,2,0:T(8,128)(2,1)}, u32[]{:S(2)}, u32[]{:S(2)}) async-start(bf16[16,128,352]{1,2,0:T(8,128)(2,1)} %bitcast.14), calls=%async_computation | async-start | bytes 2883584 | tf_op jit(solution)/shard_map/all_to_all | solution.py:629
  136.6 323.5 %all-gather.3.cloned.1.call-start = ((), (), s32[]{:S(2)}) async-start(), calls=%async_computation.4 | async-start | bytes 6684672 | tf_op jit(solution)/shard_map/all_gather | solution.py:625
  138.0 15.8 %copy-start.52 = (f32[192]{0:T(256)}, f32[192]{0:T(256)S(1)}, u32[]{:S(2)}) copy-start(f32[192]{0:T(256)S(1)} %get-tuple-element.102) | copy-start | bytes 2308
  153.8 2.9 copy-start.56
  153.8 2.9 copy-start.49
  160.2 1.9 copy-start.7
  160.2 2.6 copy-start.40
  162.8 2.3 copy-start.43
  229.7 1.5 copy-start.20
  232.8 2.1 copy-start.30
  232.8 227.2 %all-gather.5.cloned.1.call-start = ((), (), s32[]{:S(2)}) async-start(), calls=%async_computation.5 | async-start | bytes 6684672 | tf_op jit(solution)/shard_map/all_gather | solution.py:625
  262.1 31.8 %copy-start.16 = (bf16[1,192,2048]{2,1,0:T(8,128)(2,1)S(1)}, bf16[1,192,2048]{2,1,0:T(8,128)(2,1)}, u32[]{:S(2)}) copy-start(bf16[1,192,2048]{2,1,0:T(8,128)(2,1)} %param.24) | copy-start | bytes 2359300
  292.0 5.6 copy-start.11
  294.7 4.1 copy-start.4
  294.7 511.1 %reduce-scatter.3.cloned.1.call-start = ((), (), s32[]{:S(2)}) async-start(), calls=%async_computation.3 | async-start | bytes 6684672 | tf_op jit(solution)/shard_map/reduce_scatter | solution.py:633
  298.8 4.6 copy-start.37
  303.4 2.0 copy-start.34
  304.8 1.8 copy-start
  304.8 1.4 copy-start.18
  305.6 2.9 copy-start.13
  306.6 1.9 copy-start.39
  457.5 1.4 copy-start.21
  457.6 348.3 %reduce-scatter.5.cloned.1.call-start = ((), (), s32[]{:S(2)}) async-start(), calls=%async_computation.6 | async-start | bytes 6684672 | tf_op jit(solution)/shard_map/reduce_scatter | solution.py:633
  605.5 1.4 copy-start.46
  605.5 1.4 copy-start.55
  684.5 2.0 copy-start.23
  684.5 2.4 copy-start.22
  689.0 1.5 slice-start.1
  689.0 1.7 copy-start.31
  757.6 1.5 copy-start.19
  763.8 3.9 copy-start.32
  763.8 4.7 copy-start.36
  768.5 3.5 copy-start.48
  768.5 3.5 copy-start.53
  770.2 3.3 copy-start.33
  772.0 20.8 %copy-start.41 = (f32[512]{0:T(512)S(1)}, f32[512]{0:T(512)}, u32[]{:S(2)}) copy-start(f32[512]{0:T(512)} %param.29) | copy-start | bytes 6148
  773.5 19.5 %copy-start.50 = (f32[192]{0:T(256)S(1)}, f32[192]{0:T(256)}, u32[]{:S(2)}) copy-start(f32[192]{0:T(256)} %copy-done.49) | copy-start | bytes 2308
  773.5 19.5 %copy-start.57 = (f32[32]{0:T(128)S(1)}, f32[32]{0:T(128)}, u32[]{:S(2)}) copy-start(f32[32]{0:T(128)} %copy-done.56) | copy-start | bytes 388
  773.6 19.9 %copy-start.44 = (f32[192]{0:T(256)S(1)}, f32[192]{0:T(256)}, u32[]{:S(2)}) copy-start(f32[192]{0:T(256)} %copy-done.43) | copy-start | bytes 2308
  773.6 19.9 %copy-start.54 = (f32[192]{0:T(256)S(1)}, f32[192]{0:T(256)}, u32[]{:S(2)}) copy-start(f32[192]{0:T(256)} %get-tuple-element.103) | copy-start | bytes 2308
  789.0 3.8 copy-start.8
  789.0 3.8 copy-start.10
  790.8 2.8 copy-start.2
  793.6 8.9 %copy-start.17 = (bf16[16,128,576]{2,1,0:T(8,128)(2,1)S(1)}, bf16[16,128,576]{2,1,0:T(8,128)(2,1)}, u32[]{:S(2)}) copy-start(bf16[16,128,576]{2,1,0:T(8,128)(2,1)} %get-tuple-element.40) | copy-start | bytes 7077892
  802.6 2.0 copy-start.51
  (17 other events, 17.6 us)
Sparse Core Ops, SparseCore 0:
  232.9 74.9 all-gather.2
  310.2 87.3 all-gather.4
  457.7 109.6 reduce-scatter.2
  605.6 100.8 reduce-scatter.4

commit v5 on v4

--- a/solution.py
+++ b/solution.py
@@ -642,68 +642,104 @@
     return v + jnp.minimum(jnp.abs(first), 0).astype(v.dtype)
 
 
-def block_of(length):
-    return next(b for b in (512, 384, 256, 128) if length % b == 0)
-
-
-def attend_kernel(prefix_ref, q_ref, k_ref, v_ref, o_ref, lse_ref, *, block, unit):
-    i = pl.program_id(0)
+def key_blocks(start, rows, keys, length):
+    end = start + rows
+    end = jnp.where(start < length // 2, jnp.maximum(end, length // 2), end)
+    return (start + 1) // keys, (end + keys - 1) // keys
+
+
+def attend_kernel(prefix_ref, q_ref, k_ref, v_ref, o_ref, lse_ref, mixed, blocks, sent, got, local, *, members, unit):
+    me = lax.axis_index("grp")
+    tokens = blocks.shape[1]
+    block, keys = 2 * tokens, 4 * tokens
+    turns = members // 2
     prefix = prefix_ref[0]
-    start = i * block
-    q = q_ref[...]
-    inside = start < prefix
-    stop = jnp.maximum(i + 1, jnp.where(inside, (prefix + block - 1) // block, 0))
-    full = (jnp.where(inside, prefix - 1, start) + 1) // block
-    rows = start + lax.broadcasted_iota(jnp.int32, (block, 1), 0)
-    limit = jnp.where(rows < prefix, prefix - 1, rows)
-
-    def step(j, carry, masked):
-        top, total, acc = carry
-        at = pl.multiple_of(j * block, block)
-        k = k_ref[pl.ds(at, block), :]
-        v = v_ref[pl.ds(at, block), :]
-        s = dot_t(q, k)
-        if masked:
-            cols = at + lax.broadcasted_iota(jnp.int32, (1, block), 1)
-            s = jnp.where(cols <= limit, s, -1e30)
-        fresh = jnp.maximum(top, jnp.max(s, axis=1, keepdims=True))
-        p = jnp.exp2((s - fresh) * unit)
-        scale = jnp.exp2((top - fresh) * unit)
-        total = total * scale + jnp.sum(p, axis=1, keepdims=True)
-        acc = acc * scale + dot(p.astype(BF16), v)
-        return fresh, total, acc
-
-    carry = (
-        jnp.full((block, 1), -1e30, F32),
-        jnp.zeros((block, 1), F32),
-        jnp.zeros((block, VD), F32),
-    )
-    carry = lax.fori_loop(0, full, functools.partial(step, masked=False), carry)
-    top, total, acc = lax.fori_loop(full, stop, functools.partial(step, masked=True), carry)
-    o_ref[...] = acc / total
-    lse_ref[...] = top * unit + jnp.log2(total)
-
-
-def attend(prefix, q, k, v):
+
+    def block_to(n):
+        return send(blocks.at[n], mixed.at[me], sent.at[n], got.at[me], n)
+
+    def from_device(n):
+        return send(blocks.at[n], mixed.at[n], sent.at[n], got.at[n], n)
+
+    own = pltpu.make_async_copy(blocks.at[me], mixed.at[me], local)
+    meet(members)
+
+    @pl.loop(0, turns)
+    def _(n):
+        i = lax.rem(me // 2 + n, turns)
+        start = pl.multiple_of(i * block, block)
+        here = pl.ds(start, block)
+        q = q_ref[here, :]
+        rows = start + lax.broadcasted_iota(jnp.int32, (block, 1), 0)
+        limit = jnp.where(rows < prefix, prefix - 1, rows)
+        limit = jnp.maximum(limit, rows)
+
+        def step(j, carry, masked):
+            top, total, acc = carry
+            at = pl.multiple_of(j * keys, keys)
+            k = k_ref[pl.ds(at, keys), :]
+            v = v_ref[pl.ds(at, keys), :]
+            s = dot_t(q, k)
+            if masked:
+                cols = at + lax.broadcasted_iota(jnp.int32, (1, keys), 1)
+                s = jnp.where(cols <= limit, s, -1e30)
+            fresh = jnp.maximum(top, jnp.max(s, axis=1, keepdims=True))
+            p = jnp.exp2((s - fresh) * unit)
+            scale = jnp.exp2((top - fresh) * unit)
+            total = total * scale + jnp.sum(p, axis=1, keepdims=True)
+            acc = acc * scale + dot(p.astype(BF16), v)
+            return fresh, total, acc
+
+        carry = (
+            jnp.full((block, 1), -1e30, F32),
+            jnp.zeros((block, 1), F32),
+            jnp.zeros((block, VD), F32),
+        )
+        full, stop = key_blocks(start, block, keys, q_ref.shape[0])
+        carry = lax.fori_loop(0, full, functools.partial(step, masked=False), carry)
+        top, total, acc = lax.fori_loop(full, stop, functools.partial(step, masked=True), carry)
+        o = acc / total
+        o_ref[here, :] = o
+        lse_ref[here, :] = top * unit + jnp.log2(total)
+        blocks[pl.ds(2 * i, 2)] = o.astype(BF16).reshape(2, tokens, VD)
+        for t in range(2):
+            to = 2 * i + t
+
+            @pl.when(to == me)
+            def _():
+                own.start()
+
+            @pl.when(to != me)
+            def _():
+                block_to(to).start()
+
+    own.wait()
+
+    @pl.loop(1, members)
+    def _(d):
+        n = lax.rem(me + d, members)
+        from_device(n).wait_recv()
+        block_to(n).wait_send()
+
+
+def attend(prefix, q, k, v, members, collective_id):
     length = q.shape[0]
-    block = block_of(length)
+    tokens = length // members
+    vmem = pl.BlockSpec(memory_space=pltpu.VMEM)
+    sem = pltpu.SemaphoreType.DMA
     return pl.pallas_call(
-        functools.partial(attend_kernel, block=block, unit=QK**-0.5 * math.log2(math.e)),
-        grid=(length // block,),
-        in_specs=[
-            pl.BlockSpec(memory_space=pltpu.SMEM),
-            pl.BlockSpec((block, QK), lambda i: (i, 0)),
-            pl.BlockSpec((length, QK), lambda i: (0, 0)),
-            pl.BlockSpec((length, VD), lambda i: (0, 0)),
-        ],
-        out_specs=[
-            pl.BlockSpec((block, VD), lambda i: (i, 0)),
-            pl.BlockSpec((block, 1), lambda i: (i, 0)),
-        ],
+        functools.partial(attend_kernel, members=members, unit=QK**-0.5 * math.log2(math.e)),
+        in_specs=[pl.BlockSpec(memory_space=pltpu.SMEM), vmem, vmem, vmem],
+        out_specs=[vmem, vmem, pl.BlockSpec(memory_space=pl.ANY)],
         out_shape=[
             jax.ShapeDtypeStruct((length, VD), F32),
             jax.ShapeDtypeStruct((length, 1), F32),
+            jax.ShapeDtypeStruct((members, tokens, VD), BF16),
         ],
+        scratch_shapes=[pltpu.VMEM((members, tokens, VD), BF16), sem((members,)), sem((members,)), sem],
+        compiler_params=pltpu.CompilerParams(
+            collective_id=collective_id, has_side_effects=True, vmem_limit_bytes=40 * 1024 * 1024
+        ),
         cost_estimate=pl.CostEstimate(
             flops=length * length * (QK + VD), bytes_accessed=length * 1000, transcendentals=length * length // 2
         ),
@@ -712,86 +748,141 @@
 
 
 def attend_back_kernel(
-    prefix_ref, q_ref, k_ref, v_ref, d_ref, lse_ref, delta_ref, dq_ref, dk_ref, dv_ref, *, block, factor, unit
+    prefix_ref, q_ref, k_ref, v_ref, o_ref, lse_ref, d_hbm, kvb_ref, part_ref, dq_out,
+    ds_in, blocks, dk, dv, sent, got, q_sent, q_got, local, local2,
+    *, members, factor, unit
 ):
-    i = pl.program_id(0)
+    me = lax.axis_index("grp")
+    tokens = blocks.shape[1] * 2 // 3
+    block, keys = 2 * tokens, 4 * tokens
+    turns = members // 2
     prefix = prefix_ref[0]
-    start = i * block
-
-    @pl.when(i == 0)
-    def _():
-        dk_ref[...] = jnp.zeros_like(dk_ref)
-        dv_ref[...] = jnp.zeros_like(dv_ref)
-
-    q = q_ref[...]
-    d = d_ref[...]
-    lse = lse_ref[...]
-    delta = delta_ref[...]
-    inside = start < prefix
-    stop = jnp.maximum(i + 1, jnp.where(inside, (prefix + block - 1) // block, 0))
-    full = (jnp.where(inside, prefix - 1, start) + 1) // block
-    rows = start + lax.broadcasted_iota(jnp.int32, (1, block), 1)
-    limit = jnp.where(rows < prefix, prefix - 1, rows)
-
-    def step(j, dq, masked):
-        at = pl.multiple_of(j * block, block)
-        k = k_ref[pl.ds(at, block), :]
-        v = v_ref[pl.ds(at, block), :]
-        p = jnp.exp2(dot_t(k, q) * unit - lse)
-        if masked:
-            cols = at + lax.broadcasted_iota(jnp.int32, (block, 1), 0)
-            p = jnp.where(cols <= limit, p, 0.0)
-        dp = dot_t(v, d)
-        ds = (p * (dp - delta)).astype(BF16)
-        dv_ref[pl.ds(at, block), :] += dot(p.astype(BF16), d)
-        dk_ref[pl.ds(at, block), :] += dot(ds, q)
-        return dq + t_dot(ds, k)
-
-    dq = lax.fori_loop(0, full, functools.partial(step, masked=False), jnp.zeros((block, QK), F32))
-    dq = lax.fori_loop(full, stop, functools.partial(step, masked=True), dq)
-    dq_ref[...] = (dq * factor).astype(dq_ref.dtype)
-
-    @pl.when(i == pl.num_programs(0) - 1)
-    def _():
-        dk_ref[...] = dk_ref[...] * factor
-
-
-def attend_back(prefix, q, k, v, d, lse, delta):
+    exchange = Exchange(d_hbm, ds_in, sent, got, members)
+    into = pltpu.make_async_copy(d_hbm.at[me], ds_in.at[me], local)
+    own = pltpu.make_async_copy(blocks.at[me], dq_out.at[me], local2)
+
+    def block_to(n):
+        return send(blocks.at[n], dq_out.at[me], q_sent.at[n], q_got.at[me], n)
+
+    def from_device(n):
+        return send(blocks.at[n], dq_out.at[n], q_sent.at[n], q_got.at[n], n)
+
+    into.start()
+    meet(members)
+    exchange.start()
+    dk[...] = jnp.zeros_like(dk)
+    dv[...] = jnp.zeros_like(dv)
+    into.wait()
+
+    @pl.loop(0, turns)
+    def _(n):
+        i = lax.rem(me // 2 + n, turns)
+        start = pl.multiple_of(i * block, block)
+        here = pl.ds(start, block)
+        for t in range(2):
+            source = 2 * i + t
+
+            @pl.when(source != me)
+            def _():
+                send(ds_in.at[source], ds_in.at[source], sent.at[0], got.at[lax.rem(me - source + members, members)], source).wait_recv()
+
+        d = ds_in[pl.ds(2 * i, 2)].reshape(block, VD)
+        q = q_ref[here, :]
+        lse = lse_ref[pl.ds(i, 1), 0, :]
+        along = d.astype(F32) * o_ref[here, :]
+        high = along.astype(BF16)
+        low = (along - high.astype(F32)).astype(BF16)
+        ones = jnp.ones((8, VD), BF16)
+        delta = (dot_t(ones, high) + dot_t(ones, low))[0:1, :]
+        rows = start + lax.broadcasted_iota(jnp.int32, (1, block), 1)
+        limit = jnp.maximum(jnp.where(rows < prefix, prefix - 1, rows), rows)
+
+        def step(j, dq, masked):
+            at = pl.multiple_of(j * keys, keys)
+            k = k_ref[pl.ds(at, keys), :]
+            v = v_ref[pl.ds(at, keys), :]
+            p = jnp.exp2(dot_t(k, q) * unit - lse)
+            if masked:
+                cols = at + lax.broadcasted_iota(jnp.int32, (keys, 1), 0)
+                p = jnp.where(cols <= limit, p, 0.0)
+            dp = dot_t(v, d)
+            ds = (p * (dp - delta)).astype(BF16)
+            dv[pl.ds(at, keys), :] += dot(p.astype(BF16), d)
+            dk[pl.ds(at, keys), :] += dot(ds, q)
+            return dq + t_dot(ds, k)
+
+        full, stop = key_blocks(start, block, keys, q_ref.shape[0])
+        dq = lax.fori_loop(0, full, functools.partial(step, masked=False), jnp.zeros((block, QK), F32))
+        dq = lax.fori_loop(full, stop, functools.partial(step, masked=True), dq)
+        dq = (dq * factor).astype(BF16)
+        half = tokens // 2
+        for t in range(2):
+            to = 2 * i + t
+            r = t * tokens
+            blocks[to, :tokens, :] = dq[r : r + tokens, :NOPE]
+            blocks[to, tokens:, :ROPE] = dq[r : r + half, NOPE:]
+            blocks[to, tokens:, ROPE:] = dq[r + half : r + tokens, NOPE:]
+
+            @pl.when(to == me)
+            def _():
+                own.start()
+
+            @pl.when(to != me)
+            def _():
+                block_to(to).start()
+
+    @pl.loop(0, members)
+    def _(b):
+        at = pl.ds(pl.multiple_of(b * tokens, tokens), tokens)
+        d = jnp.concatenate([dk[at, :NOPE] * factor, dv[at, :]], axis=1).astype(BF16)
+        part_ref[b, :, :KVR] = dot_t(d, kvb_ref[...]).astype(BF16)
+        part_ref[b, :, KVR:] = (dk[at, NOPE:] * factor).astype(BF16)
+
+    own.wait()
+
+    @pl.loop(1, members)
+    def _(d):
+        n = lax.rem(me + d, members)
+        from_device(n).wait_recv()
+        block_to(n).wait_send()
+        exchange.copy(d).wait_send()
+
+
+def attend_back(prefix, q, k, v, o, lse, d, kvb, members, collective_id):
     length = q.shape[0]
-    block = block_of(length)
-    whole = lambda i: (0, 0)
+    tokens = length // members
+    vmem = pl.BlockSpec(memory_space=pltpu.VMEM)
+    anywhere = pl.BlockSpec(memory_space=pl.ANY)
+    sem = pltpu.SemaphoreType.DMA
     factor = QK**-0.5
+    packed = tokens + tokens // 2
     return pl.pallas_call(
-        functools.partial(attend_back_kernel, block=block, factor=factor, unit=factor * math.log2(math.e)),
-        grid=(length // block,),
-        in_specs=[
-            pl.BlockSpec(memory_space=pltpu.SMEM),
-            pl.BlockSpec((block, QK), lambda i: (i, 0)),
-            pl.BlockSpec((length, QK), whole),
-            pl.BlockSpec((length, VD), whole),
-            pl.BlockSpec((block, VD), lambda i: (i, 0)),
-            pl.BlockSpec((1, block), lambda i: (0, i)),
-            pl.BlockSpec((1, block), lambda i: (0, i)),
+        functools.partial(attend_back_kernel, members=members, factor=factor, unit=factor * math.log2(math.e)),
+        in_specs=[pl.BlockSpec(memory_space=pltpu.SMEM)] + [vmem] * 5 + [anywhere, vmem],
+        out_specs=[vmem, anywhere],
+        out_shape=[
+            jax.ShapeDtypeStruct((members, tokens, KVR + ROPE), BF16),
+            jax.ShapeDtypeStruct((members, packed, NOPE), BF16),
         ],
-        out_specs=[
-            pl.BlockSpec((block, QK), lambda i: (i, 0)),
-            pl.BlockSpec((length, QK), whole),
-            pl.BlockSpec((length, VD), whole),
+        scratch_shapes=[
+            pltpu.VMEM((members, tokens, VD), BF16),
+            pltpu.VMEM((members, packed, NOPE), BF16),
+            pltpu.VMEM((length, QK), F32),
+            pltpu.VMEM((length, VD), F32),
+            sem((members,)), sem((members,)), sem((members,)), sem((members,)), sem, sem,
         ],
-        out_shape=[
-            jax.ShapeDtypeStruct((length, QK), BF16),
-            jax.ShapeDtypeStruct((length, QK), F32),
-            jax.ShapeDtypeStruct((length, VD), F32),
-        ],
+        compiler_params=pltpu.CompilerParams(
+            collective_id=collective_id, has_side_effects=True, vmem_limit_bytes=50 * 1024 * 1024
+        ),
         cost_estimate=pl.CostEstimate(
             flops=length * length * (3 * QK + 2 * VD), bytes_accessed=length * 2000, transcendentals=length * length // 2
         ),
         name="attend_back",
-    )(prefix, q, k, v, d, lse, delta)
+    )(prefix, q, k, v, o, lse, d, kvb)
 
 
 def silu_parts(v):
-    logistic = 1.0 / (1.0 + jnp.exp(-v))
+    logistic = 0.5 * jnp.tanh(0.5 * v) + 0.5
     return v * logistic, logistic * (1.0 + v * (1.0 - logistic))
 
 
@@ -810,10 +901,10 @@
 
 
 def experts_kernel(
-    x_hbm, prob_hbm, rank_ref, back_ref, gate_hbm, up_hbm, down_hbm, own_hbm, sdown_hbm,
-    part_hbm, part2_hbm, eg_hbm, eu_hbm, eo_hbm, sh_hbm, prob_out,
+    x_hbm, prob_hbm, c_hbm, rank_ref, back_ref, gate_hbm, up_hbm, down_hbm, own_hbm, sdown_hbm,
+    part_hbm, eg_hbm, eu_hbm, eo_hbm, sh_hbm, c_out, prob_out,
     xs, probs, gate, up, down, own, sdown, tail, rows, acts, sacts, part_st, eg_st, eu_st, eo_st, sh_st,
-    sent, got, e_sent, e_got, load, store,
+    c_st, sent, got, e_sent, e_got, c_sent, c_got, load, store,
     *, members, slots, tile, wide
 ):
     me = lax.axis_index("grp")
@@ -835,10 +926,13 @@
                 (up_hbm, up),
                 (down_hbm, down),
                 (sdown_hbm, sdown),
+                (c_hbm, c_st),
             ]
         )
     ]
     gather = Gather(x_hbm, xs, sent, got, members)
+    behind = Gather(c_hbm, c_out, c_sent, c_got, members)
+    own_c = pltpu.make_async_copy(c_st, c_out.at[me], load.at[7])
     exchange = Exchange(prob_hbm, probs, e_sent, e_got, members)
     for copy in loads:
         copy.start()
@@ -847,6 +941,7 @@
     exchange.start()
     for copy in loads:
         copy.wait()
+    own_c.start()
     tail[:, :half] = gate[:, hidden - half :]
     tail[:, half:] = up[:, hidden - half :]
     gather.pass_on(z)
@@ -860,8 +955,7 @@
             pltpu.make_async_copy(a, b.at[k], store.at[n, m])
             for m, (a, b) in enumerate(
                 [
-                    (part_st.at[n, :, :, pl.ds(0, width // 2)], part_hbm),
-                    (part_st.at[n, :, :, pl.ds(width // 2, width // 2)], part2_hbm),
+                    (part_st.at[n], part_hbm),
                     (eg_st.at[n], eg_hbm),
                     (eu_st.at[n], eu_hbm),
                     (eo_st.at[n], eo_hbm),
@@ -905,6 +999,15 @@
         @pl.when(s + 1 < levels)
         def _():
             gather.pass_on(pick_from(order, z, s + 1))
+
+        @pl.when(s == levels - 3)
+        def _():
+            behind.first()
+
+        @pl.when(s >= levels - 2)
+        def _():
+            behind.relay(s - levels + 3)
+            behind.pass_on(pick_from(order, z, s - levels + 2))
 
         @pl.loop(0, width // wide)
         def _(j):
@@ -934,15 +1037,26 @@
         for copy in stores(s, k):
             copy.start()
 
+    @pl.loop(2, levels)
+    def _(s):
+        behind.relay(s + 1)
+        behind.pass_on(pick_from(order, z, s))
+
     @pl.loop(levels - 2, levels)
     def _(s):
         for copy in stores(s, pick_from(order, z, s)):
             copy.wait()
 
+    @pl.loop(0, levels)
+    def _(k):
+        behind.take_twin(k)
+
+    own_c.wait()
     gather.finish()
-
-
-def experts_forward(x, prob, rank, back, gate, up, down, own, sdown, slots, members, collective_id):
+    behind.finish()
+
+
+def experts_forward(x, prob, c, rank, back, gate, up, down, own, sdown, slots, members, collective_id):
     tokens, width = x.shape
     hidden = gate.shape[1]
     group = SIDE * CORES
@@ -961,10 +1075,11 @@
     ]
     return pl.pallas_call(
         functools.partial(experts_kernel, members=members, slots=slots, tile=tile, wide=512),
-        in_specs=[anywhere, anywhere, vmem, vmem] + [anywhere] * 5,
+        in_specs=[anywhere, anywhere, anywhere, vmem, vmem] + [anywhere] * 5,
         out_specs=[anywhere] * 6 + [vmem],
-        out_shape=[jax.ShapeDtypeStruct((*shapes[0][:3], width // 2), BF16)] * 2
-        + [jax.ShapeDtypeStruct(s, BF16) for s in shapes[1:]] + [jax.ShapeDtypeStruct(prob.shape, F32)],
+        out_shape=[jax.ShapeDtypeStruct(s, BF16) for s in shapes]
+        + [jax.ShapeDtypeStruct((members, *c.shape), BF16)]
+        + [jax.ShapeDtypeStruct(prob.shape, F32)],
         scratch_shapes=[
             pltpu.VMEM((members, tokens, width), BF16),
             pltpu.VMEM(prob.shape, F32),
@@ -979,7 +1094,9 @@
             pltpu.VMEM((group, tokens, own.shape[1] // 2), BF16),
         ]
         + [pltpu.VMEM((2, *s[1:]), BF16) for s in shapes]
-        + [sem((6, members)), sem((2, members)), sem((members,)), sem((members,)), sem((7,)), sem((2, 6))],
+        + [pltpu.VMEM(c.shape, BF16)]
+        + [sem((6, members)), sem((2, members)), sem((members,)), sem((members,))]
+        + [sem((6, members)), sem((2, members)), sem((8,)), sem((2, 5))],
         compiler_params=pltpu.CompilerParams(
             collective_id=collective_id, has_side_effects=True, vmem_limit_bytes=63 * 1024 * 1024
         ),
@@ -987,7 +1104,7 @@
             flops=12 * members * slots * width * hidden, bytes_accessed=60_000_000, transcendentals=0
         ),
         name="experts_forward",
-    )(x, prob, rank, back, gate, up, down, own, sdown)
+    )(x, prob, c, rank, back, gate, up, down, own, sdown)
 
 
 def experts_back_kernel(
@@ -1251,20 +1368,8 @@
     )
     sequences = lax.axis_size("rep")
     split = w_q.shape[0] * 3 // 128 * 16 if sequences % 2 == 0 else 0
-    (all_kva, all_q, all_o, all_router), (kvb_parts, chosen_all) = communicate(
-        [w_kva, w_q, w_o, w_router],
-        [
-            w_kvb.reshape(w_kvb.shape[0], members, -1).transpose(1, 0, 2),
-            jnp.broadcast_to(chosen_by.T[:, None, :], (experts, 8, tokens)),
-        ],
-        members,
-        1,
-        [split, split, split, 0],
-    )
-    full_kva, full_q, full_o, full_router = (
-        v.reshape(-1, v.shape[2]) for v in (all_kva, all_q, all_o, all_router)
-    )
-    own_kvb = kvb_parts.reshape(KVR, -1)
+    (all_kva, all_q, all_o), _ = communicate([w_kva, w_q, w_o], [], members, 1, [split] * 3)
+    full_kva, full_q, full_o = (v.reshape(-1, v.shape[2]) for v in (all_kva, all_q, all_o))
     hidden_slice = shared_down.shape[0]
     shared = after(jnp.stack([shared_gate, shared_up], axis=1), all_q)
     shared = shared.reshape(shared.shape[0], 2, members, hidden_slice).transpose(2, 0, 1, 3)
@@ -1281,17 +1386,25 @@
     query = jnp.concatenate(
         [query[:, :, :NOPE], rotate(query[:, :, NOPE:], cosine[:, None], sine[:, None])], axis=-1
     ).astype(BF16)
-    (all_latent,), (q_packed,) = communicate(
-        [jnp.concatenate([compressed, k_rope], axis=-1)], [after(pack(query.transpose(1, 0, 2)), own_shared)], members, 2
+    (all_latent, all_router), (q_packed, kvb_parts, chosen_all) = communicate(
+        [jnp.concatenate([compressed, k_rope], axis=-1), w_router],
+        [
+            after(pack(query.transpose(1, 0, 2)), own_shared),
+            w_kvb.reshape(w_kvb.shape[0], members, -1).transpose(1, 0, 2),
+            jnp.broadcast_to(chosen_by.T[:, None, :], (experts, 8, tokens)),
+        ],
+        members,
+        2,
     )
+    full_router = all_router.reshape(width, -1)
+    own_kvb = kvb_parts.reshape(KVR, -1)
     all_latent = all_latent.reshape(length, KVR + ROPE)
     q_head = unpack(q_packed).reshape(length, QK)
     q_head, c_first = lax.optimization_barrier((q_head, cotangent[:, : width // 2]))
     expanded = dot(all_latent[:, :KVR], own_kvb).astype(BF16)
     k_head = jnp.concatenate([expanded[:, :NOPE], all_latent[:, KVR:]], axis=-1)
     v_head = expanded[:, NOPE:]
-    mixture, lse = attend(prefix_len, q_head, k_head, v_head)
-    _, (mixed_parts,) = communicate([], [mixture.astype(BF16).reshape(members, tokens, VD)], members, 3)
+    mixture, lse, mixed_parts = attend(prefix_len, q_head, k_head, v_head, members, 3)
     mixed = mixed_parts.transpose(1, 0, 2).reshape(tokens, H * VD)
     o_small = dot(mixed, oa_down).astype(BF16)
     middle = inputs + dot(mixed, full_o) + dot(o_small, oa_up)
@@ -1299,10 +1412,7 @@
     route_probs = jax.nn.softmax(dot(ffn_in, full_router), axis=-1)
 
     half = width // 2
-    all_c = [
-        gather(c_first).reshape(members, tokens, half),
-        gather(tie(cotangent[:, half:], mixed_parts)).reshape(members, tokens, half),
-    ]
+    first_c = gather(c_first).reshape(members, tokens, half)
     chosen = chosen_all[:, 0] > 0.5
     order = jnp.arange(tokens, dtype=jnp.int32)
     before = (order[:, None] < order[None, :]).astype(BF16)
@@ -1311,16 +1421,14 @@
     rank = jnp.broadcast_to(rank[:, None, :], (members, 8, tokens))
     weights = (expert_gate[0], expert_up_weight[0], expert_down[0], own_shared, shared_down)
     prob_blocks = jnp.broadcast_to(route_probs.T[:, None, :], (experts, 8, tokens))
-    *partial, kept_gate, kept_up, kept_out, kept_shared, prob_parts = experts_forward(
-        ffn_in, prob_blocks, rank, back, *weights, slots, members, 4
+    partial, kept_gate, kept_up, kept_out, kept_shared, second_c, prob_parts = experts_forward(
+        ffn_in, prob_blocks, cotangent[:, half:], rank, back, *weights, slots, members, 4
     )
     kept = (kept_gate, kept_up, kept_out, kept_shared)
-    partial = [part.reshape(length, half) for part in partial]
-    ffn_out = [scatter_sum(partial[0])]
+    ffn_out = scatter_sum(partial.reshape(length, width))
     d_own, d_route = experts_backward(
-        all_c, rank, back, prob_parts, kept, *weights, slots, members, 5
+        (first_c, second_c), rank, back, prob_parts, kept, *weights, slots, members, 5
     )
-    ffn_out.append(scatter_sum(after(partial[1], d_own)))
     d_route = d_route[:, 0].T
     d_logits = (
         route_probs * (d_route - jnp.sum(route_probs * d_route, axis=-1, keepdims=True))
@@ -1332,22 +1440,20 @@
     d_osmall = dot_t(d_attn, oa_up).astype(BF16)
     grad_odown = t_dot(d_osmall, mixed)
     d_mixed = (dot_t(d_attn, full_o) + dot_t(d_osmall, oa_down)).astype(BF16)
-    _, (d_head,) = communicate([], [d_mixed.reshape(tokens, H, VD).transpose(1, 0, 2)], members, 6)
-    d_head = d_head.reshape(length, VD)
-    delta = jnp.sum(d_head.astype(F32) * mixture, axis=-1)
-    dq, dk, dv = attend_back(
-        prefix_len, q_head, k_head, v_head, d_head, lse.reshape(1, length), delta.reshape(1, length)
+    d_latents, d_query = attend_back(
+        prefix_len,
+        q_head,
+        k_head,
+        v_head,
+        mixture,
+        lse.reshape(members // 2, 1, 2 * tokens),
+        d_mixed.reshape(tokens, H, VD).transpose(1, 0, 2),
+        own_kvb,
+        members,
+        6,
     )
-    d_expanded = jnp.concatenate([dk[:, :NOPE], dv], axis=-1).astype(BF16)
     o_parts = jnp.concatenate([by_owner(g, members) for g in (grad_odown, grad_oup)], axis=-1)
-    d_latents, (d_query, o_landed) = reduce_blocks(
-        jnp.concatenate([dot_t(d_expanded, own_kvb), dk[:, NOPE:]], axis=-1)
-        .astype(BF16)
-        .reshape(members, tokens, KVR + ROPE),
-        [pack(dq.reshape(members, tokens, QK)), o_parts],
-        members,
-        7,
-    )
+    d_latents, (o_landed,) = reduce_blocks(d_latents, [o_parts], members, 7)
     d_latents = d_latents.astype(F32)
     d_query = unpack(d_query).transpose(1, 0, 2).astype(F32)
     d_latent = jnp.concatenate(
@@ -1365,8 +1471,8 @@
         .reshape(tokens, H * QK)
         .astype(BF16)
     )
-    first, second, _ = lax.optimization_barrier((*ffn_out, d_query))
-    output = (middle + jnp.concatenate([first, second], axis=-1).astype(F32)).astype(BF16)
+    ffn_out, _ = lax.optimization_barrier((ffn_out, d_query))
+    output = (middle + ffn_out.astype(F32)).astype(BF16)
     grad_qup = t_dot(q_small, d_query)
     d_qsmall = dot_t(d_query, qa_up).astype(BF16)
     grad_qdown = t_dot(d_qsmall, normed)

time: 820 us -> 774 us (0.944)
  Pallas kernels: 653 us -> 637 us
  other arithmetic: 36.4 us -> 23.9 us
  local copies, waits for them, and re-layouts: 49.9 us -> 40.3 us
    pallas_call x4 -> x2, Pallas kernels: 235 us -> 183 us  [communicate(): pl.pallas_call(functools.partial(comm_kernel, members=members, splits=tup...]
    pallas_call x2, Pallas kernels: 51.5 us -> 91 us  [the longest x1 61.7 us: attend_back(): pl.pallas_call(functools.partial(attend_back_kernel, members=members, fac...]
    pallas_call x1, Pallas kernels: 140 us -> 170 us  [experts_backward(): pl.pallas_call(functools.partial(experts_back_kernel, members=members, sl...]
    pallas_call x1, Pallas kernels: 63.3 us -> 40.4 us  [reduce_blocks(): pl.pallas_call(functools.partial(reduce_kernel, members=members, n_e=n_e)...]
    pallas_call x1, Pallas kernels: 149 us -> 139 us  [experts_forward(): pl.pallas_call(functools.partial(experts_kernel, members=members, slots=s...]
    unnamed x122 -> x134, local copies, waits for them, and re-layouts: 17.7 us -> 12 us
    dot_general x9 -> x8, matrix products: 24.9 us -> 22.5 us  [dot_t(): lax.dot_general(former, latter, (((1,), (1,)), ((), ())), preferred_eleme...]
  transfers between devices with their start and end apart: 5 -> 3, of which waited for: 1 -> 1; matrix products, arithmetic and copies ran while one was open for 13% -> 12% of each run, Pallas kernels for 59% -> 59%
where the time goes in v5:
time: 774 us; the launch traced here: 770 us
  Pallas kernels  637 us (82%)
  matrix products  46 us (6%)
  local copies, waits for them, and re-layouts  40.3 us (5%)
  other arithmetic  23.9 us (3%)
  between operations  16.6 us (2%)
    pallas_call x2, Pallas kernels, communicate(): pl.pallas_call(functools.partial(comm_kernel, members=members, splits=tup...  183 us
    pallas_call x1, Pallas kernels, experts_backward(): pl.pallas_call(functools.partial(experts_back_kernel, members=members, sl...  170 us
    pallas_call x1, Pallas kernels, experts_forward(): pl.pallas_call(functools.partial(experts_kernel, members=members, slots=s...  139 us
    pallas_call x1, Pallas kernels, attend_back(): pl.pallas_call(functools.partial(attend_back_kernel, members=members, fac...  61.7 us
    pallas_call x1, Pallas kernels, reduce_blocks(): pl.pallas_call(functools.partial(reduce_kernel, members=members, n_e=n_e)...  40.4 us
    pallas_call x1, Pallas kernels, attend(): pl.pallas_call(functools.partial(attend_kernel, members=members, unit=QK...  29.3 us
    dot_general x8, matrix products, dot_t(): lax.dot_general(former, latter, (((1,), (1,)), ((), ())), preferred_eleme...  22.5 us
    dot_general x10, matrix products, dot(): return jnp.dot(former, latter, preferred_element_type=F32)  19.6 us
  transfers between devices with their start and end apart: 3, of which 1 were waited for; matrix products, arithmetic and copies ran while one was open for 12% of the time, Pallas kernels for 59%

profile of v5, /device:TPU:0, one launch (start us, length us, event | category | flops | bytes accessed | tf_op | source)
XLA Modules:
  0.0 769.9 jit_solution(7056746133215592212)
XLA Ops:
  7.2 1.8 copy.100.refs_0_
  9.0 1.5 copy.106
  10.9 110.3 %communicate_1.1 = (bf16[16,128,576]{2,1,0:T(8,128)(2,1)}, bf16[16,128,3072]{2,1,0:T(8,128)(2,1)}, bf16[16,128,2048]{2,1,0:T(8,128)(2,1)}) custom-call(bf16[128,576]{1,0:T(8,128)(2,1)} %copy.100.refs_0_, bf16[128,3072]{1,0:T(8,128)(2,1)} %refs_1_.2, bf16[128,2048]{1,0:T(8,128)(2,1)} %refs_2_.1), custom_call_target="tpu_custom_call" | custom-call | bytes 186646528 | tf_op jit(solution)/shard_map/communicate_1/pallas_call | solution.py:350
  121.2 1.2 copy.107
  122.4 4.7 all-to-all-start
  128.1 1.7 fusion.99
  129.8 6.1 fusion.97
  136.5 1.2 convolution_convert_fusion.8
  137.8 2.8 convolution_add_fusion
  141.3 3.1 reshape.284
  144.6 1.1 copy.162
  146.3 1.4 multiply_cosine_fusion
  153.9 1.3 maximum_maximum_fusion.1.refs_2_
  156.6 2.6 copy.108
  159.9 72.3 %communicate_2.1 = (bf16[16,192,576]{2,1,0:T(8,128)(2,1)}, bf16[16,128,16]{2,1,0:T(8,128)(2,1)}, bf16[16,288,128]{2,1,0:T(8,128)(2,1)}, bf16[16,32,256]{2,1,0:T(8,128)(2,1)}, f32[16,8,192]{2,1,0:T(8,128)}) custom-call(bf16[192,576]{1,0:T(8,128)(2,1)} %pad_maximum_fusion.2.refs_0_, bf16[128,16]{1,0:T(8,128)(2,1)} %copy.110.refs_1_, ...), custom_call_target="tpu_custom_call" | custom-call | bytes 40763392 | tf_op jit(solution)/shard_map/communicate_2/pallas_call | solution.py:350
  232.2 1.4 fusion.105
  235.1 1.2 slice.166
  237.4 1.7 copy.113.back_ref
  239.1 3.0 convolution_convert_fusion
  243.2 29.3 %attend.1 = (f32[3072,128]{1,0:T(8,128)S(1)}, f32[3072,1]{1,0:T(8,128)S(1)}, bf16[16,192,128]{2,1,0:T(8,128)(2,1)S(1)}) custom-call(s32[1]{0:T(128)S(6)} %copy.170.prefix_ref, bf16[3072,192]{1,0:T(8,128)(2,1)S(1)} %bitcast.200, bf16[3072,192]{1,0:T(8,128)(2,1)S(1)} %pad_maximum_fusion.k_ref, bf16[3072,128]{1,0:T(8,128)(2,1)S(1)} %get-tuple-element.74.v_ref), custom_call_target="tpu_custom_call" | custom-call | flops 3019898880 | bytes 3072000 | tf_op jit(solution)/shard_map/attend/pallas_call | solution.py:730
  272.5 1.2 convolution_convert_fusion.7
  273.8 1.8 fusion.3
  275.7 1.3 multiply_reduce_fusion.1
  280.8 139.4 %experts_forward.1 = (bf16[4,4,192,2048]{3,2,1,0:T(8,128)(2,1)}, bf16[4,384,1408]{2,1,0:T(8,128)(2,1)}, bf16[4,384,1408]{2,1,0:T(8,128)(2,1)}, bf16[4,384,2048]{...) custom-call(bf16[192,2048]{1,0:T(8,128)(2,1)} %copy-done.22, ...), custom_call_target="tpu_custom_call" | custom-call | flops 53150220288 | bytes 60000000 | tf_op jit(solution)/shard_map/experts_forward/pallas_call | solution.py:1076
  420.2 1.4 copy-done.3
  421.6 1.1 reduce
  422.7 169.9 %experts_backward.1 = (bf16[192,2048]{1,0:T(8,128)(2,1)}, f32[16,8,192]{2,1,0:T(8,128)}) custom-call(bf16[4,4,192,1024]{3,2,1,0:T(8,128)(2,1)} %bitcast.231, bf16[4,4,192,1024]{3,2,1,0:T(8,128)(2,1)} %bitcast.238, f32[16,8,192]{2,1,0:T(8,128)} %broadcast_in_dim.18.rank_ref, f32[16,192,1]{2,1,0:T(8,128)} %copy.113.back_ref, ...), custom_call_target="tpu_custom_call" | custom-call | flops 53150220288 | bytes 60000000 | tf_op jit(solution)/shard_map/experts_backward/pallas_call | solution.py:1270
  594.3 2.5 multiply_reduce_fusion
  597.4 1.2 convolution_convert_fusion.6
  598.7 6.3 fusion.92
  605.0 1.3 fusion.19
  606.6 61.7 %attend_back.1 = (bf16[16,192,576]{2,1,0:T(8,128)(2,1)}, bf16[16,288,128]{2,1,0:T(8,128)(2,1)S(1)}) custom-call(s32[1]{0:T(128)S(6)} %copy.170.prefix_ref, bf16[3072,192]{1,0:T(8,128)(2,1)} %bitcast.201, bf16[3072,192]{1,0:T(8,128)(2,1)} %copy-done.1, bf16[3072,128]{1,0:T(8,128)(2,1)S(1)} %copy-done.7, f32[3072,128]{1,0:T(8,128)} %copy-done.11, ...), custom_call_target="tpu_custom_call" | custom-call | flops 7851737088 | bytes 6144000 | tf_op jit(solution)/shard_map/attend_back/pallas_call | solution.py:859
  671.0 2.0 copy.117
  673.0 3.1 convert_element_type.166
  676.3 1.6 fusion.21
  678.7 40.4 %reduce_7.1 = (bf16[192,576]{1,0:T(8,128)(2,1)}, bf16[16,16,256]{2,1,0:T(8,128)(2,1)}) custom-call(bf16[16,192,576]{2,1,0:T(8,128)(2,1)} %get-tuple-element.63.refs_0_, bf16[16,16,256]{2,1,0:T(8,128)(2,1)} %pad_maximum_fusion.4.refs_1_), custom_call_target="tpu_custom_call" | custom-call | bytes 28311552 | tf_op jit(solution)/shard_map/reduce_7/pallas_call | solution.py:524
  719.1 1.8 convert_element_type.172
  721.8 1.8 reshape.302
  724.5 1.3 convolution_convert_fusion.5
  725.9 1.1 fusion.22
  728.3 14.1 %spread_8.1 = (bf16[2,16,16,320]{3,2,1,0:T(8,128)(2,1)}, f32[2,16,384]{2,1,0:T(8,128)}) custom-call(bf16[16,16,320]{2,1,0:T(8,128)(2,1)} %pad_maximum_fusion.3.src, f32[16,384]{1,0:T(8,128)} %concatenate.63.common), custom_call_target="tpu_custom_call" | custom-call | bytes 1310720 | tf_op jit(solution)/shard_map/spread_8/pallas_call | solution.py:601
  744.2 1.1 convert_reduce_fusion
  746.3 1.1 fusion.52
  748.3 7.3 fusion.109
  755.5 1.4 convolution_add_fusion.3
  757.3 1.2 fusion.14
  759.3 1.3 fusion.26
  760.6 2.2 fusion.23
  (201 shorter events, 31.8 us)
Async XLA Ops:
  7.2 3.3 copy-start.34
  122.4 4.9 copy-start.16
  122.4 5.8 copy-start.26
  122.4 5.8 copy-start.51
  122.4 34.2 %all-to-all-start = ((bf16[16,128,352]{1,2,0:T(8,128)(2,1)}), bf16[16,128,352]{1,2,0:T(8,128)(2,1)}, u32[]{:S(2)}, u32[]{:S(2)}) async-start(bf16[16,128,352]{1,2,0:T(8,128)(2,1)} %bitcast.12), calls=%async_computation | async-start | bytes 2883584 | tf_op jit(solution)/shard_map/all_to_all | solution.py:629
  127.1 295.6 %all-gather.2.cloned.1.call-start = ((), (), s32[]{:S(2)}) async-start(), calls=%async_computation.3 | async-start | bytes 6684672 | tf_op jit(solution)/shard_map/all_gather | solution.py:625
  128.1 8.4 %copy-start.56 = (f32[192]{0:T(256)}, f32[192]{0:T(256)S(1)}, u32[]{:S(2)}) copy-start(f32[192]{0:T(256)S(1)} %get-tuple-element.96) | copy-start | bytes 2308
  137.8 2.8 copy-start.39
  137.8 2.8 copy-start.59
  140.6 5.1 copy-start.61
  150.0 1.7 copy-start.53
  150.0 1.7 copy-start.19
  150.0 2.4 copy-start.44
  234.1 8.5 %copy-start = (bf16[16,192,192]{2,1,0:T(8,128)(2,1)}, bf16[16,192,192]{2,1,0:T(8,128)(2,1)S(1)}, u32[]{:S(2)}) copy-start(bf16[16,192,192]{2,1,0:T(8,128)(2,1)S(1)} %maximum_maximum_fusion) | copy-start | bytes 3538948
  234.1 526.5 %reduce-scatter.2.cloned.1.call-start = ((), (), s32[]{:S(2)}) async-start(), calls=%async_computation.2 | async-start | bytes 13369344 | tf_op jit(solution)/shard_map/reduce_scatter | solution.py:633
  235.1 4.1 copy-start.9
  242.3 31.5 %slice-start = ((s8[8388608]{0:T(1024)(128)(4,1)}), s8[4194304]{0:T(1024)(128)(4,1)S(1)}, s32[]{:S(2)}) async-start(s8[8388608]{0:T(1024)(128)(4,1)} %bitcast.208), calls=%async_computation.4 | async-start | bytes 8388608
  242.6 29.9 %copy-start.1 = (bf16[3072,192]{1,0:T(8,128)(2,1)}, bf16[3072,192]{1,0:T(8,128)(2,1)S(1)}, u32[]{:S(2)}) copy-start(bf16[3072,192]{1,0:T(8,128)(2,1)S(1)} %pad_maximum_fusion.k_ref) | copy-start | bytes 3538948
  243.1 30.6 %slice-start.1 = ((s8[8388608]{0:T(1024)(128)(4,1)}), s8[4194304]{0:T(1024)(128)(4,1)S(1)}, s32[]{:S(2)}) async-start(s8[8388608]{0:T(1024)(128)(4,1)} %bitcast.208), calls=%async_computation.5 | async-start | bytes 8388608
  243.1 30.6 %copy-start.17 = (bf16[1,192,2048]{2,1,0:T(8,128)(2,1)S(1)}, bf16[1,192,2048]{2,1,0:T(8,128)(2,1)}, u32[]{:S(2)}) copy-start(bf16[1,192,2048]{2,1,0:T(8,128)(2,1)} %param.23) | copy-start | bytes 2359300
  272.5 3.1 copy-start.2
  272.5 3.1 copy-start.4
  272.5 3.1 copy-start.11
  273.8 1.9 copy-start.41
  275.7 2.0 copy-start.38
  277.0 1.8 copy-start.12
  277.8 3.0 copy-start.22
  278.8 1.9 copy-start.43
  594.3 2.6 copy-start.13
  594.3 2.6 copy-start.24
  594.3 2.6 copy-start.50
  594.3 2.6 copy-start.60
  597.4 7.6 copy-start.14
  673.0 3.1 copy-start.5
  673.0 3.3 copy-start.42
  678.7 42.2 %copy-start.40 = (bf16[192,16]{0,1:T(8,128)(2,1)S(1)}, bf16[192,16]{0,1:T(8,128)(2,1)}, u32[]{:S(2)}) copy-start(bf16[192,16]{0,1:T(8,128)(2,1)} %copy-done.39) | copy-start | bytes 18436
  720.9 5.0 copy-start.18
  720.9 5.0 copy-start.57
  723.5 3.4 copy-start.37
  725.9 20.3 %copy-start.45 = (f32[512]{0:T(512)S(1)}, f32[512]{0:T(512)}, u32[]{:S(2)}) copy-start(f32[512]{0:T(512)} %param.29) | copy-start | bytes 6148
  727.0 20.4 %copy-start.48 = (f32[192]{0:T(256)S(1)}, f32[192]{0:T(256)}, u32[]{:S(2)}) copy-start(f32[192]{0:T(256)} %copy-done.47) | copy-start | bytes 2308
  742.4 3.7 copy-start.20
  742.5 3.7 copy-start.21
  755.5 1.8 copy-start.27
  755.5 1.8 copy-start.52
  757.3 2.0 copy-start.15
  757.3 2.0 copy-start.55
  757.3 2.0 copy-start.58
  (19 other events, 20.7 us)
Sparse Core Ops, SparseCore 0:
  234.2 73.2 all-gather.1
  420.3 171.9 reduce-scatter.1

commit v6 on v5

--- a/solution.py
+++ b/solution.py
@@ -474,151 +474,6 @@
             pltpu.VMEM((levels, r, c), kind),
             pltpu.VMEM((levels + 1, r, c), kind),
         ] + [sem((n,)) for n in (members // CORES,) * 2 + (levels,) * 2 + (levels + 1,) * 4]
-
-
-def reduce_kernel(*refs, members, n_e):
-    p, extra, out, landed = refs[0], refs[1 : 1 + n_e], refs[1 + n_e], refs[2 + n_e : 2 + 2 * n_e]
-    bufs = refs[2 + 2 * n_e :]
-    r = Reduce(p, *bufs[:3], bufs[3:11], members)
-    stage, local, sems = bufs[11 : 11 + n_e], bufs[11 + n_e : 11 + 2 * n_e], bufs[11 + 2 * n_e :]
-    me = lax.axis_index("grp")
-    order = far_first(r.levels)
-    into = [pltpu.make_async_copy(extra[k].at[me], stage[k], local[k]) for k in range(n_e)]
-    out_of = [pltpu.make_async_copy(stage[k], landed[k].at[me], local[k]) for k in range(n_e)]
-    exchanges = [Exchange(extra[k], landed[k], sems[2 * k], sems[2 * k + 1], members) for k in range(n_e)]
-    for k in range(n_e):
-        into[k].start()
-    meet(members)
-
-    @pl.loop(0, r.levels)
-    def _(s):
-        r.start(pick_from(order, r.z, s))
-
-    for k in range(n_e):
-        exchanges[k].start()
-        into[k].wait()
-        out_of[k].start()
-
-    @pl.loop(0, r.levels)
-    def _(s):
-        r.chip(pick_from(order, r.z, s))
-
-    @pl.loop(0, r.levels - 1)
-    def _(s):
-        r.line(pick_from(order, r.z, s))
-
-    r.last(out)
-    r.finish()
-    for k in range(n_e):
-        exchanges[k].wait()
-        out_of[k].wait()
-
-
-def reduce_blocks(p, extra, members, collective_id):
-    extra = list(extra)
-    n_e = len(extra)
-    anywhere = pl.BlockSpec(memory_space=pl.ANY)
-    _, r, c = p.shape
-    sem = pltpu.SemaphoreType.DMA
-    vmem = pl.BlockSpec(memory_space=pltpu.VMEM)
-    out, *landed = pl.pallas_call(
-        functools.partial(reduce_kernel, members=members, n_e=n_e),
-        in_specs=[vmem] + [anywhere] * n_e,
-        out_specs=[vmem] + [anywhere] * n_e,
-        out_shape=[jax.ShapeDtypeStruct((r, c), p.dtype)] + [jax.ShapeDtypeStruct(e.shape, e.dtype) for e in extra],
-        scratch_shapes=Reduce.scratch(members, r, c, p.dtype)
-        + [pltpu.VMEM(e.shape[1:], e.dtype) for e in extra]
-        + [sem] * n_e
-        + [sem((members,)), sem((members,))] * n_e,
-        compiler_params=pltpu.CompilerParams(
-            collective_id=collective_id, has_side_effects=True, vmem_limit_bytes=60 * 1024 * 1024
-        ),
-        cost_estimate=pl.CostEstimate(flops=0, bytes_accessed=members * r * c * 16, transcendentals=0),
-        name=f"reduce_{collective_id}",
-    )(p, *extra)
-    return out, landed
-
-
-def spread_kernel(src, common, out, commons, stage, stage2, sent, got, sent2, got2, local, *, members, sequences):
-    me, mine = lax.axis_index("grp"), lax.axis_index("rep")
-    barrier = pltpu.get_barrier_semaphore()
-    into = [
-        pltpu.make_async_copy(src.at[me], stage, local.at[0]),
-        pltpu.make_async_copy(common, stage2, local.at[1]),
-    ]
-    out_of = [
-        pltpu.make_async_copy(stage, out.at[mine, me], local.at[0]),
-        pltpu.make_async_copy(stage2, commons.at[mine], local.at[1]),
-    ]
-    for copy in into:
-        copy.start()
-
-    def other(n):
-        return lax.rem(mine + n // members, sequences), lax.rem(me + n % members, members)
-
-    @pl.loop(1, members * sequences)
-    def _(n):
-        r, to = other(n)
-        pl.semaphore_signal(barrier, 1, device_id={"rep": r, "grp": to}, device_id_type=MESH)
-
-    pl.semaphore_wait(barrier, members * sequences - 1)
-
-    def block(n):
-        r, to = other(n)
-        return send(src.at[to], out.at[mine, me], sent.at[n], got.at[n], {"rep": r, "grp": to})
-
-    def whole(n):
-        r, to = other(n * members)
-        return send(common, commons.at[mine], sent2.at[n], got2.at[n], {"rep": r, "grp": to})
-
-    @pl.loop(1, sequences)
-    def _(n):
-        whole(n).start()
-
-    @pl.loop(1, members * sequences)
-    def _(n):
-        block(n).start()
-
-    for a, b in zip(into, out_of):
-        a.wait()
-        b.start()
-
-    @pl.loop(1, sequences)
-    def _(n):
-        whole(n).wait()
-
-    @pl.loop(1, members * sequences)
-    def _(n):
-        block(n).wait()
-
-    for copy in out_of:
-        copy.wait()
-
-
-def spread_blocks(v, common, members, sequences, collective_id):
-    anywhere = pl.BlockSpec(memory_space=pl.ANY)
-    sem = pltpu.SemaphoreType.DMA
-    return pl.pallas_call(
-        functools.partial(spread_kernel, members=members, sequences=sequences),
-        in_specs=[anywhere, anywhere],
-        out_specs=[anywhere, anywhere],
-        out_shape=[
-            jax.ShapeDtypeStruct((sequences, *v.shape), v.dtype),
-            jax.ShapeDtypeStruct((sequences, *common.shape), common.dtype),
-        ],
-        scratch_shapes=[
-            pltpu.VMEM(v.shape[1:], v.dtype),
-            pltpu.VMEM(common.shape, common.dtype),
-            sem((members * sequences,)),
-            sem((members * sequences,)),
-            sem((sequences,)),
-            sem((sequences,)),
-            sem((2,)),
-        ],
-        compiler_params=pltpu.CompilerParams(collective_id=collective_id, has_side_effects=True),
-        cost_estimate=pl.CostEstimate(flops=0, bytes_accessed=v.size * 16, transcendentals=0),
-        name=f"spread_{collective_id}",
-    )(v, common)
 
 
 def gather(v):
@@ -1305,6 +1160,187 @@
     )(*(c.reshape(levels, group, tokens, -1) for c in cs), rank, back, prob, *kept, gate, up, down, own, sdown)
 
 
+class Spread:
+    def __init__(self, src, out, common, commons, sems, members, sequences):
+        self.src, self.out, self.common, self.commons = src, out, common, commons
+        self.sent, self.got, self.sent2, self.got2 = sems
+        self.members, self.sequences = members, sequences
+        self.me, self.mine = lax.axis_index("grp"), lax.axis_index("rep")
+
+    def other(self, n):
+        r = lax.rem(self.mine + n // self.members, self.sequences)
+        return {"rep": r, "grp": lax.rem(self.me + n % self.members, self.members)}
+
+    def meet(self):
+        barrier = pltpu.get_barrier_semaphore()
+        count = self.members * self.sequences
+
+        @pl.loop(1, count)
+        def _(n):
+            pl.semaphore_signal(barrier, 1, device_id=self.other(n), device_id_type=MESH)
+
+        pl.semaphore_wait(barrier, count - 1)
+
+    def block(self, n):
+        to = self.other(n)
+        return send(self.src.at[to["grp"]], self.out.at[self.mine, self.me], self.sent.at[n], self.got.at[n], to)
+
+    def whole(self, n):
+        return send(self.common, self.commons.at[self.mine], self.sent2.at[n], self.got2.at[n], self.other(n * self.members))
+
+    def start_blocks(self):
+        @pl.loop(1, self.members * self.sequences)
+        def _(n):
+            self.block(n).start()
+
+    def start_common(self):
+        @pl.loop(1, self.sequences)
+        def _(n):
+            self.whole(n).start()
+
+    def wait(self):
+        @pl.loop(1, self.members * self.sequences)
+        def _(n):
+            self.block(n).wait()
+
+        @pl.loop(1, self.sequences)
+        def _(n):
+            self.whole(n).wait()
+
+
+def finish_kernel(
+    part, o_src, dq_ref, cos_ref, sin_ref, q_hbm, kva_ref, up_ref, down_ref, small_ref, normed_ref, latent_ref, kvg_ref,
+    x_ref, xg_ref, dmid_ref, name_ref,
+    out, q_out, o_out,
+    *bufs, members, sequences
+):
+    twin_in, side_in, line_in = bufs[:3]
+    o_in, o_common, q_parts, d_query, wq, dn, d_lat, d_latent, ds_ref = bufs[11:20]
+    o_sent, o_got, b_sent, b_got, w_sent, w_got, local = bufs[20:]
+    reduce = Reduce(part, twin_in, side_in, line_in, bufs[3:11], members)
+    exchange = Exchange(o_src, o_in, o_sent, o_got, members)
+    spread = Spread(q_parts, q_out, o_common, o_out, (b_sent, b_got, w_sent, w_got), members, sequences)
+    me, mine = spread.me, spread.mine
+    order = far_first(reduce.levels)
+    z, levels = reduce.z, reduce.levels
+    tokens, width = x_ref.shape
+    tile = 256
+    load = pltpu.make_async_copy(q_hbm, wq, local.at[0])
+    own = [
+        pltpu.make_async_copy(q_parts.at[me], q_out.at[mine, me], local.at[1]),
+        pltpu.make_async_copy(o_common, o_out.at[mine], local.at[2]),
+    ]
+    load.start()
+    spread.meet()
+
+    @pl.loop(0, levels)
+    def _(s):
+        reduce.start(pick_from(order, z, s))
+
+    exchange.start()
+    o_in[me] = o_src[me]
+    cosine, sine = cos_ref[...], sin_ref[...]
+    half = ROPE // 2
+    for pair in range(dq_ref.shape[0] // 2):
+        pieces = []
+        for h in (2 * pair, 2 * pair + 1):
+            rope = jnp.concatenate([dq_ref[h, tokens:, :ROPE], dq_ref[h, tokens:, ROPE:]], axis=0).astype(F32)
+            turned = jnp.concatenate([rope[:, half:], rope[:, :half]], axis=1)
+            pieces += [dq_ref[h, :tokens, :], (rope * cosine + turned * sine).astype(BF16)]
+        d_query[:, pair * 2 * QK : (pair + 1) * 2 * QK] = jnp.concatenate(pieces, axis=1)
+
+    @pl.loop(0, levels)
+    def _(s):
+        reduce.chip(pick_from(order, z, s))
+
+    grad_up = t_dot(small_ref[...], d_query[...])
+    ds_ref[...] = dot_t(d_query[...], up_ref[...]).astype(BF16)
+    grad_down = t_dot(ds_ref[...], normed_ref[...])
+    rows = width // members
+    for g in range(members):
+        first = g // 2 * 2 * QK
+        q_parts[g] = jnp.concatenate(
+            [grad_down[:, g * rows : (g + 1) * rows], grad_up[:, first : first + 2 * QK]], axis=1
+        ).astype(BF16)
+    spread.start_blocks()
+    own[0].start()
+    exchange.wait()
+    total = jnp.zeros(o_in.shape[1:], F32)
+    for g in range(members):
+        total = total + o_in[g].astype(F32)
+    o_common[...] = jnp.concatenate([total, name_ref[...]], axis=1)
+    spread.start_common()
+    own[1].start()
+    load.wait()
+    every = width // tile // (levels - 1)
+
+    @pl.loop(0, width // tile)
+    def _(j):
+        dn[:, tiles(j, tile)] = dot_t(d_query[...], wq[pl.ds(j * (tile // rows), tile // rows)].reshape(tile, -1))
+
+        @pl.when((j % every == every - 1) & (j // every < levels - 1))
+        def _():
+            reduce.line(pick_from(order, z, j // every))
+
+    reduce.last(d_lat)
+    gradient = d_lat[...].astype(F32)
+    latent = latent_ref[...]
+    d_latent[:, :KVR] = norm_back(latent[:, :KVR], kvg_ref[...], gradient[:, :KVR]).astype(BF16)
+    rope = gradient[:, KVR:]
+    turned = jnp.concatenate([rope[:, half:], rope[:, :half]], axis=1)
+    d_latent[:, KVR:] = (rope * cosine + turned * sine).astype(BF16)
+
+    @pl.loop(0, width // tile)
+    def _(j):
+        at = tiles(j, tile)
+        dn[:, at] += dot_t(d_latent[...], kva_ref[at, :]) + dot_t(ds_ref[...], down_ref[at, :])
+
+    out[...] = (dmid_ref[...] + norm_back(x_ref[...].astype(F32), xg_ref[...], dn[...])).astype(BF16)
+    reduce.finish()
+    spread.wait()
+    for copy in own:
+        copy.wait()
+
+
+def finish(part, o_parts, dq, cosine, sine, all_q, kva, up, down, small, normed, latent, kvg, x, xg, dmid, name, sequences, collective_id):
+    members, tokens, c = part.shape
+    width = x.shape[1]
+    rank = o_parts.shape[1]
+    vmem = pl.BlockSpec(memory_space=pltpu.VMEM)
+    anywhere = pl.BlockSpec(memory_space=pl.ANY)
+    sem = pltpu.SemaphoreType.DMA
+    share = width // members + 2 * QK
+    common = (rank, o_parts.shape[2] + name.shape[1])
+    return pl.pallas_call(
+        functools.partial(finish_kernel, members=members, sequences=sequences),
+        in_specs=[vmem] * 5 + [anywhere] + [vmem] * 11,
+        out_specs=[vmem, anywhere, anywhere],
+        out_shape=[
+            jax.ShapeDtypeStruct((tokens, width), BF16),
+            jax.ShapeDtypeStruct((sequences, members, rank, share), BF16),
+            jax.ShapeDtypeStruct((sequences, *common), F32),
+        ],
+        scratch_shapes=Reduce.scratch(members, tokens, c, BF16)
+        + [
+            pltpu.VMEM(o_parts.shape, BF16),
+            pltpu.VMEM(common, F32),
+            pltpu.VMEM((members, rank, share), BF16),
+            pltpu.VMEM((tokens, H * QK), BF16),
+            pltpu.VMEM(all_q.shape, BF16),
+            pltpu.VMEM((tokens, width), F32),
+            pltpu.VMEM((tokens, c), BF16),
+            pltpu.VMEM((tokens, c), BF16),
+            pltpu.VMEM((tokens, rank), BF16),
+        ]
+        + [sem((n,)) for n in (members,) * 2 + (members * sequences,) * 2 + (sequences,) * 2 + (3,)],
+        compiler_params=pltpu.CompilerParams(
+            collective_id=collective_id, has_side_effects=True, vmem_limit_bytes=56 * 1024 * 1024
+        ),
+        cost_estimate=pl.CostEstimate(flops=4 * tokens * width * H * QK, bytes_accessed=40_000_000, transcendentals=0),
+        name="finish",
+    )(part, o_parts, dq, cosine, sine, all_q, kva, up, down, small, normed, latent, kvg, x, xg, dmid, name)
+
+
 def by_owner(gradient, members):
     return gradient.astype(BF16).reshape(gradient.shape[0], members, -1).transpose(1, 0, 2)
 
@@ -1453,43 +1489,38 @@
         6,
     )
     o_parts = jnp.concatenate([by_owner(g, members) for g in (grad_odown, grad_oup)], axis=-1)
-    d_latents, (o_landed,) = reduce_blocks(d_latents, [o_parts], members, 7)
-    d_latents = d_latents.astype(F32)
-    d_query = unpack(d_query).transpose(1, 0, 2).astype(F32)
-    d_latent = jnp.concatenate(
-        [
-            norm_back(latent[:, :KVR], kv_gain, d_latents[:, :KVR]),
-            unrotate(d_latents[:, KVR:], cosine, sine),
-        ],
-        axis=-1,
-    ).astype(BF16)
-    d_query = (
-        jnp.concatenate(
-            [d_query[:, :, :NOPE], unrotate(d_query[:, :, NOPE:], cosine[:, None], sine[:, None])],
-            axis=-1,
-        )
-        .reshape(tokens, H * QK)
-        .astype(BF16)
+    name = jnp.broadcast_to(adapter.astype(F32), (qa_up.shape[0], 128))
+    grad_inputs, q_shares, o_shares = finish(
+        d_latents,
+        o_parts,
+        d_query,
+        jnp.concatenate([cosine, cosine], axis=1),
+        jnp.concatenate([sine, -sine], axis=1),
+        all_q,
+        full_kva,
+        qa_up,
+        qa_down,
+        q_small,
+        normed,
+        latent,
+        kv_gain[None],
+        hidden[0],
+        attn_gain[None],
+        d_middle,
+        name,
+        sequences,
+        7,
     )
     ffn_out, _ = lax.optimization_barrier((ffn_out, d_query))
     output = (middle + ffn_out.astype(F32)).astype(BF16)
-    grad_qup = t_dot(q_small, d_query)
-    d_qsmall = dot_t(d_query, qa_up).astype(BF16)
-    grad_qdown = t_dot(d_qsmall, normed)
-    d_normed = dot_t(d_query, full_q) + dot_t(d_qsmall, qa_down) + dot_t(d_latent, full_kva)
-    grad_inputs = (d_middle + norm_back(inputs, attn_gain, d_normed)).astype(BF16)
-
-    q_parts = jnp.concatenate([by_owner(g, members) for g in (grad_qdown, grad_qup)], axis=-1)
-    o_share = jnp.sum(o_landed.astype(F32), axis=0)
-    named = jnp.broadcast_to(adapter.astype(F32), (o_share.shape[0], 128))
-    q_shares, o_shares = spread_blocks(
-        q_parts, jnp.concatenate([o_share, named], axis=-1), members, sequences, 8
-    )
     numbers = o_shares[:, 0, -1].astype(jnp.int32)
-    shares = jnp.concatenate([jnp.sum(q_shares.astype(F32), axis=1), o_shares[:, :, :-128]], axis=-1)
+    q_share = jnp.sum(q_shares.astype(F32), axis=1)
+    rows = width // members
+    q_up_share = lax.dynamic_slice_in_dim(q_share[..., rows:], me % 2 * QK, QK, 2)
+    shares = jnp.concatenate([q_share[..., :rows], q_up_share, o_shares[:, :, :-128]], axis=-1)
     selector = (jnp.arange(q_down.shape[0], dtype=jnp.int32)[:, None] == numbers[None, :]).astype(F32)
     summed = jnp.sum(selector[:, :, None, None] * shares[None], axis=1)
-    sizes = [g.shape[1] // members for g in (grad_qdown, grad_qup, grad_odown, grad_oup)]
+    sizes = [rows, QK, rows, rows]
     ends = [sum(sizes[: n + 1]) for n in range(4)]
     outs = [summed[:, :, e - s : e] for e, s in zip(ends, sizes)]
     return (

time: 774 us -> 750 us (0.969); the launches traced: 770 us -> 738 us
  matrix products: 46 us -> 29.6 us
    dot_general x8 -> x4, matrix products: 22.5 us -> 11.4 us  [dot_t(): lax.dot_general(former, latter, (((1,), (1,)), ((), ())), preferred_eleme...]
    pallas_call x2 -> x1, Pallas kernels: 54.6 us -> 53.2 us  [finish(): pl.pallas_call(functools.partial(finish_kernel, members=members, sequence...]
  transfers between devices with their start and end apart: 3 -> 3, of which waited for: 1 -> 1; matrix products, arithmetic and copies ran while one was open for 12% -> 9% of each run, Pallas kernels for 59% -> 61%
where the time goes in v6:
time: 750 us; the launch traced here: 738 us
  Pallas kernels  632 us (84%)
  local copies, waits for them, and re-layouts  34.3 us (5%)
  matrix products  29.6 us (4%)
  other arithmetic  18 us (2%)
  between operations  16.4 us (2%)
    pallas_call x2, Pallas kernels, communicate(): pl.pallas_call(functools.partial(comm_kernel, members=members, splits=tup...  183 us
    pallas_call x1, Pallas kernels, experts_backward(): pl.pallas_call(functools.partial(experts_back_kernel, members=members, sl...  167 us
    pallas_call x1, Pallas kernels, experts_forward(): pl.pallas_call(functools.partial(experts_kernel, members=members, slots=s...  139 us
    pallas_call x1, Pallas kernels, attend_back(): pl.pallas_call(functools.partial(attend_back_kernel, members=members, fac...  61.3 us
    pallas_call x1, Pallas kernels, finish(): pl.pallas_call(functools.partial(finish_kernel, members=members, sequence...  53.2 us
    pallas_call x1, Pallas kernels, attend(): pl.pallas_call(functools.partial(attend_kernel, members=members, unit=QK...  29.1 us
    dot_general x10, matrix products, dot(): return jnp.dot(former, latter, preferred_element_type=F32)  17.8 us
  transfers between devices with their start and end apart: 3, of which 1 were waited for; matrix products, arithmetic and copies ran while one was open for 9% of the time, Pallas kernels for 61%

profile of v6, /device:TPU:0, one launch (start us, length us, event | category | flops | bytes accessed | tf_op | source)
XLA Modules:
  0.0 737.9 jit_solution(9974429867889680132)
XLA Ops:
  7.2 1.8 copy.79.refs_0_
  9.0 1.5 copy.86
  10.9 110.3 %communicate_1.1 = (bf16[16,128,576]{2,1,0:T(8,128)(2,1)}, bf16[16,128,3072]{2,1,0:T(8,128)(2,1)}, bf16[16,128,2048]{2,1,0:T(8,128)(2,1)}) custom-call(bf16[128,576]{1,0:T(8,128)(2,1)} %copy.79.refs_0_, bf16[128,3072]{1,0:T(8,128)(2,1)} %refs_1_.2, bf16[128,2048]{1,0:T(8,128)(2,1)} %refs_2_.1), custom_call_target="tpu_custom_call" | custom-call | bytes 186646528 | tf_op jit(solution)/shard_map/communicate_1/pallas_call | solution.py:350
  121.2 1.2 copy.87
  122.4 4.7 all-to-all-start
  127.6 1.7 fusion.56.latent_ref
  129.2 6.1 fusion.54
  135.9 0.8 constant_dynamic-slice_fusion.1
  137.4 0.9 dynamic-slice_bitcast_fusion.up_ref
  138.3 1.8 convolution_add_fusion
  140.9 3.1 reshape.243
  144.2 1.1 copy.137
  145.3 2.1 fusion.17
  147.9 1.0 subtract_convert_fusion
  151.5 0.8 pad_maximum_fusion.2.refs_0_
  152.4 1.3 maximum_maximum_fusion.1.refs_2_
  153.7 0.9 fusion.62
  154.6 2.0 all-to-all-done
  156.6 2.6 copy.88
  159.9 72.3 %communicate_2.1 = (bf16[16,192,576]{2,1,0:T(8,128)(2,1)}, bf16[16,128,16]{2,1,0:T(8,128)(2,1)}, bf16[16,288,128]{2,1,0:T(8,128)(2,1)}, bf16[16,32,256]{2,1,0:T(8,128)(2,1)}, f32[16,8,192]{2,1,0:T(8,128)}) custom-call(bf16[192,576]{1,0:T(8,128)(2,1)} %pad_maximum_fusion.2.refs_0_, bf16[128,16]{1,0:T(8,128)(2,1)} %copy.90.refs_1_, ...), custom_call_target="tpu_custom_call" | custom-call | bytes 40763392 | tf_op jit(solution)/shard_map/communicate_2/pallas_call | solution.py:350
  232.2 1.4 fusion.61
  235.3 1.2 slice.131
  236.5 0.9 slice_compare_fusion
  237.6 1.7 copy.93.back_ref
  239.3 3.0 convolution_convert_fusion
  243.4 29.1 %attend.1 = (f32[3072,128]{1,0:T(8,128)S(1)}, f32[3072,1]{1,0:T(8,128)S(1)}, bf16[16,192,128]{2,1,0:T(8,128)(2,1)S(1)}) custom-call(s32[1]{0:T(128)S(6)} %copy.144.prefix_ref, bf16[3072,192]{1,0:T(8,128)(2,1)S(1)} %bitcast.150, bf16[3072,192]{1,0:T(8,128)(2,1)S(1)} %pad_maximum_fusion.k_ref, bf16[3072,128]{1,0:T(8,128)(2,1)S(1)} %get-tuple-element.70.v_ref), custom_call_target="tpu_custom_call" | custom-call | flops 3019898880 | bytes 3072000 | tf_op jit(solution)/shard_map/attend/pallas_call | solution.py:585
  272.5 1.2 convolution_convert_fusion.5
  273.8 1.8 fusion.2
  275.7 1.3 multiply_reduce_fusion.1
  280.8 139.4 %experts_forward.1 = (bf16[4,4,192,2048]{3,2,1,0:T(8,128)(2,1)}, bf16[4,384,1408]{2,1,0:T(8,128)(2,1)}, bf16[4,384,1408]{2,1,0:T(8,128)(2,1)}, bf16[4,384,2048]{...) custom-call(bf16[192,2048]{1,0:T(8,128)(2,1)} %copy-done.19, ...), custom_call_target="tpu_custom_call" | custom-call | flops 53150220288 | bytes 60000000 | tf_op jit(solution)/shard_map/experts_forward/pallas_call | solution.py:931
  420.2 0.8 copy-done.32
  421.0 1.0 copy.80
  422.0 0.8 pad_maximum_fusion.4
  422.8 1.1 fusion.6.normed_ref
  424.0 1.1 reduce
  425.0 166.7 %experts_backward.1 = (bf16[192,2048]{1,0:T(8,128)(2,1)}, f32[16,8,192]{2,1,0:T(8,128)}) custom-call(bf16[4,4,192,1024]{3,2,1,0:T(8,128)(2,1)} %bitcast.183, bf16[4,4,192,1024]{3,2,1,0:T(8,128)(2,1)} %bitcast.190, f32[16,8,192]{2,1,0:T(8,128)} %broadcast_in_dim.25.rank_ref, f32[16,192,1]{2,1,0:T(8,128)} %copy.93.back_ref, ...), custom_call_target="tpu_custom_call" | custom-call | flops 53150220288 | bytes 60000000 | tf_op jit(solution)/shard_map/experts_backward/pallas_call | solution.py:1125
  591.8 0.9 slice.110
  593.5 2.5 multiply_reduce_fusion
  596.6 1.2 convolution_convert_fusion.4
  597.8 6.3 fusion.49
  604.2 1.3 fusion.7
  607.1 61.3 %attend_back.1 = (bf16[16,192,576]{2,1,0:T(8,128)(2,1)}, bf16[16,288,128]{2,1,0:T(8,128)(2,1)S(1)}) custom-call(s32[1]{0:T(128)S(6)} %copy.144.prefix_ref, bf16[3072,192]{1,0:T(8,128)(2,1)} %bitcast.151, bf16[3072,192]{1,0:T(8,128)(2,1)} %copy-done.1, bf16[3072,128]{1,0:T(8,128)(2,1)S(1)} %copy-done.8, f32[3072,128]{1,0:T(8,128)} %copy-done.12, ...), custom_call_target="tpu_custom_call" | custom-call | flops 7851737088 | bytes 6144000 | tf_op jit(solution)/shard_map/attend_back/pallas_call | solution.py:714
  668.4 1.0 copy-done.4
  670.1 53.2 %finish.1 = (bf16[192,2048]{1,0:T(8,128)(2,1)}, bf16[2,16,16,512]{3,2,1,0:T(8,128)(2,1)}, f32[2,16,384]{2,1,0:T(8,128)}) custom-call(bf16[16,192,576]{2,1,0:T(8,128)(2,1)} %get-tuple-element.62.part, bf16[16,16,256]{2,1,0:T(8,128)(2,1)} %pad_maximum_fusion.3.o_src, bf16[16,288,128]{2,1,0:T(8,128)(2,1)} %copy-done.4, f32[192,64]{1,0:T(8,128)} %get-tuple-element.96.cos_ref, ...), custom_call_target="tpu_custom_call" | custom-call | flops 4831838208 | bytes 40000000 | tf_op jit(solution)/shard_map/finish/pallas_call | solution.py:1314
  723.2 1.1 convert_reduce_fusion
  725.2 0.9 convert_reduce_fusion.2
  727.8 2.3 fusion.11
  730.0 0.9 copy.146
  (163 shorter events, 18.1 us)
Async XLA Ops:
  7.2 3.3 copy-start.28
  122.4 4.9 copy-start.16
  122.4 5.2 copy-start.23
  122.4 5.2 copy-start.37
  122.4 34.2 %all-to-all-start = ((bf16[16,128,352]{1,2,0:T(8,128)(2,1)}), bf16[16,128,352]{1,2,0:T(8,128)(2,1)}, u32[]{:S(2)}, u32[]{:S(2)}) async-start(bf16[16,128,352]{1,2,0:T(8,128)(2,1)} %bitcast.12), calls=%async_computation | async-start | bytes 2883584 | tf_op jit(solution)/shard_map/all_to_all | solution.py:484
  127.0 298.0 %all-gather.2.cloned.1.call-start = ((), (), s32[]{:S(2)}) async-start(), calls=%async_computation.3 | async-start | bytes 6684672 | tf_op jit(solution)/shard_map/all_gather | solution.py:480
  127.5 9.2 %copy-start.49 = (f32[192]{0:T(256)}, f32[192]{0:T(256)S(1)}, u32[]{:S(2)}) copy-start(f32[192]{0:T(256)S(1)} %add_rsqrt_fusion.2) | copy-start | bytes 2308
  137.4 2.8 copy-start.34
  138.3 1.8 copy-start.26
  138.3 1.9 copy-start.48
  149.5 1.7 copy-start.47
  149.5 1.7 copy-start.18
  149.5 1.8 copy-start.46
  152.4 1.3 copy-start.20
  232.2 1.5 copy-start.25
  234.1 8.7 %copy-start = (bf16[16,192,192]{2,1,0:T(8,128)(2,1)}, bf16[16,192,192]{2,1,0:T(8,128)(2,1)S(1)}, u32[]{:S(2)}) copy-start(bf16[16,192,192]{2,1,0:T(8,128)(2,1)S(1)} %maximum_maximum_fusion) | copy-start | bytes 3538948
  234.1 493.7 %reduce-scatter.2.cloned.1.call-start = ((), (), s32[]{:S(2)}) async-start(), calls=%async_computation.2 | async-start | bytes 13369344 | tf_op jit(solution)/shard_map/reduce_scatter | solution.py:488
  235.3 4.1 copy-start.10
  237.6 4.8 copy-start.35
  242.5 31.3 %slice-start = ((s8[8388608]{0:T(1024)(128)(4,1)}), s8[4194304]{0:T(1024)(128)(4,1)S(1)}, s32[]{:S(2)}) async-start(s8[8388608]{0:T(1024)(128)(4,1)} %bitcast.159), calls=%async_computation.4 | async-start | bytes 8388608
  242.8 29.7 %copy-start.1 = (bf16[3072,192]{1,0:T(8,128)(2,1)}, bf16[3072,192]{1,0:T(8,128)(2,1)S(1)}, u32[]{:S(2)}) copy-start(bf16[3072,192]{1,0:T(8,128)(2,1)S(1)} %pad_maximum_fusion.k_ref) | copy-start | bytes 3538948
  243.4 30.4 %slice-start.1 = ((s8[8388608]{0:T(1024)(128)(4,1)}), s8[4194304]{0:T(1024)(128)(4,1)S(1)}, s32[]{:S(2)}) async-start(s8[8388608]{0:T(1024)(128)(4,1)} %bitcast.159), calls=%async_computation.5 | async-start | bytes 8388608
  243.4 30.4 %copy-start.17 = (bf16[1,192,2048]{2,1,0:T(8,128)(2,1)S(1)}, bf16[1,192,2048]{2,1,0:T(8,128)(2,1)}, u32[]{:S(2)}) copy-start(bf16[1,192,2048]{2,1,0:T(8,128)(2,1)} %param.23) | copy-start | bytes 2359300
  272.5 3.1 copy-start.2
  272.5 3.1 copy-start.5
  272.5 3.1 copy-start.12
  273.8 1.9 copy-start.40
  275.7 1.9 copy-start.39
  277.0 1.8 copy-start.13
  277.0 1.4 copy-start.24
  277.6 1.2 copy-start.44
  277.6 2.5 copy-start.36
  278.8 1.9 copy-start.42
  279.4 1.4 copy-start.43
  420.2 1.9 copy-start.30
  420.2 2.7 copy-start.38
  420.2 2.6 copy-start.50
  421.0 3.0 copy-start.3
  593.5 2.6 copy-start.14
  593.5 2.6 copy-start.21
  593.5 2.6 copy-start.45
  593.5 2.6 copy-start.51
  596.6 9.3 %copy-start.15 = (f32[192,2048]{1,0:T(8,128)}, f32[192,2048]{1,0:T(8,128)S(1)}, u32[]{:S(2)}) copy-start(f32[192,2048]{1,0:T(8,128)S(1)} %subtract_add_fusion.dmid_ref) | copy-start | bytes 4718596
  604.2 1.5 copy-start.6
  605.7 1.4 copy-start.8
  605.7 1.4 copy-start.9
  605.7 1.4 copy-start.11
  727.8 2.3 copy-start.27
  (9 other events, 7.8 us)
Sparse Core Ops, SparseCore 0:
  234.2 73.1 all-gather.1
  420.3 171.9 reduce-scatter.1

commit v7 on v6

--- a/solution.py
+++ b/solution.py
@@ -271,98 +271,6 @@
             self.copy(d).wait()
 
 
-def comm_kernel(*refs, members, splits, n_e):
-    n_g = len(splits)
-    n = n_g + n_e
-    ins, outs = refs[:n], refs[n : 2 * n]
-    stage = refs[2 * n : 3 * n]
-    local = refs[3 * n]
-    sems = refs[3 * n + 1 :]
-    me = lax.axis_index("grp")
-    into = [
-        pltpu.make_async_copy(r if k < n_g else r.at[me], stage[k], local.at[k]) for k, r in enumerate(ins)
-    ]
-    out_of = [pltpu.make_async_copy(stage[k], outs[k].at[me], local.at[k]) for k in range(n)]
-    gathers = [
-        Gather(ins[k], outs[k], sems[2 * k], sems[2 * k + 1], members, splits[k]) for k in range(n_g)
-    ]
-    exchanges = [Exchange(ins[k], outs[k], sems[2 * k], sems[2 * k + 1], members) for k in range(n_g, n)]
-    for copy in into:
-        copy.start()
-    split = [g for g in gathers if g.split]
-    meet(members, split[0].partner if split else None)
-    for g in gathers:
-        g.first()
-    for e in exchanges:
-        e.start()
-    for a, b in zip(into, out_of):
-        a.wait()
-        b.start()
-    levels = members // (SIDE * CORES)
-    z = me // (SIDE * CORES)
-    order = near_first(levels)
-
-    def lacked(g, s):
-        k = pick_from(order, z, s)
-        g.take_lacked(k, g.x)
-        g.take_lacked(k, 1 - g.x)
-
-    if gathers:
-
-        @pl.loop(0, levels)
-        def _(s):
-            for g in gathers:
-                g.relay(s + 1)
-            for g in gathers:
-                g.pass_on(pick_from(order, z, s))
-
-            @pl.when(s >= 1)
-            def _():
-                for g in split:
-                    lacked(g, s - 1)
-
-    for g in split:
-        lacked(g, levels - 1)
-    for g in gathers:
-
-        @pl.loop(0, levels)
-        def _(k):
-            g.take_twin(k)
-
-        if g.split:
-            g.take_twin_lacked()
-        g.finish()
-    for e in exchanges:
-        e.wait()
-    for copy in out_of:
-        copy.wait()
-
-
-def communicate(gathers, exchanges, members, collective_id, splits=None):
-    gathers, exchanges = list(gathers), list(exchanges)
-    n_g, n_e = len(gathers), len(exchanges)
-    splits = splits or [0] * n_g
-    blocks = [g.shape for g in gathers] + [e.shape[1:] for e in exchanges]
-    kinds = [a.dtype for a in gathers + exchanges]
-    anywhere = pl.BlockSpec(memory_space=pl.ANY)
-    sem = pltpu.SemaphoreType.DMA
-    moved = sum(members * b[0] * b[1] * 2 for b in blocks)
-    outs = pl.pallas_call(
-        functools.partial(comm_kernel, members=members, splits=tuple(splits), n_e=n_e),
-        in_specs=[anywhere] * (n_g + n_e),
-        out_specs=[anywhere] * (n_g + n_e),
-        out_shape=[jax.ShapeDtypeStruct((members, *b), k) for b, k in zip(blocks, kinds)],
-        scratch_shapes=[pltpu.VMEM(b, k) for b, k in zip(blocks, kinds)]
-        + [sem((n_g + n_e,))]
-        + [sem((6, members)), sem((2, members))] * n_g
-        + [sem((members,)), sem((members,))] * n_e,
-        compiler_params=pltpu.CompilerParams(collective_id=collective_id, has_side_effects=True),
-        cost_estimate=pl.CostEstimate(flops=0, bytes_accessed=moved * 8, transcendentals=0),
-        name=f"communicate_{collective_id}",
-    )(*gathers, *exchanges)
-    return outs[:n_g], outs[n_g:]
-
-
 class Reduce:
     def __init__(self, p, twin_in, side_in, line_in, sems, members):
         self.p, self.twin_in, self.side_in, self.line_in = p, twin_in, side_in, line_in
@@ -480,10 +388,6 @@
     return lax.all_gather(v, "grp", axis=0, tiled=True)
 
 
-def exchange(v):
-    return lax.all_to_all(v, "grp", split_axis=0, concat_axis=0, tiled=True)
-
-
 def scatter_sum(v):
     return lax.psum_scatter(v, "grp", scatter_dimension=0, tiled=True)
 
@@ -495,6 +399,204 @@
 def tie(v, other):
     first = other[(0,) * other.ndim]
     return v + jnp.minimum(jnp.abs(first), 0).astype(v.dtype)
+
+
+def open_kernel(
+    kva_src, q_src, o_src, router_src, kvb_src, chosen_src, shared_src,
+    normed_ref, down_ref, up_ref, cos_ref, sin_ref, kvg_ref,
+    all_kva, all_q, all_o, all_router, all_lat, q_out, kvb_out, chosen_out, shared_out, latent_ref, small_ref,
+    *bufs, members, split
+):
+    stage = bufs[:7]
+    kva, wq, lat_st, qm = bufs[7:11]
+    sems = bufs[11:]
+    local, load = sems[26:]
+    pairs = [sems[2 * n : 2 * n + 2] for n in range(13)]
+    me = lax.axis_index("grp")
+    levels = members // (SIDE * CORES)
+    z = me // (SIDE * CORES)
+    order = near_first(levels)
+    tokens, width = normed_ref.shape
+    g_kva = Gather(kva_src, all_kva, *pairs[0], members, split)
+    g_q = Gather(q_src, all_q, *pairs[1], members, split)
+    g_o = Gather(o_src, all_o, *pairs[2], members, split)
+    g_router = Gather(router_src, all_router, *pairs[3], members)
+    g_lat = Gather(lat_st, all_lat, *pairs[4], members)
+    e_kvb = Exchange(kvb_src, kvb_out, *pairs[5], members)
+    e_chosen = Exchange(chosen_src, chosen_out, *pairs[6], members)
+    e_shared = Exchange(shared_src, shared_out, *pairs[7], members)
+    q_sent, q_got = pairs[8]
+    sources = [kva_src, q_src, o_src, router_src, kvb_src.at[me], chosen_src.at[me], shared_src.at[me]]
+    places = [all_kva, all_q, all_o, all_router, kvb_out, chosen_out, shared_out]
+    into = [pltpu.make_async_copy(a, stage[n], local.at[n]) for n, a in enumerate(sources)]
+    out_of = [pltpu.make_async_copy(stage[n], b.at[me], local.at[n]) for n, b in enumerate(places)]
+    own_lat = pltpu.make_async_copy(lat_st, all_lat.at[me], local.at[7])
+    own_q = pltpu.make_async_copy(qm.at[me], q_out.at[me], local.at[8])
+    loads = [pltpu.make_async_copy(all_kva, kva, load.at[0]), pltpu.make_async_copy(all_q, wq, load.at[1])]
+
+    def query_to(n):
+        return send(qm.at[n], q_out.at[me], q_sent.at[n], q_got.at[me], n)
+
+    def query_from(n):
+        return send(qm.at[n], q_out.at[n], q_sent.at[n], q_got.at[n], n)
+
+    def lacked(g, s):
+        if g.split:
+            k = pick_from(order, z, s)
+            g.take_lacked(k, g.x)
+            g.take_lacked(k, 1 - g.x)
+
+    def events(gathers, s, before):
+        for g in gathers:
+            g.relay(s + 1)
+        for g in gathers:
+            g.pass_on(pick_from(order, z, s))
+
+        @pl.when(before)
+        def _():
+            for g in gathers:
+                lacked(g, s - 1)
+
+    for copy in into:
+        copy.start()
+    meet(members, g_kva.partner if split else None)
+    for g in (g_kva, g_q, g_router):
+        g.first()
+    e_kvb.start()
+    e_chosen.start()
+    for a, b in zip(into, out_of):
+        a.wait()
+        b.start()
+
+    @pl.loop(0, levels)
+    def _(s):
+        events((g_kva, g_q, g_router), s, s >= 1)
+
+    lacked(g_kva, levels - 1)
+    lacked(g_q, levels - 1)
+    g_o.first()
+    e_shared.start()
+    for g in (g_kva, g_q):
+
+        @pl.loop(0, levels)
+        def _(k):
+            g.take_twin(k)
+
+        if split:
+            g.take_twin_lacked()
+    for copy in out_of:
+        copy.wait()
+    for copy in loads:
+        copy.start()
+    loads[0].wait()
+    latent = dot(normed_ref[...], kva[...].reshape(width, -1))
+    latent_ref[...] = latent
+    half = ROPE // 2
+
+    def turn(v):
+        turned = jnp.concatenate([v[:, half:], v[:, :half]], axis=1)
+        return (v * cos_ref[...] - turned * sin_ref[...]).astype(BF16)
+
+    lat_st[:, :KVR] = root_norm(latent[:, :KVR], kvg_ref[...]).astype(BF16)
+    lat_st[:, KVR:] = turn(latent[:, KVR:])
+    g_lat.first()
+    own_lat.start()
+    small_ref[...] = dot(normed_ref[...], down_ref[...]).astype(BF16)
+    loads[1].wait()
+    turns = members // 2
+
+    @pl.loop(0, turns)
+    def _(n):
+        pair = lax.rem(me // 2 + n, turns)
+        at = pl.ds(pl.multiple_of(pair * 2 * QK, 128), 2 * QK)
+        both = dot(normed_ref[...], wq[:, :, at].reshape(width, 2 * QK)) + dot(small_ref[...], up_ref[:, at])
+        for t in range(2):
+            to = 2 * pair + t
+            r = t * QK
+            qm[to, :tokens, :] = both[:, r : r + NOPE].astype(BF16)
+            rope = turn(both[:, r + NOPE : r + QK])
+            qm[to, tokens:, :ROPE] = rope[: tokens // 2]
+            qm[to, tokens:, ROPE:] = rope[tokens // 2 :]
+
+            @pl.when(to == me)
+            def _():
+                own_q.start()
+
+            @pl.when(to != me)
+            def _():
+                query_to(to).start()
+
+        @pl.when(n == turns // 2)
+        def _():
+            events((g_lat, g_o), 0, False)
+
+    @pl.loop(1, levels)
+    def _(s):
+        events((g_lat, g_o), s, s >= 1)
+
+    lacked(g_o, levels - 1)
+    for g in (g_lat, g_router, g_o):
+
+        @pl.loop(0, levels)
+        def _(k):
+            g.take_twin(k)
+
+        if g.split:
+            g.take_twin_lacked()
+    for g in (g_kva, g_q, g_router, g_lat, g_o):
+        g.finish()
+
+    @pl.loop(1, members)
+    def _(d):
+        n = lax.rem(me + d, members)
+        query_from(n).wait_recv()
+        query_to(n).wait_send()
+
+    for e in (e_kvb, e_chosen, e_shared):
+        e.wait()
+    own_lat.wait()
+    own_q.wait()
+
+
+def opening(kva, q, o, router, kvb, chosen, shared, normed, down, up, cosine, sine, kvg, members, split, collective_id):
+    tokens, width = normed.shape
+    vmem = pl.BlockSpec(memory_space=pltpu.VMEM)
+    anywhere = pl.BlockSpec(memory_space=pl.ANY)
+    sem = pltpu.SemaphoreType.DMA
+    packed = tokens + tokens // 2
+    grown = lambda a: jax.ShapeDtypeStruct((members, *a.shape), a.dtype)
+    same = lambda a: jax.ShapeDtypeStruct(a.shape, a.dtype)
+    g_sems = [sem((6, members)), sem((2, members))]
+    e_sems = [sem((members,)), sem((members,))]
+    return pl.pallas_call(
+        functools.partial(open_kernel, members=members, split=split),
+        in_specs=[anywhere] * 7 + [vmem] * 6,
+        out_specs=[anywhere] * 9 + [vmem] * 2,
+        out_shape=[
+            grown(kva), grown(q), grown(o), grown(router),
+            jax.ShapeDtypeStruct((members, tokens, kva.shape[1]), BF16),
+            jax.ShapeDtypeStruct((members, packed, NOPE), BF16),
+            same(kvb), same(chosen), same(shared),
+            jax.ShapeDtypeStruct((tokens, kva.shape[1]), F32),
+            jax.ShapeDtypeStruct((tokens, down.shape[1]), BF16),
+        ],
+        scratch_shapes=[pltpu.VMEM(a.shape, a.dtype) for a in (kva, q, o, router)]
+        + [pltpu.VMEM(a.shape[1:], a.dtype) for a in (kvb, chosen, shared)]
+        + [
+            pltpu.VMEM((members, *kva.shape), BF16),
+            pltpu.VMEM((members, *q.shape), BF16),
+            pltpu.VMEM((tokens, kva.shape[1]), BF16),
+            pltpu.VMEM((members, packed, NOPE), BF16),
+        ]
+        + g_sems * 5
+        + e_sems * 8
+        + [sem((9,)), sem((2,))],
+        compiler_params=pltpu.CompilerParams(
+            collective_id=collective_id, has_side_effects=True, vmem_limit_bytes=48 * 1024 * 1024
+        ),
+        cost_estimate=pl.CostEstimate(flops=2 * tokens * width * q.shape[1], bytes_accessed=200_000_000, transcendentals=0),
+        name="opening",
+    )(kva, q, o, router, kvb, chosen, shared, normed, down, up, cosine, sine, kvg)
 
 
 def key_blocks(start, rows, keys, length):
@@ -1404,36 +1506,37 @@
     )
     sequences = lax.axis_size("rep")
     split = w_q.shape[0] * 3 // 128 * 16 if sequences % 2 == 0 else 0
-    (all_kva, all_q, all_o), _ = communicate([w_kva, w_q, w_o], [], members, 1, [split] * 3)
-    full_kva, full_q, full_o = (v.reshape(-1, v.shape[2]) for v in (all_kva, all_q, all_o))
     hidden_slice = shared_down.shape[0]
-    shared = after(jnp.stack([shared_gate, shared_up], axis=1), all_q)
+    shared = jnp.stack([shared_gate, shared_up], axis=1)
     shared = shared.reshape(shared.shape[0], 2, members, hidden_slice).transpose(2, 0, 1, 3)
-    own_shared = exchange(shared.reshape(members, -1, 2 * hidden_slice)).reshape(width, 2 * hidden_slice)
-
     positions = me * tokens + jnp.arange(tokens, dtype=jnp.int32)
     cosine, sine = angles(positions, ROPE)
     normed = root_norm(inputs, attn_gain).astype(BF16)
-    latent = dot(normed, full_kva)
-    compressed = root_norm(latent[:, :KVR], kv_gain).astype(BF16)
-    k_rope = rotate(latent[:, KVR:], cosine, sine).astype(BF16)
-    q_small = dot(normed, qa_down).astype(BF16)
-    query = (dot(normed, full_q) + dot(q_small, qa_up)).reshape(tokens, H, QK)
-    query = jnp.concatenate(
-        [query[:, :, :NOPE], rotate(query[:, :, NOPE:], cosine[:, None], sine[:, None])], axis=-1
-    ).astype(BF16)
-    (all_latent, all_router), (q_packed, kvb_parts, chosen_all) = communicate(
-        [jnp.concatenate([compressed, k_rope], axis=-1), w_router],
-        [
-            after(pack(query.transpose(1, 0, 2)), own_shared),
-            w_kvb.reshape(w_kvb.shape[0], members, -1).transpose(1, 0, 2),
-            jnp.broadcast_to(chosen_by.T[:, None, :], (experts, 8, tokens)),
-        ],
+    cosine2 = jnp.concatenate([cosine, cosine], axis=1)
+    sine2 = jnp.concatenate([sine, -sine], axis=1)
+    (
+        all_kva, all_q, all_o, all_router, all_latent, q_packed, kvb_parts, chosen_all, own_shared, latent, q_small
+    ) = opening(
+        w_kva,
+        w_q,
+        w_o,
+        w_router,
+        w_kvb.reshape(w_kvb.shape[0], members, -1).transpose(1, 0, 2),
+        jnp.broadcast_to(chosen_by.T[:, None, :], (experts, 8, tokens)),
+        shared.reshape(members, -1, 2 * hidden_slice),
+        normed,
+        qa_down,
+        qa_up,
+        cosine2,
+        sine2,
+        kv_gain[None],
         members,
-        2,
+        split,
+        1,
     )
-    full_router = all_router.reshape(width, -1)
+    full_kva, full_o, full_router = (v.reshape(-1, v.shape[2]) for v in (all_kva, all_o, all_router))
     own_kvb = kvb_parts.reshape(KVR, -1)
+    own_shared = own_shared.reshape(width, -1)
     all_latent = all_latent.reshape(length, KVR + ROPE)
     q_head = unpack(q_packed).reshape(length, QK)
     q_head, c_first = lax.optimization_barrier((q_head, cotangent[:, : width // 2]))
@@ -1494,8 +1597,8 @@
         d_latents,
         o_parts,
         d_query,
-        jnp.concatenate([cosine, cosine], axis=1),
-        jnp.concatenate([sine, -sine], axis=1),
+        cosine2,
+        sine2,
         all_q,
         full_kva,
         qa_up,

time: 750 us -> 726 us (0.968); the launches traced: 738 us -> 725 us
  Pallas kernels: 632 us -> 650 us
  matrix products: 29.6 us -> 19.5 us
    pallas_call x2 -> x1, Pallas kernels: 183 us -> 193 us  [opening(): pl.pallas_call(functools.partial(open_kernel, members=members, split=spli...]
    dot_general x10 -> x6, matrix products: 17.8 us -> 7.8 us  [dot(): return jnp.dot(former, latter, preferred_element_type=F32)]
  transfers between devices with their start and end apart: 3 -> 2, of which waited for: 1 -> 0; matrix products, arithmetic and copies ran while one was open for 9% -> 5% of each run, Pallas kernels for 61% -> 63%
where the time goes in v7:
time: 726 us; the launch traced here: 725 us
  Pallas kernels  650 us (90%)
  local copies, waits for them, and re-layouts  27.5 us (4%)
  matrix products  19.5 us (3%)
  between operations  16.3 us (2%)
  other arithmetic  11.3 us (2%)
    pallas_call x1, Pallas kernels, opening(): pl.pallas_call(functools.partial(open_kernel, members=members, split=spli...  193 us
    pallas_call x1, Pallas kernels, experts_backward(): pl.pallas_call(functools.partial(experts_back_kernel, members=members, sl...  171 us
    pallas_call x1, Pallas kernels, experts_forward(): pl.pallas_call(functools.partial(experts_kernel, members=members, slots=s...  140 us
    pallas_call x1, Pallas kernels, attend_back(): pl.pallas_call(functools.partial(attend_back_kernel, members=members, fac...  60.3 us
    pallas_call x1, Pallas kernels, finish(): pl.pallas_call(functools.partial(finish_kernel, members=members, sequence...  52.9 us
    pallas_call x1, Pallas kernels, attend(): pl.pallas_call(functools.partial(attend_kernel, members=members, unit=QK...  32.8 us
  transfers between devices with their start and end apart: 2, of which 0 were waited for; matrix products, arithmetic and copies ran while one was open for 5% of the time, Pallas kernels for 63%

profile of v7, /device:TPU:0, one launch (start us, length us, event | category | flops | bytes accessed | tf_op | source)
XLA Modules:
  0.0 724.8 jit_solution(3781513600423489344)
XLA Ops:
  7.2 1.1 copy.76.kva_src
  8.4 0.8 copy.77.router_src
  9.2 1.0 copy.119
  10.1 0.7 copy.122
  10.9 1.5 copy.73
  12.9 1.6 copy.78.shared_src
  15.4 0.8 constant_dynamic-slice_fusion.1
  16.6 1.2 dynamic-slice_bitcast_fusion.up_ref
  17.8 1.4 fusion.6.normed_ref
  19.9 192.7 %opening.1 = (bf16[16,128,576]{2,1,0:T(8,128)(2,1)}, bf16[16,128,3072]{2,1,0:T(8,128)(2,1)}, bf16[16,128,2048]{2,1,0:T(8,128)(2,1)}, bf16[16,128,16]{2,1,0:T(8,1...) custom-call(bf16[128,576]{1,0:T(8,128)(2,1)S(1)} %copy.76.kva_src, ...), custom_call_target="tpu_custom_call" | custom-call | flops 2415919104 | bytes 200000000 | tf_op jit(solution)/shard_map/opening/pallas_call | solution.py:571
  213.4 0.8 copy-done.31
  214.2 0.9 fusion.47
  216.5 2.1 slice.79
  218.7 1.7 copy.81.back_ref
  220.4 3.0 convolution_convert_fusion
  223.5 1.3 copy-done.30
  225.2 32.8 %attend.1 = (f32[3072,128]{1,0:T(8,128)S(1)}, f32[3072,1]{1,0:T(8,128)S(1)}, bf16[16,192,128]{2,1,0:T(8,128)(2,1)S(1)}) custom-call(s32[1]{0:T(128)S(6)} %copy.124.prefix_ref, bf16[3072,192]{1,0:T(8,128)(2,1)S(1)} %bitcast.142, bf16[3072,192]{1,0:T(8,128)(2,1)S(1)} %pad_maximum_fusion.k_ref, bf16[3072,128]{1,0:T(8,128)(2,1)S(1)} %get-tuple-element.68.v_ref), custom_call_target="tpu_custom_call" | custom-call | flops 3019898880 | bytes 3072000 | tf_op jit(solution)/shard_map/attend/pallas_call | solution.py:687
  258.0 1.2 convolution_convert_fusion.4
  259.3 1.8 fusion.2
  261.2 1.3 multiply_reduce_fusion.1
  262.5 0.6 multiply_multiply_fusion
  264.1 0.6 copy-done.35
  264.7 0.7 broadcast_in_dim.24.prob_hbm
  265.3 0.7 broadcast_in_dim.26.rank_ref
  266.0 140.5 %experts_forward.1 = (bf16[4,4,192,2048]{3,2,1,0:T(8,128)(2,1)}, bf16[4,384,1408]{2,1,0:T(8,128)(2,1)}, bf16[4,384,1408]{2,1,0:T(8,128)(2,1)}, bf16[4,384,2048]{...) custom-call(bf16[192,2048]{1,0:T(8,128)(2,1)} %copy-done.29, ...), custom_call_target="tpu_custom_call" | custom-call | flops 53150220288 | bytes 60000000 | tf_op jit(solution)/shard_map/experts_forward/pallas_call | solution.py:1033
  406.5 1.4 copy-done.6
  407.9 1.1 reduce
  409.0 170.8 %experts_backward.1 = (bf16[192,2048]{1,0:T(8,128)(2,1)}, f32[16,8,192]{2,1,0:T(8,128)}) custom-call(bf16[4,4,192,1024]{3,2,1,0:T(8,128)(2,1)} %bitcast.171, bf16[4,4,192,1024]{3,2,1,0:T(8,128)(2,1)} %bitcast.178, f32[16,8,192]{2,1,0:T(8,128)} %broadcast_in_dim.26.rank_ref, f32[16,192,1]{2,1,0:T(8,128)} %copy.81.back_ref, ...), custom_call_target="tpu_custom_call" | custom-call | flops 53150220288 | bytes 60000000 | tf_op jit(solution)/shard_map/experts_backward/pallas_call | solution.py:1227
  579.7 0.9 slice.67
  580.7 0.7 fusion.25
  581.5 2.5 multiply_reduce_fusion
  584.0 0.5 subtract_add_fusion.dmid_ref
  584.6 1.2 convolution_convert_fusion.3
  585.8 6.3 fusion.41
  592.1 1.2 fusion.7
  593.9 0.6 copy-done.9
  594.7 0.7 pad_maximum_fusion.1.o_src
  595.4 60.3 %attend_back.1 = (bf16[16,192,576]{2,1,0:T(8,128)(2,1)}, bf16[16,288,128]{2,1,0:T(8,128)(2,1)S(1)}) custom-call(s32[1]{0:T(128)S(6)} %copy.124.prefix_ref, bf16[3072,192]{1,0:T(8,128)(2,1)} %bitcast.143, bf16[3072,192]{1,0:T(8,128)(2,1)} %copy-done.4, bf16[3072,128]{1,0:T(8,128)(2,1)S(1)} %copy-done.11, f32[3072,128]{1,0:T(8,128)} %copy-done.23, ...), custom_call_target="tpu_custom_call" | custom-call | flops 7851737088 | bytes 6144000 | tf_op jit(solution)/shard_map/attend_back/pallas_call | solution.py:816
  655.7 1.1 copy-done.7
  656.8 0.6 broadcast_in_dim.30.name_ref
  657.4 52.9 %finish.1 = (bf16[192,2048]{1,0:T(8,128)(2,1)}, bf16[2,16,16,512]{3,2,1,0:T(8,128)(2,1)}, f32[2,16,384]{2,1,0:T(8,128)}) custom-call(bf16[16,192,576]{2,1,0:T(8,128)(2,1)} %get-tuple-element.60.part, bf16[16,16,256]{2,1,0:T(8,128)(2,1)} %pad_maximum_fusion.1.o_src, bf16[16,288,128]{2,1,0:T(8,128)(2,1)} %copy-done.7, f32[192,64]{1,0:T(8,128)} %copy-done.14, ...), custom_call_target="tpu_custom_call" | custom-call | flops 4831838208 | bytes 40000000 | tf_op jit(solution)/shard_map/finish/pallas_call | solution.py:1416
  710.3 1.1 convert_reduce_fusion
  711.4 0.8 slice.71
  712.2 0.9 convert_reduce_fusion.2
  713.4 0.7 slice.85
  714.0 0.8 fusion.48
  714.8 2.3 fusion.10
  717.1 0.9 copy.126
  (130 shorter events, 5.7 us)
Async XLA Ops:
  7.2 5.2 copy-start.34
  7.2 401.8 %all-gather.2.cloned.1.call-start = ((), (), s32[]{:S(2)}) async-start(), calls=%async_computation.2 | async-start | bytes 6684672 | tf_op jit(solution)/shard_map/all_gather | solution.py:388
  12.9 1.6 copy-start.27
  14.5 3.3 copy-start.36
  16.3 3.5 copy-start.18
  16.3 3.6 copy-start.19
  16.3 3.6 copy-start.20
  16.6 196.0 %copy-start.1 = (bf16[1,2048,16]{2,1,0:T(8,128)(2,1)}, bf16[1,2048,16]{2,1,0:T(8,128)(2,1)S(1)}, u32[]{:S(2)}) copy-start(bf16[1,2048,16]{2,1,0:T(8,128)(2,1)S(1)} %copy.75) | copy-start | bytes 196612
  17.8 194.8 %copy-start.13 = (bf16[16,3072]{1,0:T(8,128)(2,1)}, bf16[16,3072]{1,0:T(8,128)(2,1)S(1)}, u32[]{:S(2)}) copy-start(bf16[16,3072]{1,0:T(8,128)(2,1)S(1)} %dynamic-slice_bitcast_fusion.up_ref) | copy-start | bytes 294916
  19.2 193.3 %copy-start = (bf16[192,2048]{1,0:T(8,128)(2,1)}, bf16[192,2048]{1,0:T(8,128)(2,1)S(1)}, u32[]{:S(2)}) copy-start(bf16[192,2048]{1,0:T(8,128)(2,1)S(1)} %fusion.6.normed_ref) | copy-start | bytes 2359300
  19.8 192.8 %copy-start.14 = (f32[192,64]{1,0:T(8,128)}, f32[192,64]{1,0:T(8,128)S(1)}, u32[]{:S(2)}) copy-start(f32[192,64]{1,0:T(8,128)S(1)} %get-tuple-element.88.cos_ref) | copy-start | bytes 147460
  19.8 192.8 %copy-start.15 = (f32[192,64]{1,0:T(8,128)}, f32[192,64]{1,0:T(8,128)S(1)}, u32[]{:S(2)}) copy-start(f32[192,64]{1,0:T(8,128)S(1)} %get-tuple-element.89.sin_ref) | copy-start | bytes 147460
  212.6 0.8 copy-start.12
  212.6 0.8 copy-start.16
  212.6 7.8 %copy-start.21 = (bf16[16,32,256]{2,1,0:T(8,128)(2,1)}, bf16[16,32,256]{2,1,0:T(8,128)(2,1)S(1)}, u32[]{:S(2)}) copy-start(bf16[16,32,256]{2,1,0:T(8,128)(2,1)S(1)} %get-tuple-element.40) | copy-start | bytes 786436
  212.6 51.1 %copy-start.2 = (bf16[16,128,16]{2,1,0:T(8,128)(2,1)}, bf16[16,128,16]{2,1,0:T(8,128)(2,1)S(1)}, u32[]{:S(2)}) copy-start(bf16[16,128,16]{2,1,0:T(8,128)(2,1)S(1)} %get-tuple-element.43) | copy-start | bytes 196612
  212.6 1.6 copy-start.31
  215.5 9.7 %copy-start.3 = (bf16[16,192,192]{2,1,0:T(8,128)(2,1)}, bf16[16,192,192]{2,1,0:T(8,128)(2,1)S(1)}, u32[]{:S(2)}) copy-start(bf16[16,192,192]{2,1,0:T(8,128)(2,1)S(1)} %maximum_maximum_fusion) | copy-start | bytes 3538948
  215.5 499.3 %reduce-scatter.2.cloned.1.call-start = ((), (), s32[]{:S(2)}) async-start(), calls=%async_computation.1 | async-start | bytes 13369344 | tf_op jit(solution)/shard_map/reduce_scatter | solution.py:392
  223.4 1.4 copy-start.30
  223.5 1.6 copy-start.10
  224.8 34.4 %slice-start = ((s8[8388608]{0:T(1024)(128)(4,1)}), s8[4194304]{0:T(1024)(128)(4,1)S(1)}, s32[]{:S(2)}) async-start(s8[8388608]{0:T(1024)(128)(4,1)} %bitcast.153), calls=%async_computation.3 | async-start | bytes 8388608
  225.1 32.9 %copy-start.4 = (bf16[3072,192]{1,0:T(8,128)(2,1)}, bf16[3072,192]{1,0:T(8,128)(2,1)S(1)}, u32[]{:S(2)}) copy-start(bf16[3072,192]{1,0:T(8,128)(2,1)S(1)} %pad_maximum_fusion.k_ref) | copy-start | bytes 3538948
  225.2 34.1 %slice-start.1 = ((s8[8388608]{0:T(1024)(128)(4,1)}), s8[4194304]{0:T(1024)(128)(4,1)S(1)}, s32[]{:S(2)}) async-start(s8[8388608]{0:T(1024)(128)(4,1)} %bitcast.153), calls=%async_computation.4 | async-start | bytes 8388608
  225.2 34.1 %copy-start.28 = (bf16[1,192,2048]{2,1,0:T(8,128)(2,1)S(1)}, bf16[1,192,2048]{2,1,0:T(8,128)(2,1)}, u32[]{:S(2)}) copy-start(bf16[1,192,2048]{2,1,0:T(8,128)(2,1)} %param.23) | copy-start | bytes 2359300
  258.0 3.1 copy-start.5
  258.0 3.1 copy-start.8
  258.0 3.1 copy-start.23
  259.3 1.9 copy-start.38
  261.2 1.9 copy-start.37
  262.5 1.5 copy-start.24
  263.3 2.7 copy-start.29
  264.0 0.6 copy-start.35
  264.1 1.9 copy-start.40
  264.6 1.3 copy-start.41
  406.5 1.4 copy-start.6
  581.4 2.6 copy-start.25
  581.4 2.6 copy-start.32
  581.4 2.6 copy-start.43
  581.4 2.6 copy-start.44
  584.6 9.0 %copy-start.26 = (f32[192,2048]{1,0:T(8,128)}, f32[192,2048]{1,0:T(8,128)S(1)}, u32[]{:S(2)}) copy-start(f32[192,2048]{1,0:T(8,128)S(1)} %subtract_add_fusion.dmid_ref) | copy-start | bytes 4718596
  592.1 1.5 copy-start.39
  593.4 1.1 copy-start.9
  593.6 1.8 copy-start.11
  593.6 1.8 copy-start.17
  593.6 1.8 copy-start.22
  655.7 1.1 copy-start.7
  714.8 2.3 copy-start.33
  (1 other events, 0.6 us)
Sparse Core Ops, SparseCore 0:
  215.7 69.9 all-gather.1
  406.6 171.6 reduce-scatter.1

commit v8 on v7

--- a/solution.py
+++ b/solution.py
@@ -251,14 +251,87 @@
                     self.to_partner(slot).wait_send()
 
 
+class SideFirst(Gather):
+    def turn(self):
+        slot = index_of(self.z, 1 - self.x, self.c)
+        self.arrive(slot)
+
+        @pl.when(self.z < self.levels - 1)
+        def _():
+            self.copy(slot, 0, self.up).start()
+
+        @pl.when(self.z > 0)
+        def _():
+            self.copy(slot, 1, self.down).start()
+
+        self.copy(slot, 3, self.twin).start()
+
+    def relay(self, s):
+        for x in (self.x, 1 - self.x):
+
+            @pl.when(self.z >= s)
+            def _():
+                slot = index_of(self.z - s, x, self.c)
+                self.arrive(slot)
+
+                @pl.when(self.z < self.levels - 1)
+                def _():
+                    self.copy(slot, 0, self.up).start()
+
+                self.copy(slot, 3, self.twin).start()
+
+            @pl.when(self.z + s < self.levels)
+            def _():
+                slot = index_of(self.z + s, x, self.c)
+                self.arrive(slot)
+
+                @pl.when(self.z > 0)
+                def _():
+                    self.copy(slot, 1, self.down).start()
+
+                self.copy(slot, 3, self.twin).start()
+
+    def finish(self):
+        self.copy(self.me, 2, self.side).wait_send()
+
+        @pl.loop(0, self.members // CORES)
+        def _(i):
+            slot = i * CORES + self.c
+            k = i // SIDE
+
+            @pl.when((k <= self.z) & (self.z < self.levels - 1))
+            def _():
+                self.copy(slot, 0, self.up).wait_send()
+
+            @pl.when((k >= self.z) & (self.z > 0))
+            def _():
+                self.copy(slot, 1, self.down).wait_send()
+
+            self.copy(slot, 3, self.twin).wait_send()
+
+
 class Exchange:
-    def __init__(self, src, out, sent, got, members):
+    def __init__(self, src, out, sent, got, members, halved=False):
         self.src, self.out, self.sent, self.got, self.members = src, out, sent, got, members
         self.me = lax.axis_index("grp")
+        self.rows = None
+        if halved:
+            half = src.shape[1] // 2
+            rep = lax.axis_index("rep")
+            odd = rep % 2
+            self.partner = {"rep": rep + 1 - 2 * odd, "grp": self.me}
+            self.rows = pl.ds(pl.multiple_of(odd * half, 16), half)
 
     def copy(self, d):
         to = lax.rem(self.me + d, self.members)
-        return send(self.src.at[to], self.out.at[self.me], self.sent.at[d], self.got.at[d], to)
+        src, dst = self.src.at[to], self.out.at[self.me]
+        if self.rows is not None:
+            src, dst = src.at[self.rows], dst.at[self.rows]
+        return send(src, dst, self.sent.at[d], self.got.at[d], to)
+
+    def to_partner(self):
+        ours = self.out.at[:, self.rows]
+        return send(ours, ours, self.sent.at[0], self.got.at[0], self.partner)
 
     def start(self):
         @pl.loop(1, self.members)
@@ -402,13 +475,13 @@
 
 
 def open_kernel(
-    kva_src, q_src, o_src, router_src, kvb_src, chosen_src, shared_src,
+    kva_src, q_src, o_src, router_src, chosen_src, kvb_ref, sgate_ref, sup_ref,
     normed_ref, down_ref, up_ref, cos_ref, sin_ref, kvg_ref,
     all_kva, all_q, all_o, all_router, all_lat, q_out, kvb_out, chosen_out, shared_out, latent_ref, small_ref,
     *bufs, members, split
 ):
-    stage = bufs[:7]
-    kva, wq, lat_st, qm = bufs[7:11]
+    stage = bufs[:5]
+    kvb_src, shared_src, kva, wq, lat_st, qm = bufs[5:11]
     sems = bufs[11:]
     local, load = sems[26:]
     pairs = [sems[2 * n : 2 * n + 2] for n in range(13)]
@@ -419,17 +492,24 @@
     tokens, width = normed_ref.shape
     g_kva = Gather(kva_src, all_kva, *pairs[0], members, split)
     g_q = Gather(q_src, all_q, *pairs[1], members, split)
-    g_o = Gather(o_src, all_o, *pairs[2], members, split)
+    g_o = Gather(o_src, all_o, *pairs[2], members, o_src.shape[0] // 2 if split else 0)
     g_router = Gather(router_src, all_router, *pairs[3], members)
     g_lat = Gather(lat_st, all_lat, *pairs[4], members)
     e_kvb = Exchange(kvb_src, kvb_out, *pairs[5], members)
     e_chosen = Exchange(chosen_src, chosen_out, *pairs[6], members)
-    e_shared = Exchange(shared_src, shared_out, *pairs[7], members)
+    e_shared = Exchange(shared_src, shared_out, *pairs[7], members, split > 0)
     q_sent, q_got = pairs[8]
-    sources = [kva_src, q_src, o_src, router_src, kvb_src.at[me], chosen_src.at[me], shared_src.at[me]]
-    places = [all_kva, all_q, all_o, all_router, kvb_out, chosen_out, shared_out]
+    sources = [kva_src, q_src, o_src, router_src, chosen_src.at[me]]
+    places = [all_kva, all_q, all_o, all_router, chosen_out]
     into = [pltpu.make_async_copy(a, stage[n], local.at[n]) for n, a in enumerate(sources)]
     out_of = [pltpu.make_async_copy(stage[n], b.at[me], local.at[n]) for n, b in enumerate(places)]
+    cut, cut_out = shared_src.at[me], shared_out.at[me]
+    if split:
+        cut, cut_out = cut.at[e_shared.rows], cut_out.at[e_shared.rows]
+    own_cut = [
+        pltpu.make_async_copy(kvb_src.at[me], kvb_out.at[me], local.at[5]),
+        pltpu.make_async_copy(cut, cut_out, local.at[6]),
+    ]
     own_lat = pltpu.make_async_copy(lat_st, all_lat.at[me], local.at[7])
     own_q = pltpu.make_async_copy(qm.at[me], q_out.at[me], local.at[8])
     loads = [pltpu.make_async_copy(all_kva, kva, load.at[0]), pltpu.make_async_copy(all_q, wq, load.at[1])]
@@ -462,8 +542,15 @@
     meet(members, g_kva.partner if split else None)
     for g in (g_kva, g_q, g_router):
         g.first()
+    e_chosen.start()
+    cols, units = kvb_src.shape[2], shared_src.shape[2] // 2
+    for g in range(members):
+        kvb_src[g] = kvb_ref[:, g * cols : (g + 1) * cols]
+        at = slice(g * units, (g + 1) * units)
+        shared_src[g] = jnp.concatenate([sgate_ref[:, at], sup_ref[:, at]], axis=1)
     e_kvb.start()
-    e_chosen.start()
+    for copy in own_cut:
+        copy.start()
     for a, b in zip(into, out_of):
         a.wait()
         b.start()
@@ -484,7 +571,7 @@
 
         if split:
             g.take_twin_lacked()
-    for copy in out_of:
+    for copy in out_of + own_cut:
         copy.wait()
     for copy in loads:
         copy.start()
@@ -534,6 +621,12 @@
     def _(s):
         events((g_lat, g_o), s, s >= 1)
 
+        @pl.when(s == 1)
+        def _():
+            e_shared.wait()
+            if split:
+                e_shared.to_partner().start()
+
     lacked(g_o, levels - 1)
     for g in (g_lat, g_router, g_o):
 
@@ -552,37 +645,43 @@
         query_from(n).wait_recv()
         query_to(n).wait_send()
 
-    for e in (e_kvb, e_chosen, e_shared):
+    for e in (e_kvb, e_chosen):
         e.wait()
+    if split:
+        e_shared.to_partner().wait()
     own_lat.wait()
     own_q.wait()
 
 
-def opening(kva, q, o, router, kvb, chosen, shared, normed, down, up, cosine, sine, kvg, members, split, collective_id):
+def opening(kva, q, o, router, chosen, kvb, sgate, sup, normed, down, up, cosine, sine, kvg, members, split, collective_id):
     tokens, width = normed.shape
     vmem = pl.BlockSpec(memory_space=pltpu.VMEM)
     anywhere = pl.BlockSpec(memory_space=pl.ANY)
     sem = pltpu.SemaphoreType.DMA
     packed = tokens + tokens // 2
+    cut = (members, kvb.shape[0], kvb.shape[1] // members)
+    slices = (members, sgate.shape[0], 2 * sgate.shape[1] // members)
     grown = lambda a: jax.ShapeDtypeStruct((members, *a.shape), a.dtype)
     same = lambda a: jax.ShapeDtypeStruct(a.shape, a.dtype)
     g_sems = [sem((6, members)), sem((2, members))]
     e_sems = [sem((members,)), sem((members,))]
     return pl.pallas_call(
         functools.partial(open_kernel, members=members, split=split),
-        in_specs=[anywhere] * 7 + [vmem] * 6,
+        in_specs=[anywhere] * 5 + [vmem] * 9,
         out_specs=[anywhere] * 9 + [vmem] * 2,
         out_shape=[
             grown(kva), grown(q), grown(o), grown(router),
             jax.ShapeDtypeStruct((members, tokens, kva.shape[1]), BF16),
             jax.ShapeDtypeStruct((members, packed, NOPE), BF16),
-            same(kvb), same(chosen), same(shared),
+            jax.ShapeDtypeStruct(cut, BF16), same(chosen), jax.ShapeDtypeStruct(slices, BF16),
             jax.ShapeDtypeStruct((tokens, kva.shape[1]), F32),
             jax.ShapeDtypeStruct((tokens, down.shape[1]), BF16),
         ],
         scratch_shapes=[pltpu.VMEM(a.shape, a.dtype) for a in (kva, q, o, router)]
-        + [pltpu.VMEM(a.shape[1:], a.dtype) for a in (kvb, chosen, shared)]
         + [
+            pltpu.VMEM(chosen.shape[1:], F32),
+            pltpu.VMEM(cut, BF16),
+            pltpu.VMEM(slices, BF16),
             pltpu.VMEM((members, *kva.shape), BF16),
             pltpu.VMEM((members, *q.shape), BF16),
             pltpu.VMEM((tokens, kva.shape[1]), BF16),
@@ -596,7 +695,7 @@
         ),
         cost_estimate=pl.CostEstimate(flops=2 * tokens * width * q.shape[1], bytes_accessed=200_000_000, transcendentals=0),
         name="opening",
-    )(kva, q, o, router, kvb, chosen, shared, normed, down, up, cosine, sine, kvg)
+    )(kva, q, o, router, chosen, kvb, sgate, sup, normed, down, up, cosine, sine, kvg)
 
 
 def key_blocks(start, rows, keys, length):
@@ -605,7 +704,10 @@
     return (start + 1) // keys, (end + keys - 1) // keys
 
 
-def attend_kernel(prefix_ref, q_ref, k_ref, v_ref, o_ref, lse_ref, mixed, blocks, sent, got, local, *, members, unit):
+def attend_kernel(
+    prefix_ref, packed, lat_ref, kvb_ref, o_ref, lse_ref, q_ref, k_ref, v_ref, mixed, blocks, sent, got, local,
+    *, members, unit
+):
     me = lax.axis_index("grp")
     tokens = blocks.shape[1]
     block, keys = 2 * tokens, 4 * tokens
@@ -619,6 +721,20 @@
         return send(blocks.at[n], mixed.at[n], sent.at[n], got.at[n], n)
 
     own = pltpu.make_async_copy(blocks.at[me], mixed.at[me], local)
+    half = tokens // 2
+
+    @pl.loop(0, members)
+    def _(b):
+        at = pl.multiple_of(b * tokens, tokens)
+        here = pl.ds(at, tokens)
+        q_ref[here, :NOPE] = packed[b, :tokens, :]
+        q_ref[pl.ds(at, half), NOPE:] = packed[b, tokens:, :ROPE]
+        q_ref[pl.ds(at + half, half), NOPE:] = packed[b, tokens:, ROPE:]
+        made = dot(lat_ref[b, :, :KVR], kvb_ref[...]).astype(BF16)
+        k_ref[here, :NOPE] = made[:, :NOPE]
+        k_ref[here, NOPE:] = lat_ref[b, :, KVR:]
+        v_ref[here, :] = made[:, NOPE:]
+
     meet(members)
 
     @pl.loop(0, turns)
@@ -679,18 +795,21 @@
         block_to(n).wait_send()
 
 
-def attend(prefix, q, k, v, members, collective_id):
-    length = q.shape[0]
-    tokens = length // members
+def attend(prefix, packed, latents, kvb, members, collective_id):
+    tokens = latents.shape[1]
+    length = tokens * members
     vmem = pl.BlockSpec(memory_space=pltpu.VMEM)
     sem = pltpu.SemaphoreType.DMA
     return pl.pallas_call(
         functools.partial(attend_kernel, members=members, unit=QK**-0.5 * math.log2(math.e)),
         in_specs=[pl.BlockSpec(memory_space=pltpu.SMEM), vmem, vmem, vmem],
-        out_specs=[vmem, vmem, pl.BlockSpec(memory_space=pl.ANY)],
+        out_specs=[vmem] * 5 + [pl.BlockSpec(memory_space=pl.ANY)],
         out_shape=[
             jax.ShapeDtypeStruct((length, VD), F32),
             jax.ShapeDtypeStruct((length, 1), F32),
+            jax.ShapeDtypeStruct((length, QK), BF16),
+            jax.ShapeDtypeStruct((length, QK), BF16),
+            jax.ShapeDtypeStruct((length, VD), BF16),
             jax.ShapeDtypeStruct((members, tokens, VD), BF16),
         ],
         scratch_shapes=[pltpu.VMEM((members, tokens, VD), BF16), sem((members,)), sem((members,)), sem],
@@ -701,7 +820,7 @@
             flops=length * length * (QK + VD), bytes_accessed=length * 1000, transcendentals=length * length // 2
         ),
         name="attend",
-    )(prefix, q, k, v)
+    )(prefix, packed, latents, kvb)
 
 
 def attend_back_kernel(
@@ -858,10 +977,10 @@
 
 
 def experts_kernel(
-    x_hbm, prob_hbm, c_hbm, rank_ref, back_ref, gate_hbm, up_hbm, down_hbm, own_hbm, sdown_hbm,
-    part_hbm, eg_hbm, eu_hbm, eo_hbm, sh_hbm, c_out, prob_out,
+    x_hbm, prob_hbm, c_hbm, c2_hbm, rank_ref, back_ref, gate_hbm, up_hbm, down_hbm, own_hbm, sdown_hbm,
+    part_hbm, eg_hbm, eu_hbm, eo_hbm, sh_hbm, c_out, c2_out, prob_out,
     xs, probs, gate, up, down, own, sdown, tail, rows, acts, sacts, part_st, eg_st, eu_st, eo_st, sh_st,
-    c_st, sent, got, e_sent, e_got, c_sent, c_got, load, store,
+    c_st, c2_st, sent, got, e_sent, e_got, c_sent, c_got, c2_sent, c2_got, load, store,
     *, members, slots, tile, wide
 ):
     me = lax.axis_index("grp")
@@ -884,12 +1003,17 @@
                 (down_hbm, down),
                 (sdown_hbm, sdown),
                 (c_hbm, c_st),
+                (c2_hbm, c2_st),
             ]
         )
     ]
     gather = Gather(x_hbm, xs, sent, got, members)
     behind = Gather(c_hbm, c_out, c_sent, c_got, members)
-    own_c = pltpu.make_async_copy(c_st, c_out.at[me], load.at[7])
+    behind2 = SideFirst(c2_hbm, c2_out, c2_sent, c2_got, members)
+    own_c = [
+        pltpu.make_async_copy(c_st, c_out.at[me], load.at[7]),
+        pltpu.make_async_copy(c2_st, c2_out.at[me], load.at[8]),
+    ]
     exchange = Exchange(prob_hbm, probs, e_sent, e_got, members)
     for copy in loads:
         copy.start()
@@ -898,7 +1022,8 @@
     exchange.start()
     for copy in loads:
         copy.wait()
-    own_c.start()
+    for copy in own_c:
+        copy.start()
     tail[:, :half] = gate[:, hidden - half :]
     tail[:, half:] = up[:, hidden - half :]
     gather.pass_on(z)
@@ -960,10 +1085,16 @@
         @pl.when(s == levels - 3)
         def _():
             behind.first()
+            behind2.first()
 
         @pl.when(s >= levels - 2)
         def _():
+            @pl.when(s == levels - 2)
+            def _():
+                behind2.turn()
+
             behind.relay(s - levels + 3)
+            behind2.relay(s - levels + 3)
             behind.pass_on(pick_from(order, z, s - levels + 2))
 
         @pl.loop(0, width // wide)
@@ -997,6 +1128,7 @@
     @pl.loop(2, levels)
     def _(s):
         behind.relay(s + 1)
+        behind2.relay(s + 1)
         behind.pass_on(pick_from(order, z, s))
 
     @pl.loop(levels - 2, levels)
@@ -1007,13 +1139,16 @@
     @pl.loop(0, levels)
     def _(k):
         behind.take_twin(k)
-
-    own_c.wait()
+        behind2.take_twin(k)
+
+    for copy in own_c:
+        copy.wait()
     gather.finish()
     behind.finish()
-
-
-def experts_forward(x, prob, c, rank, back, gate, up, down, own, sdown, slots, members, collective_id):
+    behind2.finish()
+
+
+def experts_forward(x, prob, c, c2, rank, back, gate, up, down, own, sdown, slots, members, collective_id):
     tokens, width = x.shape
     hidden = gate.shape[1]
     group = SIDE * CORES
@@ -1032,10 +1167,10 @@
     ]
     return pl.pallas_call(
         functools.partial(experts_kernel, members=members, slots=slots, tile=tile, wide=512),
-        in_specs=[anywhere, anywhere, anywhere, vmem, vmem] + [anywhere] * 5,
-        out_specs=[anywhere] * 6 + [vmem],
+        in_specs=[anywhere] * 4 + [vmem, vmem] + [anywhere] * 5,
+        out_specs=[anywhere] * 7 + [vmem],
         out_shape=[jax.ShapeDtypeStruct(s, BF16) for s in shapes]
-        + [jax.ShapeDtypeStruct((members, *c.shape), BF16)]
+        + [jax.ShapeDtypeStruct((members, *a.shape), BF16) for a in (c, c2)]
         + [jax.ShapeDtypeStruct(prob.shape, F32)],
         scratch_shapes=[
             pltpu.VMEM((members, tokens, width), BF16),
@@ -1051,9 +1186,10 @@
             pltpu.VMEM((group, tokens, own.shape[1] // 2), BF16),
         ]
         + [pltpu.VMEM((2, *s[1:]), BF16) for s in shapes]
-        + [pltpu.VMEM(c.shape, BF16)]
+        + [pltpu.VMEM(c.shape, BF16), pltpu.VMEM(c2.shape, BF16)]
         + [sem((6, members)), sem((2, members)), sem((members,)), sem((members,))]
-        + [sem((6, members)), sem((2, members)), sem((8,)), sem((2, 5))],
+        + [sem((6, members)), sem((2, members))] * 2
+        + [sem((9,)), sem((2, 5))],
         compiler_params=pltpu.CompilerParams(
             collective_id=collective_id, has_side_effects=True, vmem_limit_bytes=63 * 1024 * 1024
         ),
@@ -1061,11 +1197,11 @@
             flops=12 * members * slots * width * hidden, bytes_accessed=60_000_000, transcendentals=0
         ),
         name="experts_forward",
-    )(x, prob, c, rank, back, gate, up, down, own, sdown)
+    )(x, prob, c, c2, rank, back, gate, up, down, own, sdown)
 
 
 def experts_back_kernel(
-    c_hbm, c2_hbm, rank_ref, back_ref, prob_ref, eg_hbm, eu_hbm, eo_hbm, sh_hbm, gate_hbm, up_hbm, down_hbm, own_hbm, sdown_hbm,
+    c_hbm, c2_hbm, c3_hbm, rank_ref, back_ref, prob_ref, eg_hbm, eu_hbm, eo_hbm, sh_hbm, gate_hbm, up_hbm, down_hbm, own_hbm, sdown_hbm,
     out, dg_out,
     part, cs, eg, eu, eo, sh, gate, up, down, own, sdown, rows, d_gate, d_up, dg_st, dg_in,
     *sems, members, slots, tile, wide
@@ -1087,9 +1223,9 @@
         k = pick_from(order, z, s)
         return [
             pltpu.make_async_copy(
-                a.at[k], cs.at[s % 2, :, :, pl.ds(h * (width // 2), width // 2)], fetch.at[4 + s % 2 * 2 + h]
+                a.at[k], cs.at[s % 2, :, :, pl.ds(at, a.shape[3])], fetch.at[4 + s % 2 * 3 + h]
             )
-            for h, a in enumerate([c_hbm, c2_hbm])
+            for h, (a, at) in enumerate([(c_hbm, 0), (c2_hbm, width // 2), (c3_hbm, width // 2 + c2_hbm.shape[3])])
         ]
 
     def kept(s):
@@ -1215,7 +1351,7 @@
 
 
 def experts_backward(cs, rank, back, prob, kept, gate, up, down, own, sdown, slots, members, collective_id):
-    tokens, width = cs[0].shape[1], cs[0].shape[2] * 2
+    tokens, width = cs[0].shape[1], sum(c.shape[2] for c in cs)
     hidden = gate.shape[1]
     group = SIDE * CORES
     levels = members // group
@@ -1226,7 +1362,7 @@
     eg, eu, eo, sh = kept
     return pl.pallas_call(
         functools.partial(experts_back_kernel, members=members, slots=slots, tile=256, wide=512),
-        in_specs=[anywhere, anywhere, vmem, vmem, vmem] + [anywhere] * 9,
+        in_specs=[anywhere] * 3 + [vmem] * 3 + [anywhere] * 9,
         out_specs=[vmem, vmem],
         out_shape=[
             jax.ShapeDtypeStruct((tokens, width), BF16),
@@ -1251,7 +1387,7 @@
             pltpu.VMEM((members, 8, tokens), F32),
         ]
         + Reduce.scratch(members, tokens, width, BF16)
-        + [sem((members,)), sem((members,)), sem((5,)), sem((8,))],
+        + [sem((members,)), sem((members,)), sem((5,)), sem((10,))],
         compiler_params=pltpu.CompilerParams(
             collective_id=collective_id, has_side_effects=True, vmem_limit_bytes=67_043_328
         ),
@@ -1313,12 +1449,12 @@
 def finish_kernel(
     part, o_src, dq_ref, cos_ref, sin_ref, q_hbm, kva_ref, up_ref, down_ref, small_ref, normed_ref, latent_ref, kvg_ref,
     x_ref, xg_ref, dmid_ref, name_ref,
-    out, q_out, o_out,
+    out, gqd, gqu, god, gou,
     *bufs, members, sequences
 ):
     twin_in, side_in, line_in = bufs[:3]
-    o_in, o_common, q_parts, d_query, wq, dn, d_lat, d_latent, ds_ref = bufs[11:20]
-    o_sent, o_got, b_sent, b_got, w_sent, w_got, local = bufs[20:]
+    o_in, o_common, q_parts, d_query, wq, dn, d_lat, d_latent, ds_ref, q_out, o_out = bufs[11:22]
+    o_sent, o_got, b_sent, b_got, w_sent, w_got, local = bufs[22:]
     reduce = Reduce(part, twin_in, side_in, line_in, bufs[3:11], members)
     exchange = Exchange(o_src, o_in, o_sent, o_got, members)
     spread = Spread(q_parts, q_out, o_common, o_out, (b_sent, b_got, w_sent, w_got), members, sequences)
@@ -1328,10 +1464,6 @@
     tokens, width = x_ref.shape
     tile = 256
     load = pltpu.make_async_copy(q_hbm, wq, local.at[0])
-    own = [
-        pltpu.make_async_copy(q_parts.at[me], q_out.at[mine, me], local.at[1]),
-        pltpu.make_async_copy(o_common, o_out.at[mine], local.at[2]),
-    ]
     load.start()
     spread.meet()
 
@@ -1365,14 +1497,14 @@
             [grad_down[:, g * rows : (g + 1) * rows], grad_up[:, first : first + 2 * QK]], axis=1
         ).astype(BF16)
     spread.start_blocks()
-    own[0].start()
+    q_out[mine, me] = q_parts[me]
     exchange.wait()
     total = jnp.zeros(o_in.shape[1:], F32)
     for g in range(members):
         total = total + o_in[g].astype(F32)
     o_common[...] = jnp.concatenate([total, name_ref[...]], axis=1)
     spread.start_common()
-    own[1].start()
+    o_out[mine] = o_common[...]
     load.wait()
     every = width // tile // (levels - 1)
 
@@ -1400,11 +1532,26 @@
     out[...] = (dmid_ref[...] + norm_back(x_ref[...].astype(F32), xg_ref[...], dn[...])).astype(BF16)
     reduce.finish()
     spread.wait()
-    for copy in own:
-        copy.wait()
-
-
-def finish(part, o_parts, dq, cosine, sine, all_q, kva, up, down, small, normed, latent, kvg, x, xg, dmid, name, sequences, collective_id):
+    o_cols = gou.shape[2]
+    shares = []
+    for r in range(sequences):
+        q_share = lax.fori_loop(
+            0, members, lambda g, total: total + q_out[r, g].astype(F32), jnp.zeros(q_out.shape[2:], F32)
+        )
+        up_share = jnp.where(me % 2 == 0, q_share[:, rows : rows + QK], q_share[:, rows + QK :])
+        o_share = o_out[r]
+        number = o_share[:, 2 * o_cols : 2 * o_cols + 1]
+        shares.append((number, q_share[:, :rows], up_share, o_share[:, :o_cols], o_share[:, o_cols : 2 * o_cols]))
+    for a in range(gqd.shape[0]):
+        sums = [jnp.zeros(part.shape, F32) for part in shares[0][1:]]
+        for number, *parts in shares:
+            chosen = number == a
+            sums = [total + jnp.where(chosen, part, 0.0) for total, part in zip(sums, parts)]
+        for ref, total in zip((gqd, gqu, god, gou), sums):
+            ref[a] = total
+
+
+def finish(part, o_parts, dq, cosine, sine, all_q, kva, up, down, small, normed, latent, kvg, x, xg, dmid, name, adapters, sequences, collective_id):
     members, tokens, c = part.shape
     width = x.shape[1]
     rank = o_parts.shape[1]
@@ -1416,11 +1563,11 @@
     return pl.pallas_call(
         functools.partial(finish_kernel, members=members, sequences=sequences),
         in_specs=[vmem] * 5 + [anywhere] + [vmem] * 11,
-        out_specs=[vmem, anywhere, anywhere],
-        out_shape=[
-            jax.ShapeDtypeStruct((tokens, width), BF16),
-            jax.ShapeDtypeStruct((sequences, members, rank, share), BF16),
-            jax.ShapeDtypeStruct((sequences, *common), F32),
+        out_specs=[vmem] * 5,
+        out_shape=[jax.ShapeDtypeStruct((tokens, width), BF16)]
+        + [
+            jax.ShapeDtypeStruct((adapters, rank, n), F32)
+            for n in (width // members, QK, o_parts.shape[2] // 2, o_parts.shape[2] // 2)
         ],
         scratch_shapes=Reduce.scratch(members, tokens, c, BF16)
         + [
@@ -1433,6 +1580,8 @@
             pltpu.VMEM((tokens, c), BF16),
             pltpu.VMEM((tokens, c), BF16),
             pltpu.VMEM((tokens, rank), BF16),
+            pltpu.VMEM((sequences, members, rank, share), BF16),
+            pltpu.VMEM((sequences, *common), F32),
         ]
         + [sem((n,)) for n in (members,) * 2 + (members * sequences,) * 2 + (sequences,) * 2 + (3,)],
         compiler_params=pltpu.CompilerParams(
@@ -1445,18 +1594,6 @@
 
 def by_owner(gradient, members):
     return gradient.astype(BF16).reshape(gradient.shape[0], members, -1).transpose(1, 0, 2)
-
-
-def pack(v):
-    half = v.shape[1] // 2
-    rope = jnp.concatenate([v[:, :half, NOPE:], v[:, half:, NOPE:]], axis=-1)
-    return jnp.concatenate([v[:, :, :NOPE], rope], axis=1)
-
-
-def unpack(v):
-    rows = v.shape[1] * 2 // 3
-    rope = jnp.concatenate([v[:, rows:, :ROPE], v[:, rows:, ROPE:]], axis=1)
-    return jnp.concatenate([v[:, :rows], rope], axis=-1)
 
 
 def per_device(
@@ -1506,9 +1643,6 @@
     )
     sequences = lax.axis_size("rep")
     split = w_q.shape[0] * 3 // 128 * 16 if sequences % 2 == 0 else 0
-    hidden_slice = shared_down.shape[0]
-    shared = jnp.stack([shared_gate, shared_up], axis=1)
-    shared = shared.reshape(shared.shape[0], 2, members, hidden_slice).transpose(2, 0, 1, 3)
     positions = me * tokens + jnp.arange(tokens, dtype=jnp.int32)
     cosine, sine = angles(positions, ROPE)
     normed = root_norm(inputs, attn_gain).astype(BF16)
@@ -1521,9 +1655,10 @@
         w_q,
         w_o,
         w_router,
-        w_kvb.reshape(w_kvb.shape[0], members, -1).transpose(1, 0, 2),
         jnp.broadcast_to(chosen_by.T[:, None, :], (experts, 8, tokens)),
-        shared.reshape(members, -1, 2 * hidden_slice),
+        w_kvb,
+        shared_gate,
+        shared_up,
         normed,
         qa_down,
         qa_up,
@@ -1537,13 +1672,8 @@
     full_kva, full_o, full_router = (v.reshape(-1, v.shape[2]) for v in (all_kva, all_o, all_router))
     own_kvb = kvb_parts.reshape(KVR, -1)
     own_shared = own_shared.reshape(width, -1)
-    all_latent = all_latent.reshape(length, KVR + ROPE)
-    q_head = unpack(q_packed).reshape(length, QK)
-    q_head, c_first = lax.optimization_barrier((q_head, cotangent[:, : width // 2]))
-    expanded = dot(all_latent[:, :KVR], own_kvb).astype(BF16)
-    k_head = jnp.concatenate([expanded[:, :NOPE], all_latent[:, KVR:]], axis=-1)
-    v_head = expanded[:, NOPE:]
-    mixture, lse, mixed_parts = attend(prefix_len, q_head, k_head, v_head, members, 3)
+    q_packed, c_first = lax.optimization_barrier((q_packed, cotangent[:, : width // 2]))
+    mixture, lse, q_head, k_head, v_head, mixed_parts = attend(prefix_len, q_packed, all_latent, own_kvb, members, 3)
     mixed = mixed_parts.transpose(1, 0, 2).reshape(tokens, H * VD)
     o_small = dot(mixed, oa_down).astype(BF16)
     middle = inputs + dot(mixed, full_o) + dot(o_small, oa_up)
@@ -1560,13 +1690,13 @@
     rank = jnp.broadcast_to(rank[:, None, :], (members, 8, tokens))
     weights = (expert_gate[0], expert_up_weight[0], expert_down[0], own_shared, shared_down)
     prob_blocks = jnp.broadcast_to(route_probs.T[:, None, :], (experts, 8, tokens))
-    partial, kept_gate, kept_up, kept_out, kept_shared, second_c, prob_parts = experts_forward(
-        ffn_in, prob_blocks, cotangent[:, half:], rank, back, *weights, slots, members, 4
+    partial, kept_gate, kept_up, kept_out, kept_shared, second_c, third_c, prob_parts = experts_forward(
+        ffn_in, prob_blocks, cotangent[:, half : half + half // 2], cotangent[:, half + half // 2 :], rank, back, *weights, slots, members, 4
     )
     kept = (kept_gate, kept_up, kept_out, kept_shared)
     ffn_out = scatter_sum(partial.reshape(length, width))
     d_own, d_route = experts_backward(
-        (first_c, second_c), rank, back, prob_parts, kept, *weights, slots, members, 5
+        (first_c, second_c, third_c), rank, back, prob_parts, kept, *weights, slots, members, 5
     )
     d_route = d_route[:, 0].T
     d_logits = (
@@ -1593,7 +1723,7 @@
     )
     o_parts = jnp.concatenate([by_owner(g, members) for g in (grad_odown, grad_oup)], axis=-1)
     name = jnp.broadcast_to(adapter.astype(F32), (qa_up.shape[0], 128))
-    grad_inputs, q_shares, o_shares = finish(
+    grad_inputs, *outs = finish(
         d_latents,
         o_parts,
         d_query,
@@ -1611,21 +1741,12 @@
         attn_gain[None],
         d_middle,
         name,
+        q_down.shape[0],
         sequences,
         7,
     )
     ffn_out, _ = lax.optimization_barrier((ffn_out, d_query))
     output = (middle + ffn_out.astype(F32)).astype(BF16)
-    numbers = o_shares[:, 0, -1].astype(jnp.int32)
-    q_share = jnp.sum(q_shares.astype(F32), axis=1)
-    rows = width // members
-    q_up_share = lax.dynamic_slice_in_dim(q_share[..., rows:], me % 2 * QK, QK, 2)
-    shares = jnp.concatenate([q_share[..., :rows], q_up_share, o_shares[:, :, :-128]], axis=-1)
-    selector = (jnp.arange(q_down.shape[0], dtype=jnp.int32)[:, None] == numbers[None, :]).astype(F32)
-    summed = jnp.sum(selector[:, :, None, None] * shares[None], axis=1)
-    sizes = [rows, QK, rows, rows]
-    ends = [sum(sizes[: n + 1]) for n in range(4)]
-    outs = [summed[:, :, e - s : e] for e, s in zip(ends, sizes)]
     return (
         output[None],
         grad_inputs[None],

time: 726 us -> 720 us (level)
    pallas_call x1, Pallas kernels: 193 us -> 174 us  [opening(): pl.pallas_call(functools.partial(open_kernel, members=members, split=spli...]
    pallas_call x1, Pallas kernels: 32.8 us -> 49 us  [attend(): pl.pallas_call(functools.partial(attend_kernel, members=members, unit=QK...]
    unnamed x100 -> x112, local copies, waits for them, and re-layouts: 12.1 us -> 16 us
  transfers between devices with their start and end apart: 2 -> 2, of which waited for: 0 -> 0; matrix products, arithmetic and copies ran while one was open for 5% -> 4% of each run, Pallas kernels for 63% -> 66%
where the time goes in v8:
time: 720 us; the launch traced here: 719 us
  Pallas kernels  649 us (90%)
  local copies, waits for them, and re-layouts  25.7 us (4%)
  matrix products  16.6 us (2%)
  between operations  16.4 us (2%)
  other arithmetic  10.4 us (1%)
    pallas_call x1, Pallas kernels, opening(): pl.pallas_call(functools.partial(open_kernel, members=members, split=spli...  174 us
    pallas_call x1, Pallas kernels, experts_backward(): pl.pallas_call(functools.partial(experts_back_kernel, members=members, sl...  173 us
    pallas_call x1, Pallas kernels, experts_forward(): pl.pallas_call(functools.partial(experts_kernel, members=members, slots=s...  138 us
    pallas_call x1, Pallas kernels, attend_back(): pl.pallas_call(functools.partial(attend_back_kernel, members=members, fac...  61.8 us
    pallas_call x1, Pallas kernels, finish(): pl.pallas_call(functools.partial(finish_kernel, members=members, sequence...  53.4 us
    pallas_call x1, Pallas kernels, attend(): pl.pallas_call(functools.partial(attend_kernel, members=members, unit=QK...  49 us
    unnamed x112, local copies, waits for them, and re-layouts  16 us
  transfers between devices with their start and end apart: 2, of which 0 were waited for; matrix products, arithmetic and copies ran while one was open for 4% of the time, Pallas kernels for 66%

profile of v8, /device:TPU:0, one launch (start us, length us, event | category | flops | bytes accessed | tf_op | source)
XLA Modules:
  0.0 718.5 jit_solution(294768924622868843)
XLA Ops:
  7.2 1.1 copy.57.kva_src
  8.3 0.8 copy.58.router_src
  9.1 0.7 copy.97
  9.8 1.4 fusion.3
  11.9 0.8 constant_dynamic-slice_fusion
  13.0 1.0 dynamic-slice_bitcast_fusion.up_ref
  14.1 1.9 slice.20
  16.0 2.3 fusion.5.normed_ref
  19.0 1.1 copy-done.16
  20.1 0.9 copy-done.18
  21.0 173.6 %opening.1 = (bf16[16,128,576]{2,1,0:T(8,128)(2,1)}, bf16[16,128,3072]{2,1,0:T(8,128)(2,1)}, bf16[16,128,2048]{2,1,0:T(8,128)(2,1)}, bf16[16,128,16]{2,1,0:T(8,1...) custom-call(bf16[128,576]{1,0:T(8,128)(2,1)S(1)} %copy.57.kva_src, ...), custom_call_target="tpu_custom_call" | custom-call | flops 2415919104 | bytes 200000000 | tf_op jit(solution)/shard_map/opening/pallas_call | solution.py:668
  194.7 0.8 copy-done.7
  195.4 0.6 copy-done.11
  196.0 0.7 copy-done.19
  198.1 1.7 copy.60.back_ref
  199.9 2.1 copy-done.22
  202.0 49.0 %attend.1 = (f32[3072,128]{1,0:T(8,128)S(1)}, f32[3072,1]{1,0:T(8,128)S(1)}, bf16[3072,192]{1,0:T(8,128)(2,1)S(1)}, bf16[3072,192]{1,0:T(8,128)(2,1)S(1)}, bf16[...) custom-call(s32[1]{0:T(128)S(6)} %copy.103.prefix_ref, bf16[16,288,128]{2,1,0:T(8,128)(2,1)S(1)} %copy-done.23, ...), custom_call_target="tpu_custom_call" | custom-call | flops 3019898880 | bytes 3072000 | tf_op jit(solution)/shard_map/attend/pallas_call | solution.py:803
  251.1 1.2 convolution_convert_fusion.3
  252.4 1.8 fusion.1
  254.2 1.3 multiply_reduce_fusion.1
  255.6 0.6 multiply_multiply_fusion
  256.9 0.5 copy-done.35
  257.4 0.8 fusion.43
  258.2 0.7 broadcast_in_dim.24.prob_hbm
  258.9 0.7 broadcast_in_dim.26.rank_ref
  259.5 138.5 %experts_forward.1 = (bf16[4,4,192,2048]{3,2,1,0:T(8,128)(2,1)}, bf16[4,384,1408]{2,1,0:T(8,128)(2,1)}, bf16[4,384,1408]{2,1,0:T(8,128)(2,1)}, bf16[4,384,2048]{...) custom-call(bf16[192,2048]{1,0:T(8,128)(2,1)} %copy-done.34, ...), custom_call_target="tpu_custom_call" | custom-call | flops 53150220288 | bytes 60000000 | tf_op jit(solution)/shard_map/experts_forward/pallas_call | solution.py:1168
  398.1 1.4 copy-done.3
  399.4 1.1 reduce
  400.5 172.9 %experts_backward.1 = (bf16[192,2048]{1,0:T(8,128)(2,1)}, f32[16,8,192]{2,1,0:T(8,128)}) custom-call(bf16[4,4,192,1024]{3,2,1,0:T(8,128)(2,1)} %bitcast.147, bf16[4,4,192,512]{3,2,1,0:T(8,128)(2,1)} %bitcast.154, bf16[4,4,192,512]{3,2,1,0:T(8,128)(2,1)} %bitcast.155, f32[16,8,192]{2,1,0:T(8,128)} %broadcast_in_dim.26.rank_ref, f32[16,192,1]{2,1,0:T(8,128)} %copy.60.back_ref, ...), custom_call_target="tpu_custom_call" | custom-call | flops 53150220288 | bytes 60000000 | tf_op jit(solution)/shard_map/experts_backward/pallas_call | solution.py:1363
  573.4 0.9 slice.19
  574.4 0.7 fusion.24
  575.1 2.5 multiply_reduce_fusion
  577.7 0.5 subtract_add_fusion.dmid_ref
  578.2 1.2 convolution_convert_fusion.2
  579.5 6.3 fusion.39
  585.8 1.2 fusion.6
  587.5 0.6 copy-done.6
  588.4 0.7 pad_maximum_fusion.o_src
  589.1 61.8 %attend_back.1 = (bf16[16,192,576]{2,1,0:T(8,128)(2,1)}, bf16[16,288,128]{2,1,0:T(8,128)(2,1)S(1)}) custom-call(s32[1]{0:T(128)S(6)} %copy.103.prefix_ref, bf16[3072,192]{1,0:T(8,128)(2,1)} %copy-done.25, bf16[3072,192]{1,0:T(8,128)(2,1)} %copy-done.26, bf16[3072,128]{1,0:T(8,128)(2,1)S(1)} %copy-done.28, f32[3072,128]{1,0:T(8,128)} %copy-done.24, ...), custom_call_target="tpu_custom_call" | custom-call | flops 7851737088 | bytes 6144000 | tf_op jit(solution)/shard_map/attend_back/pallas_call | solution.py:935
  650.9 1.0 copy-done.4
  651.9 0.6 broadcast_in_dim.30.name_ref
  652.5 53.4 %finish.1 = (bf16[192,2048]{1,0:T(8,128)(2,1)}, f32[8,16,128]{2,1,0:T(8,128)}, f32[8,16,192]{2,1,0:T(8,128)}, f32[8,16,128]{2,1,0:T(8,128)}, f32[8,16,128]{2,1,0:T(8,128)}) custom-call(bf16[16,192,576]{2,1,0:T(8,128)(2,1)} %get-tuple-element.70.part, bf16[16,16,256]{2,1,0:T(8,128)(2,1)} %pad_maximum_fusion.o_src, bf16[16,288,128]{2,1,0:T(8,128)(2,1)} %copy-done.4, ...), custom_call_target="tpu_custom_call" | custom-call | flops 4831838208 | bytes 40000000 | tf_op jit(solution)/shard_map/finish/pallas_call | solution.py:1563
  706.0 2.3 fusion.9
  708.2 0.9 copy.105
  709.1 0.6 copy.106
  709.8 0.7 copy.107
  710.4 0.6 copy.108
  711.1 0.6 copy.109
  (120 shorter events, 2.8 us)
Async XLA Ops:
  7.2 8.9 %copy-start.43 = (f32[2048]{0:T(1024)S(1)}, f32[2048]{0:T(1024)}, u32[]{:S(2)}) copy-start(f32[2048]{0:T(1024)} %param.28) | copy-start | bytes 24580
  7.2 393.3 %all-gather.2.cloned.1.call-start = ((), (), s32[]{:S(2)}) async-start(), calls=%async_computation.2 | async-start | bytes 6684672 | tf_op jit(solution)/shard_map/all_gather | solution.py:461
  13.0 5.9 copy-start
  14.0 4.9 copy-start.8
  14.0 4.9 copy-start.13
  14.0 4.9 copy-start.14
  14.1 4.9 copy-start.15
  14.1 4.9 copy-start.17
  18.8 175.8 %copy-start.9 = (f32[192,64]{1,0:T(8,128)}, f32[192,64]{1,0:T(8,128)S(1)}, u32[]{:S(2)}) copy-start(f32[192,64]{1,0:T(8,128)S(1)} %get-tuple-element.93.cos_ref) | copy-start | bytes 147460
  18.9 175.8 %copy-start.10 = (f32[192,64]{1,0:T(8,128)}, f32[192,64]{1,0:T(8,128)S(1)}, u32[]{:S(2)}) copy-start(f32[192,64]{1,0:T(8,128)S(1)} %get-tuple-element.94.sin_ref) | copy-start | bytes 147460
  18.9 1.1 copy-start.16
  196.8 59.7 %copy-start.1 = (bf16[16,128,16]{2,1,0:T(8,128)(2,1)}, bf16[16,128,16]{2,1,0:T(8,128)(2,1)S(1)}, u32[]{:S(2)}) copy-start(bf16[16,128,16]{2,1,0:T(8,128)(2,1)S(1)} %get-tuple-element.49) | copy-start | bytes 196612
  196.8 3.1 copy-start.23
  196.8 3.1 copy-start.20
  196.8 509.2 %reduce-scatter.2.cloned.1.call-start = ((), (), s32[]{:S(2)}) async-start(), calls=%async_computation.1 | async-start | bytes 13369344 | tf_op jit(solution)/shard_map/reduce_scatter | solution.py:465
  199.9 2.1 copy-start.22
  202.0 50.3 %copy-start.32 = (bf16[16,128,2048]{2,1,0:T(8,128)(2,1)S(1)}, bf16[16,128,2048]{2,1,0:T(8,128)(2,1)}, u32[]{:S(2)}) copy-start(bf16[16,128,2048]{2,1,0:T(8,128)(2,1)} %get-tuple-element.48) | copy-start | bytes 25165828
  202.0 50.3 %copy-start.33 = (bf16[1,192,2048]{2,1,0:T(8,128)(2,1)S(1)}, bf16[1,192,2048]{2,1,0:T(8,128)(2,1)}, u32[]{:S(2)}) copy-start(bf16[1,192,2048]{2,1,0:T(8,128)(2,1)} %param.23) | copy-start | bytes 2359300
  251.0 3.1 copy-start.2
  251.0 3.1 copy-start.5
  251.1 3.1 copy-start.24
  251.1 3.1 copy-start.25
  251.1 3.1 copy-start.26
  251.1 3.1 copy-start.27
  252.3 1.9 copy-start.45
  254.2 2.0 copy-start.44
  255.6 1.2 copy-start.29
  256.2 1.2 copy-start.35
  256.4 3.1 copy-start.34
  256.8 1.4 copy-start.38
  256.9 2.7 copy-start.47
  256.9 2.7 copy-start.48
  398.0 1.4 copy-start.3
  575.1 2.6 copy-start.30
  575.1 2.6 copy-start.36
  575.1 2.6 copy-start.50
  575.1 2.6 copy-start.51
  578.2 9.0 %copy-start.31 = (f32[192,2048]{1,0:T(8,128)}, f32[192,2048]{1,0:T(8,128)S(1)}, u32[]{:S(2)}) copy-start(f32[192,2048]{1,0:T(8,128)S(1)} %subtract_add_fusion.dmid_ref) | copy-start | bytes 4718596
  585.8 1.5 copy-start.46
  587.0 1.1 copy-start.6
  587.3 1.8 copy-start.12
  587.3 1.8 copy-start.21
  587.3 1.8 copy-start.28
  705.9 2.3 copy-start.37
  705.9 3.2 copy-start.42
  708.2 1.5 copy-start.39
  708.2 2.2 copy-start.41
  708.2 2.8 copy-start.40
  (6 other events, 4.7 us)
Sparse Core Ops, SparseCore 0:
  196.9 90.1 all-gather.1
  398.2 174.6 reduce-scatter.1

commit v9 on v8

--- a/solution.py
+++ b/solution.py
@@ -824,8 +824,8 @@
 
 
 def attend_back_kernel(
-    prefix_ref, q_ref, k_ref, v_ref, o_ref, lse_ref, d_hbm, kvb_ref, part_ref, dq_out,
-    ds_in, blocks, dk, dv, sent, got, q_sent, q_got, local, local2,
+    prefix_ref, q_ref, k_ref, v_ref, o_ref, lse_ref, d_ref, small_ref, down_ref, wo_hbm, kvb_ref, part_ref, dq_out,
+    d_src, wo, ds_in, blocks, dk, dv, sent, got, q_sent, q_got, local, local2,
     *, members, factor, unit
 ):
     me = lax.axis_index("grp")
@@ -833,8 +833,8 @@
     block, keys = 2 * tokens, 4 * tokens
     turns = members // 2
     prefix = prefix_ref[0]
-    exchange = Exchange(d_hbm, ds_in, sent, got, members)
-    into = pltpu.make_async_copy(d_hbm.at[me], ds_in.at[me], local)
+    exchange = Exchange(d_src, ds_in, sent, got, members)
+    load = pltpu.make_async_copy(wo_hbm, wo, local)
     own = pltpu.make_async_copy(blocks.at[me], dq_out.at[me], local2)
 
     def block_to(n):
@@ -843,12 +843,29 @@
     def from_device(n):
         return send(blocks.at[n], dq_out.at[n], q_sent.at[n], q_got.at[n], n)
 
-    into.start()
-    meet(members)
-    exchange.start()
+    load.start()
     dk[...] = jnp.zeros_like(dk)
     dv[...] = jnp.zeros_like(dv)
-    into.wait()
+    meet(members)
+    load.wait()
+
+    @pl.loop(0, turns)
+    def _(n):
+        pair = lax.rem(me // 2 - n + turns, turns)
+        at = pl.ds(pl.multiple_of(pair * 2 * VD, 2 * VD), 2 * VD)
+        both = (dot_t(d_ref[...], wo[at, :]) + dot_t(small_ref[...], down_ref[at, :])).astype(BF16)
+        for t in range(2):
+            to = 2 * pair + t
+            d_src[to] = both[:, t * VD : (t + 1) * VD]
+
+            @pl.when(to == me)
+            def _():
+                ds_in[me] = both[:, t * VD : (t + 1) * VD]
+
+            @pl.when(to != me)
+            def _():
+                exchange.copy(lax.rem(to - me + members, members)).start()
+
 
     @pl.loop(0, turns)
     def _(n):
@@ -924,7 +941,7 @@
         exchange.copy(d).wait_send()
 
 
-def attend_back(prefix, q, k, v, o, lse, d, kvb, members, collective_id):
+def attend_back(prefix, q, k, v, o, lse, d, small, down, wo, kvb, members, collective_id):
     length = q.shape[0]
     tokens = length // members
     vmem = pl.BlockSpec(memory_space=pltpu.VMEM)
@@ -934,13 +951,15 @@
     packed = tokens + tokens // 2
     return pl.pallas_call(
         functools.partial(attend_back_kernel, members=members, factor=factor, unit=factor * math.log2(math.e)),
-        in_specs=[pl.BlockSpec(memory_space=pltpu.SMEM)] + [vmem] * 5 + [anywhere, vmem],
+        in_specs=[pl.BlockSpec(memory_space=pltpu.SMEM)] + [vmem] * 8 + [anywhere, vmem],
         out_specs=[vmem, anywhere],
         out_shape=[
             jax.ShapeDtypeStruct((members, tokens, KVR + ROPE), BF16),
             jax.ShapeDtypeStruct((members, packed, NOPE), BF16),
         ],
         scratch_shapes=[
+            pltpu.VMEM((members, tokens, VD), BF16),
+            pltpu.VMEM(wo.shape, BF16),
             pltpu.VMEM((members, tokens, VD), BF16),
             pltpu.VMEM((members, packed, NOPE), BF16),
             pltpu.VMEM((length, QK), F32),
@@ -954,7 +973,7 @@
             flops=length * length * (3 * QK + 2 * VD), bytes_accessed=length * 2000, transcendentals=length * length // 2
         ),
         name="attend_back",
-    )(prefix, q, k, v, o, lse, d, kvb)
+    )(prefix, q, k, v, o, lse, d, small, down, wo, kvb)
 
 
 def silu_parts(v):
@@ -1708,7 +1727,6 @@
     grad_oup = t_dot(o_small, d_attn)
     d_osmall = dot_t(d_attn, oa_up).astype(BF16)
     grad_odown = t_dot(d_osmall, mixed)
-    d_mixed = (dot_t(d_attn, full_o) + dot_t(d_osmall, oa_down)).astype(BF16)
     d_latents, d_query = attend_back(
         prefix_len,
         q_head,
@@ -1716,7 +1734,10 @@
         v_head,
         mixture,
         lse.reshape(members // 2, 1, 2 * tokens),
-        d_mixed.reshape(tokens, H, VD).transpose(1, 0, 2),
+        d_attn,
+        d_osmall,
+        oa_down,
+        full_o,
         own_kvb,
         members,
         6,

time: 720 us -> 722 us (level)
  Pallas kernels: 649 us -> 658 us
  matrix products: 16.6 us -> 8.23 us
    pallas_call x1, Pallas kernels: 61.8 us -> 71.5 us  [attend_back(): pl.pallas_call(functools.partial(attend_back_kernel, members=members, fac...]
    dot_general x4 -> x2, matrix products: 11.3 us -> 3.85 us  [dot_t(): lax.dot_general(former, latter, (((1,), (1,)), ((), ())), preferred_eleme...]
    unnamed x112 -> x114, local copies, waits for them, and re-layouts: 16 us -> 15.4 us
  transfers between devices with their start and end apart: 2 -> 2, of which waited for: 0 -> 0; matrix products, arithmetic and copies ran while one was open for 4% -> 3% of each run, Pallas kernels for 66% -> 67%
where the time goes in v9:
time: 722 us; the launch traced here: 721 us
  Pallas kernels  658 us (91%)
  local copies, waits for them, and re-layouts  26.5 us (4%)
  between operations  16.3 us (2%)
  other arithmetic  11.5 us (2%)
  matrix products  8.23 us (1%)
    pallas_call x1, Pallas kernels, opening(): pl.pallas_call(functools.partial(open_kernel, members=members, split=spli...  174 us
    pallas_call x1, Pallas kernels, experts_backward(): pl.pallas_call(functools.partial(experts_back_kernel, members=members, sl...  173 us
    pallas_call x1, Pallas kernels, experts_forward(): pl.pallas_call(functools.partial(experts_kernel, members=members, slots=s...  139 us
    pallas_call x1, Pallas kernels, attend_back(): pl.pallas_call(functools.partial(attend_back_kernel, members=members, fac...  71.5 us
    pallas_call x1, Pallas kernels, finish(): pl.pallas_call(functools.partial(finish_kernel, members=members, sequence...  52.4 us
    pallas_call x1, Pallas kernels, attend(): pl.pallas_call(functools.partial(attend_kernel, members=members, unit=QK...  49 us
    unnamed x114, local copies, waits for them, and re-layouts  15.4 us
  transfers between devices with their start and end apart: 2, of which 0 were waited for; matrix products, arithmetic and copies ran while one was open for 3% of the time, Pallas kernels for 67%

profile of v9, /device:TPU:0, one launch (start us, length us, event | category | flops | bytes accessed | tf_op | source)
XLA Modules:
  0.0 720.7 jit_solution(8857891804348089446)
XLA Ops:
  7.2 1.1 copy.61.kva_src
  8.3 0.8 copy.62.router_src
  9.1 0.7 copy.100
  9.8 1.4 fusion.2
  11.9 1.5 constant_dynamic-slice_fusion
  13.7 1.0 dynamic-slice_bitcast_fusion.up_ref
  14.7 1.9 slice.20
  16.7 2.3 fusion.4.normed_ref
  18.9 0.4 multiply_sine_fusion
  19.6 1.1 copy-done.17
  20.7 0.9 copy-done.19
  21.7 173.6 %opening.1 = (bf16[16,128,576]{2,1,0:T(8,128)(2,1)}, bf16[16,128,3072]{2,1,0:T(8,128)(2,1)}, bf16[16,128,2048]{2,1,0:T(8,128)(2,1)}, bf16[16,128,16]{2,1,0:T(8,1...) custom-call(bf16[128,576]{1,0:T(8,128)(2,1)S(1)} %copy.61.kva_src, ...), custom_call_target="tpu_custom_call" | custom-call | flops 2415919104 | bytes 200000000 | tf_op jit(solution)/shard_map/opening/pallas_call | solution.py:668
  195.3 0.8 copy-done.8
  196.1 0.6 copy-done.12
  196.7 0.7 copy-done.20
  198.8 1.7 copy.65.back_ref
  200.5 2.1 copy-done.23
  202.6 49.0 %attend.1 = (f32[3072,128]{1,0:T(8,128)S(1)}, f32[3072,1]{1,0:T(8,128)S(1)}, bf16[3072,192]{1,0:T(8,128)(2,1)S(1)}, bf16[3072,192]{1,0:T(8,128)(2,1)S(1)}, bf16[...) custom-call(s32[1]{0:T(128)S(6)} %copy.106.prefix_ref, bf16[16,288,128]{2,1,0:T(8,128)(2,1)S(1)} %copy-done.24, ...), custom_call_target="tpu_custom_call" | custom-call | flops 3019898880 | bytes 3072000 | tf_op jit(solution)/shard_map/attend/pallas_call | solution.py:803
  252.1 1.8 fusion.1
  254.1 0.5 copy-done.27
  254.8 1.3 multiply_reduce_fusion.1
  256.2 0.6 multiply_multiply_fusion
  257.0 0.3 fusion.34
  257.5 0.5 copy-done.33
  257.9 0.8 fusion.33
  258.7 0.7 broadcast_in_dim.24.prob_hbm
  259.4 0.7 broadcast_in_dim.26.rank_ref
  260.1 138.6 %experts_forward.1 = (bf16[4,4,192,2048]{3,2,1,0:T(8,128)(2,1)}, bf16[4,384,1408]{2,1,0:T(8,128)(2,1)}, bf16[4,384,1408]{2,1,0:T(8,128)(2,1)}, bf16[4,384,2048]{...) custom-call(bf16[192,2048]{1,0:T(8,128)(2,1)} %copy-done.35, ...), custom_call_target="tpu_custom_call" | custom-call | flops 53150220288 | bytes 60000000 | tf_op jit(solution)/shard_map/experts_forward/pallas_call | solution.py:1187
  398.7 1.0 copy.64
  399.7 0.6 copy-done.3
  400.2 1.1 reduce
  401.3 172.7 %experts_backward.1 = (bf16[192,2048]{1,0:T(8,128)(2,1)}, f32[16,8,192]{2,1,0:T(8,128)}) custom-call(bf16[4,4,192,1024]{3,2,1,0:T(8,128)(2,1)} %bitcast.138, bf16[4,4,192,512]{3,2,1,0:T(8,128)(2,1)} %bitcast.146, bf16[4,4,192,512]{3,2,1,0:T(8,128)(2,1)} %bitcast.147, f32[16,8,192]{2,1,0:T(8,128)} %broadcast_in_dim.26.rank_ref, f32[16,192,1]{2,1,0:T(8,128)} %copy.65.back_ref, ...), custom_call_target="tpu_custom_call" | custom-call | flops 53150220288 | bytes 60000000 | tf_op jit(solution)/shard_map/experts_backward/pallas_call | solution.py:1382
  574.1 0.9 slice.19
  575.0 0.7 fusion.19
  575.8 2.5 multiply_reduce_fusion
  578.4 1.6 fusion.32
  580.2 1.3 convolution_convert_fusion.2.small_ref
  581.9 0.7 pad_maximum_fusion.o_src
  582.5 71.5 %attend_back.1 = (bf16[16,192,576]{2,1,0:T(8,128)(2,1)}, bf16[16,288,128]{2,1,0:T(8,128)(2,1)S(1)}) custom-call(s32[1]{0:T(128)S(6)} %copy.106.prefix_ref, bf16[3072,192]{1,0:T(8,128)(2,1)} %copy-done.26, bf16[3072,192]{1,0:T(8,128)(2,1)} %copy-done.27, bf16[3072,128]{1,0:T(8,128)(2,1)S(1)} %copy-done.29, f32[3072,128]{1,0:T(8,128)} %copy-done.25, ...), custom_call_target="tpu_custom_call" | custom-call | flops 7851737088 | bytes 6144000 | tf_op jit(solution)/shard_map/attend_back/pallas_call | solution.py:952
  654.1 1.0 copy-done.4
  655.1 0.6 broadcast_in_dim.30.name_ref
  655.7 52.4 %finish.1 = (bf16[192,2048]{1,0:T(8,128)(2,1)}, f32[8,16,128]{2,1,0:T(8,128)}, f32[8,16,192]{2,1,0:T(8,128)}, f32[8,16,128]{2,1,0:T(8,128)}, f32[8,16,128]{2,1,0:T(8,128)}) custom-call(bf16[16,192,576]{2,1,0:T(8,128)(2,1)} %get-tuple-element.70.part, bf16[16,16,256]{2,1,0:T(8,128)(2,1)} %pad_maximum_fusion.o_src, bf16[16,288,128]{2,1,0:T(8,128)(2,1)} %copy-done.4, ...), custom_call_target="tpu_custom_call" | custom-call | flops 4831838208 | bytes 40000000 | tf_op jit(solution)/shard_map/finish/pallas_call | solution.py:1582
  708.2 2.3 fusion.7
  710.4 0.9 copy.108
  711.3 0.6 copy.109
  712.0 0.7 copy.110
  712.6 0.6 copy.111
  713.2 0.6 copy.112
  (120 shorter events, 2.6 us)
Async XLA Ops:
  7.2 9.5 %copy-start.43 = (f32[2048]{0:T(1024)S(1)}, f32[2048]{0:T(1024)}, u32[]{:S(2)}) copy-start(f32[2048]{0:T(1024)} %param.28) | copy-start | bytes 24580
  7.2 394.1 %all-gather.2.cloned.1.call-start = ((), (), s32[]{:S(2)}) async-start(), calls=%async_computation.2 | async-start | bytes 6684672 | tf_op jit(solution)/shard_map/all_gather | solution.py:461
  13.7 5.9 copy-start
  14.7 4.9 copy-start.9
  14.7 4.9 copy-start.14
  14.7 4.9 copy-start.15
  14.7 4.9 copy-start.16
  14.7 4.9 copy-start.18
  19.5 175.8 %copy-start.10 = (f32[192,64]{1,0:T(8,128)}, f32[192,64]{1,0:T(8,128)S(1)}, u32[]{:S(2)}) copy-start(f32[192,64]{1,0:T(8,128)S(1)} %get-tuple-element.97.cos_ref) | copy-start | bytes 147460
  19.5 175.8 %copy-start.11 = (f32[192,64]{1,0:T(8,128)}, f32[192,64]{1,0:T(8,128)S(1)}, u32[]{:S(2)}) copy-start(f32[192,64]{1,0:T(8,128)S(1)} %get-tuple-element.98.sin_ref) | copy-start | bytes 147460
  197.4 59.6 %copy-start.1 = (bf16[16,128,16]{2,1,0:T(8,128)(2,1)}, bf16[16,128,16]{2,1,0:T(8,128)(2,1)S(1)}, u32[]{:S(2)}) copy-start(bf16[16,128,16]{2,1,0:T(8,128)(2,1)S(1)} %get-tuple-element.49) | copy-start | bytes 196612
  197.4 3.1 copy-start.24
  197.4 3.1 copy-start.21
  197.4 510.7 %reduce-scatter.2.cloned.1.call-start = ((), (), s32[]{:S(2)}) async-start(), calls=%async_computation.1 | async-start | bytes 13369344 | tf_op jit(solution)/shard_map/reduce_scatter | solution.py:465
  200.5 2.1 copy-start.23
  202.6 49.1 %copy-start.38 = (bf16[1,2048,16]{1,2,0:T(8,128)(2,1)S(1)}, bf16[1,2048,16]{1,2,0:T(8,128)(2,1)}, u32[]{:S(2)}) copy-start(bf16[1,2048,16]{1,2,0:T(8,128)(2,1)} %get-tuple-element.95) | copy-start | bytes 196612
  202.6 49.4 %copy-start.32 = (bf16[1,192,2048]{2,1,0:T(8,128)(2,1)S(1)}, bf16[1,192,2048]{2,1,0:T(8,128)(2,1)}, u32[]{:S(2)}) copy-start(bf16[1,192,2048]{2,1,0:T(8,128)(2,1)} %param.23) | copy-start | bytes 2359300
  202.6 49.4 %copy-start.52 = (bf16[16,128,2048]{2,1,0:T(8,128)(2,1)S(1)}, bf16[16,128,2048]{2,1,0:T(8,128)(2,1)}, u32[]{:S(2)}) copy-start(bf16[16,128,2048]{2,1,0:T(8,128)(2,1)} %get-tuple-element.48) | copy-start | bytes 25165828
  251.7 2.2 copy-start.2
  251.7 2.2 copy-start.5
  251.7 2.2 copy-start.25
  251.7 2.4 copy-start.26
  251.7 2.8 copy-start.27
  251.7 3.1 copy-start.28
  252.0 2.8 copy-start.45
  254.8 2.0 copy-start.44
  256.1 1.2 copy-start.30
  256.8 1.2 copy-start.33
  257.0 3.1 copy-start.35
  257.4 1.3 copy-start.37
  257.4 2.7 copy-start.47
  257.4 2.6 copy-start.48
  398.6 1.6 copy-start.3
  575.7 2.6 copy-start.31
  575.7 2.6 copy-start.34
  575.8 2.6 copy-start.50
  575.8 2.6 copy-start.51
  578.3 1.6 copy-start.46
  580.0 1.6 copy-start.6
  580.0 2.6 copy-start.7
  580.0 2.6 copy-start.13
  580.0 2.6 copy-start.22
  580.0 2.5 copy-start.29
  708.1 2.3 copy-start.36
  708.1 3.2 copy-start.42
  710.4 1.5 copy-start.39
  710.4 2.2 copy-start.41
  710.4 2.8 copy-start.40
  (7 other events, 5.8 us)
Sparse Core Ops, SparseCore 0:
  197.5 90.1 all-gather.1
  398.8 174.7 reduce-scatter.1
